TPU v7x, 32 devices: a whole 2x2x4 slice. The times are simulated.
32 devices in a mesh: dev: 32 (over z, y, x, core).
Axes of the slice: x: 2, y: 2, z: 4, core: 2. Of those that a mesh axis runs over, the one named last changes fastest.
Arguments:
- tokens: bfloat16 [4608, 1536], P('dev'), may hold values from -6 to 6
- conditioning: bfloat16 [4, 1536], replicated, may hold values from -5 to 5
- text_lengths: int32 [4], replicated, may hold values from 86 to 154, as said below
- modulation_weight: bfloat16 [3072, 9216], P('dev'), may hold values from -0.15625 to 0.15625
- project_weight: bfloat16 [3072, 4608], P('dev'), may hold values from -1 to 1
- merge_weight: bfloat16 [3072, 1536], P('dev'), may hold values from -1.25 to 1.25
- up_weight: bfloat16 [3072, 6144], P('dev'), may hold values from -0.15625 to 0.15625
- down_weight: bfloat16 [12288, 1536], P('dev'), may hold values from -0.078125 to 0.078125
- cotangent: bfloat16 [4608, 1536], P('dev'), may hold values from -6 to 6
Outputs:
- layer_out: bfloat16 [4608, 1536], P('dev')
- tokens_grad: float32 [4608, 1536], P('dev')
- conditioning_grad: float32 [4, 1536], replicated
- modulation_grad: float32 [3072, 9216], P('dev')
- project_grad: float32 [3072, 4608], P('dev')
- merge_grad: float32 [3072, 1536], P('dev')
- up_grad: float32 [3072, 6144], P('dev')
- down_grad: float32 [12288, 1536], P('dev')
Inputs may be any that keep to these rules, and one draw needn't show every extreme that they name: `text_lengths`: the text tokens of all sequences sum to 512, so that the sequences fill the packed rows exactly; one sequence has exactly 154 text tokens.
All inputs are finite; a program needn't handle non-finite values.
Results may differ from a plain program's by a relative error of at most 0.025.
The roundings to bfloat16 on the way count: a program that leaves them out, or rounds other values in their place, can miss the bound.
Values may be sent and summed in bfloat16 or wider, within the bound.
A program may use at most 576 MiB of HBM per device.

v0:
```python
import jax
import jax.numpy as jnp
from jax import lax
from jax.sharding import PartitionSpec as P

HEADS = 24
HDIM = 64
IMG = 1024
REACH = 9
TXT_CAP = 144


HIGHEST_PRECISION = lax.Precision.HIGHEST
EPSILON = 1e-06
CONTRACT_LAST = (((1,), (1,)), ((), ()))
CONTRACT_FIRST = (((0,), (0,)), ((), ()))


def passed_along(x, axis, by):
    length = lax.axis_size(axis)
    pairs = [(i, i + by) for i in range(length) if 0 <= i + by < length]
    return lax.ppermute(x, axis, pairs)


def layer_norm(values):
    mean = jnp.mean(values, axis=-1, keepdims=True)
    centred = values - mean
    variance = jnp.mean(centred * centred, axis=-1, keepdims=True)
    inv_std = lax.rsqrt(variance + EPSILON)
    return (centred * inv_std, inv_std)


def norm_back(grad_normed, normed, inv_std):
    mean_grad = jnp.mean(grad_normed, axis=-1, keepdims=True)
    mean_cross = jnp.mean(grad_normed * normed, axis=-1, keepdims=True)
    return inv_std * (grad_normed - mean_grad - normed * mean_cross)


def sequence_index(positions, starts):
    return jnp.sum((starts[None, :] <= positions[:, None]).astype(jnp.int32), axis=1) - 1


def stream_dot(rows, stacked, layout):
    text_rows, text_valid, slot_of_row, is_text = layout
    half = stacked.shape[0] // 2
    image_part = jnp.dot(rows, stacked[:half], preferred_element_type=jnp.float32)
    text_part = jnp.dot(rows[text_rows], stacked[half:], preferred_element_type=jnp.float32)
    return jnp.where(is_text[:, None], text_part[slot_of_row], image_part)


def stream_rows_back(stacked, grad_low, layout):
    text_rows, text_valid, slot_of_row, is_text = layout
    half = stacked.shape[0] // 2
    image_grad = jnp.where(is_text[:, None], jnp.zeros_like(grad_low), grad_low)
    picked = grad_low[text_rows]
    text_grad = jnp.where(text_valid[:, None], picked, jnp.zeros_like(picked))
    image_back = lax.dot_general(
        image_grad, stacked[:half], CONTRACT_LAST, preferred_element_type=jnp.float32
    )
    text_back = lax.dot_general(
        text_grad, stacked[half:], CONTRACT_LAST, preferred_element_type=jnp.float32
    )
    return jnp.where(is_text[:, None], text_back[slot_of_row], image_back)


def split_streams(rows, is_text):
    zeros = jnp.zeros_like(rows)
    return jnp.concatenate(
        [jnp.where(is_text[:, None], zeros, rows), jnp.where(is_text[:, None], rows, zeros)], axis=1
    )


def term_rows(stacked_rows, grad_low):
    return lax.dot_general(
        stacked_rows, grad_low, CONTRACT_FIRST, preferred_element_type=jnp.float32
    )


def gather_tail(merge_weight, up_weight, down_weight):
    return (
        lax.all_gather(merge_weight, "dev", axis=0, tiled=True),
        lax.all_gather(up_weight, "dev", axis=0, tiled=True),
        lax.all_gather(down_weight, "dev", axis=0, tiled=True),
    )


def heads_last(stacked, count):
    return jnp.transpose(stacked, (1, 0, 2)).reshape(count, HEADS * HDIM)


def on_device(
    tokens,
    conditioning,
    text_lengths,
    modulation_weight,
    project_weight,
    merge_weight,
    up_weight,
    down_weight,
    cotangent,
):
    rows_dev = tokens.shape[0]
    width = tokens.shape[1]
    shard_rows = modulation_weight.shape[0]
    seq_count = conditioning.shape[0]
    devices = lax.axis_size("dev")
    device = lax.axis_index("dev")
    window = (2 * REACH + 1) * rows_dev
    scale = HDIM ** (-0.5)
    own_stream = device * shard_rows // width
    feature_start = device * shard_rows % width
    lengths = IMG + text_lengths
    ends = jnp.cumsum(lengths)
    starts = jnp.concatenate([jnp.zeros((1,), jnp.int32), ends[:-1]])
    positions = device * rows_dev + jnp.arange(rows_dev, dtype=jnp.int32)
    row_seq = sequence_index(positions, starts)
    row_start = jnp.max(
        jnp.where(starts[None, :] <= positions[:, None], starts[None, :], 0), axis=1
    )
    is_text = positions - row_start >= IMG
    text_count = jnp.cumsum(is_text.astype(jnp.int32))
    slot_of_row = jnp.clip(text_count - 1, 0, TXT_CAP - 1)
    slot_range = jnp.arange(TXT_CAP, dtype=jnp.int32)
    text_rows = jnp.clip(
        jnp.sum((text_count[None, :] <= slot_range[:, None]).astype(jnp.int32), axis=1),
        0,
        rows_dev - 1,
    )
    text_valid = slot_range < text_count[-1]
    layout = (text_rows, text_valid, slot_of_row, is_text)
    codes = row_seq * 2 + is_text.astype(jnp.int32)
    one_hot = (codes[:, None] == jnp.arange(2 * seq_count, dtype=jnp.int32)[None, :]).astype(
        jnp.float32
    )
    key_positions = device * rows_dev - REACH * rows_dev + jnp.arange(window, dtype=jnp.int32)
    key_valid = (key_positions >= 0) & (key_positions < devices * rows_dev)
    key_seq = sequence_index(key_positions, starts)
    mask = (row_seq[:, None] == key_seq[None, :]) & key_valid[None, :]
    cond_float = conditioning.astype(jnp.float32)
    silu_low = jax.nn.silu(cond_float).astype(jnp.bfloat16)
    silu_part = lax.dynamic_slice_in_dim(silu_low, feature_start, shard_rows, 1)
    mod_full, project_full = (
        lax.all_gather(modulation_weight, "dev", axis=0, tiled=True),
        lax.all_gather(project_weight, "dev", axis=0, tiled=True),
    )
    mod_table = jnp.einsum(
        "sd,jdc->sjc",
        silu_low,
        mod_full.reshape(2, width, 6 * width),
        preferred_element_type=jnp.float32,
    )
    mod_rows = jnp.dot(
        one_hot,
        mod_table.reshape(2 * seq_count, 6 * width),
        precision=HIGHEST_PRECISION,
        preferred_element_type=jnp.float32,
    )
    shift_a, scale_a, gate_a, shift_b, scale_b, gate_b = jnp.split(mod_rows, 6, axis=1)
    inputs = tokens.astype(jnp.float32)
    normed_a, inv_a = layer_norm(inputs)
    hidden_a = (normed_a * (1.0 + scale_a) + shift_a).astype(jnp.bfloat16)
    projected = stream_dot(hidden_a, project_full, layout).astype(jnp.bfloat16)
    queries, keys, values = jnp.split(projected, 3, axis=1)
    key_pieces = []
    value_pieces = []
    for offset in range(-REACH, REACH + 1):
        if offset == 0:
            key_pieces.append(keys)
            value_pieces.append(values)
        else:
            got_keys, got_values = passed_along((keys, values), "dev", -offset)
            key_pieces.append(got_keys)
            value_pieces.append(got_values)
    window_keys = jnp.concatenate(key_pieces, axis=0)
    window_values = jnp.concatenate(value_pieces, axis=0)

    def head_forward(head):
        query = lax.dynamic_slice_in_dim(queries, head * HDIM, HDIM, 1)
        key_cols = lax.dynamic_slice_in_dim(window_keys, head * HDIM, HDIM, 1)
        value_cols = lax.dynamic_slice_in_dim(window_values, head * HDIM, HDIM, 1)
        scores = (
            lax.dot_general(query, key_cols, CONTRACT_LAST, preferred_element_type=jnp.float32)
            * scale
        )
        masked = jnp.where(mask, scores, -jnp.inf)
        top = jnp.max(masked, axis=1, keepdims=True)
        exponent = jnp.exp(masked - top)
        total = jnp.sum(exponent, axis=1, keepdims=True)
        probs = (exponent / total).astype(jnp.bfloat16)
        attended_head = jnp.dot(probs, value_cols, preferred_element_type=jnp.float32)
        return (attended_head, (top + jnp.log(total))[:, 0])

    head_out, log_totals = lax.map(head_forward, jnp.arange(HEADS, dtype=jnp.int32))
    attended = heads_last(head_out, rows_dev).astype(jnp.bfloat16)
    merge_full, up_full, down_full = gather_tail(merge_weight, up_weight, down_weight)
    merged = stream_dot(attended, merge_full, layout)
    middle = inputs + gate_a * merged
    normed_b, inv_b = layer_norm(middle)
    hidden_b = (normed_b * (1.0 + scale_b) + shift_b).astype(jnp.bfloat16)
    upper = stream_dot(hidden_b, up_full, layout)
    activated = jax.nn.gelu(upper, approximate=True).astype(jnp.bfloat16)
    lowered = stream_dot(activated, down_full, layout)
    layer_out = (middle + gate_b * lowered).astype(jnp.bfloat16)
    grad_out = cotangent.astype(jnp.float32)
    grad_gate_b = grad_out * lowered
    grad_lowered = (gate_b * grad_out).astype(jnp.bfloat16)
    merge_again, up_again, down_again = gather_tail(merge_weight, up_weight, down_weight)
    grad_activated = stream_rows_back(down_again, grad_lowered, layout)
    activated_split = split_streams(activated, is_text)
    down_grad = lax.psum_scatter(
        term_rows(activated_split, grad_lowered), "dev", scatter_dimension=0, tiled=True
    )
    gelu_pull = jax.vjp(lambda value_in: jax.nn.gelu(value_in, approximate=True), upper)[1]
    grad_upper = gelu_pull(grad_activated)[0].astype(jnp.bfloat16)
    grad_hidden_b = stream_rows_back(up_again, grad_upper, layout)
    grad_scale_b = grad_hidden_b * normed_b
    grad_middle = grad_out + norm_back(grad_hidden_b * (1.0 + scale_b), normed_b, inv_b)
    grad_gate_a = grad_middle * merged
    grad_merged = (gate_a * grad_middle).astype(jnp.bfloat16)
    grad_attended = stream_rows_back(merge_again, grad_merged, layout).astype(jnp.bfloat16)
    attended_split = split_streams(attended, is_text)
    hidden_b_split = split_streams(hidden_b, is_text)

    def head_backward(head):
        query = lax.dynamic_slice_in_dim(queries, head * HDIM, HDIM, 1)
        key_cols = lax.dynamic_slice_in_dim(window_keys, head * HDIM, HDIM, 1)
        value_cols = lax.dynamic_slice_in_dim(window_values, head * HDIM, HDIM, 1)
        grad_head = lax.dynamic_slice_in_dim(grad_attended, head * HDIM, HDIM, 1)
        log_total = log_totals[head]
        scores = (
            lax.dot_general(query, key_cols, CONTRACT_LAST, preferred_element_type=jnp.float32)
            * scale
        )
        probs = jnp.where(mask, jnp.exp(scores - log_total[:, None]), 0.0)
        grad_probs = lax.dot_general(
            grad_head, value_cols, CONTRACT_LAST, preferred_element_type=jnp.float32
        )
        inner = jnp.sum(probs * grad_probs, axis=1, keepdims=True)
        grad_scores = (probs * (grad_probs - inner)).astype(jnp.bfloat16)
        grad_query = jnp.dot(grad_scores, key_cols, preferred_element_type=jnp.float32) * scale
        grad_key = (
            lax.dot_general(grad_scores, query, CONTRACT_FIRST, preferred_element_type=jnp.float32)
            * scale
        )
        grad_value = lax.dot_general(
            probs.astype(jnp.bfloat16),
            grad_head,
            CONTRACT_FIRST,
            preferred_element_type=jnp.float32,
        )
        return (grad_query, grad_key, grad_value)

    head_queries, head_keys, head_values = lax.map(
        head_backward, jnp.arange(HEADS, dtype=jnp.int32)
    )
    grad_queries = heads_last(head_queries, rows_dev)
    grad_keys = heads_last(head_keys, window)
    grad_values = heads_last(head_values, window)
    centre = REACH * rows_dev
    key_total = grad_keys[centre : centre + rows_dev]
    value_total = grad_values[centre : centre + rows_dev]
    for offset in range(-REACH, REACH + 1):
        if offset != 0:
            block = (offset + REACH) * rows_dev
            got_key, got_value = (
                passed_along(
                    grad_keys[block : block + rows_dev].astype(jnp.bfloat16), "dev", offset
                ).astype(jnp.float32),
                passed_along(
                    grad_values[block : block + rows_dev].astype(jnp.bfloat16), "dev", offset
                ).astype(jnp.float32),
            )
            key_total = key_total + got_key
            value_total = value_total + got_value
    grad_projected = jnp.concatenate([grad_queries, key_total, value_total], axis=1).astype(
        jnp.bfloat16
    )
    project_again = lax.all_gather(project_weight, "dev", axis=0, tiled=True)
    grad_hidden_a = stream_rows_back(project_again, grad_projected, layout)
    hidden_a_split = split_streams(hidden_a, is_text)
    summed = lax.psum_scatter(
        jnp.concatenate(
            [
                term_rows(attended_split, grad_merged),
                term_rows(hidden_b_split, grad_upper),
                term_rows(hidden_a_split, grad_projected),
            ],
            axis=1,
        ),
        "dev",
        scatter_dimension=0,
        tiled=True,
    )
    merge_grad = summed[:, :width]
    up_grad = summed[:, width : width + up_weight.shape[1]]
    project_grad = summed[:, width + up_weight.shape[1] :]
    grad_scale_a = grad_hidden_a * normed_a
    tokens_grad = grad_middle + norm_back(grad_hidden_a * (1.0 + scale_a), normed_a, inv_a)
    grad_mod_rows = jnp.concatenate(
        [grad_hidden_a, grad_scale_a, grad_gate_a, grad_hidden_b, grad_scale_b, grad_gate_b], axis=1
    )
    local_table = lax.dot_general(
        one_hot,
        grad_mod_rows,
        CONTRACT_FIRST,
        precision=HIGHEST_PRECISION,
        preferred_element_type=jnp.float32,
    )
    grad_table = lax.psum(local_table.reshape(seq_count, 2, 6 * width), "dev").astype(jnp.bfloat16)
    own_grads = lax.dynamic_index_in_dim(grad_table, own_stream, 1, keepdims=False)
    modulation_grad = lax.dot_general(
        silu_part, own_grads, CONTRACT_FIRST, preferred_element_type=jnp.float32
    )
    grad_piece = lax.dot_general(
        own_grads, modulation_weight, CONTRACT_LAST, preferred_element_type=jnp.float32
    )
    gathered = lax.all_gather(grad_piece, "dev", axis=1, tiled=True)
    grad_silu = gathered[:, :width] + gathered[:, width:]
    silu_pull = jax.vjp(jax.nn.silu, cond_float)[1]
    conditioning_grad = silu_pull(grad_silu)[0]
    return (
        layer_out,
        tokens_grad,
        conditioning_grad,
        modulation_grad,
        project_grad,
        merge_grad,
        up_grad,
        down_grad,
    )


def solution(mesh):
    return jax.shard_map(
        on_device,
        mesh=mesh,
        in_specs=(
            P("dev", None),
            P(),
            P(),
            P("dev", None),
            P("dev", None),
            P("dev", None),
            P("dev", None),
            P("dev", None),
            P("dev", None),
        ),
        out_specs=(
            P("dev", None),
            P("dev", None),
            P(),
            P("dev", None),
            P("dev", None),
            P("dev", None),
            P("dev", None),
            P("dev", None),
        ),
        check_vma=False,
    )
```

profile of v0, /device:TPU:0, one launch (start us, length us, event | category | flops | bytes accessed | tf_op | source)
XLA Modules:
  0.0 4166.6 jit_solution(7847232623532628059)
XLA Ops:
  13.0 306.8 %all-gather.7.cloned.1.call-done = bf16[3072,9216]{1,0:T(8,128)(2,1)} async-done(((bf16[96,9216]{1,0:T(8,128)(2,1)}), bf16[3072,9216]{1,0:T(8,128)(2,1)}) %all-gather.7.cloned.1.call-update) | async-done | bytes 56623120 | tf_op jit(solution)/shard_map/all_gather | solution.py:143
  319.7 20.9 fusion.179
  347.9 142.7 %all-gather.9.cloned.1.call-done = bf16[3072,4608]{1,0:T(8,128)(2,1)} async-done(((bf16[96,4608]{1,0:T(8,128)(2,1)}), bf16[3072,4608]{1,0:T(8,128)(2,1)}) %all-gather.9.cloned.1.call-update) | async-done | bytes 28311568 | tf_op jit(solution)/shard_map/all_gather | solution.py:144
  624.0 25.8 collective-permute-start.19
  649.8 26.3 collective-permute-start.20
  676.2 20.1 collective-permute-start.21
  715.7 21.0 collective-permute-start.23
  781.5 66.0 %collective-permute-done.29 = bf16[144,1536]{1,0:T(8,128)(2,1)S(1)} collective-permute-done((bf16[144,1536]{1,0:T(8,128)(2,1)S(1)}, bf16[144,1536]{1,0:T(8,128)(2,1)S(1)}, u32[]{:S(2)}, u32[]{:S(2)}) %collective-permute-start.29) | collective-permute-done | bytes 442400 | tf_op jit(solution)/shard_map/ppermute | solution.py:22
  859.3 27.8 collective-permute-done.31
  906.2 65.5 %collective-permute-done.10 = bf16[144,1536]{1,0:T(8,128)(2,1)S(1)} collective-permute-done((bf16[144,1536]{1,0:T(8,128)(2,1)S(1)}, bf16[144,1536]{1,0:T(8,128)(2,1)S(1)}, u32[]{:S(2)}, u32[]{:S(2)}) %collective-permute-start.10) | collective-permute-done | bytes 442400 | tf_op jit(solution)/shard_map/ppermute | solution.py:22
  983.1 58.3 %collective-permute-done.13 = bf16[144,1536]{1,0:T(8,128)(2,1)S(1)} collective-permute-done((bf16[144,1536]{1,0:T(8,128)(2,1)S(1)}, bf16[144,1536]{1,0:T(8,128)(2,1)S(1)}, u32[]{:S(2)}, u32[]{:S(2)}) %collective-permute-start.13) | collective-permute-done | bytes 442400 | tf_op jit(solution)/shard_map/ppermute | solution.py:22
  1041.5 19.4 collective-permute-done.14
  1064.3 164.3 %while.28 = (s32[]{:T(128)}, bf16[24,144,64]{1,2,0:T(8,128)(2,1)S(1)}, f32[24,144]{1,0:T(8,128)}, s32[24]{0:T(128)S(1)}, bf16[144,1536]{1,0:T(8,128)(2,1)S(1)}, ...) while((s32[]{:T(128)}, ...), condition=%wide.region_12.13_spmd.clone, body=%wide.region_9.12_spmd.clone.sunk | while | flops 104799600 | bytes 6301395 | solution.py:193
  1371.9 332.8 %while.29 = (s32[]{:T(128)}, bf16[24,144,64]{1,2,0:T(8,128)(2,1)S(1)}, f32[24,2736,64]{1,2,0:T(8,128)}, f32[24,2736,64]{1,2,0:T(8,128)}, s32[24]{0:T(128)S(1)}, ...) while((s32[]{:T(128)}, ...), condition=%wide.region_19.20_spmd.clone, body=%wide.region_17.19_spmd.clone.sunk | while | flops 256667760 | bytes 15618069 | solution.py:253
  1798.8 20.4 collective-permute-start.65
  1929.6 28.2 fusion.139
  1994.7 18.1 collective-permute-start.46
  2068.0 20.6 fusion.143
  2088.6 97.4 %pad_maximum_fusion = f32[3072,12288]{1,0:T(8,128)} fusion(f32[3072,4608]{1,0:T(8,128)} %fusion.143, f32[3072,6144]{1,0:T(8,128)} %fusion.139, f32[3072,1536]{1,0:T(8,128)} %fusion.135), kind=kLoop, calls=%fused_computation.61 | loop fusion | flops 75497472 | bytes 301989888 | tf_op jit(solution)/shard_map/concatenate | solution.py:282
  2188.9 29.0 fusion.86
  2254.3 105.1 %all-reduce.2 = bf16[4,2,9216]{2,0,1:T(4,128)(2,1)S(1)} all-reduce(f32[4,2,9216]{2,0,1:T(4,128)S(1)} %copy.187), channel_id=1, replica_groups=mesh['dev'=32] {'dev'}, use_global_device_ids=true, to_apply=%region_22.23 | all-reduce | flops 73728 | bytes 442368 | tf_op jit(solution)/shard_map/psum | solution.py:309
  2360.0 39.6 all-gather
  2402.8 1093.1 %reduce-scatter.3.cloned.1.call-done = f32[96,12288]{1,0:T(8,128)} async-done(((f32[3072,12288]{1,0:T(8,128)}), f32[96,12288]{1,0:T(8,128)}) %reduce-scatter.3.cloned.1.call-update) | async-done | bytes 4718608 | tf_op jit(solution)/shard_map/reduce_scatter | solution.py:281
  3503.9 655.5 %reduce-scatter.5.cloned.1.call-done = f32[384,1536]{1,0:T(8,128)} async-done(((f32[12288,1536]{1,0:T(8,128)}), f32[384,1536]{1,0:T(8,128)}) %reduce-scatter.5.cloned.1.call-update) | async-done | bytes 2359312 | tf_op jit(solution)/shard_map/reduce_scatter | solution.py:210
  (824 shorter events, 1164.4 us)
Async XLA Ops:
  7.2 312.5 %all-gather.7.cloned.1.call-start = ((), (), s32[]{:S(2)}) async-start(), calls=%async_computation.2 | async-start | bytes 58392576 | tf_op jit(solution)/shard_map/all_gather | solution.py:143
  7.9 482.6 %all-gather.9.cloned.1.call-start = ((), (), s32[]{:S(2)}) async-start(), calls=%async_computation.3 | async-start | bytes 29196288 | tf_op jit(solution)/shard_map/all_gather | solution.py:144
  8.7 1222.0 %all-gather.11.cloned.1.call-start = ((), (), s32[]{:S(2)}) async-start(), calls=%async_computation.4 | async-start | bytes 9732096 | tf_op jit(solution)/shard_map/all_gather | solution.py:81
  9.4 1238.3 %all-gather.13.cloned.1.call-start = ((), (), s32[]{:S(2)}) async-start(), calls=%async_computation.5 | async-start | bytes 38928384 | tf_op jit(solution)/shard_map/all_gather | solution.py:82
  10.0 1249.3 %all-gather.15.cloned.1.call-start = ((), (), s32[]{:S(2)}) async-start(), calls=%async_computation.6 | async-start | bytes 38928384 | tf_op jit(solution)/shard_map/all_gather | solution.py:83
  10.6 3485.4 %reduce-scatter.3.cloned.1.call-start = ((), (), s32[]{:S(2)}) async-start(), calls=%async_computation.7 | async-start | bytes 155713536 | tf_op jit(solution)/shard_map/reduce_scatter | solution.py:281
  516.3 386.2 %collective-permute-start.35 = (bf16[144,1536]{1,0:T(8,128)(2,1)S(1)}, bf16[144,1536]{1,0:T(8,128)(2,1)S(1)}, u32[]{:S(2)}, u32[]{:S(2)}) collective-permute-start(bf16[144,1536]{1,0:T(8,128)(2,1)S(1)} %get-tuple-element.282), channel_id=1, source_target_pairs={{9,0},{10,1},{11,2},{12,3},{13,4},{14,5},{15,6},{16,7},{17,8},{18,... | collective-permute-start | bytes 1327112 | tf_op jit(solution)/shard_map/ppermute | solution.py:22
  517.6 383.5 %collective-permute-start.34 = (bf16[144,1536]{1,0:T(8,128)(2,1)S(1)}, bf16[144,1536]{1,0:T(8,128)(2,1)S(1)}, u32[]{:S(2)}, u32[]{:S(2)}) collective-permute-start(bf16[144,1536]{1,0:T(8,128)(2,1)S(1)} %get-tuple-element.282), channel_id=1, source_target_pairs={{8,0},{9,1},{10,2},{11,3},{12,4},{13,5},{14,6},{15,7},{16,8},{17,9... | collective-permute-start | bytes 1327112 | tf_op jit(solution)/shard_map/ppermute | solution.py:22
  518.9 380.9 %collective-permute-start.33 = (bf16[144,1536]{1,0:T(8,128)(2,1)S(1)}, bf16[144,1536]{1,0:T(8,128)(2,1)S(1)}, u32[]{:S(2)}, u32[]{:S(2)}) collective-permute-start(bf16[144,1536]{1,0:T(8,128)(2,1)S(1)} %get-tuple-element.282), channel_id=1, source_target_pairs={{7,0},{8,1},{9,2},{10,3},{11,4},{12,5},{13,6},{14,7},{15,8},{16,9}... | collective-permute-start | bytes 1327112 | tf_op jit(solution)/shard_map/ppermute | solution.py:22
  773.8 73.6 %collective-permute-start.29 = (bf16[144,1536]{1,0:T(8,128)(2,1)S(1)}, bf16[144,1536]{1,0:T(8,128)(2,1)S(1)}, u32[]{:S(2)}, u32[]{:S(2)}) collective-permute-start(bf16[144,1536]{1,0:T(8,128)(2,1)S(1)} %get-tuple-element.282), channel_id=1, source_target_pairs={{3,0},{4,1},{5,2},{6,3},{7,4},{8,5},{9,6},{10,7},{11,8},{12,9},{13... | collective-permute-start | bytes 1327112 | tf_op jit(solution)/shard_map/ppermute | solution.py:22
  780.1 77.8 %collective-permute-start.30 = (bf16[144,1536]{1,0:T(8,128)(2,1)S(1)}, bf16[144,1536]{1,0:T(8,128)(2,1)S(1)}, u32[]{:S(2)}, u32[]{:S(2)}) collective-permute-start(bf16[144,1536]{1,0:T(8,128)(2,1)S(1)} %get-tuple-element.282), channel_id=1, source_target_pairs={{4,0},{5,1},{6,2},{7,3},{8,4},{9,5},{10,6},{11,7},{12,8},{13,9},{1... | collective-permute-start | bytes 1327112 | tf_op jit(solution)/shard_map/ppermute | solution.py:22
  887.1 173.9 %collective-permute-start.17 = (bf16[144,1536]{1,0:T(8,128)(2,1)S(1)}, bf16[144,1536]{1,0:T(8,128)(2,1)S(1)}, u32[]{:S(2)}, u32[]{:S(2)}) collective-permute-start(bf16[144,1536]{1,0:T(8,128)(2,1)S(1)} %get-tuple-element.283), channel_id=1, source_target_pairs={{9,0},{10,1},{11,2},{12,3},{13,4},{14,5},{15,6},{16,7},{17,8},{18,... | collective-permute-start | bytes 1327112 | tf_op jit(solution)/shard_map/ppermute | solution.py:22
  898.5 162.5 %collective-permute-start.16 = (bf16[144,1536]{1,0:T(8,128)(2,1)S(1)}, bf16[144,1536]{1,0:T(8,128)(2,1)S(1)}, u32[]{:S(2)}, u32[]{:S(2)}) collective-permute-start(bf16[144,1536]{1,0:T(8,128)(2,1)S(1)} %get-tuple-element.283), channel_id=1, source_target_pairs={{8,0},{9,1},{10,2},{11,3},{12,4},{13,5},{14,6},{15,7},{16,8},{17,9... | collective-permute-start | bytes 1327112 | tf_op jit(solution)/shard_map/ppermute | solution.py:22
  899.8 161.1 %collective-permute-start.15 = (bf16[144,1536]{1,0:T(8,128)(2,1)S(1)}, bf16[144,1536]{1,0:T(8,128)(2,1)S(1)}, u32[]{:S(2)}, u32[]{:S(2)}) collective-permute-start(bf16[144,1536]{1,0:T(8,128)(2,1)S(1)} %get-tuple-element.283), channel_id=1, source_target_pairs={{7,0},{8,1},{9,2},{10,3},{11,4},{12,5},{13,6},{14,7},{15,8},{16,9}... | collective-permute-start | bytes 1327112 | tf_op jit(solution)/shard_map/ppermute | solution.py:22
  904.8 70.3 %collective-permute-start.11 = (bf16[144,1536]{1,0:T(8,128)(2,1)S(1)}, bf16[144,1536]{1,0:T(8,128)(2,1)S(1)}, u32[]{:S(2)}, u32[]{:S(2)}) collective-permute-start(bf16[144,1536]{1,0:T(8,128)(2,1)S(1)} %get-tuple-element.283), channel_id=1, source_target_pairs={{3,0},{4,1},{5,2},{6,3},{7,4},{8,5},{9,6},{10,7},{11,8},{12,9},{13... | collective-permute-start | bytes 1327112 | tf_op jit(solution)/shard_map/ppermute | solution.py:22
  981.8 79.1 %collective-permute-start.14 = (bf16[144,1536]{1,0:T(8,128)(2,1)S(1)}, bf16[144,1536]{1,0:T(8,128)(2,1)S(1)}, u32[]{:S(2)}, u32[]{:S(2)}) collective-permute-start(bf16[144,1536]{1,0:T(8,128)(2,1)S(1)} %get-tuple-element.283), channel_id=1, source_target_pairs={{6,0},{7,1},{8,2},{9,3},{10,4},{11,5},{12,6},{13,7},{14,8},{15,9},... | collective-permute-start | bytes 1327112 | tf_op jit(solution)/shard_map/ppermute | solution.py:22
  1767.3 74.9 %collective-permute-start.61 = (bf16[144,1536]{1,0:T(8,128)(2,1)}, bf16[144,1536]{1,0:T(8,128)(2,1)}, u32[]{:S(2)}, u32[]{:S(2)}) collective-permute-start(bf16[144,1536]{1,0:T(8,128)(2,1)} %copy.220), channel_id=1, source_target_pairs={{2,0},{3,1},{4,2},{5,3},{6,4},{7,5},{8,6},{9,7},{10,8},{11,9},{12,... | collective-permute-start | bytes 1327112 | tf_op jit(solution)/shard_map/ppermute | solution.py:22
  1791.5 78.3 %collective-permute-start.64 = (bf16[144,1536]{1,0:T(8,128)(2,1)}, bf16[144,1536]{1,0:T(8,128)(2,1)}, u32[]{:S(2)}, u32[]{:S(2)}) collective-permute-start(bf16[144,1536]{1,0:T(8,128)(2,1)} %copy.223), channel_id=1, source_target_pairs={{0,2},{1,3},{2,4},{3,5},{4,6},{5,7},{6,8},{7,9},{8,10},{9,11},{10,... | collective-permute-start | bytes 1327112 | tf_op jit(solution)/shard_map/ppermute | solution.py:22
  1798.8 73.0 %collective-permute-start.65 = (bf16[144,1536]{1,0:T(8,128)(2,1)S(1)}, bf16[144,1536]{1,0:T(8,128)(2,1)}, u32[]{:S(2)}, u32[]{:S(2)}) collective-permute-start(bf16[144,1536]{1,0:T(8,128)(2,1)S(1)} %copy.224), channel_id=1, source_target_pairs={{0,3},{1,4},{2,5},{3,6},{4,7},{5,8},{6,9},{7,10},{8,11},{9,12},{10... | collective-permute-start | bytes 1327112 | tf_op jit(solution)/shard_map/ppermute | solution.py:22
  1922.3 72.3 %collective-permute-start.41 = (bf16[144,1536]{1,0:T(8,128)(2,1)}, bf16[144,1536]{1,0:T(8,128)(2,1)}, u32[]{:S(2)}, u32[]{:S(2)}) collective-permute-start(bf16[144,1536]{1,0:T(8,128)(2,1)} %copy.199), channel_id=1, source_target_pairs={{4,0},{5,1},{6,2},{7,3},{8,4},{9,5},{10,6},{11,7},{12,8},{13,9},{1... | collective-permute-start | bytes 1327112 | tf_op jit(solution)/shard_map/ppermute | solution.py:22
  1925.6 87.1 %collective-permute-start.42 = (bf16[144,1536]{1,0:T(8,128)(2,1)}, bf16[144,1536]{1,0:T(8,128)(2,1)}, u32[]{:S(2)}, u32[]{:S(2)}) collective-permute-start(bf16[144,1536]{1,0:T(8,128)(2,1)} %copy.200), channel_id=1, source_target_pairs={{3,0},{4,1},{5,2},{6,3},{7,4},{8,5},{9,6},{10,7},{11,8},{12,9},{13... | collective-permute-start | bytes 1327112 | tf_op jit(solution)/shard_map/ppermute | solution.py:22
  1926.9 90.0 %collective-permute-start.43 = (bf16[144,1536]{1,0:T(8,128)(2,1)}, bf16[144,1536]{1,0:T(8,128)(2,1)}, u32[]{:S(2)}, u32[]{:S(2)}) collective-permute-start(bf16[144,1536]{1,0:T(8,128)(2,1)} %copy.201), channel_id=1, source_target_pairs={{2,0},{3,1},{4,2},{5,3},{6,4},{7,5},{8,6},{9,7},{10,8},{11,9},{12,... | collective-permute-start | bytes 1327112 | tf_op jit(solution)/shard_map/ppermute | solution.py:22
  1928.2 91.4 %collective-permute-start.44 = (bf16[144,1536]{1,0:T(8,128)(2,1)}, bf16[144,1536]{1,0:T(8,128)(2,1)}, u32[]{:S(2)}, u32[]{:S(2)}) collective-permute-start(bf16[144,1536]{1,0:T(8,128)(2,1)} %copy.202), channel_id=1, source_target_pairs={{1,0},{2,1},{3,2},{4,3},{5,4},{6,5},{7,6},{8,7},{9,8},{10,9},{11,1... | collective-permute-start | bytes 1327112 | tf_op jit(solution)/shard_map/ppermute | solution.py:22
  2186.1 1973.3 %reduce-scatter.5.cloned.1.call-start = ((), (), s32[]{:S(2)}) async-start(), calls=%async_computation.8 | async-start | bytes 77856768 | tf_op jit(solution)/shard_map/reduce_scatter | solution.py:210
  (131 other events, 9052.4 us)
Sparse Core Ops, SparseCore 0:
  10.9 308.7 all-gather.6
  322.6 167.8 all-gather.8
  493.4 105.1 all-gather.10
  601.4 330.3 all-gather.12
  934.6 275.7 all-gather.14
  2186.2 1309.6 reduce-scatter.2
  3504.1 655.2 reduce-scatter.4
where the time goes:
time: 4190 us; the launch traced here: 4170 us
  waiting for transfers between devices  2590 us (62%)
  matrix products  586 us (14%)
  starting transfers between devices  366 us (9%)
  local copies, waits for them, and re-layouts  237 us (6%)
  other arithmetic  152 us (4%)
  blocking collectives  145 us (3%)
  loops' own time  78.1 us (2%)
    reduce_scatter x1, waiting for transfers between devices, on_device(): lax.psum_scatter(jnp.concatenate([term_rows(attended_split, grad_merged),...  1090 us
    reduce_scatter x1, waiting for transfers between devices, on_device(): lax.psum_scatter(term_rows(activated_split, grad_lowered), 'dev', scatter...  655 us
    ppermute x72, waiting for transfers between devices, passed_along(): return lax.ppermute(x, axis, pairs)  385 us
    ppermute x72, starting transfers between devices, passed_along(): return lax.ppermute(x, axis, pairs)  365 us
    all_gather x1, waiting for transfers between devices, on_device(): lax.all_gather(modulation_weight, 'dev', axis=0, tiled=True)  307 us
    all_gather x1, waiting for transfers between devices, on_device(): lax.all_gather(project_weight, 'dev', axis=0, tiled=True)  143 us
    psum x1, blocking collectives, on_device(): lax.psum(local_table.reshape(seq_count, 2, 6 * width), 'dev')  105 us
    concatenate x1, other arithmetic, on_device(): jnp.concatenate([term_rows(attended_split, grad_merged), term_rows(hidden...  97.4 us
  transfers between devices with their start and end apart: 79, of which 31 were waited for; matrix products, arithmetic and copies ran while one was open for 11% of the time, Pallas kernels for 0%

commit v1 on v0

v1 whole, which is shorter than its diff:
```python
import functools

import jax
import jax.numpy as jnp
import numpy as np
from jax import lax
from jax.experimental import pallas as pl
from jax.experimental.pallas import tpu as pltpu
from jax.sharding import PartitionSpec as P

HEADS = 24
HDIM = 64
IMG = 1024
TXT_MIN = 86
TXT_MAX = 154
EPSILON = 1e-06
F32 = jnp.float32
BF16 = jnp.bfloat16
CONTRACT_LAST = (((1,), (1,)), ((), ()))
CONTRACT_FIRST = (((0,), (0,)), ((), ()))
MASKED = -1e30


class Plan:
    def __init__(self, devices, sequences, rows_dev, width):
        self.devices, self.sequences, self.rows_dev, self.width = devices, sequences, rows_dev, width
        self.group = devices // sequences
        self.span = self.group * rows_dev
        mean = self.span - IMG
        up, down = TXT_MAX - mean, mean - TXT_MIN
        drift = 0
        for k in range(sequences + 1):
            drift = max(drift, min(up * k, down * (sequences - k)), min(down * k, up * (sequences - k)))
        self.edge = -(-drift // 64) * 64
        self.rows = self.span + 2 * self.edge
        self.piece = 2 * self.edge // self.group
        self.own = rows_dev + self.piece
        self.image_end = -(-(self.edge + drift + IMG) // 128) * 128
        self.text_start = (self.edge - drift + IMG) // 128 * 128
        self.heads = HEADS // self.group
        self.segments = self.edge_segments()
        self.chip_heads = devices == 4 * self.group

    def device_of(self, seq, rank):
        return seq * self.group + rank

    def place_of(self, device):
        return lax.div(device, self.group), lax.rem(device, self.group)

    def seq_groups(self):
        return [[self.device_of(s, r) for r in range(self.group)] for s in range(self.sequences)]

    def rank_groups(self):
        return [[self.device_of(s, r) for s in range(self.sequences)] for r in range(self.group)]

    def edge_row(self, rank):
        half = self.group // 2
        return jnp.where(rank < half, self.piece * rank, self.edge + self.span + self.piece * (rank - half))

    def main_row(self, rank):
        return self.edge + self.rows_dev * rank

    def edge_segments(self):
        found = []
        for rank in range(self.group):
            half = self.group // 2
            first = self.piece * rank - self.edge if rank < half else self.span + self.piece * (rank - half)
            row = 0
            while row < self.piece:
                owner, owner_row = (first + row) // self.rows_dev, (first + row) % self.rows_dev
                count = min(self.piece - row, self.rows_dev - owner_row)
                found.append((rank, row, count, owner // self.group, owner % self.group, owner_row))
                row += count
        return found


def layer_norm(values):
    mean = jnp.mean(values, axis=-1, keepdims=True)
    centred = values - mean
    variance = jnp.mean(centred * centred, axis=-1, keepdims=True)
    inv_std = lax.rsqrt(variance + EPSILON)
    return (centred * inv_std, inv_std)


def norm_back(grad_normed, normed, inv_std):
    mean_grad = jnp.mean(grad_normed, axis=-1, keepdims=True)
    mean_cross = jnp.mean(grad_normed * normed, axis=-1, keepdims=True)
    return inv_std * (grad_normed - mean_grad - normed * mean_cross)


def softmax_parts(query, key, bias):
    scores = lax.dot_general(query, key, CONTRACT_LAST, preferred_element_type=F32) + bias
    top = jnp.max(scores, axis=1, keepdims=True)
    exponent = jnp.exp(scores - top)
    total = jnp.sum(exponent, axis=1, keepdims=True)
    return exponent * (1.0 / total)


def attend_kernel(heads, q_ref, k_ref, v_ref, bias_ref, out_ref):
    bias = bias_ref[...]
    outs = []
    for head in range(heads):
        cols = slice(head * HDIM, (head + 1) * HDIM)
        query = q_ref[:, cols] * jnp.asarray(HDIM ** (-0.5), BF16)
        probs = softmax_parts(query, k_ref[:, cols], bias).astype(BF16)
        outs.append(jnp.dot(probs, v_ref[:, cols], preferred_element_type=F32))
    out_ref[...] = jnp.concatenate(outs, axis=1).astype(BF16)


def block_rows(rows):
    return 256 if rows % 256 == 0 else 128


def attend(plan, queries, keys, values, bias):
    rows, cols = queries.shape
    block = block_rows(rows)
    whole = pl.BlockSpec((rows, cols), lambda i: (0, 0))
    return pl.pallas_call(
        functools.partial(attend_kernel, plan.heads),
        out_shape=jax.ShapeDtypeStruct((rows, cols), BF16),
        grid=(rows // block,),
        in_specs=[
            pl.BlockSpec((block, cols), lambda i: (i, 0)),
            whole,
            whole,
            pl.BlockSpec((1, rows), lambda i: (0, 0)),
        ],
        out_specs=pl.BlockSpec((block, cols), lambda i: (i, 0)),
        compiler_params=pltpu.CompilerParams(vmem_limit_bytes=48 << 20),
        cost_estimate=pl.CostEstimate(flops=16 * rows * rows * cols, bytes_accessed=8 * rows * cols, transcendentals=0),
        name="attend",
    )(queries, keys, values, bias)


def attend_back_kernel(heads, steps, q_ref, k_ref, v_ref, g_ref, bias_ref, gq_ref, gk_ref, gv_ref, key_sum, value_sum):
    step = pl.program_id(0)
    scale = jnp.asarray(HDIM ** (-0.5), BF16)

    @pl.when(step == 0)
    def _():
        key_sum[...] = jnp.zeros_like(key_sum)
        value_sum[...] = jnp.zeros_like(value_sum)

    bias = bias_ref[...]
    grads = []
    for head in range(heads):
        cols = slice(head * HDIM, (head + 1) * HDIM)
        query = q_ref[:, cols] * scale
        key = k_ref[:, cols]
        grad_out = g_ref[:, cols]
        probs = softmax_parts(query, key, bias)
        grad_probs = lax.dot_general(grad_out, v_ref[:, cols], CONTRACT_LAST, preferred_element_type=F32)
        inner = jnp.sum(probs * grad_probs, axis=1, keepdims=True)
        grad_scores = (probs * (grad_probs - inner)).astype(BF16)
        grads.append(jnp.dot(grad_scores, key, preferred_element_type=F32) * HDIM ** (-0.5))
        key_sum[head] += lax.dot_general(query, grad_scores, CONTRACT_FIRST, preferred_element_type=F32)
        value_sum[head] += lax.dot_general(grad_out, probs.astype(BF16), CONTRACT_FIRST, preferred_element_type=F32)
    gq_ref[...] = jnp.concatenate(grads, axis=1).astype(BF16)

    @pl.when(step == steps - 1)
    def _():
        rows = gk_ref.shape[0]
        gk_ref[...] = key_sum[...].reshape(heads * HDIM, rows).T.astype(BF16)
        gv_ref[...] = value_sum[...].reshape(heads * HDIM, rows).T.astype(BF16)


def attend_back(plan, queries, keys, values, grad_out, bias):
    rows, cols = queries.shape
    block = block_rows(rows)
    whole = pl.BlockSpec((rows, cols), lambda i: (0, 0))
    part = pl.BlockSpec((block, cols), lambda i: (i, 0))
    shape = jax.ShapeDtypeStruct((rows, cols), BF16)
    return pl.pallas_call(
        functools.partial(attend_back_kernel, plan.heads, rows // block),
        out_shape=(shape, shape, shape),
        grid=(rows // block,),
        in_specs=[part, whole, whole, part, pl.BlockSpec((1, rows), lambda i: (0, 0))],
        out_specs=(part, whole, whole),
        scratch_shapes=[pltpu.VMEM((plan.heads, HDIM, rows), F32)] * 2,
        compiler_params=pltpu.CompilerParams(vmem_limit_bytes=56 << 20),
        cost_estimate=pl.CostEstimate(flops=40 * rows * rows * cols, bytes_accessed=14 * rows * cols, transcendentals=0),
        name="attend_back",
    )(queries, keys, values, grad_out, bias)


VMEM = pl.BlockSpec(memory_space=pltpu.VMEM)


def own_rows(plan, window, rank):
    main = lax.dynamic_slice_in_dim(window, plan.main_row(rank), plan.rows_dev, 0)
    edge = lax.dynamic_slice_in_dim(window, plan.edge_row(rank), plan.piece, 0)
    return jnp.concatenate([main, edge], axis=0)


def remote(source, target, send_sem, recv_sem, device):
    return pltpu.make_async_remote_copy(
        src_ref=source,
        dst_ref=target,
        send_sem=send_sem,
        recv_sem=recv_sem,
        device_id=(device,),
        device_id_type=pl.DeviceIdType.MESH,
    )


def here(plan):
    return plan.place_of(lax.axis_index("dev"))


def other(rank, step, size):
    return lax.rem(rank + step, size)


def meet(devices):
    barrier = pltpu.get_barrier_semaphore()
    for device in devices:
        pl.semaphore_signal(barrier, inc=1, device_id=(device,), device_id_type=pl.DeviceIdType.MESH)
    pl.semaphore_wait(barrier, len(devices))


def group_devices(plan, seq, rank):
    return [plan.device_of(seq, other(rank, step, plan.group)) for step in range(1, plan.group)]


def column_devices(plan, seq, rank):
    return [plan.device_of(other(seq, step, plan.sequences), rank) for step in range(1, plan.sequences)]


def every_device(plan, device):
    return [other(device, step, plan.devices) for step in range(1, plan.devices)]


def call(kernel, name, ident, out_shape, scratch, operands, in_specs=None, out_specs=None):
    outs = out_shape if isinstance(out_shape, tuple) else (out_shape,)
    return pl.pallas_call(
        kernel,
        out_shape=out_shape,
        in_specs=in_specs or [VMEM] * len(operands),
        out_specs=out_specs or (tuple([VMEM] * len(outs)) if isinstance(out_shape, tuple) else VMEM),
        scratch_shapes=scratch,
        compiler_params=pltpu.CompilerParams(
            collective_id=ident, has_side_effects=True, vmem_limit_bytes=40 << 20
        ),
        name=name,
    )(*operands)


def aligned(start):
    return pl.multiple_of(start, 16)


def block_parts(plan, ref, rank):
    return (
        ref.at[pl.ds(aligned(plan.main_row(rank)), plan.rows_dev)],
        ref.at[pl.ds(aligned(plan.edge_row(rank)), plan.piece)],
    )


def own_parts(plan, ref):
    return ref.at[pl.ds(0, plan.rows_dev)], ref.at[pl.ds(plan.rows_dev, plan.piece)]


def load_block(plan, ref, rank):
    main, edge = block_parts(plan, ref, rank)
    return jnp.concatenate([main[...], edge[...]], axis=0)


def sum_scratch(plan):
    half, own, width = plan.group // 2, plan.own, plan.width
    return [
        pltpu.VMEM((half, own, width), F32),
        pltpu.VMEM((half, own, width), BF16),
        pltpu.VMEM((half, own, width), BF16),
        pltpu.SemaphoreType.DMA((half, 2)),
        pltpu.SemaphoreType.DMA((half, 2)),
        pltpu.SemaphoreType.DMA((half,)),
        pltpu.SemaphoreType.DMA((half,)),
    ]


def scatter_sum(plan, seq, rank, part, pair, going, coming, pair_send, pair_recv, far_send, far_recv):
    half = plan.group // 2
    chip, core = lax.div(rank, 2), lax.rem(rank, 2)
    partner = plan.device_of(seq, 2 * chip + 1 - core)
    started = []
    order = list(range(1, half)) + [0]
    for step in order:
        chip_to = other(chip, step, half)
        copies = [
            remote(source, target, pair_send.at[step, i], pair_recv.at[step, i], partner)
            for i, (source, target) in enumerate(
                zip(block_parts(plan, part, 2 * chip_to + 1 - core), own_parts(plan, pair.at[step]))
            )
        ]
        for copy in copies:
            copy.start()
        started.append(copies)
    total, sends = None, []
    for step, copies in zip(order, started):
        for copy in copies:
            copy.wait_recv()
        chip_to = other(chip, step, half)
        both = load_block(plan, part, 2 * chip_to + core) + pair[step]
        if step == 0:
            total = both
        else:
            going[step] = both.astype(BF16)
            copy = remote(
                going.at[step], coming.at[step], far_send.at[step], far_recv.at[step], plan.device_of(seq, 2 * chip_to + core)
            )
            copy.start()
            sends.append(copy)
    for step, copy in zip(order, sends):
        copy.wait_recv()
        total = total + coming[step].astype(F32)
    for copies in started:
        for copy in copies:
            copy.wait_send()
    for copy in sends:
        copy.wait_send()
    return total


def share_scratch(plan):
    return [pltpu.SemaphoreType.DMA((plan.group, 2))] * 2 + [pltpu.SemaphoreType.DMA((plan.group, 2))]


def share_rows(plan, seq, rank, parts, window, send, recv, pass_send):
    half = plan.group // 2
    chip, core = lax.div(rank, 2), lax.rem(rank, 2)
    partner_rank = 2 * chip + 1 - core
    partner = plan.device_of(seq, partner_rank)

    def send_own(to_device, slot):
        copies = [
            remote(source, target, send.at[slot, i], recv.at[slot, i], to_device)
            for i, (source, target) in enumerate(zip(parts, block_parts(plan, window, rank)))
        ]
        for copy in copies:
            copy.start()
        return copies

    flying = {}
    for step in range(1, half):
        flying[step] = send_own(plan.device_of(seq, 2 * other(chip, step, half) + core), step)
    flying[0] = send_own(partner, 0)
    for source, target in zip(parts, block_parts(plan, window, rank)):
        target[...] = source[...]
    passed = []
    for step in range(1, half):
        for copy in flying[step]:
            copy.wait_recv()
        came = 2 * other(chip, half - step, half) + core
        copies = [
            remote(place, place, pass_send.at[step, i], recv.at[half + step, i], partner)
            for i, place in enumerate(block_parts(plan, window, came))
        ]
        for copy in copies:
            copy.start()
        passed.extend(copies)
    for copy in flying[0]:
        copy.wait_recv()
    for copy in passed:
        copy.wait_recv()
    for copies in flying.values():
        for copy in copies:
            copy.wait_send()
    for copy in passed:
        copy.wait_send()


def entry_kernel(plan, tokens, grads, mod_part, token_window, grad_window, mods, token_own, grad_own, plane, across,
                 chunk, edge_send, edge_recv, t_send, t_recv, t_pass, g_send, g_recv, g_pass, m_send, m_recv):
    device = lax.axis_index("dev")
    seq, rank = plan.place_of(device)
    meet(every_device(plan, device))
    hops = []
    for step in range(1, plan.group):
        to = other(rank, step, plan.group)
        copy = remote(mod_part.at[to], plane.at[step], m_send.at[0, step], m_recv.at[0, step], plan.device_of(seq, to))
        copy.start()
        hops.append(copy)
    arrays = ((tokens, token_own), (grads, grad_own))
    count = len(plan.segments)
    for which, (source, own) in enumerate(arrays):
        for index, (to_rank, row, rows, step, owner, owner_row) in enumerate(plan.segments):
            @pl.when(rank == owner)
            def _():
                remote(
                    source.at[pl.ds(owner_row, rows)],
                    own.at[pl.ds(row, rows)],
                    edge_send.at[which * count + index],
                    edge_recv.at[which * count + index],
                    plan.device_of(lax.rem(seq + plan.sequences - step, plan.sequences), to_rank),
                ).start()
    for copy in hops:
        copy.wait_recv()
    total = mod_part[rank]
    for step in range(1, plan.group):
        total = total + plane[step]
    plane[0] = total
    hops_across = []
    for step in range(1, plan.sequences):
        to = other(seq, step, plan.sequences)
        copy = remote(plane.at[0, to], across.at[seq], m_send.at[1, step], m_recv.at[1, step], plan.device_of(to, rank))
        copy.start()
        hops_across.append(copy)
    across[seq] = plane[0, seq]
    for which, (source, own) in enumerate(arrays):
        for index, (to_rank, row, rows, step, owner, owner_row) in enumerate(plan.segments):
            @pl.when(rank == to_rank)
            def _():
                remote(
                    source.at[pl.ds(owner_row, rows)],
                    own.at[pl.ds(row, rows)],
                    edge_send.at[which * count + index],
                    edge_recv.at[which * count + index],
                    plan.device_of(lax.rem(seq + plan.sequences + step, plan.sequences), owner),
                ).wait_recv()
    share_rows(plan, seq, rank, (tokens, token_own), token_window, t_send, t_recv, t_pass)
    for copy in hops_across:
        copy.wait_recv()
    half = plan.sequences // 2
    for stream in range(2):
        total = across[stream * half]
        for i in range(1, half):
            total = total + across[stream * half + i]
        chunk[stream] = total
    hops_back = []
    for step in range(1, plan.group):
        to = other(rank, step, plan.group)
        copy = remote(chunk, mods.at[rank], m_send.at[2, step], m_recv.at[2, step], plan.device_of(seq, to))
        copy.start()
        hops_back.append(copy)
    mods[rank] = chunk[...]
    share_rows(plan, seq, rank, (grads, grad_own), grad_window, g_send, g_recv, g_pass)
    for copy in hops_back:
        copy.wait_recv()
    for copy in hops + hops_across + hops_back:
        copy.wait_send()
    for which, (source, own) in enumerate(arrays):
        for index, (to_rank, row, rows, step, owner, owner_row) in enumerate(plan.segments):
            @pl.when(rank == owner)
            def _():
                remote(
                    source.at[pl.ds(owner_row, rows)],
                    own.at[pl.ds(row, rows)],
                    edge_send.at[which * count + index],
                    edge_recv.at[which * count + index],
                    plan.device_of(lax.rem(seq + plan.sequences - step, plan.sequences), to_rank),
                ).wait_send()


def entry(plan, tokens, grads, mod_part):
    lanes = mod_part.shape[1] // plan.group // 128
    pieces = mod_part.reshape(plan.sequences, plan.group, lanes, 128).transpose(1, 0, 2, 3)
    window = jax.ShapeDtypeStruct((plan.rows, plan.width), BF16)
    dma = pltpu.SemaphoreType.DMA
    most = max(plan.group, plan.sequences)
    token_window, grad_window, mods = call(
        functools.partial(entry_kernel, plan),
        "entry",
        1,
        (window, window, jax.ShapeDtypeStruct((plan.group, 2, lanes, 128), F32)),
        [
            pltpu.VMEM((plan.piece, plan.width), BF16),
            pltpu.VMEM((plan.piece, plan.width), BF16),
            pltpu.VMEM((plan.group, plan.sequences, lanes, 128), F32),
            pltpu.VMEM((plan.sequences, lanes, 128), F32),
            pltpu.VMEM((2, lanes, 128), F32),
            dma((2 * len(plan.segments),)),
            dma((2 * len(plan.segments),)),
        ]
        + share_scratch(plan)
        + share_scratch(plan)
        + [dma((3, most)), dma((3, most))],
        (tokens, grads, pieces),
    )
    return token_window, grad_window, mods.transpose(1, 0, 2, 3).reshape(2, -1)


def swap_kernel(plan, source, target, send, recv):
    seq, rank = here(plan)
    meet(group_devices(plan, seq, rank))
    copies = []
    for step in range(1, plan.group):
        to = other(rank, step, plan.group)
        copy = remote(source.at[to], target.at[rank], send.at[step], recv.at[step], plan.device_of(seq, to))
        copy.start()
        copies.append(copy)
    target[rank] = source[rank]
    for copy in copies:
        copy.wait()


def swap(plan, pieces, ident):
    dma = pltpu.SemaphoreType.DMA
    return call(
        functools.partial(swap_kernel, plan),
        "swap_%d" % ident,
        ident,
        jax.ShapeDtypeStruct(pieces.shape, pieces.dtype),
        [dma((plan.group,)), dma((plan.group,))],
        (pieces,),
    )


def pick_rows(table, text):
    return jnp.where(text > 0, table[1:2, :], table[0:1, :])


def norm_rows(values):
    mean = jnp.mean(values, axis=1, keepdims=True)
    centred = values - mean
    inv = lax.rsqrt(jnp.mean(centred * centred, axis=1, keepdims=True) + EPSILON)
    return centred * inv, inv


def middle_kernel(plan, part, tokens, gate_a, scale_b, shift_b, text, merged, window, own, *scratch):
    seq, rank = here(plan)
    meet(group_devices(plan, seq, rank))
    total = scatter_sum(plan, seq, rank, part, *scratch[:7])
    merged[...] = total
    mask = text[...]
    middle = tokens[...].astype(F32) + pick_rows(gate_a[...], mask) * total
    normed, _ = norm_rows(middle)
    own[...] = (normed * (1.0 + pick_rows(scale_b[...], mask)) + pick_rows(shift_b[...], mask)).astype(BF16)
    share_rows(plan, seq, rank, own_parts(plan, own), window, *scratch[7:])


def own_shape(plan, dtype=F32):
    return jax.ShapeDtypeStruct((plan.own, plan.width), dtype)


def window_shape(plan):
    return jax.ShapeDtypeStruct((plan.rows, plan.width), BF16)


def middle_rows(plan, part, tokens, gate_a, scale_b, shift_b, text):
    return call(
        functools.partial(middle_kernel, plan),
        "middle",
        2,
        (own_shape(plan), window_shape(plan)),
        [pltpu.VMEM((plan.own, plan.width), BF16)] + sum_scratch(plan) + share_scratch(plan),
        (part, tokens, gate_a, scale_b, shift_b, text),
    )


def back_kernel(plan, part, grad, middle, gate_a, scale_b, text, grad_hidden, grad_middle, window, own, *scratch):
    seq, rank = here(plan)
    meet(group_devices(plan, seq, rank))
    total = scatter_sum(plan, seq, rank, part, *scratch[:7])
    grad_hidden[...] = total
    mask = text[...]
    normed, inv = norm_rows(middle[...])
    inner = total * (1.0 + pick_rows(scale_b[...], mask))
    mean_grad = jnp.mean(inner, axis=1, keepdims=True)
    mean_cross = jnp.mean(inner * normed, axis=1, keepdims=True)
    result = grad[...].astype(F32) + inv * (inner - mean_grad - normed * mean_cross)
    grad_middle[...] = result
    own[...] = (pick_rows(gate_a[...], mask) * result).astype(BF16)
    share_rows(plan, seq, rank, own_parts(plan, own), window, *scratch[7:])


def back_rows(plan, part, grad, middle, gate_a, scale_b, text):
    return call(
        functools.partial(back_kernel, plan),
        "back",
        3,
        (own_shape(plan), own_shape(plan), window_shape(plan)),
        [pltpu.VMEM((plan.own, plan.width), BF16)] + sum_scratch(plan) + share_scratch(plan),
        (part, grad, middle, gate_a, scale_b, text),
    )


def sum_kernel(plan, part, out, *scratch):
    seq, rank = here(plan)
    meet(group_devices(plan, seq, rank))
    out[...] = scatter_sum(plan, seq, rank, part, *scratch)


def sum_rows(plan, part, ident):
    return call(
        functools.partial(sum_kernel, plan), "sum_%d" % ident, ident, own_shape(plan), sum_scratch(plan), (part,)
    )


def edge_kernel(plan, own, extra, send, recv):
    device = lax.axis_index("dev")
    seq, rank = plan.place_of(device)
    extra[...] = jnp.zeros_like(extra)
    meet(every_device(plan, device))

    def copy(index):
        from_rank, row, rows, step, owner, owner_row = plan.segments[index]
        return remote(
            own.at[pl.ds(plan.rows_dev + row, rows)],
            extra.at[pl.ds(owner_row, rows)],
            send.at[index],
            recv.at[index],
            plan.device_of(lax.rem(seq + plan.sequences + step, plan.sequences), owner),
        )

    for index, segment in enumerate(plan.segments):
        @pl.when(rank == segment[0])
        def _():
            copy(index).start()
    for index, segment in enumerate(plan.segments):
        @pl.when(rank == segment[4])
        def _():
            copy(index).wait_recv()

        @pl.when(rank == segment[0])
        def _():
            copy(index).wait_send()


def to_packed(plan, own, foreign, ident):
    dma = pltpu.SemaphoreType.DMA
    extra = call(
        functools.partial(edge_kernel, plan),
        "edges_%d" % ident,
        ident,
        jax.ShapeDtypeStruct((plan.rows_dev, plan.width), own.dtype),
        [dma((len(plan.segments),)), dma((len(plan.segments),))],
        (own,),
    )
    return jnp.where(foreign[:, None], extra, own[: plan.rows_dev])


def table_kernel(plan, local, table, first, second, mine, send, recv):
    device = lax.axis_index("dev")
    seq, rank = plan.place_of(device)
    stream = lax.div(2 * seq, plan.sequences)
    meet(every_device(plan, device))
    hops = []
    for step in range(1, plan.group):
        to = other(rank, step, plan.group)
        copy = remote(local.at[to], first.at[step], send.at[0, step], recv.at[0, step], plan.device_of(seq, to))
        copy.start()
        hops.append(copy)
    for copy in hops:
        copy.wait_recv()
    total = local[rank]
    for step in range(1, plan.group):
        total = total + first[step]
    first[0] = total
    across = []
    for step in range(1, plan.sequences):
        to = other(seq, step, plan.sequences)
        to_stream = lax.div(2 * to, plan.sequences)
        copy = remote(first.at[0, to_stream], second.at[seq], send.at[1, step], recv.at[1, step], plan.device_of(to, rank))
        copy.start()
        across.append(copy)
    second[seq] = first[0, stream]
    for copy in across:
        copy.wait_recv()
    mine[...] = second[...]
    last = []
    for step in range(1, plan.group):
        to = other(rank, step, plan.group)
        copy = remote(mine, table.at[rank], send.at[2, step], recv.at[2, step], plan.device_of(seq, to))
        copy.start()
        last.append(copy)
    table[rank] = mine[...]
    for copy in last:
        copy.wait_recv()
    for copy in hops + across + last:
        copy.wait_send()


def stream_table(plan, local, ident):
    lanes = local.shape[1] // plan.group // 128
    pieces = local.reshape(2, plan.group, lanes, 128).transpose(1, 0, 2, 3)
    dma = pltpu.SemaphoreType.DMA
    most = max(plan.group, plan.sequences)
    table = call(
        functools.partial(table_kernel, plan),
        "mod_table",
        ident,
        jax.ShapeDtypeStruct((plan.group, plan.sequences, lanes, 128), F32),
        [
            pltpu.VMEM((plan.group, 2, lanes, 128), F32),
            pltpu.VMEM((plan.sequences, lanes, 128), F32),
            pltpu.VMEM((plan.sequences, lanes, 128), F32),
            dma((3, most)),
            dma((3, most)),
        ],
        (pieces,),
    )
    return table.transpose(1, 0, 2, 3).reshape(plan.sequences, -1)


def spread_kernel(plan, piece, everyone, send, recv):
    device = lax.axis_index("dev")
    seq, rank = plan.place_of(device)
    meet(group_devices(plan, seq, rank) + column_devices(plan, seq, rank))
    copies = []
    everyone[seq, rank] = piece[...]
    for step in range(1, plan.group):
        to = other(rank, step, plan.group)
        copy = remote(piece, everyone.at[seq, rank], send.at[0, step], recv.at[0, step], plan.device_of(seq, to))
        copy.start()
        copies.append(copy)
    for copy in copies:
        copy.wait_recv()
    across = []
    for step in range(1, plan.sequences):
        to = other(seq, step, plan.sequences)
        copy = remote(everyone.at[seq], everyone.at[seq], send.at[1, step], recv.at[1, step], plan.device_of(to, rank))
        copy.start()
        across.append(copy)
    for copy in across:
        copy.wait_recv()
    for copy in copies + across:
        copy.wait_send()


def spread(plan, piece, ident):
    dma = pltpu.SemaphoreType.DMA
    most = max(plan.group, plan.sequences)
    return call(
        functools.partial(spread_kernel, plan),
        "spread",
        ident,
        jax.ShapeDtypeStruct((plan.sequences, plan.group) + piece.shape, piece.dtype),
        [dma((2, most)), dma((2, most))],
        (piece,),
    )


def project_slices(plan, weight):
    rows, share = weight.shape[0], plan.width // plan.group
    view = weight.reshape(rows, 3, 2, plan.group // 2, share).transpose(3, 2, 0, 1, 4)
    got = swap(plan, view.reshape(plan.group, rows, 3 * share), 4)
    got = lax.all_gather(got, "dev", axis=0, axis_index_groups=plan.rank_groups())
    return got.reshape(2, plan.width, 3 * share)


def up_slices(plan, weight):
    rows, cols = weight.shape
    planes = plan.sequences // 2
    share = cols // planes // plan.group
    view = weight.reshape(rows, planes, plan.group, share).transpose(2, 0, 1, 3)
    got = swap(plan, view.reshape(plan.group, rows, planes * share), 5)
    got = lax.all_gather(got, "dev", axis=0, axis_index_groups=plan.rank_groups())
    return got.reshape(2, plan.width, planes * share)


def sum_to_owners(plan, grad, rows, ident):
    cols = grad.shape[2]
    pieces = grad.astype(BF16).reshape(plan.sequences, plan.group, rows, cols)
    got = lax.psum_scatter(pieces, "dev", scatter_dimension=0, axis_index_groups=plan.rank_groups())
    return swap(plan, got, ident)


def project_grads(plan, grad, rows):
    share = plan.width // plan.group
    got = sum_to_owners(plan, grad, rows, 6)
    got = got.reshape(plan.group // 2, 2, rows, 3, share).transpose(2, 3, 1, 0, 4)
    return got.reshape(rows, -1).astype(F32)


def up_grads(plan, grad, rows):
    planes = plan.sequences // 2
    got = sum_to_owners(plan, grad, rows, 7)
    got = got.reshape(plan.group, rows, planes, -1).transpose(1, 2, 0, 3)
    return got.reshape(rows, -1).astype(F32)


def chip_groups(plan):
    return [
        [plan.device_of(s, 2 * q + core) for s in range(plan.sequences) for core in range(2)]
        for q in range(plan.group // 2)
    ]


def merge_slices(plan, weight, rank):
    half = plan.group // 2
    rows = weight.shape[0]
    share = plan.width // plan.group
    if plan.chip_heads:
        full = lax.all_gather(weight, "dev", axis=0, axis_index_groups=chip_groups(plan))
        full = full.reshape(2, 2, share, weight.shape[1])
        return lax.dynamic_index_in_dim(full, lax.rem(rank, 2), 1, keepdims=False)
    full = lax.all_gather(weight, "dev", axis=0, tiled=True)
    full = full.reshape(2, 2, half, share, weight.shape[1])
    full = lax.dynamic_index_in_dim(full, lax.rem(rank, 2), 1, keepdims=False)
    return lax.dynamic_index_in_dim(full, lax.div(rank, 2), 1, keepdims=False)


def merge_grads(plan, grad, rank):
    half = plan.group // 2
    _, share, cols = grad.shape
    core = lax.rem(rank, 2)
    grad = grad.astype(BF16)
    mine = [jnp.where(core == k, grad, jnp.zeros((), BF16)) for k in range(2)]
    if plan.chip_heads:
        full = jnp.stack(mine, axis=1).reshape(2 * plan.sequences, -1, cols)
        out = lax.psum_scatter(full, "dev", scatter_dimension=0, axis_index_groups=chip_groups(plan))
        return out.astype(F32)
    full = jnp.zeros((2, 2, half, share, cols), BF16)
    full = lax.dynamic_update_slice_in_dim(full, jnp.stack(mine, axis=1)[:, :, None], lax.div(rank, 2), 2)
    return lax.psum_scatter(full.reshape(-1, cols), "dev", scatter_dimension=0, tiled=True).astype(F32)


def down_slices(plan, weight):
    full = lax.all_gather(weight, "dev", axis=0, axis_index_groups=plan.rank_groups())
    return full.reshape(2, -1, weight.shape[1])


def down_grads(plan, grad):
    cols = grad.shape[2]
    pieces = grad.astype(BF16).reshape(plan.sequences, -1, cols)
    return lax.psum_scatter(pieces, "dev", scatter_dimension=0, axis_index_groups=plan.rank_groups()).astype(F32)


def by_stream(plan, image_part, text_part, is_text):
    start, end = plan.text_start, plan.image_end
    mixed = jnp.where(is_text[start:end, None], text_part[: end - start], image_part[start:])
    return jnp.concatenate([image_part[:start], mixed, text_part[end - start :]], axis=0)


def stream_dot(plan, rows, pair, is_text):
    image_part = jnp.dot(rows[: plan.image_end], pair[0], preferred_element_type=F32)
    text_part = jnp.dot(rows[plan.text_start :], pair[1], preferred_element_type=F32)
    return by_stream(plan, image_part, text_part, is_text)


def stream_dot_back(plan, grads, pair, is_text):
    image_part = lax.dot_general(grads[: plan.image_end], pair[0], CONTRACT_LAST, preferred_element_type=F32)
    text_part = lax.dot_general(grads[plan.text_start :], pair[1], CONTRACT_LAST, preferred_element_type=F32)
    return by_stream(plan, image_part, text_part, is_text)


def weight_terms(plan, rows, grads, is_text):
    zero = jnp.zeros((), grads.dtype)
    image = jnp.where(is_text[: plan.image_end, None], zero, grads[: plan.image_end])
    text = jnp.where(is_text[plan.text_start :, None], grads[plan.text_start :], zero)
    image_term = lax.dot_general(rows[: plan.image_end], image, CONTRACT_FIRST, preferred_element_type=F32)
    text_term = lax.dot_general(rows[plan.text_start :], text, CONTRACT_FIRST, preferred_element_type=F32)
    return jnp.stack([image_term, text_term])


def pick(table, text_rows):
    return jnp.where(text_rows[:, None], table[1][None, :], table[0][None, :])


def on_device(
    tokens,
    conditioning,
    text_lengths,
    modulation_weight,
    project_weight,
    merge_weight,
    up_weight,
    down_weight,
    cotangent,
):
    rows_dev, width = tokens.shape
    mod_rows = modulation_weight.shape[0]
    plan = Plan(lax.axis_size("dev"), conditioning.shape[0], rows_dev, width)
    device = lax.axis_index("dev")
    seq, rank = plan.place_of(device)
    feature_start = device * mod_rows % width

    ends = jnp.cumsum(IMG + text_lengths)
    starts = jnp.concatenate([jnp.zeros((1,), jnp.int32), ends[:-1]])
    positions = device * rows_dev + jnp.arange(rows_dev, dtype=jnp.int32)
    row_seq = jnp.sum((starts[None, :] <= positions[:, None]).astype(jnp.int32), axis=1) - 1
    offset = plan.span * seq - plan.edge + jnp.arange(plan.rows, dtype=jnp.int32) - starts[seq]
    valid = (offset >= 0) & (offset < IMG + text_lengths[seq])
    is_text = offset >= IMG
    bias = jnp.where(valid, 0.0, MASKED).astype(F32)[None, :]
    own_valid = own_rows(plan, valid[:, None], rank)[:, 0]
    own_text = own_rows(plan, is_text[:, None], rank)[:, 0]

    cond_float = conditioning.astype(F32)
    silu_low = jax.nn.silu(cond_float).astype(BF16)
    silu_part = lax.dynamic_slice_in_dim(silu_low, feature_start, mod_rows, 1)
    mod_part = jnp.dot(silu_part, modulation_weight, preferred_element_type=F32)

    merge_pair = merge_slices(plan, merge_weight, rank)
    project_pair = project_slices(plan, project_weight)
    up_pair = up_slices(plan, up_weight)
    down_pair = down_slices(plan, down_weight)

    token_window, grad_window, mods = entry(plan, tokens, cotangent, mod_part)
    shift_a, scale_a, gate_a, shift_b, scale_b, gate_b = jnp.split(mods, 6, axis=1)
    grad_window = jnp.where(valid[:, None], grad_window, jnp.zeros((), BF16))

    normed_full, _ = layer_norm(token_window.astype(F32))
    hidden_a = (normed_full * (1.0 + pick(scale_a, is_text)) + pick(shift_a, is_text)).astype(BF16)
    projected = stream_dot(plan, hidden_a, project_pair, is_text).astype(BF16)
    queries, keys, values = jnp.split(projected, 3, axis=1)
    attended = attend(plan, queries, keys, values, bias)

    own_tokens = own_rows(plan, token_window, rank)
    own_grad = own_rows(plan, grad_window, rank)
    text_mask = own_text.astype(F32)[:, None]
    merged, hidden_b = middle_rows(
        plan, stream_dot(plan, attended, merge_pair, is_text), own_tokens, gate_a, scale_b, shift_b, text_mask
    )
    middle = own_tokens.astype(F32) + pick(gate_a, own_text) * merged
    normed_b, inv_b = layer_norm(middle)

    upper = stream_dot(plan, hidden_b, up_pair, is_text)
    activated = jax.nn.gelu(upper, approximate=True).astype(BF16)
    grad_lowered = (pick(gate_b, is_text) * grad_window.astype(F32)).astype(BF16)
    down_term = weight_terms(plan, activated, grad_lowered, is_text)
    down_grad = down_grads(plan, down_term)
    grad_activated = stream_dot_back(plan, grad_lowered, down_pair, is_text)
    gelu_pull = jax.vjp(lambda value_in: jax.nn.gelu(value_in, approximate=True), upper)[1]
    grad_upper = gelu_pull(grad_activated)[0].astype(BF16)
    up_term = weight_terms(plan, hidden_b, grad_upper, is_text)
    up_grad = up_grads(plan, up_term, mod_rows)
    grad_hidden_b, grad_middle, grad_merged = back_rows(
        plan, stream_dot_back(plan, grad_upper, up_pair, is_text), own_grad, middle, gate_a, scale_b, text_mask
    )
    lowered = sum_rows(plan, stream_dot(plan, activated, down_pair, is_text), 8)
    foreign = row_seq != seq
    layer_out = to_packed(plan, (middle + pick(gate_b, own_text) * lowered).astype(BF16), foreign, 9)
    grad_gate_b = own_grad.astype(F32) * lowered
    grad_scale_b = grad_hidden_b * normed_b
    grad_gate_a = grad_middle * merged
    grad_attended = stream_dot_back(plan, grad_merged, merge_pair, is_text).astype(BF16)
    merge_grad = merge_grads(plan, weight_terms(plan, attended, grad_merged, is_text), rank)

    grad_projected = jnp.concatenate(attend_back(plan, queries, keys, values, grad_attended, bias), axis=1)
    project_grad = project_grads(plan, weight_terms(plan, hidden_a, grad_projected, is_text), mod_rows)
    grad_hidden_a = sum_rows(plan, stream_dot_back(plan, grad_projected, project_pair, is_text), 10)

    normed_a, inv_a = layer_norm(own_tokens.astype(F32))
    grad_scale_a = grad_hidden_a * normed_a
    own_back = grad_middle + norm_back(grad_hidden_a * (1.0 + pick(scale_a, own_text)), normed_a, inv_a)
    tokens_grad = to_packed(plan, own_back, foreign, 11)

    rows_of = jnp.stack([own_valid & ~own_text, own_valid & own_text]).astype(F32)
    sums = [
        jnp.stack([jnp.sum(jnp.where(own[:, None] > 0, part, 0.0), axis=0) for own in rows_of])
        for part in (grad_hidden_a, grad_scale_a, grad_gate_a, grad_hidden_b, grad_scale_b, grad_gate_b)
    ]
    local_mods = jnp.concatenate(sums, axis=1)
    own_grads = stream_table(plan, local_mods, 12).astype(BF16)
    modulation_grad = lax.dot_general(silu_part, own_grads, CONTRACT_FIRST, preferred_element_type=F32)
    grad_piece = lax.dot_general(own_grads, modulation_weight, CONTRACT_LAST, preferred_element_type=F32)
    everyone = spread(plan, grad_piece.reshape(-1, 128), 13)
    everyone = everyone.reshape(2, plan.devices // 2, plan.sequences, mod_rows)
    grad_silu = (everyone[0] + everyone[1]).transpose(1, 0, 2).reshape(plan.sequences, width)
    conditioning_grad = jax.vjp(jax.nn.silu, cond_float)[1](grad_silu)[0]
    return (
        layer_out,
        tokens_grad,
        conditioning_grad,
        modulation_grad,
        project_grad,
        merge_grad,
        up_grad,
        down_grad,
    )


def solution(mesh):
    shard, whole = P("dev", None), P()
    return jax.shard_map(
        on_device,
        mesh=mesh,
        in_specs=(shard, whole, whole, shard, shard, shard, shard, shard, shard),
        out_specs=(shard, shard, whole, shard, shard, shard, shard, shard),
        check_vma=False,
    )
```

time: 4190 us -> 728 us (0.17)
  waiting for transfers between devices: 2590 us -> 92.5 us
  matrix products: 586 us -> 64.5 us
  Pallas kernels: 0 us -> 397 us
  starting transfers between devices: 366 us -> 0.54 us
  local copies, waits for them, and re-layouts: 237 us -> 92 us
  blocking collectives: 145 us -> 0 us
  other arithmetic: 152 us -> 56.1 us
  loops' own time: 78.1 us -> 0 us
    reduce_scatter x2 -> x4, waiting for transfers between devices: 1750 us -> 37.9 us  [the longest x1 37.9 us: down_grads(): lax.psum_scatter(pieces, 'dev', scatter_dimension=0, axis_index_groups=pl...]
    dot_general x191 -> x25, matrix products: 583 us -> 61.5 us  [the longest x4 17 us: stream_dot_back(): lax.dot_general(grads[:plan.image_end], pair[0], CONTRACT_LAST, preferred...]
    pallas_call x0 -> x15, Pallas kernels: none -> 397 us  [the longest x13 363 us: call(): pl.pallas_call(kernel, out_shape=out_shape, in_specs=in_specs or [VMEM] *...]
    all_gather x5 -> x4, waiting for transfers between devices: 449 us -> 53.3 us  [the longest x1 53.3 us: down_slices(): lax.all_gather(weight, 'dev', axis=0, axis_index_groups=plan.rank_groups())]
    ppermute x72 -> x0, waiting for transfers between devices: 385 us -> none  [passed_along(): return lax.ppermute(x, axis, pairs)]
    ppermute x72 -> x0, starting transfers between devices: 365 us -> none  [passed_along(): return lax.ppermute(x, axis, pairs)]
    psum x1 -> x0, blocking collectives: 105 us -> none  [on_device(): lax.psum(local_table.reshape(seq_count, 2, 6 * width), 'dev')]
    concatenate x3 -> x11, other arithmetic: 98.6 us -> 11.3 us  [the longest x6 9.57 us: by_stream(): jnp.concatenate([image_part[:start], mixed, text_part[end - start:]], axi...]
  transfers between devices with their start and end apart: 79 -> 8, of which waited for: 31 -> 2; matrix products, arithmetic and copies ran while one was open for 11% -> 21% of each run, Pallas kernels for 0% -> 45%
where the time goes in v1:
time: 728 us; the launch traced here: 720 us
  Pallas kernels  397 us (55%)
  waiting for transfers between devices  92.5 us (13%)
  local copies, waits for them, and re-layouts  92 us (13%)
  matrix products  64.5 us (9%)
  other arithmetic  56.1 us (8%)
  between operations  16.7 us (2%)
    pallas_call x13, Pallas kernels, call(): pl.pallas_call(kernel, out_shape=out_shape, in_specs=in_specs or [VMEM] *...  363 us
    all_gather x1, waiting for transfers between devices, down_slices(): lax.all_gather(weight, 'dev', axis=0, axis_index_groups=plan.rank_groups())  53.3 us
    reduce_scatter x1, waiting for transfers between devices, down_grads(): lax.psum_scatter(pieces, 'dev', scatter_dimension=0, axis_index_groups=pl...  37.9 us
    unnamed x166, local copies, waits for them, and re-layouts  37.9 us
    pallas_call x1, Pallas kernels, attend_back(): pl.pallas_call(functools.partial(attend_back_kernel, plan.heads, rows //...  22.2 us
    dot_general x4, matrix products, stream_dot_back(): lax.dot_general(grads[:plan.image_end], pair[0], CONTRACT_LAST, preferred...  17 us
  transfers between devices with their start and end apart: 8, of which 2 were waited for; matrix products, arithmetic and copies ran while one was open for 21% of the time, Pallas kernels for 45%

profile of v1, /device:TPU:0, one launch (start us, length us, event | category | flops | bytes accessed | tf_op | source)
XLA Modules:
  0.0 719.8 jit_solution(17196346279463400453)
XLA Ops:
  14.3 16.1 %swap_4.1 = bf16[8,96,576]{2,1,0:T(8,128)(2,1)} custom-call(bf16[8,96,576]{2,1,0:T(8,128)(2,1)S(1)} %copy.121.source), custom_call_target="tpu_custom_call" | custom-call | tf_op jit(solution)/shard_map/swap_4/pallas_call | solution.py:235
  37.9 17.2 %swap_5.1 = bf16[8,96,768]{2,1,0:T(8,128)(2,1)} custom-call(bf16[8,96,768]{2,1,0:T(8,128)(2,1)S(1)} %reshape.345.source), custom_call_target="tpu_custom_call" | custom-call | tf_op jit(solution)/shard_map/swap_5/pallas_call | solution.py:235
  60.5 83.5 %entry.1 = (bf16[1280,1536]{1,0:T(8,128)(2,1)S(1)}, bf16[1280,1536]{1,0:T(8,128)(2,1)S(1)}, f32[8,2,9,128]{3,2,1,0:T(8,128)S(1)}) custom-call(bf16[144,1536]{1,0:T(8,128)(2,1)S(1)} %copy-done.17, bf16[144,1536]{1,0:T(8,128)(2,1)S(1)} %copy-done.18, f32[8,4,9,128]{3,2,1,0:T(8,128)S(1)} %bitcast.105), custom_call_target="tpu_custom_call" | custom-call | tf_op jit(solution)/shard_map/entry/pallas_call | solution.py:235
  147.4 9.9 %multiply_convert_fusion = (bf16[1280,1536]{1,0:T(8,128)(2,1)}, bf16[1280,1536]{1,0:T(8,128)(2,1)S(1)}, bf16[1280,1536]{1,0:T(8,128)(2,1)}) fusion(f32[1536]{0:T(1024)S(1)} %get-tuple-element.45, f32[1536]{0:T(1024)S(1)} %get-tuple-element.44, pred[1280]{0:T(1024)(128)(4,1)S(1)} %fusion.129, bf16[1280,1536]{1,0:T(8,128)(2,1)} %copy-done.3, ...), kind=kLoop, calls=%fused_computation.12 | loop fusion | flops 27525120 | bytes 19710464 | tf_op jit(solution)/shard_map/convert_element_type | solution.py:910
  182.1 12.3 %attend.1 = bf16[1280,192]{1,0:T(8,128)(2,1)S(1)} custom-call(bf16[1280,192]{1,0:T(8,128)(2,1)S(1)} %get-tuple-element.72.q_ref, bf16[1280,192]{1,0:T(8,128)(2,1)S(1)} %get-tuple-element.71.k_ref, bf16[1280,192]{1,0:T(8,128)(2,1)S(1)} %get-tuple-element.70.v_ref, f32[1,1280]{1,0:T(1,128)S(1)} %and_select_fusion.bias_ref), custom_call_target="tpu_custom_call" | custom-call | flops 5033164800 | bytes 1966080 | tf_op jit(solution)/shard_map/attend/pallas_call | solution.py:118
  203.3 54.6 %middle.1 = (f32[160,1536]{1,0:T(8,128)S(1)}, bf16[1280,1536]{1,0:T(8,128)(2,1)S(1)}) custom-call(f32[1280,1536]{1,0:T(8,128)S(1)} %pad_maximum_fusion.part, bf16[160,1536]{1,0:T(8,128)(2,1)S(1)} %pad_maximum_fusion.14.tokens, f32[2,1536]{1,0:T(2,128)S(1)} %get-tuple-element.97.gate_a, f32[2,1536]{1,0:T(2,128)S(1)} %get-tuple-element.96.scale_b, ...), custom_call_target="tpu_custom_call" | custom-call | tf_op jit(solution)/shard_map/middle/pallas_call | solution.py:235
  271.2 53.3 %all-gather.15.cloned.1.call-done = bf16[1536,1536]{1,0:T(8,128)(2,1)} async-done(((bf16[384,1536]{1,0:T(8,128)(2,1)}), bf16[1536,1536]{1,0:T(8,128)(2,1)}) %all-gather.15.cloned.1.call-update) | async-done | bytes 4718608 | tf_op jit(solution)/shard_map/all_gather | solution.py:809
  324.5 5.7 fusion.23
  347.9 58.3 %back.1 = (f32[160,1536]{1,0:T(8,128)S(1)}, f32[160,1536]{1,0:T(8,128)S(1)}, bf16[1280,1536]{1,0:T(8,128)(2,1)S(1)}) custom-call(f32[1280,1536]{1,0:T(8,128)} %pad_maximum_fusion.2.part, bf16[160,1536]{1,0:T(8,128)(2,1)S(1)} %pad_maximum_fusion.15.grad, f32[160,1536]{1,0:T(8,128)S(1)} %get-tuple-element.59.middle, f32[2,1536]{1,0:T(2,128)S(1)} %get-tuple-element.97.gate_a, ...), custom_call_target="tpu_custom_call" | custom-call | tf_op jit(solution)/shard_map/back/pallas_call | solution.py:235
  422.0 22.2 %attend_back.1 = (bf16[1280,192]{1,0:T(8,128)(2,1)}, bf16[1280,192]{1,0:T(8,128)(2,1)}, bf16[1280,192]{1,0:T(8,128)(2,1)}) custom-call(bf16[1280,192]{1,0:T(8,128)(2,1)} %copy-done.16, bf16[1280,192]{1,0:T(8,128)(2,1)} %copy-done.15, bf16[1280,192]{1,0:T(8,128)(2,1)} %copy-done.14, bf16[1280,192]{1,0:T(8,128)(2,1)} %pad_maximum_fusion.13.g_ref, ...), custom_call_target="tpu_custom_call" | custom-call | flops 12582912000 | bytes 3440640 | tf_op jit(solution)/shard_map/attend_back/pallas_call | solution.py:173
  452.9 6.0 copy.135
  461.2 5.8 fusion.38
  470.5 5.2 fusion.61
  490.4 5.0 fusion.76
  505.1 28.3 %sum_8.1 = f32[160,1536]{1,0:T(8,128)S(1)} custom-call(f32[1280,1536]{1,0:T(8,128)S(1)} %pad_maximum_fusion.1.part), custom_call_target="tpu_custom_call" | custom-call | tf_op jit(solution)/shard_map/sum_8/pallas_call | solution.py:235
  534.2 28.6 %sum_10.1 = f32[160,1536]{1,0:T(8,128)S(1)} custom-call(f32[1280,1536]{1,0:T(8,128)S(1)} %pad_maximum_fusion.3.part), custom_call_target="tpu_custom_call" | custom-call | tf_op jit(solution)/shard_map/sum_10/pallas_call | solution.py:235
  567.5 14.9 %mod_table.1 = f32[8,4,9,128]{3,2,1,0:T(8,128)S(1)} custom-call(f32[8,2,9,128]{3,2,1,0:T(8,128)S(1)} %bitcast.107), custom_call_target="tpu_custom_call" | custom-call | tf_op jit(solution)/shard_map/mod_table/pallas_call | solution.py:235
  583.2 10.1 %spread.1 = f32[4,8,3,128]{3,2,1,0:T(4,128)S(1)} custom-call(f32[3,128]{1,0:T(4,128)S(1)} %reshape.347.piece), custom_call_target="tpu_custom_call" | custom-call | tf_op jit(solution)/shard_map/spread/pallas_call | solution.py:235
  593.6 11.7 %edges_11.1 = f32[144,1536]{1,0:T(8,128)S(1)} custom-call(f32[160,1536]{1,0:T(8,128)S(1)} %copy-done.2), custom_call_target="tpu_custom_call" | custom-call | tf_op jit(solution)/shard_map/edges_11/pallas_call | solution.py:235
  605.3 11.1 %edges_9.1 = bf16[144,1536]{1,0:T(8,128)(2,1)S(1)} custom-call(bf16[160,1536]{1,0:T(8,128)(2,1)S(1)} %get-tuple-element.83.own), custom_call_target="tpu_custom_call" | custom-call | tf_op jit(solution)/shard_map/edges_9/pallas_call | solution.py:235
  624.5 11.6 %swap_6.1 = bf16[8,96,576]{2,1,0:T(8,128)(2,1)S(1)} custom-call(bf16[8,96,576]{2,1,0:T(8,128)(2,1)S(1)} %bitcast.106), custom_call_target="tpu_custom_call" | custom-call | tf_op jit(solution)/shard_map/swap_6/pallas_call | solution.py:235
  637.9 4.5 copy.137
  647.6 16.7 %swap_7.1 = bf16[8,96,768]{2,1,0:T(8,128)(2,1)S(1)} custom-call(bf16[8,96,768]{2,1,0:T(8,128)(2,1)S(1)} %bitcast.104), custom_call_target="tpu_custom_call" | custom-call | tf_op jit(solution)/shard_map/swap_7/pallas_call | solution.py:235
  672.0 37.9 %reduce-scatter.11.cloned.1.call-done = bf16[1,384,1536]{2,1,0:T(8,128)(2,1)} async-done(((bf16[4,384,1536]{2,1,0:T(8,128)(2,1)}), bf16[1,384,1536]{2,1,0:T(8,128)(2,1)}) %reduce-scatter.11.cloned.1.call-update) | async-done | bytes 1179664 | tf_op jit(solution)/shard_map/reduce_scatter | solution.py:816
  (344 shorter events, 172.6 us)
Async XLA Ops:
  7.2 52.9 %copy-start = (bf16[96,9216]{1,0:T(8,128)(2,1)S(1)}, bf16[96,9216]{1,0:T(8,128)(2,1)}, u32[]{:S(2)}) copy-start(bf16[96,9216]{1,0:T(8,128)(2,1)} %param.12) | copy-start | bytes 5308420
  7.2 157.2 %all-gather.9.cloned.1.call-start = ((), (), s32[]{:S(2)}) async-start(), calls=%async_computation.8 | async-start | bytes 4915200 | tf_op jit(solution)/shard_map/all_gather | solution.py:737
  30.5 167.3 %all-gather.11.cloned.1.call-start = ((), (), s32[]{:S(2)}) async-start(), calls=%async_computation.9 | async-start | bytes 2654208 | tf_op jit(solution)/shard_map/all_gather | solution.py:784
  31.2 230.0 %all-gather.13.cloned.1.call-start = ((), (), s32[]{:S(2)}) async-start(), calls=%async_computation.10 | async-start | bytes 5898240 | tf_op jit(solution)/shard_map/all_gather | solution.py:747
  55.1 269.4 %all-gather.15.cloned.1.call-start = ((), (), s32[]{:S(2)}) async-start(), calls=%async_computation.11 | async-start | bytes 5898240 | tf_op jit(solution)/shard_map/all_gather | solution.py:809
  55.7 565.7 %reduce-scatter.7.cloned.1.call-start = ((), (), s32[]{:S(2)}) async-start(), calls=%async_computation.5 | async-start | bytes 2654208 | tf_op jit(solution)/shard_map/reduce_scatter | solution.py:801
  59.9 122.2 %copy-start.21 = (f32[1,1280]{1,0:T(1,128)}, f32[1,1280]{1,0:T(1,128)S(1)}, u32[]{:S(2)}) copy-start(f32[1,1280]{1,0:T(1,128)S(1)} %and_select_fusion.bias_ref) | copy-start | bytes 15364
  60.0 84.6 %copy-start.61 = (bf16[4,96]{1,0:T(4,128)(2,1)}, bf16[4,96]{1,0:T(4,128)(2,1)S(1)}, u32[]{:S(2)}) copy-start(bf16[4,96]{1,0:T(4,128)(2,1)S(1)} %fusion.132) | copy-start | bytes 2308
  162.2 244.0 %copy-start.67 = (pred[256]{0:T(512)(128)(4,1)}, pred[256]{0:T(512)(128)(4,1)S(1)}, u32[]{:S(2)}) copy-start(pred[256]{0:T(512)(128)(4,1)S(1)} %slice.422) | copy-start | bytes 772
  163.3 96.4 %copy-start.63 = (pred[160]{0:T(512)(128)(4,1)}, pred[160]{0:T(512)(128)(4,1)S(1)}, u32[]{:S(2)}) copy-start(pred[160]{0:T(512)(128)(4,1)S(1)} %reduce) | copy-start | bytes 484
  203.2 57.4 %copy-start.25 = (bf16[144,1536]{1,0:T(8,128)(2,1)S(1)}, bf16[144,1536]{1,0:T(8,128)(2,1)}, u32[]{:S(2)}) copy-start(bf16[144,1536]{1,0:T(8,128)(2,1)} %copy-done.24) | copy-start | bytes 1327108
  347.9 58.4 %copy-start.7 = (bf16[1280,192]{1,0:T(8,128)(2,1)S(1)}, bf16[1280,192]{1,0:T(8,128)(2,1)}, u32[]{:S(2)}) copy-start(bf16[1280,192]{1,0:T(8,128)(2,1)} %copy-done.6) | copy-start | bytes 1474564
  410.6 212.7 %reduce-scatter.5.cloned.1.call-start = ((), (), s32[]{:S(2)}) async-start(), calls=%async_computation.4 | async-start | bytes 4915200 | tf_op jit(solution)/shard_map/reduce_scatter | solution.py:754
  458.9 187.4 %reduce-scatter.9.cloned.1.call-start = ((), (), s32[]{:S(2)}) async-start(), calls=%async_computation.6 | async-start | bytes 5898240 | tf_op jit(solution)/shard_map/reduce_scatter | solution.py:754
  469.7 240.2 %reduce-scatter.11.cloned.1.call-start = ((), (), s32[]{:S(2)}) async-start(), calls=%async_computation.7 | async-start | bytes 5898240 | tf_op jit(solution)/shard_map/reduce_scatter | solution.py:816
  534.1 28.7 %copy-start.26 = (bf16[144,1536]{1,0:T(8,128)(2,1)S(1)}, bf16[144,1536]{1,0:T(8,128)(2,1)}, u32[]{:S(2)}) copy-start(bf16[144,1536]{1,0:T(8,128)(2,1)} %copy-done.24) | copy-start | bytes 1327108
  534.1 28.7 %copy-start.37 = (bf16[144,1536]{1,0:T(8,128)(2,1)S(1)}, bf16[144,1536]{1,0:T(8,128)(2,1)}, u32[]{:S(2)}) copy-start(bf16[144,1536]{1,0:T(8,128)(2,1)} %get-tuple-element.107) | copy-start | bytes 1327108
  534.1 28.7 %copy-start.50 = (bf16[16,1536]{1,0:T(8,128)(2,1)S(1)}, bf16[16,1536]{1,0:T(8,128)(2,1)}, u32[]{:S(2)}) copy-start(bf16[16,1536]{1,0:T(8,128)(2,1)} %copy-done.49) | copy-start | bytes 147460
  534.2 28.7 %copy-start.52 = (f32[1536]{0:T(1024)S(1)}, f32[1536]{0:T(1024)}, u32[]{:S(2)}) copy-start(f32[1536]{0:T(1024)} %copy-done.51) | copy-start | bytes 18436
  534.2 28.7 %copy-start.54 = (f32[1536]{0:T(1024)S(1)}, f32[1536]{0:T(1024)}, u32[]{:S(2)}) copy-start(f32[1536]{0:T(1024)} %copy-done.53) | copy-start | bytes 18436
  534.2 28.7 %copy-start.58 = (f32[1536]{0:T(1024)S(1)}, f32[1536]{0:T(1024)}, u32[]{:S(2)}) copy-start(f32[1536]{0:T(1024)} %copy-done.57) | copy-start | bytes 18436
  534.2 28.7 %copy-start.60 = (f32[1536]{0:T(1024)S(1)}, f32[1536]{0:T(1024)}, u32[]{:S(2)}) copy-start(f32[1536]{0:T(1024)} %copy-done.59) | copy-start | bytes 18436
  567.1 49.3 %copy-start.62 = (bf16[4,96]{1,0:T(4,128)(2,1)S(1)}, bf16[4,96]{1,0:T(4,128)(2,1)}, u32[]{:S(2)}) copy-start(bf16[4,96]{1,0:T(4,128)(2,1)} %copy-done.61) | copy-start | bytes 2308
  583.1 35.8 %copy-start.56 = (bf16[4,1536]{1,0:T(4,128)(2,1)S(1)}, bf16[4,1536]{1,0:T(4,128)(2,1)}, u32[]{:S(2)}) copy-start(bf16[4,1536]{1,0:T(4,128)(2,1)} %param.10) | copy-start | bytes 36868
  (64 other events, 389.7 us)
Sparse Core Ops, SparseCore 0:
  30.6 82.5 all-gather.8
  114.8 30.2 all-gather.10
  146.6 88.5 all-gather.12
  236.6 87.8 all-gather.14
  410.7 33.9 reduce-scatter.6
  459.0 70.5 reduce-scatter.4
  531.9 89.8 reduce-scatter.8
  624.1 85.7 reduce-scatter.10

commit v2 on v1

--- a/solution.py
+++ b/solution.py
@@ -479,9 +479,19 @@
     return token_window, grad_window, mods.transpose(1, 0, 2, 3).reshape(2, -1)
 
 
-def swap_kernel(plan, source, target, send, recv):
-    seq, rank = here(plan)
-    meet(group_devices(plan, seq, rank))
+def project_columns(plan, rank):
+    share = plan.width // plan.group
+    first = (rank % 2) * (plan.width // 2) + (rank // 2) * share
+    return [part * plan.width + first for part in range(3)], share
+
+
+def up_columns(plan, rank, cols):
+    planes = plan.sequences // 2
+    share = cols // planes // plan.group
+    return [plane * plan.group * share + rank * share for plane in range(planes)], share
+
+
+def start_swap(plan, seq, rank, source, target, send, recv):
     copies = []
     for step in range(1, plan.group):
         to = other(rank, step, plan.group)
@@ -489,18 +499,60 @@
         copy.start()
         copies.append(copy)
     target[rank] = source[rank]
+    return copies
+
+
+def swap_in_kernel(plan, project, up, project_out, up_out, project_cut, up_cut, p_send, p_recv, u_send, u_recv):
+    seq, rank = here(plan)
+    for to in range(plan.group):
+        starts, share = project_columns(plan, to)
+        project_cut[to] = jnp.concatenate([project[:, c : c + share] for c in starts], axis=1)
+    meet(group_devices(plan, seq, rank))
+    copies = start_swap(plan, seq, rank, project_cut, project_out, p_send, p_recv)
+    for to in range(plan.group):
+        starts, share = up_columns(plan, to, up.shape[1])
+        up_cut[to] = jnp.concatenate([up[:, c : c + share] for c in starts], axis=1)
+    copies += start_swap(plan, seq, rank, up_cut, up_out, u_send, u_recv)
     for copy in copies:
         copy.wait()
 
 
-def swap(plan, pieces, ident):
+def swap_in(plan, project, up):
+    rows = project.shape[0]
     dma = pltpu.SemaphoreType.DMA
+    shapes = [(plan.group, rows, project.shape[1] // plan.group), (plan.group, rows, up.shape[1] // plan.group)]
     return call(
-        functools.partial(swap_kernel, plan),
-        "swap_%d" % ident,
+        functools.partial(swap_in_kernel, plan),
+        "swap_in",
+        4,
+        tuple(jax.ShapeDtypeStruct(shape, BF16) for shape in shapes),
+        [pltpu.VMEM(shape, BF16) for shape in shapes] + [dma((plan.group,))] * 4,
+        (project, up),
+    )
+
+
+def swap_out_kernel(plan, columns, pieces, out, got, send, recv):
+    seq, rank = here(plan)
+    meet(group_devices(plan, seq, rank))
+    copies = start_swap(plan, seq, rank, pieces, got, send, recv)
+    for copy in copies:
+        copy.wait()
+    for source in range(plan.group):
+        starts, share = columns(plan, source)
+        piece = got[source].astype(F32)
+        for i, c in enumerate(starts):
+            out[:, c : c + share] = piece[:, i * share : (i + 1) * share]
+
+
+def swap_out(plan, pieces, columns, name, ident):
+    dma = pltpu.SemaphoreType.DMA
+    group, rows, cols = pieces.shape
+    return call(
+        functools.partial(swap_out_kernel, plan, columns),
+        name,
         ident,
-        jax.ShapeDtypeStruct(pieces.shape, pieces.dtype),
-        [dma((plan.group,)), dma((plan.group,))],
+        jax.ShapeDtypeStruct((rows, group * cols), F32),
+        [pltpu.VMEM(pieces.shape, BF16), dma((plan.group,)), dma((plan.group,))],
         (pieces,),
     )
 
@@ -574,122 +626,155 @@
     )
 
 
-def sum_kernel(plan, part, out, *scratch):
-    seq, rank = here(plan)
-    meet(group_devices(plan, seq, rank))
-    out[...] = scatter_sum(plan, seq, rank, part, *scratch)
-
-
-def sum_rows(plan, part, ident):
-    return call(
-        functools.partial(sum_kernel, plan), "sum_%d" % ident, ident, own_shape(plan), sum_scratch(plan), (part,)
-    )
-
-
-def edge_kernel(plan, own, extra, send, recv):
+def edge_copy(plan, seq, source, first_row, target, send, recv, index):
+    from_rank, row, rows, step, owner, owner_row = plan.segments[index]
+    return remote(
+        source.at[pl.ds(first_row + row, rows)],
+        target.at[pl.ds(owner_row, rows)],
+        send.at[index],
+        recv.at[index],
+        plan.device_of(lax.rem(seq + plan.sequences + step, plan.sequences), owner),
+    )
+
+
+def start_edges(plan, seq, rank, *refs):
+    for index, segment in enumerate(plan.segments):
+        @pl.when(rank == segment[0])
+        def _():
+            edge_copy(plan, seq, *refs, index).start()
+
+
+def finish_edges(plan, seq, rank, *refs):
+    for index, segment in enumerate(plan.segments):
+        @pl.when(rank == segment[4])
+        def _():
+            edge_copy(plan, seq, *refs, index).wait_recv()
+
+        @pl.when(rank == segment[0])
+        def _():
+            edge_copy(plan, seq, *refs, index).wait_send()
+
+
+def edge_scratch(plan):
+    return [pltpu.SemaphoreType.DMA((len(plan.segments),))] * 2
+
+
+def output_kernel(plan, part, middle, gate_b, text, lowered, out, extra, own, *scratch):
     device = lax.axis_index("dev")
     seq, rank = plan.place_of(device)
     extra[...] = jnp.zeros_like(extra)
     meet(every_device(plan, device))
-
-    def copy(index):
-        from_rank, row, rows, step, owner, owner_row = plan.segments[index]
-        return remote(
-            own.at[pl.ds(plan.rows_dev + row, rows)],
-            extra.at[pl.ds(owner_row, rows)],
-            send.at[index],
-            recv.at[index],
-            plan.device_of(lax.rem(seq + plan.sequences + step, plan.sequences), owner),
-        )
-
-    for index, segment in enumerate(plan.segments):
-        @pl.when(rank == segment[0])
-        def _():
-            copy(index).start()
-    for index, segment in enumerate(plan.segments):
-        @pl.when(rank == segment[4])
-        def _():
-            copy(index).wait_recv()
-
-        @pl.when(rank == segment[0])
-        def _():
-            copy(index).wait_send()
-
-
-def to_packed(plan, own, foreign, ident):
-    dma = pltpu.SemaphoreType.DMA
-    extra = call(
-        functools.partial(edge_kernel, plan),
-        "edges_%d" % ident,
-        ident,
-        jax.ShapeDtypeStruct((plan.rows_dev, plan.width), own.dtype),
-        [dma((len(plan.segments),)), dma((len(plan.segments),))],
-        (own,),
-    )
-    return jnp.where(foreign[:, None], extra, own[: plan.rows_dev])
-
-
-def table_kernel(plan, local, table, first, second, mine, send, recv):
+    total = scatter_sum(plan, seq, rank, part, *scratch[:7])
+    lowered[...] = total
+    own[...] = (middle[...] + pick_rows(gate_b[...], text[...]) * total).astype(BF16)
+    refs = (own, plan.rows_dev, extra) + scratch[7:]
+    start_edges(plan, seq, rank, *refs)
+    out[...] = own[pl.ds(0, plan.rows_dev)]
+    finish_edges(plan, seq, rank, *refs)
+
+
+def output_rows(plan, part, middle, gate_b, text):
+    rows = jax.ShapeDtypeStruct((plan.rows_dev, plan.width), BF16)
+    return call(
+        functools.partial(output_kernel, plan),
+        "output",
+        8,
+        (own_shape(plan), rows, rows),
+        [pltpu.VMEM((plan.own, plan.width), BF16)] + sum_scratch(plan) + edge_scratch(plan),
+        (part, middle, gate_b, text),
+    )
+
+
+def stream_sums(values, masks):
+    return jnp.concatenate([jnp.sum(values * mask, axis=0, keepdims=True) for mask in masks], axis=0)
+
+
+def last_kernel(plan, part, tokens, grad_middle, scale_a, text, masks, rest, out, extra, table,
+                own, local, first, second, mine, t_send, t_recv, *scratch):
     device = lax.axis_index("dev")
     seq, rank = plan.place_of(device)
     stream = lax.div(2 * seq, plan.sequences)
+    extra[...] = jnp.zeros_like(extra)
     meet(every_device(plan, device))
+    total = scatter_sum(plan, seq, rank, part, *scratch[:7])
+    normed, inv = norm_rows(tokens[...].astype(F32))
+    streams = (masks[:, 0:1], masks[:, 1:2])
+    local[:, : plan.width] = stream_sums(total, streams)
+    local[:, plan.width : 2 * plan.width] = stream_sums(total * normed, streams)
+    local[:, 2 * plan.width :] = rest[...]
+    cols = 6 * plan.width // plan.group
+
+    def chunk(index):
+        return pl.ds(pl.multiple_of(index * cols, 128), cols)
+
     hops = []
     for step in range(1, plan.group):
         to = other(rank, step, plan.group)
-        copy = remote(local.at[to], first.at[step], send.at[0, step], recv.at[0, step], plan.device_of(seq, to))
+        copy = remote(local.at[:, chunk(to)], first.at[step], t_send.at[0, step], t_recv.at[0, step], plan.device_of(seq, to))
         copy.start()
         hops.append(copy)
+    inner = total * (1.0 + pick_rows(scale_a[...], text[...]))
+    mean_grad = jnp.mean(inner, axis=1, keepdims=True)
+    mean_cross = jnp.mean(inner * normed, axis=1, keepdims=True)
+    own[...] = grad_middle[...] + inv * (inner - mean_grad - normed * mean_cross)
+    refs = (own, plan.rows_dev, extra) + scratch[7:]
+    start_edges(plan, seq, rank, *refs)
     for copy in hops:
         copy.wait_recv()
-    total = local[rank]
+    sums = local[:, chunk(rank)]
     for step in range(1, plan.group):
-        total = total + first[step]
-    first[0] = total
+        sums = sums + first[step]
+    for i in range(2):
+        mine[i] = sums[i : i + 1]
     across = []
     for step in range(1, plan.sequences):
         to = other(seq, step, plan.sequences)
         to_stream = lax.div(2 * to, plan.sequences)
-        copy = remote(first.at[0, to_stream], second.at[seq], send.at[1, step], recv.at[1, step], plan.device_of(to, rank))
+        copy = remote(mine.at[to_stream], second.at[seq], t_send.at[1, step], t_recv.at[1, step], plan.device_of(to, rank))
         copy.start()
         across.append(copy)
-    second[seq] = first[0, stream]
+    second[seq] = mine[stream]
+    out[...] = own[pl.ds(0, plan.rows_dev)]
     for copy in across:
         copy.wait_recv()
-    mine[...] = second[...]
     last = []
     for step in range(1, plan.group):
         to = other(rank, step, plan.group)
-        copy = remote(mine, table.at[rank], send.at[2, step], recv.at[2, step], plan.device_of(seq, to))
+        copy = remote(second, table.at[rank], t_send.at[2, step], t_recv.at[2, step], plan.device_of(seq, to))
         copy.start()
         last.append(copy)
-    table[rank] = mine[...]
+    table[rank] = second[...]
     for copy in last:
         copy.wait_recv()
     for copy in hops + across + last:
         copy.wait_send()
-
-
-def stream_table(plan, local, ident):
-    lanes = local.shape[1] // plan.group // 128
-    pieces = local.reshape(2, plan.group, lanes, 128).transpose(1, 0, 2, 3)
+    finish_edges(plan, seq, rank, *refs)
+
+
+def last_rows(plan, part, tokens, grad_middle, scale_a, text, masks, rest):
+    rows = jax.ShapeDtypeStruct((plan.rows_dev, plan.width), F32)
+    cols = 6 * plan.width // plan.group
     dma = pltpu.SemaphoreType.DMA
     most = max(plan.group, plan.sequences)
-    table = call(
-        functools.partial(table_kernel, plan),
-        "mod_table",
-        ident,
-        jax.ShapeDtypeStruct((plan.group, plan.sequences, lanes, 128), F32),
+    out, extra, table = call(
+        functools.partial(last_kernel, plan),
+        "last",
+        10,
+        (rows, rows, jax.ShapeDtypeStruct((plan.group, plan.sequences, 1, cols), F32)),
         [
-            pltpu.VMEM((plan.group, 2, lanes, 128), F32),
-            pltpu.VMEM((plan.sequences, lanes, 128), F32),
-            pltpu.VMEM((plan.sequences, lanes, 128), F32),
+            pltpu.VMEM((plan.own, plan.width), F32),
+            pltpu.VMEM((2, 6 * plan.width), F32),
+            pltpu.VMEM((plan.group, 2, cols), F32),
+            pltpu.VMEM((plan.sequences, 1, cols), F32),
+            pltpu.VMEM((2, 1, cols), F32),
             dma((3, most)),
             dma((3, most)),
-        ],
-        (pieces,),
-    )
-    return table.transpose(1, 0, 2, 3).reshape(plan.sequences, -1)
+        ]
+        + sum_scratch(plan)
+        + edge_scratch(plan),
+        (part, tokens, grad_middle, scale_a, text, masks, rest),
+    )
+    return out, extra, table[:, :, 0].transpose(1, 0, 2).reshape(plan.sequences, -1)
 
 
 def spread_kernel(plan, piece, everyone, send, recv):
@@ -730,43 +815,17 @@
     )
 
 
-def project_slices(plan, weight):
-    rows, share = weight.shape[0], plan.width // plan.group
-    view = weight.reshape(rows, 3, 2, plan.group // 2, share).transpose(3, 2, 0, 1, 4)
-    got = swap(plan, view.reshape(plan.group, rows, 3 * share), 4)
-    got = lax.all_gather(got, "dev", axis=0, axis_index_groups=plan.rank_groups())
-    return got.reshape(2, plan.width, 3 * share)
-
-
-def up_slices(plan, weight):
-    rows, cols = weight.shape
-    planes = plan.sequences // 2
-    share = cols // planes // plan.group
-    view = weight.reshape(rows, planes, plan.group, share).transpose(2, 0, 1, 3)
-    got = swap(plan, view.reshape(plan.group, rows, planes * share), 5)
-    got = lax.all_gather(got, "dev", axis=0, axis_index_groups=plan.rank_groups())
-    return got.reshape(2, plan.width, planes * share)
-
-
-def sum_to_owners(plan, grad, rows, ident):
-    cols = grad.shape[2]
-    pieces = grad.astype(BF16).reshape(plan.sequences, plan.group, rows, cols)
-    got = lax.psum_scatter(pieces, "dev", scatter_dimension=0, axis_index_groups=plan.rank_groups())
-    return swap(plan, got, ident)
-
-
-def project_grads(plan, grad, rows):
-    share = plan.width // plan.group
-    got = sum_to_owners(plan, grad, rows, 6)
-    got = got.reshape(plan.group // 2, 2, rows, 3, share).transpose(2, 3, 1, 0, 4)
-    return got.reshape(rows, -1).astype(F32)
-
-
-def up_grads(plan, grad, rows):
-    planes = plan.sequences // 2
-    got = sum_to_owners(plan, grad, rows, 7)
-    got = got.reshape(plan.group, rows, planes, -1).transpose(1, 2, 0, 3)
-    return got.reshape(rows, -1).astype(F32)
+def over_sequences(plan, pieces):
+    full = lax.all_gather(pieces, "dev", axis=0, axis_index_groups=plan.rank_groups())
+    return full.reshape(2, plan.width, pieces.shape[2])
+
+
+def terms_to_send(plan, grad, rows):
+    return grad.astype(BF16).reshape(plan.sequences, plan.group, rows, grad.shape[2])
+
+
+def over_sequences_sum(plan, pieces):
+    return lax.psum_scatter(pieces, "dev", scatter_dimension=0, axis_index_groups=plan.rank_groups())
 
 
 def chip_groups(plan):
@@ -808,12 +867,6 @@
 def down_slices(plan, weight):
     full = lax.all_gather(weight, "dev", axis=0, axis_index_groups=plan.rank_groups())
     return full.reshape(2, -1, weight.shape[1])
-
-
-def down_grads(plan, grad):
-    cols = grad.shape[2]
-    pieces = grad.astype(BF16).reshape(plan.sequences, -1, cols)
-    return lax.psum_scatter(pieces, "dev", scatter_dimension=0, axis_index_groups=plan.rank_groups()).astype(F32)
 
 
 def by_stream(plan, image_part, text_part, is_text):
@@ -882,8 +935,10 @@
     mod_part = jnp.dot(silu_part, modulation_weight, preferred_element_type=F32)
 
     merge_pair = merge_slices(plan, merge_weight, rank)
-    project_pair = project_slices(plan, project_weight)
-    up_pair = up_slices(plan, up_weight)
+    project_pieces, up_pieces = swap_in(plan, project_weight, up_weight)
+    project_pieces, up_pieces, merge_pair = lax.optimization_barrier((project_pieces, up_pieces, merge_pair))
+    project_pair = over_sequences(plan, project_pieces)
+    up_pair = over_sequences(plan, up_pieces)
     down_pair = down_slices(plan, down_weight)
 
     token_window, grad_window, mods = entry(plan, tokens, cotangent, mod_part)
@@ -908,41 +963,57 @@
     upper = stream_dot(plan, hidden_b, up_pair, is_text)
     activated = jax.nn.gelu(upper, approximate=True).astype(BF16)
     grad_lowered = (pick(gate_b, is_text) * grad_window.astype(F32)).astype(BF16)
-    down_term = weight_terms(plan, activated, grad_lowered, is_text)
-    down_grad = down_grads(plan, down_term)
+    down_term = weight_terms(plan, activated, grad_lowered, is_text).astype(BF16)
+    down_term = down_term.reshape(plan.sequences, -1, width)
+    down_term, grad_lowered = lax.optimization_barrier((down_term, grad_lowered))
+    down_sum = over_sequences_sum(plan, down_term)
     grad_activated = stream_dot_back(plan, grad_lowered, down_pair, is_text)
     gelu_pull = jax.vjp(lambda value_in: jax.nn.gelu(value_in, approximate=True), upper)[1]
     grad_upper = gelu_pull(grad_activated)[0].astype(BF16)
-    up_term = weight_terms(plan, hidden_b, grad_upper, is_text)
-    up_grad = up_grads(plan, up_term, mod_rows)
+    up_term = terms_to_send(plan, weight_terms(plan, hidden_b, grad_upper, is_text), mod_rows)
+    back_part = stream_dot_back(plan, grad_upper, up_pair, is_text)
+    back_part, up_term = lax.optimization_barrier((back_part, up_term))
+    up_sum = over_sequences_sum(plan, up_term)
     grad_hidden_b, grad_middle, grad_merged = back_rows(
-        plan, stream_dot_back(plan, grad_upper, up_pair, is_text), own_grad, middle, gate_a, scale_b, text_mask
-    )
-    lowered = sum_rows(plan, stream_dot(plan, activated, down_pair, is_text), 8)
-    foreign = row_seq != seq
-    layer_out = to_packed(plan, (middle + pick(gate_b, own_text) * lowered).astype(BF16), foreign, 9)
-    grad_gate_b = own_grad.astype(F32) * lowered
-    grad_scale_b = grad_hidden_b * normed_b
-    grad_gate_a = grad_middle * merged
+        plan, back_part, own_grad, middle, gate_a, scale_b, text_mask
+    )
+    foreign = (row_seq != seq)[:, None]
+    lowered, out_here, out_there = output_rows(
+        plan, stream_dot(plan, activated, down_pair, is_text), middle, gate_b, text_mask
+    )
+    layer_out = jnp.where(foreign, out_there, out_here)
     grad_attended = stream_dot_back(plan, grad_merged, merge_pair, is_text).astype(BF16)
     merge_grad = merge_grads(plan, weight_terms(plan, attended, grad_merged, is_text), rank)
 
     grad_projected = jnp.concatenate(attend_back(plan, queries, keys, values, grad_attended, bias), axis=1)
-    project_grad = project_grads(plan, weight_terms(plan, hidden_a, grad_projected, is_text), mod_rows)
-    grad_hidden_a = sum_rows(plan, stream_dot_back(plan, grad_projected, project_pair, is_text), 10)
-
-    normed_a, inv_a = layer_norm(own_tokens.astype(F32))
-    grad_scale_a = grad_hidden_a * normed_a
-    own_back = grad_middle + norm_back(grad_hidden_a * (1.0 + pick(scale_a, own_text)), normed_a, inv_a)
-    tokens_grad = to_packed(plan, own_back, foreign, 11)
-
-    rows_of = jnp.stack([own_valid & ~own_text, own_valid & own_text]).astype(F32)
-    sums = [
-        jnp.stack([jnp.sum(jnp.where(own[:, None] > 0, part, 0.0), axis=0) for own in rows_of])
-        for part in (grad_hidden_a, grad_scale_a, grad_gate_a, grad_hidden_b, grad_scale_b, grad_gate_b)
-    ]
-    local_mods = jnp.concatenate(sums, axis=1)
-    own_grads = stream_table(plan, local_mods, 12).astype(BF16)
+    grad_projected, down_sum = lax.optimization_barrier((grad_projected, down_sum))
+    down_grad = down_sum.astype(F32)
+    project_term = terms_to_send(plan, weight_terms(plan, hidden_a, grad_projected, is_text), mod_rows)
+    last_part = stream_dot_back(plan, grad_projected, project_pair, is_text)
+    last_part, project_term = lax.optimization_barrier((last_part, project_term))
+    project_sum = over_sequences_sum(plan, project_term)
+
+    masks = jnp.stack([own_valid & ~own_text, own_valid & own_text], axis=1).astype(F32)
+    rest = jnp.concatenate(
+        [
+            jnp.stack([jnp.sum(value * masks[:, j : j + 1], axis=0) for j in range(2)])
+            for value in (
+                grad_middle * merged,
+                grad_hidden_b,
+                grad_hidden_b * normed_b,
+                own_grad.astype(F32) * lowered,
+            )
+        ],
+        axis=1,
+    )
+    rest, up_sum = lax.optimization_barrier((rest, up_sum))
+    back_here, back_there, grad_table = last_rows(
+        plan, last_part, own_tokens, grad_middle, scale_a, text_mask, masks, rest
+    )
+    tokens_grad = jnp.where(foreign, back_there, back_here)
+    own_grads = grad_table.astype(BF16)
+    up_grad = swap_out(plan, up_sum, lambda p, r: up_columns(p, r, up_weight.shape[1]), "up_out", 7)
+    project_grad = swap_out(plan, project_sum, project_columns, "project_out", 6)
     modulation_grad = lax.dot_general(silu_part, own_grads, CONTRACT_FIRST, preferred_element_type=F32)
     grad_piece = lax.dot_general(own_grads, modulation_weight, CONTRACT_LAST, preferred_element_type=F32)
     everyone = spread(plan, grad_piece.reshape(-1, 128), 13)

time: 728 us -> 648 us (0.89)
  waiting for transfers between devices: 92.5 us -> 37 us
  Pallas kernels: 397 us -> 376 us
  other arithmetic: 56.1 us -> 68 us
  local copies, waits for them, and re-layouts: 92 us -> 84 us
    reduce_scatter x3, waiting for transfers between devices: 37.9 us -> 0.04 us  [over_sequences_sum(): lax.psum_scatter(pieces, 'dev', scatter_dimension=0, axis_index_groups=pl...]
    all_gather x1, waiting for transfers between devices: 53.3 us -> 30.2 us  [down_slices(): lax.all_gather(weight, 'dev', axis=0, axis_index_groups=plan.rank_groups())]
    pallas_call x13 -> x9, Pallas kernels: 363 us -> 341 us  [call(): pl.pallas_call(kernel, out_shape=out_shape, in_specs=in_specs or [VMEM] *...]
    convert_element_type x7 -> x1, local copies, waits for them, and re-layouts: 15.7 us -> 0.01 us  [on_device(): own_grads = grad_table.astype(BF16)]
    reshape x7 -> x0, local copies, waits for them, and re-layouts: 12.2 us -> none  [the longest x2 5.42 us: project_slices(): weight.reshape(rows, 3, 2, plan.group // 2, share).transpose(3, 2, 0, 1, 4)]
    unnamed x166 -> x189, local copies, waits for them, and re-layouts: 37.9 us -> 48 us
    concatenate x6, other arithmetic: 9.57 us -> 19.2 us  [by_stream(): jnp.concatenate([image_part[:start], mixed, text_part[end - start:]], axi...]
  transfers between devices with their start and end apart: 8 -> 8, of which waited for: 2 -> 2; matrix products, arithmetic and copies ran while one was open for 21% -> 26% of each run, Pallas kernels for 45% -> 56%
where the time goes in v2:
time: 648 us; the launch traced here: 642 us
  Pallas kernels  376 us (58%)
  local copies, waits for them, and re-layouts  84 us (13%)
  other arithmetic  68 us (10%)
  matrix products  60.3 us (9%)
  waiting for transfers between devices  37 us (6%)
  between operations  16.5 us (3%)
    pallas_call x9, Pallas kernels, call(): pl.pallas_call(kernel, out_shape=out_shape, in_specs=in_specs or [VMEM] *...  341 us
    unnamed x189, local copies, waits for them, and re-layouts  48 us
    all_gather x1, waiting for transfers between devices, down_slices(): lax.all_gather(weight, 'dev', axis=0, axis_index_groups=plan.rank_groups())  30.2 us
    pallas_call x1, Pallas kernels, attend_back(): pl.pallas_call(functools.partial(attend_back_kernel, plan.heads, rows //...  21.9 us
    concatenate x6, other arithmetic, by_stream(): jnp.concatenate([image_part[:start], mixed, text_part[end - start:]], axi...  19.2 us
    dot_general x4, matrix products, stream_dot_back(): lax.dot_general(grads[:plan.image_end], pair[0], CONTRACT_LAST, preferred...  17.1 us
    dot_general x4, matrix products, stream_dot(): jnp.dot(rows[:plan.image_end], pair[0], preferred_element_type=F32)  14.5 us
    slice x9, local copies, waits for them, and re-layouts, by_stream(): image_part[:start]  13.8 us
  transfers between devices with their start and end apart: 8, of which 2 were waited for; matrix products, arithmetic and copies ran while one was open for 26% of the time, Pallas kernels for 56%

profile of v2, /device:TPU:0, one launch (start us, length us, event | category | flops | bytes accessed | tf_op | source)
XLA Modules:
  0.0 641.9 jit_solution(14836370290762184017)
XLA Ops:
  10.4 29.5 %swap_in.1 = (bf16[8,96,576]{2,1,0:T(8,128)(2,1)}, bf16[8,96,768]{2,1,0:T(8,128)(2,1)}) custom-call(bf16[96,4608]{1,0:T(8,128)(2,1)S(1)} %copy-done.24, bf16[96,6144]{1,0:T(8,128)(2,1)S(1)} %copy-done.16), custom_call_target="tpu_custom_call" | custom-call | tf_op jit(solution)/shard_map/swap_in/pallas_call | solution.py:235
  39.9 4.1 all-gather.9.cloned.1.call-done
  53.1 77.9 %entry.1 = (bf16[1280,1536]{1,0:T(8,128)(2,1)S(1)}, bf16[1280,1536]{1,0:T(8,128)(2,1)S(1)}, f32[8,2,9,128]{3,2,1,0:T(8,128)S(1)}) custom-call(bf16[144,1536]{1,0:T(8,128)(2,1)S(1)} %copy-done.28, bf16[144,1536]{1,0:T(8,128)(2,1)S(1)} %copy-done.29, f32[8,4,9,128]{3,2,1,0:T(8,128)S(1)} %bitcast.81), custom_call_target="tpu_custom_call" | custom-call | tf_op jit(solution)/shard_map/entry/pallas_call | solution.py:235
  140.4 9.7 %multiply_convert_fusion = (bf16[1280,1536]{1,0:T(8,128)(2,1)}, bf16[1280,1536]{1,0:T(8,128)(2,1)S(1)}, bf16[1280,1536]{1,0:T(8,128)(2,1)}) fusion(f32[1536]{0:T(1024)S(1)} %get-tuple-element.83, f32[1536]{0:T(1024)S(1)} %get-tuple-element.82, pred[1280]{0:T(1024)(128)(4,1)S(1)} %fusion.121, bf16[1280,1536]{1,0:T(8,128)(2,1)} %copy-done.6, ...), kind=kLoop, calls=%fused_computation.12 | loop fusion | flops 27525120 | bytes 19710464 | tf_op jit(solution)/shard_map/convert_element_type | solution.py:965
  155.1 3.8 fusion.135
  162.4 5.1 fusion.23
  175.7 12.3 %attend.1 = bf16[1280,192]{1,0:T(8,128)(2,1)S(1)} custom-call(bf16[1280,192]{1,0:T(8,128)(2,1)S(1)} %get-tuple-element.106.q_ref, bf16[1280,192]{1,0:T(8,128)(2,1)S(1)} %get-tuple-element.105.k_ref, bf16[1280,192]{1,0:T(8,128)(2,1)S(1)} %get-tuple-element.104.v_ref, f32[1,1280]{1,0:T(1,128)S(1)} %and_select_fusion.bias_ref), custom_call_target="tpu_custom_call" | custom-call | flops 5033164800 | bytes 1966080 | tf_op jit(solution)/shard_map/attend/pallas_call | solution.py:118
  192.8 4.0 pad_maximum_fusion.part
  196.8 54.4 %middle.1 = (f32[160,1536]{1,0:T(8,128)S(1)}, bf16[1280,1536]{1,0:T(8,128)(2,1)S(1)}) custom-call(f32[1280,1536]{1,0:T(8,128)S(1)} %pad_maximum_fusion.part, bf16[160,1536]{1,0:T(8,128)(2,1)S(1)} %pad_maximum_fusion.14.tokens, f32[2,1536]{1,0:T(2,128)S(1)} %get-tuple-element.127.gate_a, f32[2,1536]{1,0:T(2,128)S(1)} %get-tuple-element.126.scale_b, ...), custom_call_target="tpu_custom_call" | custom-call | tf_op jit(solution)/shard_map/middle/pallas_call | solution.py:235
  275.0 30.2 %all-gather.15.cloned.1.call-done = bf16[1536,1536]{1,0:T(8,128)(2,1)} async-done(((bf16[384,1536]{1,0:T(8,128)(2,1)}), bf16[1536,1536]{1,0:T(8,128)(2,1)}) %all-gather.15.cloned.1.call-update) | async-done | bytes 4718608 | tf_op jit(solution)/shard_map/all_gather | solution.py:868
  305.2 5.7 fusion.16
  332.8 3.9 pad_maximum_fusion.2.part
  337.7 58.5 %back.1 = (f32[160,1536]{1,0:T(8,128)S(1)}, f32[160,1536]{1,0:T(8,128)S(1)}, bf16[1280,1536]{1,0:T(8,128)(2,1)S(1)}) custom-call(f32[1280,1536]{1,0:T(8,128)} %pad_maximum_fusion.2.part, bf16[160,1536]{1,0:T(8,128)(2,1)S(1)} %copy-done.12, f32[160,1536]{1,0:T(8,128)S(1)} %get-tuple-element.95.middle, f32[2,1536]{1,0:T(2,128)S(1)} %get-tuple-element.127.gate_a, ...), custom_call_target="tpu_custom_call" | custom-call | tf_op jit(solution)/shard_map/back/pallas_call | solution.py:235
  416.0 21.9 %attend_back.1 = (bf16[1280,192]{1,0:T(8,128)(2,1)}, bf16[1280,192]{1,0:T(8,128)(2,1)}, bf16[1280,192]{1,0:T(8,128)(2,1)}) custom-call(bf16[1280,192]{1,0:T(8,128)(2,1)} %copy-done.27, bf16[1280,192]{1,0:T(8,128)(2,1)} %copy-done.26, bf16[1280,192]{1,0:T(8,128)(2,1)} %copy-done.25, bf16[1280,192]{1,0:T(8,128)(2,1)} %pad_maximum_fusion.13.g_ref, ...), custom_call_target="tpu_custom_call" | custom-call | flops 12582912000 | bytes 3440640 | tf_op jit(solution)/shard_map/attend_back/pallas_call | solution.py:173
  443.3 5.4 fusion.55
  448.7 5.0 fusion.70
  464.4 6.0 copy.104
  482.5 5.8 slice.394
  490.1 4.1 pad_maximum_fusion.1.part
  494.3 35.8 %output.1 = (f32[160,1536]{1,0:T(8,128)S(1)}, bf16[144,1536]{1,0:T(8,128)(2,1)S(1)}, bf16[144,1536]{1,0:T(8,128)(2,1)S(1)}) custom-call(f32[1280,1536]{1,0:T(8,128)S(1)} %pad_maximum_fusion.1.part, f32[160,1536]{1,0:T(8,128)S(1)} %get-tuple-element.95.middle, f32[2,1536]{1,0:T(2,128)S(1)} %get-tuple-element.128.gate_b, f32[160,1]{1,0:T(8,128)S(1)} %convert_element_type.101.text), custom_call_target="tpu_custom_call" | custom-call | tf_op jit(solution)/shard_map/output/pallas_call | solution.py:235
  535.9 45.2 %last.1 = (f32[144,1536]{1,0:T(8,128)S(1)}, f32[144,1536]{1,0:T(8,128)S(1)}, f32[8,4,1,1152]{3,2,1,0:T(1,128)S(1)}) custom-call(f32[1280,1536]{1,0:T(8,128)S(1)} %copy-done.3, bf16[160,1536]{1,0:T(8,128)(2,1)S(1)} %pad_maximum_fusion.14.tokens, f32[160,1536]{1,0:T(8,128)S(1)} %copy-done.11, f32[2,1536]{1,0:T(2,128)S(1)} %get-tuple-element.125.scale_a, ...), custom_call_target="tpu_custom_call" | custom-call | tf_op jit(solution)/shard_map/last/pallas_call | solution.py:235
  583.7 10.0 %spread.1 = f32[4,8,3,128]{3,2,1,0:T(4,128)S(1)} custom-call(f32[3,128]{1,0:T(4,128)S(1)} %reshape.340.piece), custom_call_target="tpu_custom_call" | custom-call | tf_op jit(solution)/shard_map/spread/pallas_call | solution.py:235
  594.0 15.8 %up_out.1 = f32[96,6144]{1,0:T(8,128)S(1)} custom-call(bf16[8,96,768]{2,1,0:T(8,128)(2,1)S(1)} %bitcast.80), custom_call_target="tpu_custom_call" | custom-call | tf_op jit(solution)/shard_map/up_out/pallas_call | solution.py:235
  618.0 14.3 %project_out.1 = f32[96,4608]{1,0:T(8,128)S(1)} custom-call(bf16[8,96,576]{2,1,0:T(8,128)(2,1)S(1)} %bitcast.82), custom_call_target="tpu_custom_call" | custom-call | tf_op jit(solution)/shard_map/project_out/pallas_call | solution.py:235
  (338 shorter events, 157.1 us)
Async XLA Ops:
  7.2 45.4 %copy-start = (bf16[96,9216]{1,0:T(8,128)(2,1)S(1)}, bf16[96,9216]{1,0:T(8,128)(2,1)}, u32[]{:S(2)}) copy-start(bf16[96,9216]{1,0:T(8,128)(2,1)} %param.12) | copy-start | bytes 5308420
  7.2 36.8 %all-gather.9.cloned.1.call-start = ((), (), s32[]{:S(2)}) async-start(), calls=%async_computation.8 | async-start | bytes 2654208 | tf_op jit(solution)/shard_map/all_gather | solution.py:843
  7.9 147.1 %all-gather.11.cloned.1.call-start = ((), (), s32[]{:S(2)}) async-start(), calls=%async_computation.9 | async-start | bytes 4915200 | tf_op jit(solution)/shard_map/all_gather | solution.py:819
  10.4 37.4 %copy-start.67 = (bf16[4,1536]{1,0:T(4,128)(2,1)S(1)}, bf16[4,1536]{1,0:T(4,128)(2,1)}, u32[]{:S(2)}) copy-start(bf16[4,1536]{1,0:T(4,128)(2,1)} %param.10) | copy-start | bytes 36868
  10.4 37.4 %copy-start.86 = (s32[4]{0:T(128)S(1)}, s32[4]{0:T(128)}, u32[]{:S(2)}) copy-start(s32[4]{0:T(128)} %param.11) | copy-start | bytes 52
  46.4 207.7 %all-gather.13.cloned.1.call-start = ((), (), s32[]{:S(2)}) async-start(), calls=%async_computation.10 | async-start | bytes 5898240 | tf_op jit(solution)/shard_map/all_gather | solution.py:819
  47.2 258.1 %all-gather.15.cloned.1.call-start = ((), (), s32[]{:S(2)}) async-start(), calls=%async_computation.11 | async-start | bytes 5898240 | tf_op jit(solution)/shard_map/all_gather | solution.py:868
  47.7 401.0 %reduce-scatter.5.cloned.1.call-start = ((), (), s32[]{:S(2)}) async-start(), calls=%async_computation.4 | async-start | bytes 5898240 | tf_op jit(solution)/shard_map/reduce_scatter | solution.py:828
  50.0 104.1 %copy-start.70 = (pred[1280]{0:T(1024)(128)(4,1)}, pred[1280]{0:T(1024)(128)(4,1)S(1)}, u32[]{:S(2)}) copy-start(pred[1280]{0:T(1024)(128)(4,1)S(1)} %fusion.121) | copy-start | bytes 3844
  52.5 123.1 %copy-start.37 = (f32[1,1280]{1,0:T(1,128)}, f32[1,1280]{1,0:T(1,128)S(1)}, u32[]{:S(2)}) copy-start(f32[1,1280]{1,0:T(1,128)S(1)} %and_select_fusion.bias_ref) | copy-start | bytes 15364
  52.6 82.3 %copy-start.74 = (bf16[4,96]{1,0:T(4,128)(2,1)}, bf16[4,96]{1,0:T(4,128)(2,1)S(1)}, u32[]{:S(2)}) copy-start(bf16[4,96]{1,0:T(4,128)(2,1)S(1)} %fusion.123) | copy-start | bytes 2308
  154.0 118.6 %copy-start.50 = (bf16[144,1536]{1,0:T(8,128)(2,1)}, bf16[144,1536]{1,0:T(8,128)(2,1)S(1)}, u32[]{:S(2)}) copy-start(bf16[144,1536]{1,0:T(8,128)(2,1)S(1)} %get-tuple-element.139) | copy-start | bytes 1327108
  271.9 216.4 %reduce-scatter.11.cloned.1.call-start = ((), (), s32[]{:S(2)}) async-start(), calls=%async_computation.7 | async-start | bytes 2654208 | tf_op jit(solution)/shard_map/reduce_scatter | solution.py:860
  337.7 58.5 %copy-start.14 = (bf16[1280,192]{1,0:T(8,128)(2,1)S(1)}, bf16[1280,192]{1,0:T(8,128)(2,1)}, u32[]{:S(2)}) copy-start(bf16[1280,192]{1,0:T(8,128)(2,1)} %copy-done.13) | copy-start | bytes 1474564
  400.5 130.9 %reduce-scatter.7.cloned.1.call-start = ((), (), s32[]{:S(2)}) async-start(), calls=%async_computation.5 | async-start | bytes 5898240 | tf_op jit(solution)/shard_map/reduce_scatter | solution.py:828
  401.3 215.4 %reduce-scatter.9.cloned.1.call-start = ((), (), s32[]{:S(2)}) async-start(), calls=%async_computation.6 | async-start | bytes 4915200 | tf_op jit(solution)/shard_map/reduce_scatter | solution.py:828
  413.8 27.6 %slice-start.1 = ((s8[4718592]{0:T(1024)(128)(4,1)}), s8[4194304]{0:T(1024)(128)(4,1)S(1)}, s32[]{:S(2)}) async-start(s8[4718592]{0:T(1024)(128)(4,1)} %bitcast.106), calls=%async_computation.13 | async-start | bytes 8388608
  416.0 25.4 %slice-start.2 = ((s8[4718592]{0:T(1024)(128)(4,1)}), s8[524288]{0:T(1024)(128)(4,1)S(1)}, s32[]{:S(2)}) async-start(s8[4718592]{0:T(1024)(128)(4,1)} %bitcast.106), calls=%async_computation.14 | async-start | bytes 1048576
  494.3 35.9 %copy-start.8 = (f32[160,1536]{1,0:T(8,128)S(1)}, f32[160,1536]{1,0:T(8,128)}, u32[]{:S(2)}) copy-start(f32[160,1536]{1,0:T(8,128)} %copy-done.7) | copy-start | bytes 2949124
  494.3 35.9 %copy-start.10 = (f32[160,1536]{1,0:T(8,128)S(1)}, f32[160,1536]{1,0:T(8,128)}, u32[]{:S(2)}) copy-start(f32[160,1536]{1,0:T(8,128)} %copy-done.9) | copy-start | bytes 2949124
  494.3 35.9 %copy-start.18 = (f32[160,1536]{1,0:T(8,128)S(1)}, f32[160,1536]{1,0:T(8,128)}, u32[]{:S(2)}) copy-start(f32[160,1536]{1,0:T(8,128)} %copy-done.17) | copy-start | bytes 2949124
  494.3 35.9 %copy-start.51 = (bf16[144,1536]{1,0:T(8,128)(2,1)S(1)}, bf16[144,1536]{1,0:T(8,128)(2,1)}, u32[]{:S(2)}) copy-start(bf16[144,1536]{1,0:T(8,128)(2,1)} %copy-done.50) | copy-start | bytes 1327108
  494.3 35.9 %copy-start.82 = (f32[160]{0:T(256)S(1)}, f32[160]{0:T(256)}, u32[]{:S(2)}) copy-start(f32[160]{0:T(256)} %get-tuple-element.81) | copy-start | bytes 1924
  594.0 17.6 %copy-start.75 = (bf16[4,96]{1,0:T(4,128)(2,1)S(1)}, bf16[4,96]{1,0:T(4,128)(2,1)}, u32[]{:S(2)}) copy-start(bf16[4,96]{1,0:T(4,128)(2,1)} %copy-done.74) | copy-start | bytes 2308
  (74 other events, 294.0 us)
Sparse Core Ops, SparseCore 0:
  9.7 34.3 all-gather.8
  46.5 80.0 all-gather.10
  128.2 87.7 all-gather.12
  217.3 87.8 all-gather.14
  307.4 83.6 reduce-scatter.4
  400.7 33.7 reduce-scatter.10
  436.8 84.5 reduce-scatter.6
  523.6 76.3 reduce-scatter.8

commit v3 on v2

--- a/solution.py
+++ b/solution.py
@@ -17,6 +17,7 @@
 F32 = jnp.float32
 BF16 = jnp.bfloat16
 CONTRACT_LAST = (((1,), (1,)), ((), ()))
+PLAIN = (((1,), (0,)), ((), ()))
 CONTRACT_FIRST = (((0,), (0,)), ((), ()))
 MASKED = -1e30
 
@@ -269,38 +270,46 @@
     half, own, width = plan.group // 2, plan.own, plan.width
     return [
         pltpu.VMEM((half, own, width), F32),
+        pltpu.VMEM((half, own, width), F32),
         pltpu.VMEM((half, own, width), BF16),
         pltpu.VMEM((half, own, width), BF16),
-        pltpu.SemaphoreType.DMA((half, 2)),
-        pltpu.SemaphoreType.DMA((half, 2)),
+        pltpu.SemaphoreType.DMA((half,)),
+        pltpu.SemaphoreType.DMA((half,)),
         pltpu.SemaphoreType.DMA((half,)),
         pltpu.SemaphoreType.DMA((half,)),
     ]
 
 
-def scatter_sum(plan, seq, rank, part, pair, going, coming, pair_send, pair_recv, far_send, far_recv):
+SUM_SCRATCH = 8
+
+
+def product(plan, rows, pair, text, dims, rank):
+    block = load_block(plan, rows, rank)
+    mask = load_block(plan, text, rank)
+    parts = [lax.dot_general(block, pair[j], dims, preferred_element_type=F32) for j in range(2)]
+    return jnp.where(mask > 0, parts[1], parts[0])
+
+
+def scatter_sum(plan, seq, rank, rows, pair, text, dims, away, near, going, coming, pair_send, pair_recv, far_send, far_recv):
     half = plan.group // 2
     chip, core = lax.div(rank, 2), lax.rem(rank, 2)
     partner = plan.device_of(seq, 2 * chip + 1 - core)
-    started = []
     order = list(range(1, half)) + [0]
-    for step in order:
+
+    def for_partner(step):
+        away[step] = product(plan, rows, pair, text, dims, 2 * other(chip, step, half) + 1 - core)
+        copy = remote(away.at[step], near.at[step], pair_send.at[step], pair_recv.at[step], partner)
+        copy.start()
+        return copy
+
+    pairs, sends = [for_partner(order[0])], []
+    for i, step in enumerate(order):
         chip_to = other(chip, step, half)
-        copies = [
-            remote(source, target, pair_send.at[step, i], pair_recv.at[step, i], partner)
-            for i, (source, target) in enumerate(
-                zip(block_parts(plan, part, 2 * chip_to + 1 - core), own_parts(plan, pair.at[step]))
-            )
-        ]
-        for copy in copies:
-            copy.start()
-        started.append(copies)
-    total, sends = None, []
-    for step, copies in zip(order, started):
-        for copy in copies:
-            copy.wait_recv()
-        chip_to = other(chip, step, half)
-        both = load_block(plan, part, 2 * chip_to + core) + pair[step]
+        mine = product(plan, rows, pair, text, dims, 2 * chip_to + core)
+        if i + 1 < half:
+            pairs.append(for_partner(order[i + 1]))
+        pairs[i].wait_recv()
+        both = mine + near[step]
         if step == 0:
             total = both
         else:
@@ -313,10 +322,7 @@
     for step, copy in zip(order, sends):
         copy.wait_recv()
         total = total + coming[step].astype(F32)
-    for copies in started:
-        for copy in copies:
-            copy.wait_send()
-    for copy in sends:
+    for copy in pairs + sends:
         copy.wait_send()
     return total
 
@@ -369,11 +375,30 @@
         copy.wait_send()
 
 
-def entry_kernel(plan, tokens, grads, mod_part, token_window, grad_window, mods, token_own, grad_own, plane, across,
-                 chunk, edge_send, edge_recv, t_send, t_recv, t_pass, g_send, g_recv, g_pass, m_send, m_recv):
+def entry_kernel(plan, tokens, grads, mod_part, *refs):
+    if plan.chip_heads:
+        merge, merge_out, *refs = refs[:1] + refs[4:5] + refs[1:4] + refs[5:]
+        merge_send, merge_recv, *refs = refs[-2:] + refs[:-2]
+    (token_window, grad_window, mods, token_own, grad_own, plane, across, chunk, edge_send, edge_recv,
+     t_send, t_recv, t_pass, g_send, g_recv, g_pass, m_send, m_recv) = refs
     device = lax.axis_index("dev")
     seq, rank = plan.place_of(device)
     meet(every_device(plan, device))
+    swaps = []
+    if plan.chip_heads:
+        core = lax.rem(rank, 2)
+        partner = plan.device_of(seq, 2 * lax.div(rank, 2) + 1 - core)
+        for stream in range(2):
+            copy = remote(
+                merge.at[2 * stream + 1 - core],
+                merge_out.at[stream, core],
+                merge_send.at[stream],
+                merge_recv.at[stream],
+                partner,
+            )
+            copy.start()
+            swaps.append(copy)
+            merge_out[stream, core] = merge[2 * stream + core]
     hops = []
     for step in range(1, plan.group):
         to = other(rank, step, plan.group)
@@ -438,6 +463,8 @@
         copy.wait_recv()
     for copy in hops + hops_across + hops_back:
         copy.wait_send()
+    for copy in swaps:
+        copy.wait()
     for which, (source, own) in enumerate(arrays):
         for index, (to_rank, row, rows, step, owner, owner_row) in enumerate(plan.segments):
             @pl.when(rank == owner)
@@ -451,17 +478,15 @@
                 ).wait_send()
 
 
-def entry(plan, tokens, grads, mod_part):
+def entry(plan, tokens, grads, mod_part, merge):
     lanes = mod_part.shape[1] // plan.group // 128
     pieces = mod_part.reshape(plan.sequences, plan.group, lanes, 128).transpose(1, 0, 2, 3)
     window = jax.ShapeDtypeStruct((plan.rows, plan.width), BF16)
     dma = pltpu.SemaphoreType.DMA
     most = max(plan.group, plan.sequences)
-    token_window, grad_window, mods = call(
-        functools.partial(entry_kernel, plan),
-        "entry",
-        1,
-        (window, window, jax.ShapeDtypeStruct((plan.group, 2, lanes, 128), F32)),
+    shapes = (window, window, jax.ShapeDtypeStruct((plan.group, 2, lanes, 128), F32))
+    operands = (tokens, grads, pieces)
+    scratch = (
         [
             pltpu.VMEM((plan.piece, plan.width), BF16),
             pltpu.VMEM((plan.piece, plan.width), BF16),
@@ -473,10 +498,17 @@
         ]
         + share_scratch(plan)
         + share_scratch(plan)
-        + [dma((3, most)), dma((3, most))],
-        (tokens, grads, pieces),
-    )
-    return token_window, grad_window, mods.transpose(1, 0, 2, 3).reshape(2, -1)
+        + [dma((3, most)), dma((3, most))]
+    )
+    if plan.chip_heads:
+        shapes += (jax.ShapeDtypeStruct((2, 2) + merge.shape[1:], BF16),)
+        operands += (merge,)
+        scratch += [dma((2,)), dma((2,))]
+    token_window, grad_window, mods, *rest = call(
+        functools.partial(entry_kernel, plan), "entry", 1, shapes, scratch, operands
+    )
+    merge_pair = rest[0].reshape(2, -1, plan.width) if plan.chip_heads else merge
+    return token_window, grad_window, mods.transpose(1, 0, 2, 3).reshape(2, -1), merge_pair
 
 
 def project_columns(plan, rank):
@@ -568,16 +600,16 @@
     return centred * inv, inv
 
 
-def middle_kernel(plan, part, tokens, gate_a, scale_b, shift_b, text, merged, window, own, *scratch):
+def middle_kernel(plan, rows, pair, window_text, tokens, gate_a, scale_b, shift_b, text, merged, window, own, *scratch):
     seq, rank = here(plan)
     meet(group_devices(plan, seq, rank))
-    total = scatter_sum(plan, seq, rank, part, *scratch[:7])
+    total = scatter_sum(plan, seq, rank, rows, pair, window_text, PLAIN, *scratch[:SUM_SCRATCH])
     merged[...] = total
     mask = text[...]
     middle = tokens[...].astype(F32) + pick_rows(gate_a[...], mask) * total
     normed, _ = norm_rows(middle)
     own[...] = (normed * (1.0 + pick_rows(scale_b[...], mask)) + pick_rows(shift_b[...], mask)).astype(BF16)
-    share_rows(plan, seq, rank, own_parts(plan, own), window, *scratch[7:])
+    share_rows(plan, seq, rank, own_parts(plan, own), window, *scratch[SUM_SCRATCH:])
 
 
 def own_shape(plan, dtype=F32):
@@ -588,21 +620,21 @@
     return jax.ShapeDtypeStruct((plan.rows, plan.width), BF16)
 
 
-def middle_rows(plan, part, tokens, gate_a, scale_b, shift_b, text):
+def middle_rows(plan, rows, pair, window_text, tokens, gate_a, scale_b, shift_b, text):
     return call(
         functools.partial(middle_kernel, plan),
         "middle",
         2,
         (own_shape(plan), window_shape(plan)),
         [pltpu.VMEM((plan.own, plan.width), BF16)] + sum_scratch(plan) + share_scratch(plan),
-        (part, tokens, gate_a, scale_b, shift_b, text),
-    )
-
-
-def back_kernel(plan, part, grad, middle, gate_a, scale_b, text, grad_hidden, grad_middle, window, own, *scratch):
+        (rows, pair, window_text, tokens, gate_a, scale_b, shift_b, text),
+    )
+
+
+def back_kernel(plan, rows, pair, window_text, grad, middle, gate_a, scale_b, text, grad_hidden, grad_middle, window, own, *scratch):
     seq, rank = here(plan)
     meet(group_devices(plan, seq, rank))
-    total = scatter_sum(plan, seq, rank, part, *scratch[:7])
+    total = scatter_sum(plan, seq, rank, rows, pair, window_text, CONTRACT_LAST, *scratch[:SUM_SCRATCH])
     grad_hidden[...] = total
     mask = text[...]
     normed, inv = norm_rows(middle[...])
@@ -612,17 +644,17 @@
     result = grad[...].astype(F32) + inv * (inner - mean_grad - normed * mean_cross)
     grad_middle[...] = result
     own[...] = (pick_rows(gate_a[...], mask) * result).astype(BF16)
-    share_rows(plan, seq, rank, own_parts(plan, own), window, *scratch[7:])
-
-
-def back_rows(plan, part, grad, middle, gate_a, scale_b, text):
+    share_rows(plan, seq, rank, own_parts(plan, own), window, *scratch[SUM_SCRATCH:])
+
+
+def back_rows(plan, rows, pair, window_text, grad, middle, gate_a, scale_b, text):
     return call(
         functools.partial(back_kernel, plan),
         "back",
         3,
         (own_shape(plan), own_shape(plan), window_shape(plan)),
         [pltpu.VMEM((plan.own, plan.width), BF16)] + sum_scratch(plan) + share_scratch(plan),
-        (part, grad, middle, gate_a, scale_b, text),
+        (rows, pair, window_text, grad, middle, gate_a, scale_b, text),
     )
 
 
@@ -659,44 +691,64 @@
     return [pltpu.SemaphoreType.DMA((len(plan.segments),))] * 2
 
 
-def output_kernel(plan, part, middle, gate_b, text, lowered, out, extra, own, *scratch):
+def output_kernel(plan, rows, pair, window_text, middle, gate_b, text, *refs):
+    if plan.chip_heads:
+        term, lowered, out, extra, term_out, own, term_send, term_recv, *scratch = refs
+    else:
+        lowered, out, extra, own, *scratch = refs
     device = lax.axis_index("dev")
     seq, rank = plan.place_of(device)
     extra[...] = jnp.zeros_like(extra)
     meet(every_device(plan, device))
-    total = scatter_sum(plan, seq, rank, part, *scratch[:7])
+    swaps = []
+    if plan.chip_heads:
+        core = lax.rem(rank, 2)
+        partner = plan.device_of(seq, 2 * lax.div(rank, 2) + 1 - core)
+        for stream in range(2):
+            copy = remote(
+                term.at[stream, 1 - core], term_out.at[2 * stream + core], term_send.at[stream], term_recv.at[stream], partner
+            )
+            copy.start()
+            swaps.append(copy)
+            term_out[2 * stream + core] = term[stream, core]
+    total = scatter_sum(plan, seq, rank, rows, pair, window_text, PLAIN, *scratch[:SUM_SCRATCH])
     lowered[...] = total
     own[...] = (middle[...] + pick_rows(gate_b[...], text[...]) * total).astype(BF16)
-    refs = (own, plan.rows_dev, extra) + scratch[7:]
-    start_edges(plan, seq, rank, *refs)
+    edges = (own, plan.rows_dev, extra) + tuple(scratch[SUM_SCRATCH:])
+    start_edges(plan, seq, rank, *edges)
     out[...] = own[pl.ds(0, plan.rows_dev)]
-    finish_edges(plan, seq, rank, *refs)
-
-
-def output_rows(plan, part, middle, gate_b, text):
-    rows = jax.ShapeDtypeStruct((plan.rows_dev, plan.width), BF16)
-    return call(
-        functools.partial(output_kernel, plan),
-        "output",
-        8,
-        (own_shape(plan), rows, rows),
-        [pltpu.VMEM((plan.own, plan.width), BF16)] + sum_scratch(plan) + edge_scratch(plan),
-        (part, middle, gate_b, text),
-    )
+    for copy in swaps:
+        copy.wait()
+    finish_edges(plan, seq, rank, *edges)
+
+
+def output_rows(plan, rows, pair, window_text, middle, gate_b, text, term):
+    placed = jax.ShapeDtypeStruct((plan.rows_dev, plan.width), BF16)
+    shapes = (own_shape(plan), placed, placed)
+    operands = (rows, pair, window_text, middle, gate_b, text)
+    scratch = [pltpu.VMEM((plan.own, plan.width), BF16)]
+    if plan.chip_heads:
+        share = plan.width // plan.group // 2
+        shapes += (jax.ShapeDtypeStruct((plan.sequences, share, plan.width), BF16),)
+        operands += (term.reshape(2, 2, share, plan.width),)
+        scratch += [pltpu.SemaphoreType.DMA((2,))] * 2
+    scratch += sum_scratch(plan) + edge_scratch(plan)
+    outs = call(functools.partial(output_kernel, plan), "output", 8, shapes, scratch, operands)
+    return outs if plan.chip_heads else outs + [None] if isinstance(outs, list) else outs + (None,)
 
 
 def stream_sums(values, masks):
     return jnp.concatenate([jnp.sum(values * mask, axis=0, keepdims=True) for mask in masks], axis=0)
 
 
-def last_kernel(plan, part, tokens, grad_middle, scale_a, text, masks, rest, out, extra, table,
+def last_kernel(plan, rows, pair, window_text, tokens, grad_middle, scale_a, text, masks, rest, out, extra, table,
                 own, local, first, second, mine, t_send, t_recv, *scratch):
     device = lax.axis_index("dev")
     seq, rank = plan.place_of(device)
     stream = lax.div(2 * seq, plan.sequences)
     extra[...] = jnp.zeros_like(extra)
     meet(every_device(plan, device))
-    total = scatter_sum(plan, seq, rank, part, *scratch[:7])
+    total = scatter_sum(plan, seq, rank, rows, pair, window_text, CONTRACT_LAST, *scratch[:SUM_SCRATCH])
     normed, inv = norm_rows(tokens[...].astype(F32))
     streams = (masks[:, 0:1], masks[:, 1:2])
     local[:, : plan.width] = stream_sums(total, streams)
@@ -717,7 +769,7 @@
     mean_grad = jnp.mean(inner, axis=1, keepdims=True)
     mean_cross = jnp.mean(inner * normed, axis=1, keepdims=True)
     own[...] = grad_middle[...] + inv * (inner - mean_grad - normed * mean_cross)
-    refs = (own, plan.rows_dev, extra) + scratch[7:]
+    refs = (own, plan.rows_dev, extra) + scratch[SUM_SCRATCH:]
     start_edges(plan, seq, rank, *refs)
     for copy in hops:
         copy.wait_recv()
@@ -751,8 +803,8 @@
     finish_edges(plan, seq, rank, *refs)
 
 
-def last_rows(plan, part, tokens, grad_middle, scale_a, text, masks, rest):
-    rows = jax.ShapeDtypeStruct((plan.rows_dev, plan.width), F32)
+def last_rows(plan, rows, pair, window_text, tokens, grad_middle, scale_a, text, masks, rest):
+    placed = jax.ShapeDtypeStruct((plan.rows_dev, plan.width), F32)
     cols = 6 * plan.width // plan.group
     dma = pltpu.SemaphoreType.DMA
     most = max(plan.group, plan.sequences)
@@ -760,7 +812,7 @@
         functools.partial(last_kernel, plan),
         "last",
         10,
-        (rows, rows, jax.ShapeDtypeStruct((plan.group, plan.sequences, 1, cols), F32)),
+        (placed, placed, jax.ShapeDtypeStruct((plan.group, plan.sequences, 1, cols), F32)),
         [
             pltpu.VMEM((plan.own, plan.width), F32),
             pltpu.VMEM((2, 6 * plan.width), F32),
@@ -772,7 +824,7 @@
         ]
         + sum_scratch(plan)
         + edge_scratch(plan),
-        (part, tokens, grad_middle, scale_a, text, masks, rest),
+        (rows, pair, window_text, tokens, grad_middle, scale_a, text, masks, rest),
     )
     return out, extra, table[:, :, 0].transpose(1, 0, 2).reshape(plan.sequences, -1)
 
@@ -828,40 +880,25 @@
     return lax.psum_scatter(pieces, "dev", scatter_dimension=0, axis_index_groups=plan.rank_groups())
 
 
-def chip_groups(plan):
-    return [
-        [plan.device_of(s, 2 * q + core) for s in range(plan.sequences) for core in range(2)]
-        for q in range(plan.group // 2)
-    ]
-
-
-def merge_slices(plan, weight, rank):
-    half = plan.group // 2
-    rows = weight.shape[0]
+def merge_rows(plan, weight, rank):
+    if plan.chip_heads:
+        return lax.all_gather(weight, "dev", axis=0, axis_index_groups=plan.rank_groups())
     share = plan.width // plan.group
-    if plan.chip_heads:
-        full = lax.all_gather(weight, "dev", axis=0, axis_index_groups=chip_groups(plan))
-        full = full.reshape(2, 2, share, weight.shape[1])
-        return lax.dynamic_index_in_dim(full, lax.rem(rank, 2), 1, keepdims=False)
     full = lax.all_gather(weight, "dev", axis=0, tiled=True)
-    full = full.reshape(2, 2, half, share, weight.shape[1])
+    full = full.reshape(2, 2, plan.group // 2, share, weight.shape[1])
     full = lax.dynamic_index_in_dim(full, lax.rem(rank, 2), 1, keepdims=False)
     return lax.dynamic_index_in_dim(full, lax.div(rank, 2), 1, keepdims=False)
 
 
-def merge_grads(plan, grad, rank):
+def merge_sum(plan, term, term_out, rank):
+    if plan.chip_heads:
+        return over_sequences_sum(plan, term_out)
     half = plan.group // 2
-    _, share, cols = grad.shape
-    core = lax.rem(rank, 2)
-    grad = grad.astype(BF16)
-    mine = [jnp.where(core == k, grad, jnp.zeros((), BF16)) for k in range(2)]
-    if plan.chip_heads:
-        full = jnp.stack(mine, axis=1).reshape(2 * plan.sequences, -1, cols)
-        out = lax.psum_scatter(full, "dev", scatter_dimension=0, axis_index_groups=chip_groups(plan))
-        return out.astype(F32)
+    _, share, cols = term.shape
+    mine = [jnp.where(lax.rem(rank, 2) == k, term, jnp.zeros((), BF16)) for k in range(2)]
     full = jnp.zeros((2, 2, half, share, cols), BF16)
     full = lax.dynamic_update_slice_in_dim(full, jnp.stack(mine, axis=1)[:, :, None], lax.div(rank, 2), 2)
-    return lax.psum_scatter(full.reshape(-1, cols), "dev", scatter_dimension=0, tiled=True).astype(F32)
+    return lax.psum_scatter(full.reshape(-1, cols), "dev", scatter_dimension=0, tiled=True)
 
 
 def down_slices(plan, weight):
@@ -934,14 +971,14 @@
     silu_part = lax.dynamic_slice_in_dim(silu_low, feature_start, mod_rows, 1)
     mod_part = jnp.dot(silu_part, modulation_weight, preferred_element_type=F32)
 
-    merge_pair = merge_slices(plan, merge_weight, rank)
+    merge_pair = merge_rows(plan, merge_weight, rank)
     project_pieces, up_pieces = swap_in(plan, project_weight, up_weight)
     project_pieces, up_pieces, merge_pair = lax.optimization_barrier((project_pieces, up_pieces, merge_pair))
     project_pair = over_sequences(plan, project_pieces)
     up_pair = over_sequences(plan, up_pieces)
     down_pair = down_slices(plan, down_weight)
 
-    token_window, grad_window, mods = entry(plan, tokens, cotangent, mod_part)
+    token_window, grad_window, mods, merge_pair = entry(plan, tokens, cotangent, mod_part, merge_pair)
     shift_a, scale_a, gate_a, shift_b, scale_b, gate_b = jnp.split(mods, 6, axis=1)
     grad_window = jnp.where(valid[:, None], grad_window, jnp.zeros((), BF16))
 
@@ -954,8 +991,9 @@
     own_tokens = own_rows(plan, token_window, rank)
     own_grad = own_rows(plan, grad_window, rank)
     text_mask = own_text.astype(F32)[:, None]
+    window_text = is_text.astype(F32)[:, None]
     merged, hidden_b = middle_rows(
-        plan, stream_dot(plan, attended, merge_pair, is_text), own_tokens, gate_a, scale_b, shift_b, text_mask
+        plan, attended, merge_pair, window_text, own_tokens, gate_a, scale_b, shift_b, text_mask
     )
     middle = own_tokens.astype(F32) + pick(gate_a, own_text) * merged
     normed_b, inv_b = layer_norm(middle)
@@ -971,27 +1009,26 @@
     gelu_pull = jax.vjp(lambda value_in: jax.nn.gelu(value_in, approximate=True), upper)[1]
     grad_upper = gelu_pull(grad_activated)[0].astype(BF16)
     up_term = terms_to_send(plan, weight_terms(plan, hidden_b, grad_upper, is_text), mod_rows)
-    back_part = stream_dot_back(plan, grad_upper, up_pair, is_text)
-    back_part, up_term = lax.optimization_barrier((back_part, up_term))
+    grad_upper, up_term = lax.optimization_barrier((grad_upper, up_term))
     up_sum = over_sequences_sum(plan, up_term)
     grad_hidden_b, grad_middle, grad_merged = back_rows(
-        plan, back_part, own_grad, middle, gate_a, scale_b, text_mask
+        plan, grad_upper, up_pair, window_text, own_grad, middle, gate_a, scale_b, text_mask
     )
     foreign = (row_seq != seq)[:, None]
-    lowered, out_here, out_there = output_rows(
-        plan, stream_dot(plan, activated, down_pair, is_text), middle, gate_b, text_mask
-    )
-    layer_out = jnp.where(foreign, out_there, out_here)
     grad_attended = stream_dot_back(plan, grad_merged, merge_pair, is_text).astype(BF16)
-    merge_grad = merge_grads(plan, weight_terms(plan, attended, grad_merged, is_text), rank)
+    merge_term = weight_terms(plan, attended, grad_merged, is_text).astype(BF16)
 
     grad_projected = jnp.concatenate(attend_back(plan, queries, keys, values, grad_attended, bias), axis=1)
     grad_projected, down_sum = lax.optimization_barrier((grad_projected, down_sum))
     down_grad = down_sum.astype(F32)
     project_term = terms_to_send(plan, weight_terms(plan, hidden_a, grad_projected, is_text), mod_rows)
-    last_part = stream_dot_back(plan, grad_projected, project_pair, is_text)
-    last_part, project_term = lax.optimization_barrier((last_part, project_term))
+    grad_projected, project_term = lax.optimization_barrier((grad_projected, project_term))
     project_sum = over_sequences_sum(plan, project_term)
+    activated, project_term = lax.optimization_barrier((activated, project_term))
+    lowered, out_here, out_there, merge_out = output_rows(
+        plan, activated, down_pair, window_text, middle, gate_b, text_mask, merge_term
+    )
+    layer_out = jnp.where(foreign, out_there, out_here)
 
     masks = jnp.stack([own_valid & ~own_text, own_valid & own_text], axis=1).astype(F32)
     rest = jnp.concatenate(
@@ -1008,14 +1045,18 @@
     )
     rest, up_sum = lax.optimization_barrier((rest, up_sum))
     back_here, back_there, grad_table = last_rows(
-        plan, last_part, own_tokens, grad_middle, scale_a, text_mask, masks, rest
+        plan, grad_projected, project_pair, window_text, own_tokens, grad_middle, scale_a, text_mask, masks, rest
     )
     tokens_grad = jnp.where(foreign, back_there, back_here)
     own_grads = grad_table.astype(BF16)
+    modulation_grad = lax.dot_general(silu_part, own_grads, CONTRACT_FIRST, preferred_element_type=F32)
+    grad_piece = lax.dot_general(own_grads, modulation_weight, CONTRACT_LAST, preferred_element_type=F32)
+    merge_out, merge_term, project_sum, own_grads = lax.optimization_barrier(
+        (merge_out, merge_term, project_sum, own_grads)
+    )
+    merge_grad = merge_sum(plan, merge_term, merge_out, rank).reshape(merge_weight.shape).astype(F32)
     up_grad = swap_out(plan, up_sum, lambda p, r: up_columns(p, r, up_weight.shape[1]), "up_out", 7)
     project_grad = swap_out(plan, project_sum, project_columns, "project_out", 6)
-    modulation_grad = lax.dot_general(silu_part, own_grads, CONTRACT_FIRST, preferred_element_type=F32)
-    grad_piece = lax.dot_general(own_grads, modulation_weight, CONTRACT_LAST, preferred_element_type=F32)
     everyone = spread(plan, grad_piece.reshape(-1, 128), 13)
     everyone = everyone.reshape(2, plan.devices // 2, plan.sequences, mod_rows)
     grad_silu = (everyone[0] + everyone[1]).transpose(1, 0, 2).reshape(plan.sequences, width)

time: 648 us -> 625 us (0.965)
  matrix products: 60.3 us -> 41.2 us
  other arithmetic: 68 us -> 49.8 us
  waiting for transfers between devices: 37 us -> 54.4 us
  local copies, waits for them, and re-layouts: 84 us -> 70.1 us
  Pallas kernels: 376 us -> 386 us
    all_gather x1, waiting for transfers between devices: 30.2 us -> 46 us  [down_slices(): lax.all_gather(weight, 'dev', axis=0, axis_index_groups=plan.rank_groups())]
    concatenate x6 -> x2, other arithmetic: 19.2 us -> 3.5 us  [by_stream(): jnp.concatenate([image_part[:start], mixed, text_part[end - start:]], axi...]
    slice x9 -> x4, local copies, waits for them, and re-layouts: 13.8 us -> 2.37 us  [by_stream(): image_part[:start]]
    pallas_call x9, Pallas kernels: 341 us -> 352 us  [call(): pl.pallas_call(kernel, out_shape=out_shape, in_specs=in_specs or [VMEM] *...]
    dot_general x4 -> x2, matrix products: 17.1 us -> 6.97 us  [stream_dot_back(): lax.dot_general(grads[:plan.image_end], pair[0], CONTRACT_LAST, preferred...]
    dot_general x4 -> x2, matrix products: 14.5 us -> 5.58 us  [stream_dot(): jnp.dot(rows[:plan.image_end], pair[0], preferred_element_type=F32)]
    unnamed x189 -> x195, local copies, waits for them, and re-layouts: 48 us -> 43.9 us
  transfers between devices with their start and end apart: 8 -> 8, of which waited for: 2 -> 3; matrix products, arithmetic and copies ran while one was open for 26% -> 20% of each run, Pallas kernels for 56% -> 62%
where the time goes in v3:
time: 625 us; the launch traced here: 619 us
  Pallas kernels  386 us (62%)
  local copies, waits for them, and re-layouts  70.1 us (11%)
  waiting for transfers between devices  54.4 us (9%)
  other arithmetic  49.8 us (8%)
  matrix products  41.2 us (7%)
  between operations  16.5 us (3%)
    pallas_call x9, Pallas kernels, call(): pl.pallas_call(kernel, out_shape=out_shape, in_specs=in_specs or [VMEM] *...  352 us
    all_gather x1, waiting for transfers between devices, down_slices(): lax.all_gather(weight, 'dev', axis=0, axis_index_groups=plan.rank_groups())  46 us
    unnamed x195, local copies, waits for them, and re-layouts  43.9 us
    pallas_call x1, Pallas kernels, attend_back(): pl.pallas_call(functools.partial(attend_back_kernel, plan.heads, rows //...  22.1 us
    dot_general x4, matrix products, weight_terms(): lax.dot_general(rows[:plan.image_end], image, CONTRACT_FIRST, preferred_e...  15 us
  transfers between devices with their start and end apart: 8, of which 3 were waited for; matrix products, arithmetic and copies ran while one was open for 20% of the time, Pallas kernels for 62%

profile of v3, /device:TPU:0, one launch (start us, length us, event | category | flops | bytes accessed | tf_op | source)
XLA Modules:
  0.0 619.1 jit_solution(3706669539014260656)
XLA Ops:
  10.4 29.5 %swap_in.1 = (bf16[8,96,576]{2,1,0:T(8,128)(2,1)}, bf16[8,96,768]{2,1,0:T(8,128)(2,1)}) custom-call(bf16[96,4608]{1,0:T(8,128)(2,1)S(1)} %copy-done.35, bf16[96,6144]{1,0:T(8,128)(2,1)S(1)} %copy-done.27), custom_call_target="tpu_custom_call" | custom-call | tf_op jit(solution)/shard_map/swap_in/pallas_call | solution.py:236
  57.1 78.5 %entry.1 = (bf16[1280,1536]{1,0:T(8,128)(2,1)S(1)}, bf16[1280,1536]{1,0:T(8,128)(2,1)S(1)}, f32[8,2,9,128]{3,2,1,0:T(8,128)S(1)}, bf16[2,2,96,1536]{3,2,1,0:T(8,128)(2,1)S(1)}) custom-call(bf16[144,1536]{1,0:T(8,128)(2,1)S(1)} %copy-done.44, bf16[144,1536]{1,0:T(8,128)(2,1)S(1)} %copy-done.45, f32[8,4,9,128]{3,2,1,0:T(8,128)S(1)} %bitcast.76, ...), custom_call_target="tpu_custom_call" | custom-call | tf_op jit(solution)/shard_map/entry/pallas_call | solution.py:236
  140.6 3.4 fusion.2
  144.8 9.3 %multiply_convert_fusion = (bf16[1280,1536]{1,0:T(8,128)(2,1)}, bf16[1280,1536]{1,0:T(8,128)(2,1)}, bf16[1280,1536]{1,0:T(8,128)(2,1)}) fusion(f32[1536]{0:T(1024)S(1)} %get-tuple-element.94, f32[1536]{0:T(1024)S(1)} %get-tuple-element.95, pred[1280]{0:T(1024)(128)(4,1)S(1)} %copy-done.69, bf16[1280,1536]{1,0:T(8,128)(2,1)} %copy-done.16, ...), kind=kLoop, calls=%fused_computation.8 | loop fusion | flops 27525120 | bytes 19710464 | tf_op jit(solution)/shard_map/convert_element_type | solution.py:1003
  169.5 12.5 %attend.1.rows = bf16[1280,192]{1,0:T(8,128)(2,1)S(1)} custom-call(bf16[1280,192]{1,0:T(8,128)(2,1)S(1)} %get-tuple-element.116.q_ref, bf16[1280,192]{1,0:T(8,128)(2,1)S(1)} %get-tuple-element.115.k_ref, bf16[1280,192]{1,0:T(8,128)(2,1)S(1)} %get-tuple-element.114.v_ref, f32[1,1280]{1,0:T(1,128)S(1)} %and_select_fusion.bias_ref), custom_call_target="tpu_custom_call" | custom-call | flops 5033164800 | bytes 1966080 | tf_op jit(solution)/shard_map/attend/pallas_call | solution.py:119
  182.0 54.9 %middle.1 = (f32[160,1536]{1,0:T(8,128)S(1)}, bf16[1280,1536]{1,0:T(8,128)(2,1)S(1)}) custom-call(bf16[1280,192]{1,0:T(8,128)(2,1)S(1)} %attend.1.rows, bf16[2,192,1536]{2,1,0:T(8,128)(2,1)S(1)} %bitcast.73, f32[1280,1]{1,0:T(8,128)S(1)} %fusion.72.window_text, bf16[160,1536]{1,0:T(8,128)(2,1)S(1)} %pad_maximum_fusion.9.tokens, ...), custom_call_target="tpu_custom_call" | custom-call | tf_op jit(solution)/shard_map/middle/pallas_call | solution.py:236
  251.5 3.3 fusion.39
  257.4 46.0 %all-gather.15.cloned.1.call-done = bf16[1536,1536]{1,0:T(8,128)(2,1)} async-done(((bf16[384,1536]{1,0:T(8,128)(2,1)}), bf16[1536,1536]{1,0:T(8,128)(2,1)}) %all-gather.15.cloned.1.call-update) | async-done | bytes 4718608 | tf_op jit(solution)/shard_map/all_gather | solution.py:905
  303.3 5.7 fusion.16
  309.2 2.9 copy-done.11
  318.4 3.4 fusion.35
  331.3 61.3 %back.1 = (f32[160,1536]{1,0:T(8,128)S(1)}, f32[160,1536]{1,0:T(8,128)S(1)}, bf16[1280,1536]{1,0:T(8,128)(2,1)S(1)}) custom-call(bf16[1280,768]{1,0:T(8,128)(2,1)S(1)} %copy-done.5, bf16[2,1536,768]{2,1,0:T(8,128)(2,1)} %bitcast.79, f32[1280,1]{1,0:T(8,128)S(1)} %fusion.72.window_text, bf16[160,1536]{1,0:T(8,128)(2,1)S(1)} %pad_maximum_fusion.10.grad, ...), custom_call_target="tpu_custom_call" | custom-call | tf_op jit(solution)/shard_map/back/pallas_call | solution.py:236
  406.7 22.1 %attend_back.1 = (bf16[1280,192]{1,0:T(8,128)(2,1)}, bf16[1280,192]{1,0:T(8,128)(2,1)}, bf16[1280,192]{1,0:T(8,128)(2,1)}) custom-call(bf16[1280,192]{1,0:T(8,128)(2,1)} %copy-done.39, bf16[1280,192]{1,0:T(8,128)(2,1)} %copy-done.38, bf16[1280,192]{1,0:T(8,128)(2,1)} %copy-done.37, bf16[1280,192]{1,0:T(8,128)(2,1)} %pad_maximum_fusion.8.g_ref, ...), custom_call_target="tpu_custom_call" | custom-call | flops 12582912000 | bytes 3440640 | tf_op jit(solution)/shard_map/attend_back/pallas_call | solution.py:174
  428.8 3.3 pad_maximum_fusion.6.rows
  434.0 5.0 fusion.41
  441.2 5.9 copy.104
  451.0 3.3 fusion.44
  455.8 38.6 %output.1 = (f32[160,1536]{1,0:T(8,128)S(1)}, bf16[144,1536]{1,0:T(8,128)(2,1)S(1)}, bf16[144,1536]{1,0:T(8,128)(2,1)S(1)}, bf16[4,96,1536]{2,1,0:T(8,128)(2,1)S(1)}) custom-call(bf16[1280,768]{1,0:T(8,128)(2,1)S(1)} %copy-done.7, bf16[2,768,1536]{2,1,0:T(8,128)(2,1)S(1)} %bitcast.72, f32[1280,1]{1,0:T(8,128)S(1)} %fusion.72.window_text, ...), custom_call_target="tpu_custom_call" | custom-call | tf_op jit(solution)/shard_map/output/pallas_call | solution.py:236
  502.5 47.9 %last.1 = (f32[144,1536]{1,0:T(8,128)S(1)}, f32[144,1536]{1,0:T(8,128)S(1)}, f32[8,4,1,1152]{3,2,1,0:T(1,128)S(1)}) custom-call(bf16[1280,576]{1,0:T(8,128)(2,1)S(1)} %copy-done.10, bf16[2,1536,576]{2,1,0:T(8,128)(2,1)S(1)} %bitcast.69, f32[1280,1]{1,0:T(8,128)S(1)} %fusion.72.window_text, bf16[160,1536]{1,0:T(8,128)(2,1)S(1)} %copy-done.15, ...), custom_call_target="tpu_custom_call" | custom-call | tf_op jit(solution)/shard_map/last/pallas_call | solution.py:236
  552.5 3.6 reduce-scatter.9.cloned.1.call-done
  556.1 3.0 convert_element_type.119
  559.7 10.6 %spread.1 = f32[4,8,3,128]{3,2,1,0:T(4,128)S(1)} custom-call(f32[3,128]{1,0:T(4,128)S(1)} %reshape.314.piece), custom_call_target="tpu_custom_call" | custom-call | tf_op jit(solution)/shard_map/spread/pallas_call | solution.py:236
  570.6 15.7 %up_out.1 = f32[96,6144]{1,0:T(8,128)S(1)} custom-call(bf16[8,96,768]{2,1,0:T(8,128)(2,1)S(1)} %bitcast.74), custom_call_target="tpu_custom_call" | custom-call | tf_op jit(solution)/shard_map/up_out/pallas_call | solution.py:236
  592.7 14.7 %project_out.1 = f32[96,4608]{1,0:T(8,128)S(1)} custom-call(bf16[8,96,576]{2,1,0:T(8,128)(2,1)S(1)} %bitcast.77), custom_call_target="tpu_custom_call" | custom-call | tf_op jit(solution)/shard_map/project_out/pallas_call | solution.py:236
  (326 shorter events, 118.3 us)
Async XLA Ops:
  7.2 44.9 %copy-start = (bf16[96,9216]{1,0:T(8,128)(2,1)S(1)}, bf16[96,9216]{1,0:T(8,128)(2,1)}, u32[]{:S(2)}) copy-start(bf16[96,9216]{1,0:T(8,128)(2,1)} %param.12) | copy-start | bytes 5308420
  7.2 37.0 %copy-start.89 = (s32[4]{0:T(128)S(1)}, s32[4]{0:T(128)}, u32[]{:S(2)}) copy-start(s32[4]{0:T(128)} %param.11) | copy-start | bytes 52
  7.2 42.8 %copy-start.63 = (bf16[4,1536]{1,0:T(4,128)(2,1)S(1)}, bf16[4,1536]{1,0:T(4,128)(2,1)}, u32[]{:S(2)}) copy-start(bf16[4,1536]{1,0:T(4,128)(2,1)} %param.10) | copy-start | bytes 36868
  7.2 35.6 %all-gather.9.cloned.1.call-start = ((), (), s32[]{:S(2)}) async-start(), calls=%async_computation.8 | async-start | bytes 1474560 | tf_op jit(solution)/shard_map/all_gather | solution.py:885
  7.9 146.3 %all-gather.11.cloned.1.call-start = ((), (), s32[]{:S(2)}) async-start(), calls=%async_computation.9 | async-start | bytes 4915200 | tf_op jit(solution)/shard_map/all_gather | solution.py:871
  42.8 197.8 %all-gather.13.cloned.1.call-start = ((), (), s32[]{:S(2)}) async-start(), calls=%async_computation.10 | async-start | bytes 5898240 | tf_op jit(solution)/shard_map/all_gather | solution.py:871
  43.5 259.8 %all-gather.15.cloned.1.call-start = ((), (), s32[]{:S(2)}) async-start(), calls=%async_computation.11 | async-start | bytes 5898240 | tf_op jit(solution)/shard_map/all_gather | solution.py:905
  44.1 387.9 %reduce-scatter.5.cloned.1.call-start = ((), (), s32[]{:S(2)}) async-start(), calls=%async_computation.4 | async-start | bytes 5898240 | tf_op jit(solution)/shard_map/reduce_scatter | solution.py:880
  46.9 92.2 %copy-start.68 = (pred[1280]{0:T(1024)(128)(4,1)}, pred[1280]{0:T(1024)(128)(4,1)S(1)}, u32[]{:S(2)}) copy-start(pred[1280]{0:T(1024)(128)(4,1)S(1)} %fusion.88) | copy-start | bytes 3844
  49.3 89.8 %copy-start.66 = (pred[1280]{0:T(1024)(128)(4,1)}, pred[1280]{0:T(1024)(128)(4,1)S(1)}, u32[]{:S(2)}) copy-start(pred[1280]{0:T(1024)(128)(4,1)S(1)} %fusion.89) | copy-start | bytes 3844
  50.0 119.5 %copy-start.49 = (f32[1,1280]{1,0:T(1,128)}, f32[1,1280]{1,0:T(1,128)S(1)}, u32[]{:S(2)}) copy-start(f32[1,1280]{1,0:T(1,128)S(1)} %and_select_fusion.bias_ref) | copy-start | bytes 15364
  51.1 88.1 %copy-start.84 = (pred[144,1]{0,1:T(4,128)(4,1)}, pred[144,1]{0,1:T(4,128)(4,1)S(1)}, u32[]{:S(2)}) copy-start(pred[144,1]{0,1:T(4,128)(4,1)S(1)} %concatenate.86) | copy-start | bytes 436
  51.8 87.3 %copy-start.72 = (pred[160,1]{0,1:T(4,128)(4,1)}, pred[160,1]{0,1:T(4,128)(4,1)S(1)}, u32[]{:S(2)}) copy-start(pred[160,1]{0,1:T(4,128)(4,1)S(1)} %get-tuple-element.107) | copy-start | bytes 484
  52.1 87.1 %copy-start.74 = (bf16[4,96]{1,0:T(4,128)(2,1)}, bf16[4,96]{1,0:T(4,128)(2,1)S(1)}, u32[]{:S(2)}) copy-start(bf16[4,96]{1,0:T(4,128)(2,1)S(1)} %fusion.90) | copy-start | bytes 2308
  144.8 37.2 %copy-start.14 = (bf16[160,1536]{1,0:T(8,128)(2,1)}, bf16[160,1536]{1,0:T(8,128)(2,1)S(1)}, u32[]{:S(2)}) copy-start(bf16[160,1536]{1,0:T(8,128)(2,1)S(1)} %pad_maximum_fusion.9.tokens) | copy-start | bytes 1474564
  257.3 238.5 %reduce-scatter.7.cloned.1.call-start = ((), (), s32[]{:S(2)}) async-start(), calls=%async_computation.5 | async-start | bytes 5898240 | tf_op jit(solution)/shard_map/reduce_scatter | solution.py:880
  324.4 231.6 %reduce-scatter.9.cloned.1.call-start = ((), (), s32[]{:S(2)}) async-start(), calls=%async_computation.6 | async-start | bytes 4915200 | tf_op jit(solution)/shard_map/reduce_scatter | solution.py:880
  447.1 160.2 %reduce-scatter.11.cloned.1.call-start = ((), (), s32[]{:S(2)}) async-start(), calls=%async_computation.7 | async-start | bytes 1474560 | tf_op jit(solution)/shard_map/reduce_scatter | solution.py:880
  455.8 38.6 %copy-start.18 = (f32[160,1536]{1,0:T(8,128)S(1)}, f32[160,1536]{1,0:T(8,128)}, u32[]{:S(2)}) copy-start(f32[160,1536]{1,0:T(8,128)} %copy-done.17) | copy-start | bytes 2949124
  455.8 38.6 %copy-start.20 = (f32[160,1536]{1,0:T(8,128)S(1)}, f32[160,1536]{1,0:T(8,128)}, u32[]{:S(2)}) copy-start(f32[160,1536]{1,0:T(8,128)} %copy-done.19) | copy-start | bytes 2949124
  455.8 38.7 %copy-start.29 = (f32[160,1536]{1,0:T(8,128)S(1)}, f32[160,1536]{1,0:T(8,128)}, u32[]{:S(2)}) copy-start(f32[160,1536]{1,0:T(8,128)} %copy-done.28) | copy-start | bytes 2949124
  455.8 38.7 %copy-start.56 = (bf16[144,1536]{1,0:T(8,128)(2,1)S(1)}, bf16[144,1536]{1,0:T(8,128)(2,1)}, u32[]{:S(2)}) copy-start(bf16[144,1536]{1,0:T(8,128)(2,1)} %copy-done.55) | copy-start | bytes 1327108
  455.8 38.7 %copy-start.61 = (bf16[16,1536]{1,0:T(8,128)(2,1)S(1)}, bf16[16,1536]{1,0:T(8,128)(2,1)}, u32[]{:S(2)}) copy-start(bf16[16,1536]{1,0:T(8,128)(2,1)} %copy-done.60) | copy-start | bytes 147460
  559.0 28.6 %copy-start.75 = (bf16[4,96]{1,0:T(4,128)(2,1)S(1)}, bf16[4,96]{1,0:T(4,128)(2,1)}, u32[]{:S(2)}) copy-start(bf16[4,96]{1,0:T(4,128)(2,1)} %copy-done.74) | copy-start | bytes 2308
  (76 other events, 365.2 us)
Sparse Core Ops, SparseCore 0:
  9.6 33.1 all-gather.8
  44.4 79.9 all-gather.10
  126.0 88.0 all-gather.12
  215.4 87.8 all-gather.14
  305.5 83.6 reduce-scatter.4
  391.4 85.7 reduce-scatter.6
  479.5 76.4 reduce-scatter.8
  558.3 30.2 reduce-scatter.10

commit v4 on v3

--- a/solution.py
+++ b/solution.py
@@ -97,14 +97,19 @@
     return exponent * (1.0 / total)
 
 
-def attend_kernel(heads, q_ref, k_ref, v_ref, bias_ref, out_ref):
+def head_columns(heads, part, head):
+    first = (part * heads + head) * HDIM
+    return slice(first, first + HDIM)
+
+
+def attend_kernel(heads, block, projected, bias_ref, out_ref):
+    rows = pl.ds(pl.multiple_of(pl.program_id(0) * block, block), block)
     bias = bias_ref[...]
     outs = []
     for head in range(heads):
-        cols = slice(head * HDIM, (head + 1) * HDIM)
-        query = q_ref[:, cols] * jnp.asarray(HDIM ** (-0.5), BF16)
-        probs = softmax_parts(query, k_ref[:, cols], bias).astype(BF16)
-        outs.append(jnp.dot(probs, v_ref[:, cols], preferred_element_type=F32))
+        query = projected[rows, head_columns(heads, 0, head)] * jnp.asarray(HDIM ** (-0.5), BF16)
+        probs = softmax_parts(query, projected[:, head_columns(heads, 1, head)], bias).astype(BF16)
+        outs.append(jnp.dot(probs, projected[:, head_columns(heads, 2, head)], preferred_element_type=F32))
     out_ref[...] = jnp.concatenate(outs, axis=1).astype(BF16)
 
 
@@ -112,28 +117,28 @@
     return 256 if rows % 256 == 0 else 128
 
 
-def attend(plan, queries, keys, values, bias):
-    rows, cols = queries.shape
+def constant(shape):
+    return pl.BlockSpec(shape, lambda i: (0,) * len(shape))
+
+
+def attend(plan, projected, bias):
+    rows, cols = projected.shape[0], projected.shape[1] // 3
     block = block_rows(rows)
-    whole = pl.BlockSpec((rows, cols), lambda i: (0, 0))
     return pl.pallas_call(
-        functools.partial(attend_kernel, plan.heads),
+        functools.partial(attend_kernel, plan.heads, block),
         out_shape=jax.ShapeDtypeStruct((rows, cols), BF16),
         grid=(rows // block,),
-        in_specs=[
-            pl.BlockSpec((block, cols), lambda i: (i, 0)),
-            whole,
-            whole,
-            pl.BlockSpec((1, rows), lambda i: (0, 0)),
-        ],
+        in_specs=[constant(projected.shape), constant(bias.shape)],
         out_specs=pl.BlockSpec((block, cols), lambda i: (i, 0)),
         compiler_params=pltpu.CompilerParams(vmem_limit_bytes=48 << 20),
         cost_estimate=pl.CostEstimate(flops=16 * rows * rows * cols, bytes_accessed=8 * rows * cols, transcendentals=0),
         name="attend",
-    )(queries, keys, values, bias)
-
-
-def attend_back_kernel(heads, steps, q_ref, k_ref, v_ref, g_ref, bias_ref, gq_ref, gk_ref, gv_ref, key_sum, value_sum):
+    )(projected, bias)
+
+
+def attend_back_kernel(
+    heads, steps, block, projected, grad_merged, merge_pair, text, bias_ref, out, key_sum, value_sum
+):
     step = pl.program_id(0)
     scale = jnp.asarray(HDIM ** (-0.5), BF16)
 
@@ -142,46 +147,98 @@
         key_sum[...] = jnp.zeros_like(key_sum)
         value_sum[...] = jnp.zeros_like(value_sum)
 
+    rows = pl.ds(pl.multiple_of(step * block, block), block)
     bias = bias_ref[...]
+    image, other_stream = [
+        lax.dot_general(grad_merged[...], merge_pair[j], CONTRACT_LAST, preferred_element_type=F32) for j in range(2)
+    ]
+    grad_attended = jnp.where(text[...] > 0, other_stream, image).astype(BF16)
     grads = []
     for head in range(heads):
-        cols = slice(head * HDIM, (head + 1) * HDIM)
-        query = q_ref[:, cols] * scale
-        key = k_ref[:, cols]
-        grad_out = g_ref[:, cols]
+        query = projected[rows, head_columns(heads, 0, head)] * scale
+        key = projected[:, head_columns(heads, 1, head)]
+        grad_out = grad_attended[:, head * HDIM : (head + 1) * HDIM]
         probs = softmax_parts(query, key, bias)
-        grad_probs = lax.dot_general(grad_out, v_ref[:, cols], CONTRACT_LAST, preferred_element_type=F32)
+        grad_probs = lax.dot_general(
+            grad_out, projected[:, head_columns(heads, 2, head)], CONTRACT_LAST, preferred_element_type=F32
+        )
         inner = jnp.sum(probs * grad_probs, axis=1, keepdims=True)
         grad_scores = (probs * (grad_probs - inner)).astype(BF16)
         grads.append(jnp.dot(grad_scores, key, preferred_element_type=F32) * HDIM ** (-0.5))
         key_sum[head] += lax.dot_general(query, grad_scores, CONTRACT_FIRST, preferred_element_type=F32)
         value_sum[head] += lax.dot_general(grad_out, probs.astype(BF16), CONTRACT_FIRST, preferred_element_type=F32)
-    gq_ref[...] = jnp.concatenate(grads, axis=1).astype(BF16)
+    cols = heads * HDIM
+    out[rows, :cols] = jnp.concatenate(grads, axis=1).astype(BF16)
 
     @pl.when(step == steps - 1)
     def _():
-        rows = gk_ref.shape[0]
-        gk_ref[...] = key_sum[...].reshape(heads * HDIM, rows).T.astype(BF16)
-        gv_ref[...] = value_sum[...].reshape(heads * HDIM, rows).T.astype(BF16)
-
-
-def attend_back(plan, queries, keys, values, grad_out, bias):
-    rows, cols = queries.shape
+        total = out.shape[0]
+        out[:, cols : 2 * cols] = key_sum[...].reshape(cols, total).T.astype(BF16)
+        out[:, 2 * cols :] = value_sum[...].reshape(cols, total).T.astype(BF16)
+
+
+def attend_back(plan, projected, grad_merged, merge_pair, text, bias):
+    rows, cols = projected.shape[0], projected.shape[1] // 3
     block = block_rows(rows)
-    whole = pl.BlockSpec((rows, cols), lambda i: (0, 0))
-    part = pl.BlockSpec((block, cols), lambda i: (i, 0))
-    shape = jax.ShapeDtypeStruct((rows, cols), BF16)
     return pl.pallas_call(
-        functools.partial(attend_back_kernel, plan.heads, rows // block),
-        out_shape=(shape, shape, shape),
+        functools.partial(attend_back_kernel, plan.heads, rows // block, block),
+        out_shape=jax.ShapeDtypeStruct(projected.shape, BF16),
         grid=(rows // block,),
-        in_specs=[part, whole, whole, part, pl.BlockSpec((1, rows), lambda i: (0, 0))],
-        out_specs=(part, whole, whole),
+        in_specs=[
+            constant(projected.shape),
+            pl.BlockSpec((block, plan.width), lambda i: (i, 0)),
+            constant(merge_pair.shape),
+            pl.BlockSpec((block, 1), lambda i: (i, 0)),
+            constant(bias.shape),
+        ],
+        out_specs=constant(projected.shape),
         scratch_shapes=[pltpu.VMEM((plan.heads, HDIM, rows), F32)] * 2,
         compiler_params=pltpu.CompilerParams(vmem_limit_bytes=56 << 20),
         cost_estimate=pl.CostEstimate(flops=40 * rows * rows * cols, bytes_accessed=14 * rows * cols, transcendentals=0),
         name="attend_back",
-    )(queries, keys, values, grad_out, bias)
+    )(projected, grad_merged, merge_pair, text, bias)
+
+
+def fold_rows(piece):
+    half = piece.shape[0] // 2
+    return jnp.concatenate([piece[:half], piece[half:]], axis=1)
+
+
+def unfold_rows(piece):
+    half = piece.shape[1] // 2
+    return jnp.concatenate([piece[:, :half], piece[:, half:]], axis=0)
+
+
+def project_terms_kernel(plan, rows_of, hidden, grads, text, out):
+    cols = grads.shape[1]
+    spans = ((0, plan.image_end), (plan.text_start, plan.rows))
+    chunk = 4 * 96
+    for stream, (first, last) in enumerate(spans):
+        mask = text[pl.ds(first, last - first)]
+        keep = (mask > 0) if stream else (mask <= 0)
+        part = jnp.where(keep, grads[pl.ds(first, last - first)], jnp.zeros((), BF16))
+        for start in range(0, plan.width, chunk):
+            term = lax.dot_general(
+                hidden[pl.ds(first, last - first), start : start + chunk], part, CONTRACT_FIRST, preferred_element_type=F32
+            ).astype(BF16)
+            for i in range(chunk // rows_of):
+                owner = (stream * plan.width + start) // rows_of + i
+                out[owner] = fold_rows(term[i * rows_of : (i + 1) * rows_of])
+
+
+def project_terms(plan, hidden, grads, text, rows):
+    cols = grads.shape[1]
+    shape = (plan.devices, rows // 2, 2 * cols)
+    out = pl.pallas_call(
+        functools.partial(project_terms_kernel, plan, rows),
+        out_shape=jax.ShapeDtypeStruct(shape, BF16),
+        in_specs=[pl.BlockSpec(memory_space=pltpu.VMEM)] * 3,
+        out_specs=pl.BlockSpec(memory_space=pltpu.VMEM),
+        compiler_params=pltpu.CompilerParams(vmem_limit_bytes=40 << 20),
+        cost_estimate=pl.CostEstimate(flops=4 * plan.rows * plan.width * cols, bytes_accessed=1 << 23, transcendentals=0),
+        name="project_terms",
+    )(hidden, grads, text)
+    return out.reshape((plan.sequences, plan.group) + shape[1:])
 
 
 VMEM = pl.BlockSpec(memory_space=pltpu.VMEM)
@@ -538,7 +595,7 @@
     seq, rank = here(plan)
     for to in range(plan.group):
         starts, share = project_columns(plan, to)
-        project_cut[to] = jnp.concatenate([project[:, c : c + share] for c in starts], axis=1)
+        project_cut[to] = fold_rows(jnp.concatenate([project[:, c : c + share] for c in starts], axis=1))
     meet(group_devices(plan, seq, rank))
     copies = start_swap(plan, seq, rank, project_cut, project_out, p_send, p_recv)
     for to in range(plan.group):
@@ -552,7 +609,10 @@
 def swap_in(plan, project, up):
     rows = project.shape[0]
     dma = pltpu.SemaphoreType.DMA
-    shapes = [(plan.group, rows, project.shape[1] // plan.group), (plan.group, rows, up.shape[1] // plan.group)]
+    shapes = [
+        (plan.group, rows // 2, 2 * project.shape[1] // plan.group),
+        (plan.group, rows, up.shape[1] // plan.group),
+    ]
     return call(
         functools.partial(swap_in_kernel, plan),
         "swap_in",
@@ -563,29 +623,65 @@
     )
 
 
-def swap_out_kernel(plan, columns, pieces, out, got, send, recv):
-    seq, rank = here(plan)
-    meet(group_devices(plan, seq, rank))
-    copies = start_swap(plan, seq, rank, pieces, got, send, recv)
-    for copy in copies:
-        copy.wait()
+def place_columns(plan, got, out, columns, unfold):
     for source in range(plan.group):
         starts, share = columns(plan, source)
-        piece = got[source].astype(F32)
+        piece = got[source]
+        piece = (unfold_rows(piece) if unfold else piece).astype(F32)
         for i, c in enumerate(starts):
             out[:, c : c + share] = piece[:, i * share : (i + 1) * share]
 
 
-def swap_out(plan, pieces, columns, name, ident):
+def finish_kernel(plan, up, project, piece, up_out, project_out, everyone, up_got, project_got,
+                  u_send, u_recv, p_send, p_recv, send, recv):
+    seq, rank = here(plan)
+    meet(group_devices(plan, seq, rank) + column_devices(plan, seq, rank))
+    near = []
+    everyone[seq, rank] = piece[...]
+    for step in range(1, plan.group):
+        to = other(rank, step, plan.group)
+        copy = remote(piece, everyone.at[seq, rank], send.at[0, step], recv.at[0, step], plan.device_of(seq, to))
+        copy.start()
+        near.append(copy)
+    ups = start_swap(plan, seq, rank, up, up_got, u_send, u_recv)
+    projects = start_swap(plan, seq, rank, project, project_got, p_send, p_recv)
+    for copy in near:
+        copy.wait_recv()
+    far = []
+    for step in range(1, plan.sequences):
+        to = other(seq, step, plan.sequences)
+        copy = remote(everyone.at[seq], everyone.at[seq], send.at[1, step], recv.at[1, step], plan.device_of(to, rank))
+        copy.start()
+        far.append(copy)
+    for copy in ups:
+        copy.wait()
+    place_columns(plan, up_got, up_out, lambda p, r: up_columns(p, r, up_out.shape[1]), False)
+    for copy in projects:
+        copy.wait()
+    place_columns(plan, project_got, project_out, project_columns, True)
+    for copy in far:
+        copy.wait_recv()
+    for copy in near + far:
+        copy.wait_send()
+
+
+def finish(plan, up, project, piece):
     dma = pltpu.SemaphoreType.DMA
-    group, rows, cols = pieces.shape
+    most = max(plan.group, plan.sequences)
+    rows = up.shape[1]
     return call(
-        functools.partial(swap_out_kernel, plan, columns),
-        name,
-        ident,
-        jax.ShapeDtypeStruct((rows, group * cols), F32),
-        [pltpu.VMEM(pieces.shape, BF16), dma((plan.group,)), dma((plan.group,))],
-        (pieces,),
+        functools.partial(finish_kernel, plan),
+        "finish",
+        6,
+        (
+            jax.ShapeDtypeStruct((rows, plan.group * up.shape[2]), F32),
+            jax.ShapeDtypeStruct((rows, plan.group * project.shape[2] // 2), F32),
+            jax.ShapeDtypeStruct((plan.sequences, plan.group) + piece.shape, F32),
+        ),
+        [pltpu.VMEM(up.shape, BF16), pltpu.VMEM(project.shape, BF16)]
+        + [dma((plan.group,))] * 4
+        + [dma((2, most))] * 2,
+        (up, project, piece),
     )
 
 
@@ -829,47 +925,9 @@
     return out, extra, table[:, :, 0].transpose(1, 0, 2).reshape(plan.sequences, -1)
 
 
-def spread_kernel(plan, piece, everyone, send, recv):
-    device = lax.axis_index("dev")
-    seq, rank = plan.place_of(device)
-    meet(group_devices(plan, seq, rank) + column_devices(plan, seq, rank))
-    copies = []
-    everyone[seq, rank] = piece[...]
-    for step in range(1, plan.group):
-        to = other(rank, step, plan.group)
-        copy = remote(piece, everyone.at[seq, rank], send.at[0, step], recv.at[0, step], plan.device_of(seq, to))
-        copy.start()
-        copies.append(copy)
-    for copy in copies:
-        copy.wait_recv()
-    across = []
-    for step in range(1, plan.sequences):
-        to = other(seq, step, plan.sequences)
-        copy = remote(everyone.at[seq], everyone.at[seq], send.at[1, step], recv.at[1, step], plan.device_of(to, rank))
-        copy.start()
-        across.append(copy)
-    for copy in across:
-        copy.wait_recv()
-    for copy in copies + across:
-        copy.wait_send()
-
-
-def spread(plan, piece, ident):
-    dma = pltpu.SemaphoreType.DMA
-    most = max(plan.group, plan.sequences)
-    return call(
-        functools.partial(spread_kernel, plan),
-        "spread",
-        ident,
-        jax.ShapeDtypeStruct((plan.sequences, plan.group) + piece.shape, piece.dtype),
-        [dma((2, most)), dma((2, most))],
-        (piece,),
-    )
-
-
 def over_sequences(plan, pieces):
     full = lax.all_gather(pieces, "dev", axis=0, axis_index_groups=plan.rank_groups())
-    return full.reshape(2, plan.width, pieces.shape[2])
+    return full.reshape((plan.devices,) + pieces.shape[1:])
 
 
 def terms_to_send(plan, grad, rows):
@@ -975,7 +1033,10 @@
     project_pieces, up_pieces = swap_in(plan, project_weight, up_weight)
     project_pieces, up_pieces, merge_pair = lax.optimization_barrier((project_pieces, up_pieces, merge_pair))
     project_pair = over_sequences(plan, project_pieces)
-    up_pair = over_sequences(plan, up_pieces)
+    share = project_pair.shape[2] // 2
+    project_pair = jnp.concatenate([project_pair[:, :, :share], project_pair[:, :, share:]], axis=1)
+    project_pair = project_pair.reshape(2, width, share)
+    up_pair = over_sequences(plan, up_pieces).reshape(2, width, -1)
     down_pair = down_slices(plan, down_weight)
 
     token_window, grad_window, mods, merge_pair = entry(plan, tokens, cotangent, mod_part, merge_pair)
@@ -985,8 +1046,7 @@
     normed_full, _ = layer_norm(token_window.astype(F32))
     hidden_a = (normed_full * (1.0 + pick(scale_a, is_text)) + pick(shift_a, is_text)).astype(BF16)
     projected = stream_dot(plan, hidden_a, project_pair, is_text).astype(BF16)
-    queries, keys, values = jnp.split(projected, 3, axis=1)
-    attended = attend(plan, queries, keys, values, bias)
+    attended = attend(plan, projected, bias)
 
     own_tokens = own_rows(plan, token_window, rank)
     own_grad = own_rows(plan, grad_window, rank)
@@ -1015,13 +1075,12 @@
         plan, grad_upper, up_pair, window_text, own_grad, middle, gate_a, scale_b, text_mask
     )
     foreign = (row_seq != seq)[:, None]
-    grad_attended = stream_dot_back(plan, grad_merged, merge_pair, is_text).astype(BF16)
     merge_term = weight_terms(plan, attended, grad_merged, is_text).astype(BF16)
 
-    grad_projected = jnp.concatenate(attend_back(plan, queries, keys, values, grad_attended, bias), axis=1)
+    grad_projected = attend_back(plan, projected, grad_merged, merge_pair, window_text, bias)
     grad_projected, down_sum = lax.optimization_barrier((grad_projected, down_sum))
     down_grad = down_sum.astype(F32)
-    project_term = terms_to_send(plan, weight_terms(plan, hidden_a, grad_projected, is_text), mod_rows)
+    project_term = project_terms(plan, hidden_a, grad_projected, window_text, mod_rows)
     grad_projected, project_term = lax.optimization_barrier((grad_projected, project_term))
     project_sum = over_sequences_sum(plan, project_term)
     activated, project_term = lax.optimization_barrier((activated, project_term))
@@ -1051,13 +1110,11 @@
     own_grads = grad_table.astype(BF16)
     modulation_grad = lax.dot_general(silu_part, own_grads, CONTRACT_FIRST, preferred_element_type=F32)
     grad_piece = lax.dot_general(own_grads, modulation_weight, CONTRACT_LAST, preferred_element_type=F32)
-    merge_out, merge_term, project_sum, own_grads = lax.optimization_barrier(
-        (merge_out, merge_term, project_sum, own_grads)
+    merge_out, merge_term, project_sum, modulation_grad, down_grad, layer_out, tokens_grad = lax.optimization_barrier(
+        (merge_out, merge_term, project_sum, modulation_grad, down_grad, layer_out, tokens_grad)
     )
     merge_grad = merge_sum(plan, merge_term, merge_out, rank).reshape(merge_weight.shape).astype(F32)
-    up_grad = swap_out(plan, up_sum, lambda p, r: up_columns(p, r, up_weight.shape[1]), "up_out", 7)
-    project_grad = swap_out(plan, project_sum, project_columns, "project_out", 6)
-    everyone = spread(plan, grad_piece.reshape(-1, 128), 13)
+    up_grad, project_grad, everyone = finish(plan, up_sum, project_sum, grad_piece.reshape(-1, 128))
     everyone = everyone.reshape(2, plan.devices // 2, plan.sequences, mod_rows)
     grad_silu = (everyone[0] + everyone[1]).transpose(1, 0, 2).reshape(plan.sequences, width)
     conditioning_grad = jax.vjp(jax.nn.silu, cond_float)[1](grad_silu)[0]

time: 625 us -> 599 us (0.958)
  matrix products: 41.2 us -> 28.2 us
    pallas_call x9 -> x7, Pallas kernels: 352 us -> 339 us  [call(): pl.pallas_call(kernel, out_shape=out_shape, in_specs=in_specs or [VMEM] *...]
    all_gather x1, waiting for transfers between devices: 46 us -> 34 us  [down_slices(): lax.all_gather(weight, 'dev', axis=0, axis_index_groups=plan.rank_groups())]
    unnamed x195 -> x187, local copies, waits for them, and re-layouts: 43.9 us -> 54.6 us
    dot_general x4 -> x3, matrix products: 15 us -> 7.73 us  [weight_terms(): lax.dot_general(rows[:plan.image_end], image, CONTRACT_FIRST, preferred_e...]
    pallas_call x1 -> x2, Pallas kernels: 12.5 us -> 16.7 us  [the longest x1 12.8 us: attend(): pl.pallas_call(functools.partial(attend_kernel, plan.heads, block), out_s...]
  transfers between devices with their start and end apart: 8 -> 8, of which waited for: 3 -> 3; matrix products, arithmetic and copies ran while one was open for 20% -> 16% of each run, Pallas kernels for 62% -> 64%
where the time goes in v4:
time: 599 us; the launch traced here: 593 us
  Pallas kernels  381 us (64%)
  local copies, waits for them, and re-layouts  73 us (12%)
  waiting for transfers between devices  49.2 us (8%)
  other arithmetic  44.3 us (7%)
  matrix products  28.2 us (5%)
  between operations  16.3 us (3%)
    pallas_call x7, Pallas kernels, call(): pl.pallas_call(kernel, out_shape=out_shape, in_specs=in_specs or [VMEM] *...  339 us
    unnamed x187, local copies, waits for them, and re-layouts  54.6 us
    all_gather x1, waiting for transfers between devices, down_slices(): lax.all_gather(weight, 'dev', axis=0, axis_index_groups=plan.rank_groups())  34 us
    pallas_call x1, Pallas kernels, attend_back(): pl.pallas_call(functools.partial(attend_back_kernel, plan.heads, rows //...  25.1 us
    pallas_call x1, Pallas kernels, attend(): pl.pallas_call(functools.partial(attend_kernel, plan.heads, block), out_s...  12.8 us
  transfers between devices with their start and end apart: 8, of which 3 were waited for; matrix products, arithmetic and copies ran while one was open for 16% of the time, Pallas kernels for 64%

profile of v4, /device:TPU:0, one launch (start us, length us, event | category | flops | bytes accessed | tf_op | source)
XLA Modules:
  0.0 592.7 jit_solution(5670834286186165566)
XLA Ops:
  10.4 28.8 %swap_in.1 = (bf16[8,48,1152]{2,1,0:T(8,128)(2,1)}, bf16[8,96,768]{2,1,0:T(8,128)(2,1)}) custom-call(bf16[96,4608]{1,0:T(8,128)(2,1)S(1)} %copy-done.38, bf16[96,6144]{1,0:T(8,128)(2,1)S(1)} %copy-done.34), custom_call_target="tpu_custom_call" | custom-call | tf_op jit(solution)/shard_map/swap_in/pallas_call | solution.py:293
  39.3 3.5 all-gather.9.cloned.1.call-done
  54.7 78.8 %entry.1 = (bf16[1280,1536]{1,0:T(8,128)(2,1)S(1)}, bf16[1280,1536]{1,0:T(8,128)(2,1)S(1)}, f32[8,2,9,128]{3,2,1,0:T(8,128)S(1)}, bf16[2,2,96,1536]{3,2,1,0:T(8,128)(2,1)S(1)}) custom-call(bf16[144,1536]{1,0:T(8,128)(2,1)S(1)} %copy-done.45, bf16[144,1536]{1,0:T(8,128)(2,1)S(1)} %copy-done.46, f32[8,4,9,128]{3,2,1,0:T(8,128)S(1)} %bitcast.70, ...), custom_call_target="tpu_custom_call" | custom-call | tf_op jit(solution)/shard_map/entry/pallas_call | solution.py:293
  139.2 3.1 convert_reduce_fusion
  143.6 6.0 %multiply_convert_fusion = (bf16[1280,1536]{1,0:T(8,128)(2,1)}, bf16[1280,1536]{1,0:T(8,128)(2,1)S(1)}, bf16[1280,1536]{1,0:T(8,128)(2,1)}) fusion(f32[1536]{0:T(1024)S(1)} %get-tuple-element.102, f32[1536]{0:T(1024)S(1)} %get-tuple-element.103, pred[1280]{0:T(1024)(128)(4,1)S(1)} %copy-done.75, bf16[1280,1536]{1,0:T(8,128)(2,1)S(1)} %copy-done.16, ...), kind=kLoop, calls=%fused_computation.8 | loop fusion | flops 27525120 | bytes 19710464 | tf_op jit(solution)/shard_map/convert_element_type | solution.py:1063
  151.1 3.4 fusion.80
  174.5 12.8 %attend.1.rows = bf16[1280,192]{1,0:T(8,128)(2,1)S(1)} custom-call(bf16[1280,576]{1,0:T(8,128)(2,1)S(1)} %pad_maximum_fusion.5.projected, f32[1,1280]{1,0:T(1,128)S(1)} %and_select_fusion.bias_ref), custom_call_target="tpu_custom_call" | custom-call | flops 5033164800 | bytes 1966080 | tf_op jit(solution)/shard_map/attend/pallas_call | solution.py:127
  187.3 54.8 %middle.1 = (f32[160,1536]{1,0:T(8,128)S(1)}, bf16[1280,1536]{1,0:T(8,128)(2,1)S(1)}) custom-call(bf16[1280,192]{1,0:T(8,128)(2,1)S(1)} %attend.1.rows, bf16[2,192,1536]{2,1,0:T(8,128)(2,1)S(1)} %bitcast.68, f32[1280,1]{1,0:T(8,128)S(1)} %fusion.56.window_text.text, bf16[160,1536]{1,0:T(8,128)(2,1)S(1)} %pad_maximum_fusion.7.tokens, ...), custom_call_target="tpu_custom_call" | custom-call | tf_op jit(solution)/shard_map/middle/pallas_call | solution.py:293
  245.9 2.9 fusion.79
  249.5 2.9 fusion.25
  256.9 3.3 fusion.32
  262.8 34.0 %all-gather.15.cloned.1.call-done = bf16[1536,1536]{1,0:T(8,128)(2,1)} async-done(((bf16[384,1536]{1,0:T(8,128)(2,1)}), bf16[1536,1536]{1,0:T(8,128)(2,1)}) %all-gather.15.cloned.1.call-update) | async-done | bytes 4718608 | tf_op jit(solution)/shard_map/all_gather | solution.py:963
  296.9 5.7 fusion.19
  302.8 2.9 copy-done.10
  308.0 3.2 fusion.12.rows
  312.4 3.4 fusion.28
  321.7 61.2 %back.1 = (f32[160,1536]{1,0:T(8,128)S(1)}, f32[160,1536]{1,0:T(8,128)S(1)}, bf16[1280,1536]{1,0:T(8,128)(2,1)S(1)}) custom-call(bf16[1280,768]{1,0:T(8,128)(2,1)S(1)} %copy-done.7, bf16[2,1536,768]{2,1,0:T(8,128)(2,1)} %bitcast.73, f32[1280,1]{1,0:T(8,128)S(1)} %fusion.56.window_text.text, bf16[160,1536]{1,0:T(8,128)(2,1)S(1)} %pad_maximum_fusion.8.grad, ...), custom_call_target="tpu_custom_call" | custom-call | tf_op jit(solution)/shard_map/back/pallas_call | solution.py:293
  386.9 25.1 %attend_back.1.grads.rows = bf16[1280,576]{1,0:T(8,128)(2,1)} custom-call(bf16[1280,576]{1,0:T(8,128)(2,1)} %copy-done.27, bf16[1280,1536]{1,0:T(8,128)(2,1)} %copy-done.51, bf16[2,192,1536]{2,1,0:T(8,128)(2,1)} %bitcast.67, f32[1280,1]{1,0:T(8,128)} %copy-done.3, f32[1,1280]{1,0:T(1,128)} %copy-done.50), custom_call_target="tpu_custom_call" | custom-call | flops 12582912000 | bytes 3440640 | tf_op jit(solution)/shard_map/attend_back/pallas_call | solution.py:183
  415.5 3.9 project_terms.1
  423.2 4.6 pad_maximum_fusion
  430.9 40.2 %output.1 = (f32[160,1536]{1,0:T(8,128)S(1)}, bf16[144,1536]{1,0:T(8,128)(2,1)S(1)}, bf16[144,1536]{1,0:T(8,128)(2,1)S(1)}, bf16[4,96,1536]{2,1,0:T(8,128)(2,1)}) custom-call(bf16[1280,768]{1,0:T(8,128)(2,1)S(1)} %copy-done.9, bf16[2,768,1536]{2,1,0:T(8,128)(2,1)S(1)} %bitcast.64, f32[1280,1]{1,0:T(8,128)S(1)} %copy-done.4, ...), custom_call_target="tpu_custom_call" | custom-call | tf_op jit(solution)/shard_map/output/pallas_call | solution.py:293
  479.2 48.3 %last.1 = (f32[144,1536]{1,0:T(8,128)S(1)}, f32[144,1536]{1,0:T(8,128)S(1)}, f32[8,4,1,1152]{3,2,1,0:T(1,128)S(1)}) custom-call(bf16[1280,576]{1,0:T(8,128)(2,1)S(1)} %copy-done.26, bf16[2,1536,576]{2,1,0:T(8,128)(2,1)S(1)} %bitcast.61, f32[1280,1]{1,0:T(8,128)S(1)} %copy-done.4, bf16[160,1536]{1,0:T(8,128)(2,1)S(1)} %copy-done.12, ...), custom_call_target="tpu_custom_call" | custom-call | tf_op jit(solution)/shard_map/last/pallas_call | solution.py:293
  533.7 9.7 %reduce-scatter.7.cloned.1.call-done = bf16[1,8,48,1152]{3,2,1,0:T(8,128)(2,1)} async-done(((bf16[4,8,48,1152]{3,2,1,0:T(8,128)(2,1)}), bf16[1,8,48,1152]{3,2,1,0:T(8,128)(2,1)}) %reduce-scatter.7.cloned.1.call-update) | async-done | bytes 884752 | tf_op jit(solution)/shard_map/reduce_scatter | solution.py:938
  546.5 26.9 %finish.1 = (f32[96,6144]{1,0:T(8,128)S(1)}, f32[96,4608]{1,0:T(8,128)S(1)}, f32[4,8,3,128]{3,2,1,0:T(4,128)S(1)}) custom-call(bf16[8,96,768]{2,1,0:T(8,128)(2,1)S(1)} %bitcast.66, bf16[8,48,1152]{2,1,0:T(8,128)(2,1)S(1)} %bitcast.71, f32[3,128]{1,0:T(4,128)S(1)} %reshape.311.piece), custom_call_target="tpu_custom_call" | custom-call | tf_op jit(solution)/shard_map/finish/pallas_call | solution.py:293
  (303 shorter events, 107.0 us)
Async XLA Ops:
  7.2 43.2 %copy-start = (bf16[96,9216]{1,0:T(8,128)(2,1)S(1)}, bf16[96,9216]{1,0:T(8,128)(2,1)}, u32[]{:S(2)}) copy-start(bf16[96,9216]{1,0:T(8,128)(2,1)} %param.12) | copy-start | bytes 5308420
  7.2 37.0 %copy-start.69 = (bf16[4,1536]{1,0:T(4,128)(2,1)S(1)}, bf16[4,1536]{1,0:T(4,128)(2,1)}, u32[]{:S(2)}) copy-start(bf16[4,1536]{1,0:T(4,128)(2,1)} %param.10) | copy-start | bytes 36868
  7.2 37.1 %copy-start.87 = (s32[4]{0:T(128)S(1)}, s32[4]{0:T(128)}, u32[]{:S(2)}) copy-start(s32[4]{0:T(128)} %param.11) | copy-start | bytes 52
  7.2 35.6 %all-gather.9.cloned.1.call-start = ((), (), s32[]{:S(2)}) async-start(), calls=%async_computation.8 | async-start | bytes 1474560 | tf_op jit(solution)/shard_map/all_gather | solution.py:943
  7.9 143.2 %all-gather.11.cloned.1.call-start = ((), (), s32[]{:S(2)}) async-start(), calls=%async_computation.9 | async-start | bytes 4423680 | tf_op jit(solution)/shard_map/all_gather | solution.py:929
  42.8 203.1 %all-gather.13.cloned.1.call-start = ((), (), s32[]{:S(2)}) async-start(), calls=%async_computation.10 | async-start | bytes 5898240 | tf_op jit(solution)/shard_map/all_gather | solution.py:929
  43.5 253.3 %all-gather.15.cloned.1.call-start = ((), (), s32[]{:S(2)}) async-start(), calls=%async_computation.11 | async-start | bytes 5898240 | tf_op jit(solution)/shard_map/all_gather | solution.py:963
  44.1 367.8 %reduce-scatter.5.cloned.1.call-start = ((), (), s32[]{:S(2)}) async-start(), calls=%async_computation.4 | async-start | bytes 5898240 | tf_op jit(solution)/shard_map/reduce_scatter | solution.py:938
  46.4 92.1 %copy-start.74 = (pred[1280]{0:T(1024)(128)(4,1)}, pred[1280]{0:T(1024)(128)(4,1)S(1)}, u32[]{:S(2)}) copy-start(pred[1280]{0:T(1024)(128)(4,1)S(1)} %fusion.68) | copy-start | bytes 3844
  47.7 90.8 %copy-start.72 = (pred[1280]{0:T(1024)(128)(4,1)}, pred[1280]{0:T(1024)(128)(4,1)S(1)}, u32[]{:S(2)}) copy-start(pred[1280]{0:T(1024)(128)(4,1)S(1)} %fusion.69) | copy-start | bytes 3844
  48.4 126.1 %copy-start.50 = (f32[1,1280]{1,0:T(1,128)}, f32[1,1280]{1,0:T(1,128)S(1)}, u32[]{:S(2)}) copy-start(f32[1,1280]{1,0:T(1,128)S(1)} %and_select_fusion.bias_ref) | copy-start | bytes 15364
  49.1 272.6 %copy-start.3 = (f32[1280,1]{1,0:T(8,128)}, f32[1280,1]{1,0:T(8,128)S(1)}, u32[]{:S(2)}) copy-start(f32[1280,1]{1,0:T(8,128)S(1)} %fusion.56.window_text.text) | copy-start | bytes 15364
  149.7 169.7 %copy-start.58 = (bf16[144,1536]{1,0:T(8,128)(2,1)}, bf16[144,1536]{1,0:T(8,128)(2,1)S(1)}, u32[]{:S(2)}) copy-start(bf16[144,1536]{1,0:T(8,128)(2,1)S(1)} %get-tuple-element.142) | copy-start | bytes 1327108
  151.0 36.2 %copy-start.11 = (bf16[160,1536]{1,0:T(8,128)(2,1)}, bf16[160,1536]{1,0:T(8,128)(2,1)S(1)}, u32[]{:S(2)}) copy-start(bf16[160,1536]{1,0:T(8,128)(2,1)S(1)} %pad_maximum_fusion.7.tokens) | copy-start | bytes 1474564
  262.8 209.7 %reduce-scatter.9.cloned.1.call-start = ((), (), s32[]{:S(2)}) async-start(), calls=%async_computation.6 | async-start | bytes 5898240 | tf_op jit(solution)/shard_map/reduce_scatter | solution.py:938
  318.5 224.9 %reduce-scatter.7.cloned.1.call-start = ((), (), s32[]{:S(2)}) async-start(), calls=%async_computation.5 | async-start | bytes 4423680 | tf_op jit(solution)/shard_map/reduce_scatter | solution.py:938
  421.3 159.8 %reduce-scatter.11.cloned.1.call-start = ((), (), s32[]{:S(2)}) async-start(), calls=%async_computation.7 | async-start | bytes 1474560 | tf_op jit(solution)/shard_map/reduce_scatter | solution.py:938
  430.9 40.2 %copy-start.18 = (f32[160,1536]{1,0:T(8,128)S(1)}, f32[160,1536]{1,0:T(8,128)}, u32[]{:S(2)}) copy-start(f32[160,1536]{1,0:T(8,128)} %copy-done.17) | copy-start | bytes 2949124
  430.9 40.2 %copy-start.20 = (f32[160,1536]{1,0:T(8,128)S(1)}, f32[160,1536]{1,0:T(8,128)}, u32[]{:S(2)}) copy-start(f32[160,1536]{1,0:T(8,128)} %copy-done.19) | copy-start | bytes 2949124
  430.9 40.2 %copy-start.36 = (f32[160,1536]{1,0:T(8,128)S(1)}, f32[160,1536]{1,0:T(8,128)}, u32[]{:S(2)}) copy-start(f32[160,1536]{1,0:T(8,128)} %copy-done.35) | copy-start | bytes 2949124
  430.9 40.2 %copy-start.59 = (bf16[144,1536]{1,0:T(8,128)(2,1)S(1)}, bf16[144,1536]{1,0:T(8,128)(2,1)}, u32[]{:S(2)}) copy-start(bf16[144,1536]{1,0:T(8,128)(2,1)} %copy-done.58) | copy-start | bytes 1327108
  430.9 40.2 %copy-start.67 = (bf16[16,1536]{1,0:T(8,128)(2,1)S(1)}, bf16[16,1536]{1,0:T(8,128)(2,1)}, u32[]{:S(2)}) copy-start(bf16[16,1536]{1,0:T(8,128)(2,1)} %get-tuple-element.140) | copy-start | bytes 147460
  479.2 48.5 %copy-start.63 = (bf16[1,384,1536]{2,1,0:T(8,128)(2,1)S(1)}, bf16[1,384,1536]{2,1,0:T(8,128)(2,1)}, u32[]{:S(2)}) copy-start(bf16[1,384,1536]{2,1,0:T(8,128)(2,1)} %reduce-scatter.5.cloned.1.call-done) | copy-start | bytes 3538948
  532.7 47.1 %copy-start.70 = (bf16[4,1536]{1,0:T(4,128)(2,1)S(1)}, bf16[4,1536]{1,0:T(4,128)(2,1)}, u32[]{:S(2)}) copy-start(bf16[4,1536]{1,0:T(4,128)(2,1)} %param.10) | copy-start | bytes 36868
  (74 other events, 252.6 us)
Sparse Core Ops, SparseCore 0:
  9.6 33.1 all-gather.8
  44.4 73.5 all-gather.10
  119.5 88.0 all-gather.12
  209.0 87.8 all-gather.14
  299.0 83.6 reduce-scatter.4
  384.9 86.8 reduce-scatter.8
  474.1 69.2 reduce-scatter.6
  545.7 30.2 reduce-scatter.10

commit v5 on v4

--- a/solution.py
+++ b/solution.py
@@ -1,4 +1,5 @@
 import functools
+import types
 
 import jax
 import jax.numpy as jnp
@@ -209,36 +210,49 @@
     return jnp.concatenate([piece[:, :half], piece[:, half:]], axis=0)
 
 
-def project_terms_kernel(plan, rows_of, hidden, grads, text, out):
-    cols = grads.shape[1]
-    spans = ((0, plan.image_end), (plan.text_start, plan.rows))
-    chunk = 4 * 96
-    for stream, (first, last) in enumerate(spans):
-        mask = text[pl.ds(first, last - first)]
+def terms_kernel(plan, fold, chunk, rows, grads, text, out, kept):
+    width = rows.shape[1]
+    for stream, (first, last) in enumerate(((0, plan.image_end), (plan.text_start, plan.rows))):
+        count = last - first
+        mask = text[pl.ds(first, count)]
         keep = (mask > 0) if stream else (mask <= 0)
-        part = jnp.where(keep, grads[pl.ds(first, last - first)], jnp.zeros((), BF16))
-        for start in range(0, plan.width, chunk):
+        kept[pl.ds(0, count)] = jnp.where(keep, grads[pl.ds(first, count)], jnp.zeros((), BF16))
+
+        def step(i, carry):
+            start = pl.multiple_of(i * chunk, chunk)
             term = lax.dot_general(
-                hidden[pl.ds(first, last - first), start : start + chunk], part, CONTRACT_FIRST, preferred_element_type=F32
+                rows[pl.ds(first, count), pl.ds(start, chunk)],
+                kept[pl.ds(0, count)],
+                CONTRACT_FIRST,
+                preferred_element_type=F32,
             ).astype(BF16)
-            for i in range(chunk // rows_of):
-                owner = (stream * plan.width + start) // rows_of + i
-                out[owner] = fold_rows(term[i * rows_of : (i + 1) * rows_of])
-
-
-def project_terms(plan, hidden, grads, text, rows):
-    cols = grads.shape[1]
-    shape = (plan.devices, rows // 2, 2 * cols)
-    out = pl.pallas_call(
-        functools.partial(project_terms_kernel, plan, rows),
+            if fold:
+                for j in range(chunk // fold):
+                    out[(stream * width) // fold + i * (chunk // fold) + j] = fold_rows(term[j * fold : (j + 1) * fold])
+            else:
+                out[stream, pl.ds(start, chunk)] = term
+            return carry
+
+        if width == chunk:
+            step(0, 0)
+        else:
+            lax.fori_loop(0, width // chunk, step, 0)
+
+
+def weight_terms(plan, rows, grads, text, name, fold=0):
+    width, cols = rows.shape[1], grads.shape[1]
+    chunk = 384 if width % 384 == 0 else width
+    shape = (2 * width // fold, fold // 2, 2 * cols) if fold else (2, width, cols)
+    return pl.pallas_call(
+        functools.partial(terms_kernel, plan, fold, chunk),
         out_shape=jax.ShapeDtypeStruct(shape, BF16),
         in_specs=[pl.BlockSpec(memory_space=pltpu.VMEM)] * 3,
         out_specs=pl.BlockSpec(memory_space=pltpu.VMEM),
+        scratch_shapes=[pltpu.VMEM((plan.image_end, cols), BF16)],
         compiler_params=pltpu.CompilerParams(vmem_limit_bytes=40 << 20),
-        cost_estimate=pl.CostEstimate(flops=4 * plan.rows * plan.width * cols, bytes_accessed=1 << 23, transcendentals=0),
-        name="project_terms",
-    )(hidden, grads, text)
-    return out.reshape((plan.sequences, plan.group) + shape[1:])
+        cost_estimate=pl.CostEstimate(flops=3 * plan.rows * width * cols, bytes_accessed=1 << 23, transcendentals=0),
+        name=name,
+    )(rows, grads, text)
 
 
 VMEM = pl.BlockSpec(memory_space=pltpu.VMEM)
@@ -288,7 +302,7 @@
     return [other(device, step, plan.devices) for step in range(1, plan.devices)]
 
 
-def call(kernel, name, ident, out_shape, scratch, operands, in_specs=None, out_specs=None):
+def call(kernel, name, ident, out_shape, scratch, operands, in_specs=None, out_specs=None, vmem=40 << 20):
     outs = out_shape if isinstance(out_shape, tuple) else (out_shape,)
     return pl.pallas_call(
         kernel,
@@ -297,7 +311,7 @@
         out_specs=out_specs or (tuple([VMEM] * len(outs)) if isinstance(out_shape, tuple) else VMEM),
         scratch_shapes=scratch,
         compiler_params=pltpu.CompilerParams(
-            collective_id=ident, has_side_effects=True, vmem_limit_bytes=40 << 20
+            collective_id=ident, has_side_effects=True, vmem_limit_bytes=vmem
         ),
         name=name,
     )(*operands)
@@ -328,8 +342,9 @@
     return [
         pltpu.VMEM((half, own, width), F32),
         pltpu.VMEM((half, own, width), F32),
-        pltpu.VMEM((half, own, width), BF16),
-        pltpu.VMEM((half, own, width), BF16),
+        pltpu.VMEM((own, width), F32),
+        pltpu.VMEM((half - 1, own, width), BF16),
+        pltpu.VMEM((half - 1, own, width), BF16),
         pltpu.SemaphoreType.DMA((half,)),
         pltpu.SemaphoreType.DMA((half,)),
         pltpu.SemaphoreType.DMA((half,)),
@@ -337,51 +352,77 @@
     ]
 
 
-SUM_SCRATCH = 8
-
-
-def product(plan, rows, pair, text, dims, rank):
+SUM_SCRATCH = 9
+
+
+def product(plan, rows, pair, text, dims, rank, out):
     block = load_block(plan, rows, rank)
-    mask = load_block(plan, text, rank)
-    parts = [lax.dot_general(block, pair[j], dims, preferred_element_type=F32) for j in range(2)]
-    return jnp.where(mask > 0, parts[1], parts[0])
-
-
-def scatter_sum(plan, seq, rank, rows, pair, text, dims, away, near, going, coming, pair_send, pair_recv, far_send, far_recv):
+    text_row = load_block(plan, text, rank) > 0
+    chunk = plan.width // 4
+
+    def step(i, carry):
+        cols = pl.ds(pl.multiple_of(i * chunk, chunk), chunk)
+        parts = []
+        for stream in range(2):
+            weight = pair[stream, cols, :] if dims is CONTRACT_LAST else pair[stream, :, cols]
+            parts.append(lax.dot_general(block, weight, dims, preferred_element_type=F32))
+        out[:, cols] = jnp.where(text_row, parts[1], parts[0])
+        return carry
+
+    lax.fori_loop(0, 4, step, 0)
+
+
+def scatter_sum(*args):
+    return scatter_start(*args)()
+
+
+def scatter_start(plan, seq, rank, rows, pair, text, dims, away, near, mine, going, coming,
+                  pair_send, pair_recv, far_send, far_recv):
     half = plan.group // 2
     chip, core = lax.div(rank, 2), lax.rem(rank, 2)
     partner = plan.device_of(seq, 2 * chip + 1 - core)
     order = list(range(1, half)) + [0]
 
-    def for_partner(step):
-        away[step] = product(plan, rows, pair, text, dims, 2 * other(chip, step, half) + 1 - core)
-        copy = remote(away.at[step], near.at[step], pair_send.at[step], pair_recv.at[step], partner)
-        copy.start()
-        return copy
-
-    pairs, sends = [for_partner(order[0])], []
-    for i, step in enumerate(order):
-        chip_to = other(chip, step, half)
-        mine = product(plan, rows, pair, text, dims, 2 * chip_to + core)
-        if i + 1 < half:
-            pairs.append(for_partner(order[i + 1]))
-        pairs[i].wait_recv()
-        both = mine + near[step]
-        if step == 0:
-            total = both
-        else:
-            going[step] = both.astype(BF16)
-            copy = remote(
-                going.at[step], coming.at[step], far_send.at[step], far_recv.at[step], plan.device_of(seq, 2 * chip_to + core)
-            )
-            copy.start()
-            sends.append(copy)
-    for step, copy in zip(order, sends):
-        copy.wait_recv()
-        total = total + coming[step].astype(F32)
-    for copy in pairs + sends:
-        copy.wait_send()
-    return total
+    def pair_copy(step):
+        return remote(away.at[step], near.at[step], pair_send.at[step], pair_recv.at[step], partner)
+
+    def far_copy(step):
+        to = plan.device_of(seq, 2 * other(chip, step, half) + core)
+        return remote(going.at[step - 1], coming.at[step - 1], far_send.at[step], far_recv.at[step], to)
+
+    def for_owner(step):
+        product(plan, rows, pair, text, dims, 2 * other(chip, step, half) + core, mine)
+        pair_copy(step).wait_recv()
+        mine[...] += near[step]
+
+    def turn(i, carry):
+        step = other(i, 1, half)
+        product(plan, rows, pair, text, dims, 2 * other(chip, step, half) + 1 - core, away.at[step])
+        pair_copy(step).start()
+
+        @pl.when(i > 0)
+        def _():
+            for_owner(i)
+            going[i - 1] = mine[...].astype(BF16)
+            far_copy(i).start()
+
+        return carry
+
+    lax.fori_loop(0, half, turn, 0)
+
+    def result():
+        for_owner(0)
+        total = mine[...]
+        for step in range(1, half):
+            far_copy(step).wait_recv()
+            total = total + coming[step - 1].astype(F32)
+        for step in range(half):
+            pair_copy(step).wait_send()
+        for step in range(1, half):
+            far_copy(step).wait_send()
+        return total
+
+    return result
 
 
 def share_scratch(plan):
@@ -626,63 +667,39 @@
 def place_columns(plan, got, out, columns, unfold):
     for source in range(plan.group):
         starts, share = columns(plan, source)
-        piece = got[source]
-        piece = (unfold_rows(piece) if unfold else piece).astype(F32)
+        piece = unfold_rows(got[source]) if unfold else got[source]
         for i, c in enumerate(starts):
             out[:, c : c + share] = piece[:, i * share : (i + 1) * share]
 
 
-def finish_kernel(plan, up, project, piece, up_out, project_out, everyone, up_got, project_got,
-                  u_send, u_recv, p_send, p_recv, send, recv):
+def finish_kernel(plan, up, project, up_out, project_out, up_got, project_got, u_send, u_recv, p_send, p_recv):
     seq, rank = here(plan)
-    meet(group_devices(plan, seq, rank) + column_devices(plan, seq, rank))
-    near = []
-    everyone[seq, rank] = piece[...]
-    for step in range(1, plan.group):
-        to = other(rank, step, plan.group)
-        copy = remote(piece, everyone.at[seq, rank], send.at[0, step], recv.at[0, step], plan.device_of(seq, to))
-        copy.start()
-        near.append(copy)
+    meet(group_devices(plan, seq, rank))
     ups = start_swap(plan, seq, rank, up, up_got, u_send, u_recv)
     projects = start_swap(plan, seq, rank, project, project_got, p_send, p_recv)
-    for copy in near:
-        copy.wait_recv()
-    far = []
-    for step in range(1, plan.sequences):
-        to = other(seq, step, plan.sequences)
-        copy = remote(everyone.at[seq], everyone.at[seq], send.at[1, step], recv.at[1, step], plan.device_of(to, rank))
-        copy.start()
-        far.append(copy)
     for copy in ups:
         copy.wait()
     place_columns(plan, up_got, up_out, lambda p, r: up_columns(p, r, up_out.shape[1]), False)
     for copy in projects:
         copy.wait()
     place_columns(plan, project_got, project_out, project_columns, True)
-    for copy in far:
-        copy.wait_recv()
-    for copy in near + far:
-        copy.wait_send()
-
-
-def finish(plan, up, project, piece):
+
+
+def finish(plan, up, project):
     dma = pltpu.SemaphoreType.DMA
-    most = max(plan.group, plan.sequences)
     rows = up.shape[1]
-    return call(
+    up_grad, project_grad = call(
         functools.partial(finish_kernel, plan),
         "finish",
         6,
         (
-            jax.ShapeDtypeStruct((rows, plan.group * up.shape[2]), F32),
-            jax.ShapeDtypeStruct((rows, plan.group * project.shape[2] // 2), F32),
-            jax.ShapeDtypeStruct((plan.sequences, plan.group) + piece.shape, F32),
+            jax.ShapeDtypeStruct((rows, plan.group * up.shape[2]), BF16),
+            jax.ShapeDtypeStruct((rows, plan.group * project.shape[2] // 2), BF16),
         ),
-        [pltpu.VMEM(up.shape, BF16), pltpu.VMEM(project.shape, BF16)]
-        + [dma((plan.group,))] * 4
-        + [dma((2, most))] * 2,
-        (up, project, piece),
-    )
+        [pltpu.VMEM(up.shape, BF16), pltpu.VMEM(project.shape, BF16)] + [dma((plan.group,))] * 4,
+        (up, project),
+    )
+    return up_grad.astype(F32), project_grad.astype(F32)
 
 
 def pick_rows(table, text):
@@ -787,70 +804,50 @@
     return [pltpu.SemaphoreType.DMA((len(plan.segments),))] * 2
 
 
-def output_kernel(plan, rows, pair, window_text, middle, gate_b, text, *refs):
-    if plan.chip_heads:
-        term, lowered, out, extra, term_out, own, term_send, term_recv, *scratch = refs
-    else:
-        lowered, out, extra, own, *scratch = refs
+def stream_sums(values, masks):
+    return jnp.concatenate([jnp.sum(values * mask, axis=0, keepdims=True) for mask in masks], axis=0)
+
+
+def last_kernel(plan, names, *refs):
+    at = types.SimpleNamespace(**dict(zip(names, refs)))
+    low_scratch = refs[len(names) : len(names) + SUM_SCRATCH]
+    back_scratch = refs[len(names) + SUM_SCRATCH : len(names) + 2 * SUM_SCRATCH]
     device = lax.axis_index("dev")
     seq, rank = plan.place_of(device)
-    extra[...] = jnp.zeros_like(extra)
+    stream = lax.div(2 * seq, plan.sequences)
+    at.layer_extra[...] = jnp.zeros_like(at.layer_extra)
+    at.token_extra[...] = jnp.zeros_like(at.token_extra)
     meet(every_device(plan, device))
+    low_sum = scatter_start(plan, seq, rank, at.activated, at.down_pair, at.window_text, PLAIN, *low_scratch)
+    back_sum = scatter_start(plan, seq, rank, at.grads, at.project_pair, at.window_text, CONTRACT_LAST, *back_scratch)
     swaps = []
     if plan.chip_heads:
         core = lax.rem(rank, 2)
         partner = plan.device_of(seq, 2 * lax.div(rank, 2) + 1 - core)
-        for stream in range(2):
+        for j in range(2):
             copy = remote(
-                term.at[stream, 1 - core], term_out.at[2 * stream + core], term_send.at[stream], term_recv.at[stream], partner
+                at.term.at[j, 1 - core], at.term_out.at[2 * j + core], at.term_send.at[j], at.term_recv.at[j], partner
             )
             copy.start()
             swaps.append(copy)
-            term_out[2 * stream + core] = term[stream, core]
-    total = scatter_sum(plan, seq, rank, rows, pair, window_text, PLAIN, *scratch[:SUM_SCRATCH])
-    lowered[...] = total
-    own[...] = (middle[...] + pick_rows(gate_b[...], text[...]) * total).astype(BF16)
-    edges = (own, plan.rows_dev, extra) + tuple(scratch[SUM_SCRATCH:])
-    start_edges(plan, seq, rank, *edges)
-    out[...] = own[pl.ds(0, plan.rows_dev)]
-    for copy in swaps:
-        copy.wait()
-    finish_edges(plan, seq, rank, *edges)
-
-
-def output_rows(plan, rows, pair, window_text, middle, gate_b, text, term):
-    placed = jax.ShapeDtypeStruct((plan.rows_dev, plan.width), BF16)
-    shapes = (own_shape(plan), placed, placed)
-    operands = (rows, pair, window_text, middle, gate_b, text)
-    scratch = [pltpu.VMEM((plan.own, plan.width), BF16)]
-    if plan.chip_heads:
-        share = plan.width // plan.group // 2
-        shapes += (jax.ShapeDtypeStruct((plan.sequences, share, plan.width), BF16),)
-        operands += (term.reshape(2, 2, share, plan.width),)
-        scratch += [pltpu.SemaphoreType.DMA((2,))] * 2
-    scratch += sum_scratch(plan) + edge_scratch(plan)
-    outs = call(functools.partial(output_kernel, plan), "output", 8, shapes, scratch, operands)
-    return outs if plan.chip_heads else outs + [None] if isinstance(outs, list) else outs + (None,)
-
-
-def stream_sums(values, masks):
-    return jnp.concatenate([jnp.sum(values * mask, axis=0, keepdims=True) for mask in masks], axis=0)
-
-
-def last_kernel(plan, rows, pair, window_text, tokens, grad_middle, scale_a, text, masks, rest, out, extra, table,
-                own, local, first, second, mine, t_send, t_recv, *scratch):
-    device = lax.axis_index("dev")
-    seq, rank = plan.place_of(device)
-    stream = lax.div(2 * seq, plan.sequences)
-    extra[...] = jnp.zeros_like(extra)
-    meet(every_device(plan, device))
-    total = scatter_sum(plan, seq, rank, rows, pair, window_text, CONTRACT_LAST, *scratch[:SUM_SCRATCH])
-    normed, inv = norm_rows(tokens[...].astype(F32))
-    streams = (masks[:, 0:1], masks[:, 1:2])
-    local[:, : plan.width] = stream_sums(total, streams)
-    local[:, plan.width : 2 * plan.width] = stream_sums(total * normed, streams)
-    local[:, 2 * plan.width :] = rest[...]
-    cols = 6 * plan.width // plan.group
+            at.term_out[2 * j + core] = at.term[j, core]
+    text = at.text[...]
+    streams = (at.masks[:, 0:1], at.masks[:, 1:2])
+    width = plan.width
+
+    lowered = low_sum()
+    at.layer_own[...] = (at.middle[...] + pick_rows(at.gate_b[...], text) * lowered).astype(BF16)
+    layer_edges = (at.layer_own, plan.rows_dev, at.layer_extra, at.l_send, at.l_recv)
+    start_edges(plan, seq, rank, *layer_edges)
+    at.local[:, 5 * width :] = stream_sums(at.grad[...].astype(F32) * lowered, streams)
+    at.local[:, 2 * width : 5 * width] = at.rest[...]
+    at.layer[...] = at.layer_own[pl.ds(0, plan.rows_dev)]
+
+    total = back_sum()
+    normed, inv = norm_rows(at.tokens[...].astype(F32))
+    at.local[:, :width] = stream_sums(total, streams)
+    at.local[:, width : 2 * width] = stream_sums(total * normed, streams)
+    cols = 6 * width // plan.group
 
     def chunk(index):
         return pl.ds(pl.multiple_of(index * cols, 128), cols)
@@ -858,80 +855,142 @@
     hops = []
     for step in range(1, plan.group):
         to = other(rank, step, plan.group)
-        copy = remote(local.at[:, chunk(to)], first.at[step], t_send.at[0, step], t_recv.at[0, step], plan.device_of(seq, to))
+        copy = remote(
+            at.local.at[:, chunk(to)], at.first.at[step], at.t_send.at[0, step], at.t_recv.at[0, step], plan.device_of(seq, to)
+        )
         copy.start()
         hops.append(copy)
-    inner = total * (1.0 + pick_rows(scale_a[...], text[...]))
+    inner = total * (1.0 + pick_rows(at.scale_a[...], text))
     mean_grad = jnp.mean(inner, axis=1, keepdims=True)
     mean_cross = jnp.mean(inner * normed, axis=1, keepdims=True)
-    own[...] = grad_middle[...] + inv * (inner - mean_grad - normed * mean_cross)
-    refs = (own, plan.rows_dev, extra) + scratch[SUM_SCRATCH:]
-    start_edges(plan, seq, rank, *refs)
+    at.token_own[...] = at.grad_middle[...] + inv * (inner - mean_grad - normed * mean_cross)
+    token_edges = (at.token_own, plan.rows_dev, at.token_extra, at.e_send, at.e_recv)
+    start_edges(plan, seq, rank, *token_edges)
     for copy in hops:
         copy.wait_recv()
-    sums = local[:, chunk(rank)]
+    sums = at.local[:, chunk(rank)]
     for step in range(1, plan.group):
-        sums = sums + first[step]
+        sums = sums + at.first[step]
     for i in range(2):
-        mine[i] = sums[i : i + 1]
+        at.mine[i] = sums[i : i + 1]
     across = []
     for step in range(1, plan.sequences):
         to = other(seq, step, plan.sequences)
         to_stream = lax.div(2 * to, plan.sequences)
-        copy = remote(mine.at[to_stream], second.at[seq], t_send.at[1, step], t_recv.at[1, step], plan.device_of(to, rank))
+        copy = remote(
+            at.mine.at[to_stream], at.second.at[seq], at.t_send.at[1, step], at.t_recv.at[1, step], plan.device_of(to, rank)
+        )
         copy.start()
         across.append(copy)
-    second[seq] = mine[stream]
-    out[...] = own[pl.ds(0, plan.rows_dev)]
+    at.second[seq] = at.mine[stream]
+    at.token[...] = at.token_own[pl.ds(0, plan.rows_dev)]
     for copy in across:
         copy.wait_recv()
     last = []
     for step in range(1, plan.group):
         to = other(rank, step, plan.group)
-        copy = remote(second, table.at[rank], t_send.at[2, step], t_recv.at[2, step], plan.device_of(seq, to))
+        copy = remote(at.second, at.table.at[rank], at.t_send.at[2, step], at.t_recv.at[2, step], plan.device_of(seq, to))
         copy.start()
         last.append(copy)
-    table[rank] = second[...]
+    at.table[rank] = at.second[...]
     for copy in last:
         copy.wait_recv()
-    for copy in hops + across + last:
+
+    piece = None
+    for index in range(plan.group):
+        grads = jnp.concatenate([at.table[index, s] for s in range(plan.sequences)], axis=0).astype(BF16)
+        part = lax.dot_general(
+            grads, at.weight[:, index * cols : (index + 1) * cols], CONTRACT_LAST, preferred_element_type=F32
+        )
+        piece = part if piece is None else piece + part
+    at.piece[...] = piece
+    at.everyone[seq, rank] = piece
+    spread = []
+    for step in range(1, plan.group):
+        to = other(rank, step, plan.group)
+        copy = remote(
+            at.piece, at.everyone.at[seq, rank], at.c_send.at[0, step], at.c_recv.at[0, step], plan.device_of(seq, to)
+        )
+        copy.start()
+        spread.append(copy)
+    for copy in spread:
+        copy.wait_recv()
+    for step in range(1, plan.sequences):
+        to = other(seq, step, plan.sequences)
+        copy = remote(
+            at.everyone.at[seq], at.everyone.at[seq], at.c_send.at[1, step], at.c_recv.at[1, step], plan.device_of(to, rank)
+        )
+        copy.start()
+        spread.append(copy)
+    for copy in spread[plan.group - 1 :]:
+        copy.wait_recv()
+    for copy in hops + across + last + spread:
         copy.wait_send()
-    finish_edges(plan, seq, rank, *refs)
-
-
-def last_rows(plan, rows, pair, window_text, tokens, grad_middle, scale_a, text, masks, rest):
-    placed = jax.ShapeDtypeStruct((plan.rows_dev, plan.width), F32)
+    for copy in swaps:
+        copy.wait()
+    finish_edges(plan, seq, rank, *layer_edges)
+    finish_edges(plan, seq, rank, *token_edges)
+
+
+def last_rows(plan, term, weight, **operands):
+    rows, share = weight.shape[0], plan.width // plan.group // 2
     cols = 6 * plan.width // plan.group
+    most = max(plan.group, plan.sequences)
     dma = pltpu.SemaphoreType.DMA
-    most = max(plan.group, plan.sequences)
-    out, extra, table = call(
-        functools.partial(last_kernel, plan),
+
+    def placed(dtype):
+        return jax.ShapeDtypeStruct((plan.rows_dev, plan.width), dtype)
+
+    operands = dict(operands, weight=weight)
+    outs = dict(
+        layer=placed(BF16),
+        layer_extra=placed(BF16),
+        token=placed(F32),
+        token_extra=placed(F32),
+        table=jax.ShapeDtypeStruct((plan.group, plan.sequences, 1, cols), F32),
+        everyone=jax.ShapeDtypeStruct((plan.sequences, plan.group, plan.sequences, rows), F32),
+    )
+    edges = len(plan.segments)
+    scratch = dict(
+        layer_own=pltpu.VMEM((plan.own, plan.width), BF16),
+        token_own=pltpu.VMEM((plan.own, plan.width), F32),
+        local=pltpu.VMEM((2, 6 * plan.width), F32),
+        first=pltpu.VMEM((plan.group, 2, cols), F32),
+        second=pltpu.VMEM((plan.sequences, 1, cols), F32),
+        mine=pltpu.VMEM((2, 1, cols), F32),
+        piece=pltpu.VMEM((plan.sequences, rows), F32),
+        t_send=dma((3, most)),
+        t_recv=dma((3, most)),
+        c_send=dma((2, most)),
+        c_recv=dma((2, most)),
+        l_send=dma((edges,)),
+        l_recv=dma((edges,)),
+        e_send=dma((edges,)),
+        e_recv=dma((edges,)),
+    )
+    if plan.chip_heads:
+        operands["term"] = term.reshape(2, 2, share, plan.width)
+        outs["term_out"] = jax.ShapeDtypeStruct((plan.sequences, share, plan.width), BF16)
+        scratch.update(term_send=dma((2,)), term_recv=dma((2,)))
+    names = tuple(operands) + tuple(outs) + tuple(scratch)
+    got = call(
+        functools.partial(last_kernel, plan, names),
         "last",
         10,
-        (placed, placed, jax.ShapeDtypeStruct((plan.group, plan.sequences, 1, cols), F32)),
-        [
-            pltpu.VMEM((plan.own, plan.width), F32),
-            pltpu.VMEM((2, 6 * plan.width), F32),
-            pltpu.VMEM((plan.group, 2, cols), F32),
-            pltpu.VMEM((plan.sequences, 1, cols), F32),
-            pltpu.VMEM((2, 1, cols), F32),
-            dma((3, most)),
-            dma((3, most)),
-        ]
-        + sum_scratch(plan)
-        + edge_scratch(plan),
-        (rows, pair, window_text, tokens, grad_middle, scale_a, text, masks, rest),
-    )
-    return out, extra, table[:, :, 0].transpose(1, 0, 2).reshape(plan.sequences, -1)
+        tuple(outs.values()),
+        list(scratch.values()) + sum_scratch(plan) + sum_scratch(plan),
+        tuple(operands.values()),
+        vmem=58 << 20,
+    )
+    got = types.SimpleNamespace(**dict(zip(outs, got)))
+    got.table = got.table[:, :, 0].transpose(1, 0, 2).reshape(plan.sequences, -1)
+    got.term = got.term_out if plan.chip_heads else term
+    return got
 
 
 def over_sequences(plan, pieces):
     full = lax.all_gather(pieces, "dev", axis=0, axis_index_groups=plan.rank_groups())
     return full.reshape((plan.devices,) + pieces.shape[1:])
-
-
-def terms_to_send(plan, grad, rows):
-    return grad.astype(BF16).reshape(plan.sequences, plan.group, rows, grad.shape[2])
 
 
 def over_sequences_sum(plan, pieces):
@@ -948,9 +1007,9 @@
     return lax.dynamic_index_in_dim(full, lax.div(rank, 2), 1, keepdims=False)
 
 
-def merge_sum(plan, term, term_out, rank):
+def merge_sum(plan, term, rank):
     if plan.chip_heads:
-        return over_sequences_sum(plan, term_out)
+        return over_sequences_sum(plan, term)
     half = plan.group // 2
     _, share, cols = term.shape
     mine = [jnp.where(lax.rem(rank, 2) == k, term, jnp.zeros((), BF16)) for k in range(2)]
@@ -980,15 +1039,6 @@
     image_part = lax.dot_general(grads[: plan.image_end], pair[0], CONTRACT_LAST, preferred_element_type=F32)
     text_part = lax.dot_general(grads[plan.text_start :], pair[1], CONTRACT_LAST, preferred_element_type=F32)
     return by_stream(plan, image_part, text_part, is_text)
-
-
-def weight_terms(plan, rows, grads, is_text):
-    zero = jnp.zeros((), grads.dtype)
-    image = jnp.where(is_text[: plan.image_end, None], zero, grads[: plan.image_end])
-    text = jnp.where(is_text[plan.text_start :, None], grads[plan.text_start :], zero)
-    image_term = lax.dot_general(rows[: plan.image_end], image, CONTRACT_FIRST, preferred_element_type=F32)
-    text_term = lax.dot_general(rows[plan.text_start :], text, CONTRACT_FIRST, preferred_element_type=F32)
-    return jnp.stack([image_term, text_term])
 
 
 def pick(table, text_rows):
@@ -1021,6 +1071,7 @@
     valid = (offset >= 0) & (offset < IMG + text_lengths[seq])
     is_text = offset >= IMG
     bias = jnp.where(valid, 0.0, MASKED).astype(F32)[None, :]
+    window_text = is_text.astype(F32)[:, None]
     own_valid = own_rows(plan, valid[:, None], rank)[:, 0]
     own_text = own_rows(plan, is_text[:, None], rank)[:, 0]
 
@@ -1035,7 +1086,7 @@
     project_pair = over_sequences(plan, project_pieces)
     share = project_pair.shape[2] // 2
     project_pair = jnp.concatenate([project_pair[:, :, :share], project_pair[:, :, share:]], axis=1)
-    project_pair = project_pair.reshape(2, width, share)
+    project_pair = lax.optimization_barrier(project_pair.reshape(2, width, share))
     up_pair = over_sequences(plan, up_pieces).reshape(2, width, -1)
     down_pair = down_slices(plan, down_weight)
 
@@ -1051,7 +1102,6 @@
     own_tokens = own_rows(plan, token_window, rank)
     own_grad = own_rows(plan, grad_window, rank)
     text_mask = own_text.astype(F32)[:, None]
-    window_text = is_text.astype(F32)[:, None]
     merged, hidden_b = middle_rows(
         plan, attended, merge_pair, window_text, own_tokens, gate_a, scale_b, shift_b, text_mask
     )
@@ -1061,63 +1111,72 @@
     upper = stream_dot(plan, hidden_b, up_pair, is_text)
     activated = jax.nn.gelu(upper, approximate=True).astype(BF16)
     grad_lowered = (pick(gate_b, is_text) * grad_window.astype(F32)).astype(BF16)
-    down_term = weight_terms(plan, activated, grad_lowered, is_text).astype(BF16)
+    down_term = weight_terms(plan, activated, grad_lowered, window_text, "down_terms")
     down_term = down_term.reshape(plan.sequences, -1, width)
     down_term, grad_lowered = lax.optimization_barrier((down_term, grad_lowered))
     down_sum = over_sequences_sum(plan, down_term)
     grad_activated = stream_dot_back(plan, grad_lowered, down_pair, is_text)
     gelu_pull = jax.vjp(lambda value_in: jax.nn.gelu(value_in, approximate=True), upper)[1]
     grad_upper = gelu_pull(grad_activated)[0].astype(BF16)
-    up_term = terms_to_send(plan, weight_terms(plan, hidden_b, grad_upper, is_text), mod_rows)
+    up_term = weight_terms(plan, hidden_b, grad_upper, window_text, "up_terms")
+    up_term = up_term.reshape(plan.sequences, plan.group, mod_rows, -1)
     grad_upper, up_term = lax.optimization_barrier((grad_upper, up_term))
     up_sum = over_sequences_sum(plan, up_term)
     grad_hidden_b, grad_middle, grad_merged = back_rows(
         plan, grad_upper, up_pair, window_text, own_grad, middle, gate_a, scale_b, text_mask
     )
-    foreign = (row_seq != seq)[:, None]
-    merge_term = weight_terms(plan, attended, grad_merged, is_text).astype(BF16)
+    merge_term = weight_terms(plan, attended, grad_merged, window_text, "merge_terms")
 
     grad_projected = attend_back(plan, projected, grad_merged, merge_pair, window_text, bias)
     grad_projected, down_sum = lax.optimization_barrier((grad_projected, down_sum))
     down_grad = down_sum.astype(F32)
-    project_term = project_terms(plan, hidden_a, grad_projected, window_text, mod_rows)
+    project_term = weight_terms(plan, hidden_a, grad_projected, window_text, "project_terms", mod_rows)
+    project_term = project_term.reshape((plan.sequences, plan.group) + project_term.shape[1:])
     grad_projected, project_term = lax.optimization_barrier((grad_projected, project_term))
     project_sum = over_sequences_sum(plan, project_term)
-    activated, project_term = lax.optimization_barrier((activated, project_term))
-    lowered, out_here, out_there, merge_out = output_rows(
-        plan, activated, down_pair, window_text, middle, gate_b, text_mask, merge_term
-    )
-    layer_out = jnp.where(foreign, out_there, out_here)
 
     masks = jnp.stack([own_valid & ~own_text, own_valid & own_text], axis=1).astype(F32)
     rest = jnp.concatenate(
         [
             jnp.stack([jnp.sum(value * masks[:, j : j + 1], axis=0) for j in range(2)])
-            for value in (
-                grad_middle * merged,
-                grad_hidden_b,
-                grad_hidden_b * normed_b,
-                own_grad.astype(F32) * lowered,
-            )
+            for value in (grad_middle * merged, grad_hidden_b, grad_hidden_b * normed_b)
         ],
         axis=1,
     )
-    rest, up_sum = lax.optimization_barrier((rest, up_sum))
-    back_here, back_there, grad_table = last_rows(
-        plan, grad_projected, project_pair, window_text, own_tokens, grad_middle, scale_a, text_mask, masks, rest
-    )
-    tokens_grad = jnp.where(foreign, back_there, back_here)
-    own_grads = grad_table.astype(BF16)
+    got = last_rows(
+        plan,
+        merge_term,
+        modulation_weight,
+        activated=activated,
+        down_pair=down_pair,
+        grads=grad_projected,
+        project_pair=project_pair,
+        window_text=window_text,
+        tokens=own_tokens,
+        middle=middle,
+        grad=own_grad,
+        grad_middle=grad_middle,
+        gate_b=gate_b,
+        scale_a=scale_a,
+        text=text_mask,
+        masks=masks,
+        rest=rest,
+    )
+    foreign = (row_seq != seq)[:, None]
+    layer_out = jnp.where(foreign, got.layer_extra, got.layer)
+    tokens_grad = jnp.where(foreign, got.token_extra, got.token)
+    own_grads = got.table.astype(BF16)
     modulation_grad = lax.dot_general(silu_part, own_grads, CONTRACT_FIRST, preferred_element_type=F32)
-    grad_piece = lax.dot_general(own_grads, modulation_weight, CONTRACT_LAST, preferred_element_type=F32)
-    merge_out, merge_term, project_sum, modulation_grad, down_grad, layer_out, tokens_grad = lax.optimization_barrier(
-        (merge_out, merge_term, project_sum, modulation_grad, down_grad, layer_out, tokens_grad)
-    )
-    merge_grad = merge_sum(plan, merge_term, merge_out, rank).reshape(merge_weight.shape).astype(F32)
-    up_grad, project_grad, everyone = finish(plan, up_sum, project_sum, grad_piece.reshape(-1, 128))
-    everyone = everyone.reshape(2, plan.devices // 2, plan.sequences, mod_rows)
+    everyone = got.everyone.reshape(2, plan.devices // 2, plan.sequences, mod_rows)
     grad_silu = (everyone[0] + everyone[1]).transpose(1, 0, 2).reshape(plan.sequences, width)
     conditioning_grad = jax.vjp(jax.nn.silu, cond_float)[1](grad_silu)[0]
+    modulation_grad, up_sum = lax.optimization_barrier((modulation_grad, up_sum))
+    merge_out, project_sum, *done = lax.optimization_barrier(
+        (got.term, project_sum, modulation_grad, down_grad, layer_out, tokens_grad, conditioning_grad)
+    )
+    modulation_grad, down_grad, layer_out, tokens_grad, conditioning_grad = done
+    merge_grad = merge_sum(plan, merge_out, rank).reshape(merge_weight.shape).astype(F32)
+    up_grad, project_grad = finish(plan, up_sum, project_sum)
     return (
         layer_out,
         tokens_grad,

time: 599 us -> 589 us (0.983)
  local copies, waits for them, and re-layouts: 73 us -> 50.7 us
  Pallas kernels: 381 us -> 402 us
  waiting for transfers between devices: 49.2 us -> 59.4 us
  matrix products: 28.2 us -> 19.4 us
  other arithmetic: 44.3 us -> 35.6 us
    unnamed x187 -> x109, local copies, waits for them, and re-layouts: 54.6 us -> 39.1 us
    pallas_call x1 -> x4, Pallas kernels: 3.91 us -> 18.2 us  [weight_terms(): pl.pallas_call(functools.partial(terms_kernel, plan, fold, chunk), out_sh...]
    all_gather x1, waiting for transfers between devices: 34 us -> 45.2 us  [down_slices(): lax.all_gather(weight, 'dev', axis=0, axis_index_groups=plan.rank_groups())]
    dot_general x7 -> x0, matrix products: 10.4 us -> none  [the longest x3 7.73 us: weight_terms(): lax.dot_general(rows[:plan.image_end], image, CONTRACT_FIRST, preferred_e...]
    pallas_call x7 -> x6, Pallas kernels: 339 us -> 346 us  [call(): pl.pallas_call(kernel, out_shape=out_shape, in_specs=in_specs or [VMEM] *...]
    another operation x5 -> x2, other arithmetic: 6.57 us -> 0.27 us  [the longest x3 5.3 us: weight_terms(): return jnp.stack([image_term, text_term])]
  transfers between devices with their start and end apart: 8 -> 8, of which waited for: 3 -> 4; matrix products, arithmetic and copies ran while one was open for 16% -> 11% of each run, Pallas kernels for 64% -> 69%
where the time goes in v5:
time: 589 us; the launch traced here: 584 us
  Pallas kernels  402 us (68%)
  waiting for transfers between devices  59.4 us (10%)
  local copies, waits for them, and re-layouts  50.7 us (9%)
  other arithmetic  35.6 us (6%)
  matrix products  19.4 us (3%)
  between operations  16.1 us (3%)
    pallas_call x6, Pallas kernels, call(): pl.pallas_call(kernel, out_shape=out_shape, in_specs=in_specs or [VMEM] *...  346 us
    all_gather x1, waiting for transfers between devices, down_slices(): lax.all_gather(weight, 'dev', axis=0, axis_index_groups=plan.rank_groups())  45.2 us
    unnamed x109, local copies, waits for them, and re-layouts  39.1 us
    pallas_call x1, Pallas kernels, attend_back(): pl.pallas_call(functools.partial(attend_back_kernel, plan.heads, rows //...  25.7 us
    pallas_call x4, Pallas kernels, weight_terms(): pl.pallas_call(functools.partial(terms_kernel, plan, fold, chunk), out_sh...  18.2 us
    pallas_call x1, Pallas kernels, attend(): pl.pallas_call(functools.partial(attend_kernel, plan.heads, block), out_s...  12.5 us
  transfers between devices with their start and end apart: 8, of which 4 were waited for; matrix products, arithmetic and copies ran while one was open for 11% of the time, Pallas kernels for 69%

profile of v5, /device:TPU:0, one launch (start us, length us, event | category | flops | bytes accessed | tf_op | source)
XLA Modules:
  0.0 584.1 jit_solution(10473670905949340834)
XLA Ops:
  10.4 28.8 %swap_in.1 = (bf16[8,48,1152]{2,1,0:T(8,128)(2,1)}, bf16[8,96,768]{2,1,0:T(8,128)(2,1)}) custom-call(bf16[96,4608]{1,0:T(8,128)(2,1)S(1)} %copy-done.31, bf16[96,6144]{1,0:T(8,128)(2,1)S(1)} %copy-done.28), custom_call_target="tpu_custom_call" | custom-call | tf_op jit(solution)/shard_map/swap_in/pallas_call | solution.py:307
  39.3 3.5 all-gather.9.cloned.1.call-done
  51.9 79.4 %entry.1 = (bf16[1280,1536]{1,0:T(8,128)(2,1)S(1)}, bf16[1280,1536]{1,0:T(8,128)(2,1)S(1)}, f32[8,2,9,128]{3,2,1,0:T(8,128)S(1)}, bf16[2,2,96,1536]{3,2,1,0:T(8,128)(2,1)S(1)}) custom-call(bf16[144,1536]{1,0:T(8,128)(2,1)S(1)} %copy-done.33, bf16[144,1536]{1,0:T(8,128)(2,1)S(1)} %copy-done.34, f32[8,4,9,128]{3,2,1,0:T(8,128)S(1)} %bitcast.61, ...), custom_call_target="tpu_custom_call" | custom-call | tf_op jit(solution)/shard_map/entry/pallas_call | solution.py:307
  136.3 2.8 convert_reduce_fusion
  140.9 6.2 %multiply_convert_fusion = (bf16[1280,1536]{1,0:T(8,128)(2,1)}, bf16[1280,1536]{1,0:T(8,128)(2,1)S(1)}, bf16[1280,1536]{1,0:T(8,128)(2,1)}) fusion(f32[1536]{0:T(1024)S(1)} %get-tuple-element.98, f32[1536]{0:T(1024)S(1)} %get-tuple-element.99, pred[1280]{0:T(1024)(128)(4,1)S(1)} %fusion.32, bf16[1280,1536]{1,0:T(8,128)(2,1)S(1)} %copy-done.19, ...), kind=kLoop, calls=%fused_computation.8 | loop fusion | flops 27525120 | bytes 19710464 | tf_op jit(solution)/shard_map/convert_element_type | solution.py:1113
  149.5 3.3 fusion.38
  153.1 3.1 copy-done.13
  163.5 12.5 %attend.1.rows = bf16[1280,192]{1,0:T(8,128)(2,1)S(1)} custom-call(bf16[1280,576]{1,0:T(8,128)(2,1)S(1)} %pad_maximum_fusion.3.projected, f32[1,1280]{1,0:T(1,128)S(1)} %and_select_fusion.bias_ref), custom_call_target="tpu_custom_call" | custom-call | flops 5033164800 | bytes 1966080 | tf_op jit(solution)/shard_map/attend/pallas_call | solution.py:128
  176.1 56.2 %middle.1 = (f32[160,1536]{1,0:T(8,128)S(1)}, bf16[1280,1536]{1,0:T(8,128)(2,1)S(1)}) custom-call(bf16[1280,192]{1,0:T(8,128)(2,1)S(1)} %attend.1.rows, bf16[2,192,1536]{2,1,0:T(8,128)(2,1)S(1)} %bitcast.58, f32[1280,1]{1,0:T(8,128)S(1)} %fusion.27.window_text.text.refs_4_, bf16[160,1536]{1,0:T(8,128)(2,1)S(1)} %pad_maximum_fusion.4.tokens.refs_5_, ...), custom_call_target="tpu_custom_call" | custom-call | tf_op jit(solution)/shard_map/middle/pallas_call | solution.py:307
  234.4 2.9 fusion.37
  238.0 2.9 fusion.17
  244.5 4.9 down_terms.1
  251.7 45.2 %all-gather.15.cloned.1.call-done = bf16[1536,1536]{1,0:T(8,128)(2,1)} async-done(((bf16[384,1536]{1,0:T(8,128)(2,1)}), bf16[1536,1536]{1,0:T(8,128)(2,1)}) %all-gather.15.cloned.1.call-update) | async-done | bytes 4718608 | tf_op jit(solution)/shard_map/all_gather | solution.py:1022
  296.8 5.7 fusion.15
  302.7 2.9 copy-done.42
  307.9 2.7 fusion.12.grads.rows
  310.7 5.8 up_terms.1
  323.1 63.6 %back.1 = (f32[160,1536]{1,0:T(8,128)S(1)}, f32[160,1536]{1,0:T(8,128)S(1)}, bf16[1280,1536]{1,0:T(8,128)(2,1)S(1)}) custom-call(bf16[1280,768]{1,0:T(8,128)(2,1)S(1)} %copy-done.6, bf16[2,1536,768]{2,1,0:T(8,128)(2,1)} %bitcast.64, f32[1280,1]{1,0:T(8,128)S(1)} %fusion.27.window_text.text.refs_4_, bf16[160,1536]{1,0:T(8,128)(2,1)S(1)} %pad_maximum_fusion.5.grad.refs_7_, ...), custom_call_target="tpu_custom_call" | custom-call | tf_op jit(solution)/shard_map/back/pallas_call | solution.py:307
  390.6 25.7 %attend_back.1.grads.refs_2_ = bf16[1280,576]{1,0:T(8,128)(2,1)} custom-call(bf16[1280,576]{1,0:T(8,128)(2,1)} %copy-done.23, bf16[1280,1536]{1,0:T(8,128)(2,1)} %copy-done.16, bf16[2,192,1536]{2,1,0:T(8,128)(2,1)} %bitcast.57, f32[1280,1]{1,0:T(8,128)} %copy-done.3, f32[1,1280]{1,0:T(1,128)} %copy-done.35), custom_call_target="tpu_custom_call" | custom-call | flops 12582912000 | bytes 3440640 | tf_op jit(solution)/shard_map/attend_back/pallas_call | solution.py:184
  419.8 6.3 %project_terms.1 = bf16[32,48,1152]{2,1,0:T(8,128)(2,1)S(1)} custom-call(bf16[1280,1536]{1,0:T(8,128)(2,1)S(1)} %copy-done.14, bf16[1280,576]{1,0:T(8,128)(2,1)S(1)} %copy-done.22, f32[1280,1]{1,0:T(8,128)S(1)} %copy-done.4), custom_call_target="tpu_custom_call" | custom-call | flops 3397386240 | bytes 8388608 | tf_op jit(solution)/shard_map/project_terms/pallas_call | solution.py:246
  429.0 2.7 multiply_reduce_fusion.1
  434.7 91.5 %last.1 = (bf16[144,1536]{1,0:T(8,128)(2,1)}, bf16[144,1536]{1,0:T(8,128)(2,1)}, f32[144,1536]{1,0:T(8,128)}, f32[144,1536]{1,0:T(8,128)}, f32[8,4,1,1152]{3,2,1...) custom-call(bf16[1280,768]{1,0:T(8,128)(2,1)} %copy-done.7, bf16[2,768,1536]{2,1,0:T(8,128)(2,1)} %bitcast.68, ...), custom_call_target="tpu_custom_call" | custom-call | tf_op jit(solution)/shard_map/last/pallas_call | solution.py:307
  536.0 7.3 %reduce-scatter.7.cloned.1.call-done = bf16[1,8,48,1152]{3,2,1,0:T(8,128)(2,1)} async-done(((bf16[4,8,48,1152]{3,2,1,0:T(8,128)(2,1)}), bf16[1,8,48,1152]{3,2,1,0:T(8,128)(2,1)}) %reduce-scatter.7.cloned.1.call-update) | async-done | bytes 884752 | tf_op jit(solution)/shard_map/reduce_scatter | solution.py:997
  544.6 26.2 %finish.1 = (bf16[96,6144]{1,0:T(8,128)(2,1)S(1)}, bf16[96,4608]{1,0:T(8,128)(2,1)S(1)}) custom-call(bf16[8,96,768]{2,1,0:T(8,128)(2,1)S(1)} %bitcast.60, bf16[8,48,1152]{2,1,0:T(8,128)(2,1)S(1)} %bitcast.62), custom_call_target="tpu_custom_call" | custom-call | tf_op jit(solution)/shard_map/finish/pallas_call | solution.py:307
  (212 shorter events, 75.9 us)
Async XLA Ops:
  7.2 37.0 %copy-start.51 = (s32[4]{0:T(128)S(1)}, s32[4]{0:T(128)}, u32[]{:S(2)}) copy-start(s32[4]{0:T(128)} %param.11) | copy-start | bytes 52
  7.2 41.1 %copy-start.50 = (bf16[4,1536]{1,0:T(4,128)(2,1)S(1)}, bf16[4,1536]{1,0:T(4,128)(2,1)}, u32[]{:S(2)}) copy-start(bf16[4,1536]{1,0:T(4,128)(2,1)} %param.10) | copy-start | bytes 36868
  7.2 35.6 %all-gather.9.cloned.1.call-start = ((), (), s32[]{:S(2)}) async-start(), calls=%async_computation.8 | async-start | bytes 1474560 | tf_op jit(solution)/shard_map/all_gather | solution.py:1002
  7.9 141.5 %all-gather.11.cloned.1.call-start = ((), (), s32[]{:S(2)}) async-start(), calls=%async_computation.9 | async-start | bytes 4423680 | tf_op jit(solution)/shard_map/all_gather | solution.py:992
  39.3 12.6 %copy-start.33 = (bf16[144,1536]{1,0:T(8,128)(2,1)S(1)}, bf16[144,1536]{1,0:T(8,128)(2,1)}, u32[]{:S(2)}) copy-start(bf16[144,1536]{1,0:T(8,128)(2,1)} %tokens.1) | copy-start | bytes 1327108
  39.3 12.6 %copy-start.34 = (bf16[144,1536]{1,0:T(8,128)(2,1)S(1)}, bf16[144,1536]{1,0:T(8,128)(2,1)}, u32[]{:S(2)}) copy-start(bf16[144,1536]{1,0:T(8,128)(2,1)} %grads.1) | copy-start | bytes 1327108
  42.8 9.1 %copy-start.27 = (bf16[384,1536]{1,0:T(8,128)(2,1)S(1)}, bf16[384,1536]{1,0:T(8,128)(2,1)}, u32[]{:S(2)}) copy-start(bf16[384,1536]{1,0:T(8,128)(2,1)} %all-gather.9.cloned.1.call-done) | copy-start | bytes 3538948
  42.8 191.6 %all-gather.13.cloned.1.call-start = ((), (), s32[]{:S(2)}) async-start(), calls=%async_computation.10 | async-start | bytes 5898240 | tf_op jit(solution)/shard_map/all_gather | solution.py:992
  43.5 253.3 %all-gather.15.cloned.1.call-start = ((), (), s32[]{:S(2)}) async-start(), calls=%async_computation.11 | async-start | bytes 5898240 | tf_op jit(solution)/shard_map/all_gather | solution.py:1022
  44.1 372.2 %reduce-scatter.5.cloned.1.call-start = ((), (), s32[]{:S(2)}) async-start(), calls=%async_computation.4 | async-start | bytes 5898240 | tf_op jit(solution)/shard_map/reduce_scatter | solution.py:997
  48.3 115.2 %copy-start.35 = (f32[1,1280]{1,0:T(1,128)}, f32[1,1280]{1,0:T(1,128)S(1)}, u32[]{:S(2)}) copy-start(f32[1,1280]{1,0:T(1,128)S(1)} %and_select_fusion.bias_ref) | copy-start | bytes 15364
  49.1 272.1 %copy-start.3 = (f32[1280,1]{1,0:T(8,128)}, f32[1280,1]{1,0:T(8,128)S(1)}, u32[]{:S(2)}) copy-start(f32[1280,1]{1,0:T(8,128)S(1)} %fusion.27.window_text.text.refs_4_) | copy-start | bytes 15364
  49.7 271.5 %copy-start.24 = (f32[160,1]{1,0:T(8,128)}, f32[160,1]{1,0:T(8,128)S(1)}, u32[]{:S(2)}) copy-start(f32[160,1]{1,0:T(8,128)S(1)} %convert_element_type.86.text.refs_11_) | copy-start | bytes 1924
  148.8 27.3 %copy-start.11 = (bf16[160,1536]{1,0:T(8,128)(2,1)}, bf16[160,1536]{1,0:T(8,128)(2,1)S(1)}, u32[]{:S(2)}) copy-start(bf16[160,1536]{1,0:T(8,128)(2,1)S(1)} %pad_maximum_fusion.4.tokens.refs_5_) | copy-start | bytes 1474564
  163.5 12.6 %copy-start.23 = (bf16[1280,576]{1,0:T(8,128)(2,1)}, bf16[1280,576]{1,0:T(8,128)(2,1)S(1)}, u32[]{:S(2)}) copy-start(bf16[1280,576]{1,0:T(8,128)(2,1)S(1)} %pad_maximum_fusion.3.projected) | copy-start | bytes 4423684
  163.5 12.6 %copy-start.26 = (bf16[2,2,96,1536]{3,2,1,0:T(8,128)(2,1)S(1)}, bf16[2,2,96,1536]{3,2,1,0:T(8,128)(2,1)}, u32[]{:S(2)}) copy-start(bf16[2,2,96,1536]{3,2,1,0:T(8,128)(2,1)} %copy-done.25) | copy-start | bytes 3538948
  251.6 280.8 %reduce-scatter.9.cloned.1.call-start = ((), (), s32[]{:S(2)}) async-start(), calls=%async_computation.6 | async-start | bytes 5898240 | tf_op jit(solution)/shard_map/reduce_scatter | solution.py:997
  318.6 224.7 %reduce-scatter.7.cloned.1.call-start = ((), (), s32[]{:S(2)}) async-start(), calls=%async_computation.5 | async-start | bytes 4423680 | tf_op jit(solution)/shard_map/reduce_scatter | solution.py:997
  319.7 67.1 %copy-start.12 = (bf16[160,1536]{1,0:T(8,128)(2,1)}, bf16[160,1536]{1,0:T(8,128)(2,1)S(1)}, u32[]{:S(2)}) copy-start(bf16[160,1536]{1,0:T(8,128)(2,1)S(1)} %pad_maximum_fusion.5.grad.refs_7_) | copy-start | bytes 1474564
  321.2 107.8 %copy-start.2 = (f32[160,1536]{1,0:T(8,128)}, f32[160,1536]{1,0:T(8,128)S(1)}, u32[]{:S(2)}) copy-start(f32[160,1536]{1,0:T(8,128)S(1)} %get-tuple-element.107.middle.refs_6_) | copy-start | bytes 2949124
  390.6 25.7 %copy-start.4 = (f32[1280,1]{1,0:T(8,128)S(1)}, f32[1280,1]{1,0:T(8,128)}, u32[]{:S(2)}) copy-start(f32[1280,1]{1,0:T(8,128)} %copy-done.3) | copy-start | bytes 15364
  427.9 147.3 %reduce-scatter.11.cloned.1.call-start = ((), (), s32[]{:S(2)}) async-start(), calls=%async_computation.7 | async-start | bytes 1474560 | tf_op jit(solution)/shard_map/reduce_scatter | solution.py:997
  434.7 93.5 %copy-start.46 = (bf16[1,384,1536]{2,1,0:T(8,128)(2,1)S(1)}, bf16[1,384,1536]{2,1,0:T(8,128)(2,1)}, u32[]{:S(2)}) copy-start(bf16[1,384,1536]{2,1,0:T(8,128)(2,1)} %reduce-scatter.5.cloned.1.call-done) | copy-start | bytes 3538948
  532.4 11.0 %copy-start.29 = (bf16[1,8,96,768]{3,2,1,0:T(8,128)(2,1)S(1)}, bf16[1,8,96,768]{3,2,1,0:T(8,128)(2,1)}, u32[]{:S(2)}) copy-start(bf16[1,8,96,768]{3,2,1,0:T(8,128)(2,1)} %reduce-scatter.9.cloned.1.call-done) | copy-start | bytes 3538948
  (36 other events, 103.1 us)
Sparse Core Ops, SparseCore 0:
  9.6 33.1 all-gather.8
  44.3 73.5 all-gather.10
  119.5 87.9 all-gather.12
  208.9 87.8 all-gather.14
  299.0 83.6 reduce-scatter.4
  384.9 85.7 reduce-scatter.8
  473.0 70.2 reduce-scatter.6
  545.7 29.5 reduce-scatter.10

commit v6 on v5

--- a/solution.py
+++ b/solution.py
@@ -337,14 +337,14 @@
     return jnp.concatenate([main[...], edge[...]], axis=0)
 
 
-def sum_scratch(plan):
+def sum_scratch(plan, wire=BF16):
     half, own, width = plan.group // 2, plan.own, plan.width
     return [
         pltpu.VMEM((half, own, width), F32),
         pltpu.VMEM((half, own, width), F32),
         pltpu.VMEM((own, width), F32),
-        pltpu.VMEM((half - 1, own, width), BF16),
-        pltpu.VMEM((half - 1, own, width), BF16),
+        pltpu.VMEM((half - 1, own, width), wire),
+        pltpu.VMEM((half - 1, own, width), wire),
         pltpu.SemaphoreType.DMA((half,)),
         pltpu.SemaphoreType.DMA((half,)),
         pltpu.SemaphoreType.DMA((half,)),
@@ -403,7 +403,7 @@
         @pl.when(i > 0)
         def _():
             for_owner(i)
-            going[i - 1] = mine[...].astype(BF16)
+            going[i - 1] = mine[...].astype(going.dtype)
             far_copy(i).start()
 
         return carry
@@ -739,7 +739,7 @@
         "middle",
         2,
         (own_shape(plan), window_shape(plan)),
-        [pltpu.VMEM((plan.own, plan.width), BF16)] + sum_scratch(plan) + share_scratch(plan),
+        [pltpu.VMEM((plan.own, plan.width), BF16)] + sum_scratch(plan, F32) + share_scratch(plan),
         (rows, pair, window_text, tokens, gate_a, scale_b, shift_b, text),
     )
 

time: 589 us -> 589 us (level)
  Pallas kernels: 402 us -> 423 us
  waiting for transfers between devices: 59.4 us -> 38.7 us
    pallas_call x6, Pallas kernels: 346 us -> 367 us  [call(): pl.pallas_call(kernel, out_shape=out_shape, in_specs=in_specs or [VMEM] *...]
    all_gather x1, waiting for transfers between devices: 45.2 us -> 24.4 us  [down_slices(): lax.all_gather(weight, 'dev', axis=0, axis_index_groups=plan.rank_groups())]
  transfers between devices with their start and end apart: 8 -> 8, of which waited for: 4 -> 4; matrix products, arithmetic and copies ran while one was open for 11% -> 11% of each run, Pallas kernels for 69% -> 72%
where the time goes in v6:
time: 589 us; the launch traced here: 584 us
  Pallas kernels  423 us (72%)
  local copies, waits for them, and re-layouts  50.4 us (9%)
  waiting for transfers between devices  38.7 us (7%)
  other arithmetic  35.6 us (6%)
  matrix products  19.4 us (3%)
  between operations  16.1 us (3%)
    pallas_call x6, Pallas kernels, call(): pl.pallas_call(kernel, out_shape=out_shape, in_specs=in_specs or [VMEM] *...  367 us
    unnamed x109, local copies, waits for them, and re-layouts  38.9 us
    pallas_call x1, Pallas kernels, attend_back(): pl.pallas_call(functools.partial(attend_back_kernel, plan.heads, rows //...  25.7 us
    all_gather x1, waiting for transfers between devices, down_slices(): lax.all_gather(weight, 'dev', axis=0, axis_index_groups=plan.rank_groups())  24.4 us
    pallas_call x4, Pallas kernels, weight_terms(): pl.pallas_call(functools.partial(terms_kernel, plan, fold, chunk), out_sh...  18.2 us
    pallas_call x1, Pallas kernels, attend(): pl.pallas_call(functools.partial(attend_kernel, plan.heads, block), out_s...  12.5 us
  transfers between devices with their start and end apart: 8, of which 4 were waited for; matrix products, arithmetic and copies ran while one was open for 11% of the time, Pallas kernels for 72%

profile of v6, /device:TPU:0, one launch (start us, length us, event | category | flops | bytes accessed | tf_op | source)
XLA Modules:
  0.0 584.1 jit_solution(9500336382549382976)
XLA Ops:
  10.4 28.8 %swap_in.1 = (bf16[8,48,1152]{2,1,0:T(8,128)(2,1)}, bf16[8,96,768]{2,1,0:T(8,128)(2,1)}) custom-call(bf16[96,4608]{1,0:T(8,128)(2,1)S(1)} %copy-done.31, bf16[96,6144]{1,0:T(8,128)(2,1)S(1)} %copy-done.28), custom_call_target="tpu_custom_call" | custom-call | tf_op jit(solution)/shard_map/swap_in/pallas_call | solution.py:307
  39.3 3.5 all-gather.9.cloned.1.call-done
  51.9 79.4 %entry.1 = (bf16[1280,1536]{1,0:T(8,128)(2,1)S(1)}, bf16[1280,1536]{1,0:T(8,128)(2,1)S(1)}, f32[8,2,9,128]{3,2,1,0:T(8,128)S(1)}, bf16[2,2,96,1536]{3,2,1,0:T(8,128)(2,1)S(1)}) custom-call(bf16[144,1536]{1,0:T(8,128)(2,1)S(1)} %copy-done.33, bf16[144,1536]{1,0:T(8,128)(2,1)S(1)} %copy-done.34, f32[8,4,9,128]{3,2,1,0:T(8,128)S(1)} %bitcast.61, ...), custom_call_target="tpu_custom_call" | custom-call | tf_op jit(solution)/shard_map/entry/pallas_call | solution.py:307
  136.3 2.8 convert_reduce_fusion
  140.9 6.2 %multiply_convert_fusion = (bf16[1280,1536]{1,0:T(8,128)(2,1)}, bf16[1280,1536]{1,0:T(8,128)(2,1)S(1)}, bf16[1280,1536]{1,0:T(8,128)(2,1)}) fusion(f32[1536]{0:T(1024)S(1)} %get-tuple-element.98, f32[1536]{0:T(1024)S(1)} %get-tuple-element.99, pred[1280]{0:T(1024)(128)(4,1)S(1)} %fusion.32, bf16[1280,1536]{1,0:T(8,128)(2,1)S(1)} %copy-done.19, ...), kind=kLoop, calls=%fused_computation.8 | loop fusion | flops 27525120 | bytes 19710464 | tf_op jit(solution)/shard_map/convert_element_type | solution.py:1113
  149.5 3.3 fusion.38
  153.1 3.1 copy-done.13
  163.5 12.5 %attend.1.rows = bf16[1280,192]{1,0:T(8,128)(2,1)S(1)} custom-call(bf16[1280,576]{1,0:T(8,128)(2,1)S(1)} %pad_maximum_fusion.3.projected, f32[1,1280]{1,0:T(1,128)S(1)} %and_select_fusion.bias_ref), custom_call_target="tpu_custom_call" | custom-call | flops 5033164800 | bytes 1966080 | tf_op jit(solution)/shard_map/attend/pallas_call | solution.py:128
  176.1 77.2 %middle.1 = (f32[160,1536]{1,0:T(8,128)S(1)}, bf16[1280,1536]{1,0:T(8,128)(2,1)S(1)}) custom-call(bf16[1280,192]{1,0:T(8,128)(2,1)S(1)} %attend.1.rows, bf16[2,192,1536]{2,1,0:T(8,128)(2,1)S(1)} %bitcast.58, f32[1280,1]{1,0:T(8,128)S(1)} %fusion.27.window_text.text.refs_4_, bf16[160,1536]{1,0:T(8,128)(2,1)S(1)} %pad_maximum_fusion.4.tokens.refs_5_, ...), custom_call_target="tpu_custom_call" | custom-call | tf_op jit(solution)/shard_map/middle/pallas_call | solution.py:307
  255.3 2.8 fusion.37
  258.9 2.9 fusion.17
  265.3 4.9 down_terms.1
  272.4 24.4 %all-gather.15.cloned.1.call-done = bf16[1536,1536]{1,0:T(8,128)(2,1)} async-done(((bf16[384,1536]{1,0:T(8,128)(2,1)}), bf16[1536,1536]{1,0:T(8,128)(2,1)}) %all-gather.15.cloned.1.call-update) | async-done | bytes 4718608 | tf_op jit(solution)/shard_map/all_gather | solution.py:1022
  296.8 5.7 fusion.15
  302.7 2.9 copy-done.42
  307.9 2.7 fusion.12.grads.rows
  310.7 5.8 up_terms.1
  323.1 63.6 %back.1 = (f32[160,1536]{1,0:T(8,128)S(1)}, f32[160,1536]{1,0:T(8,128)S(1)}, bf16[1280,1536]{1,0:T(8,128)(2,1)S(1)}) custom-call(bf16[1280,768]{1,0:T(8,128)(2,1)S(1)} %copy-done.6, bf16[2,1536,768]{2,1,0:T(8,128)(2,1)} %bitcast.64, f32[1280,1]{1,0:T(8,128)S(1)} %fusion.27.window_text.text.refs_4_, bf16[160,1536]{1,0:T(8,128)(2,1)S(1)} %pad_maximum_fusion.5.grad.refs_7_, ...), custom_call_target="tpu_custom_call" | custom-call | tf_op jit(solution)/shard_map/back/pallas_call | solution.py:307
  390.6 25.7 %attend_back.1.grads.refs_2_ = bf16[1280,576]{1,0:T(8,128)(2,1)} custom-call(bf16[1280,576]{1,0:T(8,128)(2,1)} %copy-done.23, bf16[1280,1536]{1,0:T(8,128)(2,1)} %copy-done.16, bf16[2,192,1536]{2,1,0:T(8,128)(2,1)} %bitcast.57, f32[1280,1]{1,0:T(8,128)} %copy-done.3, f32[1,1280]{1,0:T(1,128)} %copy-done.35), custom_call_target="tpu_custom_call" | custom-call | flops 12582912000 | bytes 3440640 | tf_op jit(solution)/shard_map/attend_back/pallas_call | solution.py:184
  419.8 6.3 %project_terms.1 = bf16[32,48,1152]{2,1,0:T(8,128)(2,1)S(1)} custom-call(bf16[1280,1536]{1,0:T(8,128)(2,1)S(1)} %copy-done.14, bf16[1280,576]{1,0:T(8,128)(2,1)S(1)} %copy-done.22, f32[1280,1]{1,0:T(8,128)S(1)} %copy-done.4), custom_call_target="tpu_custom_call" | custom-call | flops 3397386240 | bytes 8388608 | tf_op jit(solution)/shard_map/project_terms/pallas_call | solution.py:246
  429.0 2.7 multiply_reduce_fusion.1
  434.7 91.5 %last.1 = (bf16[144,1536]{1,0:T(8,128)(2,1)}, bf16[144,1536]{1,0:T(8,128)(2,1)}, f32[144,1536]{1,0:T(8,128)}, f32[144,1536]{1,0:T(8,128)}, f32[8,4,1,1152]{3,2,1...) custom-call(bf16[1280,768]{1,0:T(8,128)(2,1)} %copy-done.7, bf16[2,768,1536]{2,1,0:T(8,128)(2,1)} %bitcast.68, ...), custom_call_target="tpu_custom_call" | custom-call | tf_op jit(solution)/shard_map/last/pallas_call | solution.py:307
  536.0 7.3 %reduce-scatter.7.cloned.1.call-done = bf16[1,8,48,1152]{3,2,1,0:T(8,128)(2,1)} async-done(((bf16[4,8,48,1152]{3,2,1,0:T(8,128)(2,1)}), bf16[1,8,48,1152]{3,2,1,0:T(8,128)(2,1)}) %reduce-scatter.7.cloned.1.call-update) | async-done | bytes 884752 | tf_op jit(solution)/shard_map/reduce_scatter | solution.py:997
  544.6 26.2 %finish.1 = (bf16[96,6144]{1,0:T(8,128)(2,1)S(1)}, bf16[96,4608]{1,0:T(8,128)(2,1)S(1)}) custom-call(bf16[8,96,768]{2,1,0:T(8,128)(2,1)S(1)} %bitcast.60, bf16[8,48,1152]{2,1,0:T(8,128)(2,1)S(1)} %bitcast.62), custom_call_target="tpu_custom_call" | custom-call | tf_op jit(solution)/shard_map/finish/pallas_call | solution.py:307
  (212 shorter events, 75.7 us)
Async XLA Ops:
  7.2 37.0 %copy-start.51 = (s32[4]{0:T(128)S(1)}, s32[4]{0:T(128)}, u32[]{:S(2)}) copy-start(s32[4]{0:T(128)} %param.11) | copy-start | bytes 52
  7.2 41.1 %copy-start.50 = (bf16[4,1536]{1,0:T(4,128)(2,1)S(1)}, bf16[4,1536]{1,0:T(4,128)(2,1)}, u32[]{:S(2)}) copy-start(bf16[4,1536]{1,0:T(4,128)(2,1)} %param.10) | copy-start | bytes 36868
  7.2 35.6 %all-gather.9.cloned.1.call-start = ((), (), s32[]{:S(2)}) async-start(), calls=%async_computation.8 | async-start | bytes 1474560 | tf_op jit(solution)/shard_map/all_gather | solution.py:1002
  7.9 141.5 %all-gather.11.cloned.1.call-start = ((), (), s32[]{:S(2)}) async-start(), calls=%async_computation.9 | async-start | bytes 4423680 | tf_op jit(solution)/shard_map/all_gather | solution.py:992
  39.3 12.6 %copy-start.33 = (bf16[144,1536]{1,0:T(8,128)(2,1)S(1)}, bf16[144,1536]{1,0:T(8,128)(2,1)}, u32[]{:S(2)}) copy-start(bf16[144,1536]{1,0:T(8,128)(2,1)} %tokens.1) | copy-start | bytes 1327108
  39.3 12.6 %copy-start.34 = (bf16[144,1536]{1,0:T(8,128)(2,1)S(1)}, bf16[144,1536]{1,0:T(8,128)(2,1)}, u32[]{:S(2)}) copy-start(bf16[144,1536]{1,0:T(8,128)(2,1)} %grads.1) | copy-start | bytes 1327108
  42.8 9.1 %copy-start.27 = (bf16[384,1536]{1,0:T(8,128)(2,1)S(1)}, bf16[384,1536]{1,0:T(8,128)(2,1)}, u32[]{:S(2)}) copy-start(bf16[384,1536]{1,0:T(8,128)(2,1)} %all-gather.9.cloned.1.call-done) | copy-start | bytes 3538948
  42.8 212.5 %all-gather.13.cloned.1.call-start = ((), (), s32[]{:S(2)}) async-start(), calls=%async_computation.10 | async-start | bytes 5898240 | tf_op jit(solution)/shard_map/all_gather | solution.py:992
  43.5 253.3 %all-gather.15.cloned.1.call-start = ((), (), s32[]{:S(2)}) async-start(), calls=%async_computation.11 | async-start | bytes 5898240 | tf_op jit(solution)/shard_map/all_gather | solution.py:1022
  44.1 372.2 %reduce-scatter.5.cloned.1.call-start = ((), (), s32[]{:S(2)}) async-start(), calls=%async_computation.4 | async-start | bytes 5898240 | tf_op jit(solution)/shard_map/reduce_scatter | solution.py:997
  48.3 115.2 %copy-start.35 = (f32[1,1280]{1,0:T(1,128)}, f32[1,1280]{1,0:T(1,128)S(1)}, u32[]{:S(2)}) copy-start(f32[1,1280]{1,0:T(1,128)S(1)} %and_select_fusion.bias_ref) | copy-start | bytes 15364
  49.1 272.1 %copy-start.3 = (f32[1280,1]{1,0:T(8,128)}, f32[1280,1]{1,0:T(8,128)S(1)}, u32[]{:S(2)}) copy-start(f32[1280,1]{1,0:T(8,128)S(1)} %fusion.27.window_text.text.refs_4_) | copy-start | bytes 15364
  49.7 271.5 %copy-start.24 = (f32[160,1]{1,0:T(8,128)}, f32[160,1]{1,0:T(8,128)S(1)}, u32[]{:S(2)}) copy-start(f32[160,1]{1,0:T(8,128)S(1)} %convert_element_type.86.text.refs_11_) | copy-start | bytes 1924
  148.8 27.3 %copy-start.11 = (bf16[160,1536]{1,0:T(8,128)(2,1)}, bf16[160,1536]{1,0:T(8,128)(2,1)S(1)}, u32[]{:S(2)}) copy-start(bf16[160,1536]{1,0:T(8,128)(2,1)S(1)} %pad_maximum_fusion.4.tokens.refs_5_) | copy-start | bytes 1474564
  163.5 12.6 %copy-start.23 = (bf16[1280,576]{1,0:T(8,128)(2,1)}, bf16[1280,576]{1,0:T(8,128)(2,1)S(1)}, u32[]{:S(2)}) copy-start(bf16[1280,576]{1,0:T(8,128)(2,1)S(1)} %pad_maximum_fusion.3.projected) | copy-start | bytes 4423684
  163.5 12.6 %copy-start.26 = (bf16[2,2,96,1536]{3,2,1,0:T(8,128)(2,1)S(1)}, bf16[2,2,96,1536]{3,2,1,0:T(8,128)(2,1)}, u32[]{:S(2)}) copy-start(bf16[2,2,96,1536]{3,2,1,0:T(8,128)(2,1)} %copy-done.25) | copy-start | bytes 3538948
  272.4 260.1 %reduce-scatter.9.cloned.1.call-start = ((), (), s32[]{:S(2)}) async-start(), calls=%async_computation.6 | async-start | bytes 5898240 | tf_op jit(solution)/shard_map/reduce_scatter | solution.py:997
  318.6 224.7 %reduce-scatter.7.cloned.1.call-start = ((), (), s32[]{:S(2)}) async-start(), calls=%async_computation.5 | async-start | bytes 4423680 | tf_op jit(solution)/shard_map/reduce_scatter | solution.py:997
  319.7 67.1 %copy-start.12 = (bf16[160,1536]{1,0:T(8,128)(2,1)}, bf16[160,1536]{1,0:T(8,128)(2,1)S(1)}, u32[]{:S(2)}) copy-start(bf16[160,1536]{1,0:T(8,128)(2,1)S(1)} %pad_maximum_fusion.5.grad.refs_7_) | copy-start | bytes 1474564
  321.2 107.8 %copy-start.2 = (f32[160,1536]{1,0:T(8,128)}, f32[160,1536]{1,0:T(8,128)S(1)}, u32[]{:S(2)}) copy-start(f32[160,1536]{1,0:T(8,128)S(1)} %get-tuple-element.107.middle.refs_6_) | copy-start | bytes 2949124
  390.6 25.7 %copy-start.4 = (f32[1280,1]{1,0:T(8,128)S(1)}, f32[1280,1]{1,0:T(8,128)}, u32[]{:S(2)}) copy-start(f32[1280,1]{1,0:T(8,128)} %copy-done.3) | copy-start | bytes 15364
  427.9 147.3 %reduce-scatter.11.cloned.1.call-start = ((), (), s32[]{:S(2)}) async-start(), calls=%async_computation.7 | async-start | bytes 1474560 | tf_op jit(solution)/shard_map/reduce_scatter | solution.py:997
  434.7 93.5 %copy-start.46 = (bf16[1,384,1536]{2,1,0:T(8,128)(2,1)S(1)}, bf16[1,384,1536]{2,1,0:T(8,128)(2,1)}, u32[]{:S(2)}) copy-start(bf16[1,384,1536]{2,1,0:T(8,128)(2,1)} %reduce-scatter.5.cloned.1.call-done) | copy-start | bytes 3538948
  532.4 11.0 %copy-start.29 = (bf16[1,8,96,768]{3,2,1,0:T(8,128)(2,1)S(1)}, bf16[1,8,96,768]{3,2,1,0:T(8,128)(2,1)}, u32[]{:S(2)}) copy-start(bf16[1,8,96,768]{3,2,1,0:T(8,128)(2,1)} %reduce-scatter.9.cloned.1.call-done) | copy-start | bytes 3538948
  (36 other events, 102.7 us)
Sparse Core Ops, SparseCore 0:
  9.6 33.1 all-gather.8
  44.3 73.5 all-gather.10
  119.5 87.9 all-gather.12
  208.9 87.8 all-gather.14
  299.0 83.6 reduce-scatter.4
  384.9 85.7 reduce-scatter.8
  473.0 70.2 reduce-scatter.6
  545.7 29.5 reduce-scatter.10

commit v7 on v6

--- a/solution.py
+++ b/solution.py
@@ -632,35 +632,43 @@
     return copies
 
 
-def swap_in_kernel(plan, project, up, project_out, up_out, project_cut, up_cut, p_send, p_recv, u_send, u_recv):
+def swap_in_kernel(plan, project, up, down, project_out, up_out, down_out, project_cut, up_cut,
+                   p_send, p_recv, u_send, u_recv, d_send, d_recv):
     seq, rank = here(plan)
     for to in range(plan.group):
         starts, share = project_columns(plan, to)
         project_cut[to] = fold_rows(jnp.concatenate([project[:, c : c + share] for c in starts], axis=1))
-    meet(group_devices(plan, seq, rank))
+    meet(group_devices(plan, seq, rank) + column_devices(plan, seq, rank))
     copies = start_swap(plan, seq, rank, project_cut, project_out, p_send, p_recv)
+    for step in range(1, plan.sequences):
+        to = other(seq, step, plan.sequences)
+        copy = remote(down, down_out.at[seq], d_send.at[step], d_recv.at[step], plan.device_of(to, rank))
+        copy.start()
+        copies.append(copy)
     for to in range(plan.group):
         starts, share = up_columns(plan, to, up.shape[1])
         up_cut[to] = jnp.concatenate([up[:, c : c + share] for c in starts], axis=1)
     copies += start_swap(plan, seq, rank, up_cut, up_out, u_send, u_recv)
+    down_out[seq] = down[...]
     for copy in copies:
         copy.wait()
 
 
-def swap_in(plan, project, up):
+def swap_in(plan, project, up, down):
     rows = project.shape[0]
     dma = pltpu.SemaphoreType.DMA
     shapes = [
         (plan.group, rows // 2, 2 * project.shape[1] // plan.group),
         (plan.group, rows, up.shape[1] // plan.group),
     ]
+    whole = (plan.sequences,) + down.shape
     return call(
         functools.partial(swap_in_kernel, plan),
         "swap_in",
         4,
-        tuple(jax.ShapeDtypeStruct(shape, BF16) for shape in shapes),
-        [pltpu.VMEM(shape, BF16) for shape in shapes] + [dma((plan.group,))] * 4,
-        (project, up),
+        tuple(jax.ShapeDtypeStruct(shape, BF16) for shape in shapes + [whole]),
+        [pltpu.VMEM(shape, BF16) for shape in shapes] + [dma((plan.group,))] * 4 + [dma((plan.sequences,))] * 2,
+        (project, up, down),
     )
 
 
@@ -1018,11 +1026,6 @@
     return lax.psum_scatter(full.reshape(-1, cols), "dev", scatter_dimension=0, tiled=True)
 
 
-def down_slices(plan, weight):
-    full = lax.all_gather(weight, "dev", axis=0, axis_index_groups=plan.rank_groups())
-    return full.reshape(2, -1, weight.shape[1])
-
-
 def by_stream(plan, image_part, text_part, is_text):
     start, end = plan.text_start, plan.image_end
     mixed = jnp.where(is_text[start:end, None], text_part[: end - start], image_part[start:])
@@ -1081,14 +1084,17 @@
     mod_part = jnp.dot(silu_part, modulation_weight, preferred_element_type=F32)
 
     merge_pair = merge_rows(plan, merge_weight, rank)
-    project_pieces, up_pieces = swap_in(plan, project_weight, up_weight)
+    early = down_weight.shape[0] // 6
+    project_pieces, up_pieces, down_early = swap_in(plan, project_weight, up_weight, down_weight[:early])
     project_pieces, up_pieces, merge_pair = lax.optimization_barrier((project_pieces, up_pieces, merge_pair))
     project_pair = over_sequences(plan, project_pieces)
     share = project_pair.shape[2] // 2
     project_pair = jnp.concatenate([project_pair[:, :, :share], project_pair[:, :, share:]], axis=1)
     project_pair = lax.optimization_barrier(project_pair.reshape(2, width, share))
     up_pair = over_sequences(plan, up_pieces).reshape(2, width, -1)
-    down_pair = down_slices(plan, down_weight)
+    down_late = lax.all_gather(down_weight[early:], "dev", axis=0, axis_index_groups=plan.rank_groups())
+    down_pair = jnp.concatenate([down_early, down_late], axis=1).reshape(2, -1, width)
+    down_pair = lax.optimization_barrier(down_pair)
 
     token_window, grad_window, mods, merge_pair = entry(plan, tokens, cotangent, mod_part, merge_pair)
     shift_a, scale_a, gate_a, shift_b, scale_b, gate_b = jnp.split(mods, 6, axis=1)

time: 589 us -> 590 us (level)
  other arithmetic: 35.6 us -> 42 us
    all_gather x1, waiting for transfers between devices: 24.4 us -> 7.42 us  [on_device(): lax.all_gather(down_weight[early:], 'dev', axis=0, axis_index_groups=plan...]
    all_gather x1, waiting for transfers between devices: 3.49 us -> 12.4 us  [merge_rows(): lax.all_gather(weight, 'dev', axis=0, axis_index_groups=plan.rank_groups())]
    unnamed x109 -> x119, local copies, waits for them, and re-layouts: 38.9 us -> 38 us
  transfers between devices with their start and end apart: 8 -> 8, of which waited for: 4 -> 4; matrix products, arithmetic and copies ran while one was open for 11% -> 13% of each run, Pallas kernels for 72% -> 72%
where the time goes in v7:
time: 590 us; the launch traced here: 585 us
  Pallas kernels  424 us (72%)
  local copies, waits for them, and re-layouts  53.9 us (9%)
  other arithmetic  42 us (7%)
  waiting for transfers between devices  32.9 us (6%)
  between operations  16.4 us (3%)
  matrix products  15.5 us (3%)
    pallas_call x6, Pallas kernels, call(): pl.pallas_call(kernel, out_shape=out_shape, in_specs=in_specs or [VMEM] *...  367 us
    unnamed x119, local copies, waits for them, and re-layouts  38 us
    pallas_call x1, Pallas kernels, attend_back(): pl.pallas_call(functools.partial(attend_back_kernel, plan.heads, rows //...  25.4 us
    pallas_call x4, Pallas kernels, weight_terms(): pl.pallas_call(functools.partial(terms_kernel, plan, fold, chunk), out_sh...  18.2 us
    pallas_call x1, Pallas kernels, attend(): pl.pallas_call(functools.partial(attend_kernel, plan.heads, block), out_s...  12.5 us
    all_gather x1, waiting for transfers between devices, merge_rows(): lax.all_gather(weight, 'dev', axis=0, axis_index_groups=plan.rank_groups())  12.4 us
  transfers between devices with their start and end apart: 8, of which 4 were waited for; matrix products, arithmetic and copies ran while one was open for 13% of the time, Pallas kernels for 72%

profile of v7, /device:TPU:0, one launch (start us, length us, event | category | flops | bytes accessed | tf_op | source)
XLA Modules:
  0.0 584.7 jit_solution(7476299145486631035)
XLA Ops:
  11.4 30.5 %swap_in.1 = (bf16[8,48,1152]{2,1,0:T(8,128)(2,1)}, bf16[8,96,768]{2,1,0:T(8,128)(2,1)}, bf16[4,64,1536]{2,1,0:T(8,128)(2,1)S(1)}) custom-call(bf16[96,4608]{1,0:T(8,128)(2,1)S(1)} %copy-done.31, bf16[96,6144]{1,0:T(8,128)(2,1)S(1)} %copy-done.25, bf16[64,1536]{1,0:T(8,128)(2,1)S(1)} %slice.149.down), custom_call_target="tpu_custom_call" | custom-call | tf_op jit(solution)/shard_map/swap_in/pallas_call | solution.py:307
  42.8 12.4 %all-gather.9.cloned.1.call-done = bf16[384,1536]{1,0:T(8,128)(2,1)} async-done(((bf16[96,1536]{1,0:T(8,128)(2,1)}), bf16[384,1536]{1,0:T(8,128)(2,1)}) %all-gather.9.cloned.1.call-update) | async-done | bytes 1179664 | tf_op jit(solution)/shard_map/all_gather | solution.py:1010
  65.5 79.9 %entry.1 = (bf16[1280,1536]{1,0:T(8,128)(2,1)S(1)}, bf16[1280,1536]{1,0:T(8,128)(2,1)S(1)}, f32[8,2,9,128]{3,2,1,0:T(8,128)S(1)}, bf16[2,2,96,1536]{3,2,1,0:T(8,128)(2,1)S(1)}) custom-call(bf16[144,1536]{1,0:T(8,128)(2,1)S(1)} %copy-done.35, bf16[144,1536]{1,0:T(8,128)(2,1)S(1)} %copy-done.36, f32[8,4,9,128]{3,2,1,0:T(8,128)S(1)} %bitcast.68, ...), custom_call_target="tpu_custom_call" | custom-call | tf_op jit(solution)/shard_map/entry/pallas_call | solution.py:307
  150.3 3.5 fusion.2
  153.9 9.2 %multiply_convert_fusion = (bf16[1280,1536]{1,0:T(8,128)(2,1)}, bf16[1280,1536]{1,0:T(8,128)(2,1)}, bf16[1280,1536]{1,0:T(8,128)(2,1)}) fusion(f32[1536]{0:T(1024)S(1)} %get-tuple-element.100, f32[1536]{0:T(1024)S(1)} %get-tuple-element.101, pred[1280]{0:T(1024)(128)(4,1)S(1)} %get-tuple-element.132, bf16[1280,1536]{1,0:T(8,128)(2,1)} %copy-done.19, ...), kind=kLoop, calls=%fused_computation.8 | loop fusion | flops 27525120 | bytes 19710464 | tf_op jit(solution)/shard_map/convert_element_type | solution.py:1119
  163.8 3.3 fusion.36
  167.5 3.1 copy-done.13
  170.7 2.7 fusion.13
  180.0 12.5 %attend.1.rows = bf16[1280,192]{1,0:T(8,128)(2,1)S(1)} custom-call(bf16[1280,576]{1,0:T(8,128)(2,1)S(1)} %pad_maximum_fusion.4.projected, f32[1,1280]{1,0:T(1,128)S(1)} %and_select_fusion.bias_ref), custom_call_target="tpu_custom_call" | custom-call | flops 5033164800 | bytes 1966080 | tf_op jit(solution)/shard_map/attend/pallas_call | solution.py:128
  192.5 77.2 %middle.1 = (f32[160,1536]{1,0:T(8,128)S(1)}, bf16[1280,1536]{1,0:T(8,128)(2,1)S(1)}) custom-call(bf16[1280,192]{1,0:T(8,128)(2,1)S(1)} %attend.1.rows, bf16[2,192,1536]{2,1,0:T(8,128)(2,1)S(1)} %bitcast.65, f32[1280,1]{1,0:T(8,128)S(1)} %fusion.25.window_text.text.refs_4_, bf16[160,1536]{1,0:T(8,128)(2,1)S(1)} %pad_maximum_fusion.5.tokens.refs_5_, ...), custom_call_target="tpu_custom_call" | custom-call | tf_op jit(solution)/shard_map/middle/pallas_call | solution.py:307
  271.7 2.9 fusion.35
  275.3 2.9 fusion.17
  282.6 4.9 down_terms.1
  289.8 7.4 %all-gather.15.cloned.1.call-done = bf16[1280,1536]{1,0:T(8,128)(2,1)} async-done(((bf16[320,1536]{1,0:T(8,128)(2,1)}), bf16[1280,1536]{1,0:T(8,128)(2,1)}) %all-gather.15.cloned.1.call-update) | async-done | bytes 3932176 | tf_op jit(solution)/shard_map/all_gather | solution.py:1095
  300.5 3.0 fusion.15
  306.2 2.9 fusion.12.grads.rows
  309.1 5.8 up_terms.1
  322.6 63.7 %back.1 = (f32[160,1536]{1,0:T(8,128)S(1)}, f32[160,1536]{1,0:T(8,128)S(1)}, bf16[1280,1536]{1,0:T(8,128)(2,1)S(1)}) custom-call(bf16[1280,768]{1,0:T(8,128)(2,1)S(1)} %copy-done.6, bf16[2,1536,768]{2,1,0:T(8,128)(2,1)} %bitcast.71, f32[1280,1]{1,0:T(8,128)S(1)} %fusion.25.window_text.text.refs_4_, bf16[160,1536]{1,0:T(8,128)(2,1)S(1)} %pad_maximum_fusion.6.grad.refs_7_, ...), custom_call_target="tpu_custom_call" | custom-call | tf_op jit(solution)/shard_map/back/pallas_call | solution.py:307
  390.1 25.4 %attend_back.1.grads.refs_2_ = bf16[1280,576]{1,0:T(8,128)(2,1)} custom-call(bf16[1280,576]{1,0:T(8,128)(2,1)} %copy-done.23, bf16[1280,1536]{1,0:T(8,128)(2,1)} %copy-done.17, bf16[2,192,1536]{2,1,0:T(8,128)(2,1)} %bitcast.64, f32[1280,1]{1,0:T(8,128)} %copy-done.3, f32[1,1280]{1,0:T(1,128)} %copy-done.37), custom_call_target="tpu_custom_call" | custom-call | flops 12582912000 | bytes 3440640 | tf_op jit(solution)/shard_map/attend_back/pallas_call | solution.py:184
  419.0 6.3 %project_terms.1 = bf16[32,48,1152]{2,1,0:T(8,128)(2,1)S(1)} custom-call(bf16[1280,1536]{1,0:T(8,128)(2,1)S(1)} %copy-done.14, bf16[1280,576]{1,0:T(8,128)(2,1)S(1)} %copy-done.22, f32[1280,1]{1,0:T(8,128)S(1)} %copy-done.4), custom_call_target="tpu_custom_call" | custom-call | flops 3397386240 | bytes 8388608 | tf_op jit(solution)/shard_map/project_terms/pallas_call | solution.py:246
  428.2 2.6 multiply_reduce_fusion.1
  433.9 90.2 %last.1 = (bf16[144,1536]{1,0:T(8,128)(2,1)}, bf16[144,1536]{1,0:T(8,128)(2,1)}, f32[144,1536]{1,0:T(8,128)}, f32[144,1536]{1,0:T(8,128)}, f32[8,4,1,1152]{3,2,1...) custom-call(bf16[1280,768]{1,0:T(8,128)(2,1)} %copy-done.7, bf16[2,768,1536]{2,1,0:T(8,128)(2,1)} %bitcast.74, ...), custom_call_target="tpu_custom_call" | custom-call | tf_op jit(solution)/shard_map/last/pallas_call | solution.py:307
  533.9 9.9 %reduce-scatter.7.cloned.1.call-done = bf16[1,8,48,1152]{3,2,1,0:T(8,128)(2,1)} async-done(((bf16[4,8,48,1152]{3,2,1,0:T(8,128)(2,1)}), bf16[1,8,48,1152]{3,2,1,0:T(8,128)(2,1)}) %reduce-scatter.7.cloned.1.call-update) | async-done | bytes 884752 | tf_op jit(solution)/shard_map/reduce_scatter | solution.py:1005
  545.0 26.0 %finish.1 = (bf16[96,6144]{1,0:T(8,128)(2,1)S(1)}, bf16[96,4608]{1,0:T(8,128)(2,1)S(1)}) custom-call(bf16[8,96,768]{2,1,0:T(8,128)(2,1)S(1)} %bitcast.67, bf16[8,48,1152]{2,1,0:T(8,128)(2,1)S(1)} %bitcast.69), custom_call_target="tpu_custom_call" | custom-call | tf_op jit(solution)/shard_map/finish/pallas_call | solution.py:307
  (227 shorter events, 80.3 us)
Async XLA Ops:
  7.2 48.0 %all-gather.9.cloned.1.call-start = ((), (), s32[]{:S(2)}) async-start(), calls=%async_computation.8 | async-start | bytes 1474560 | tf_op jit(solution)/shard_map/all_gather | solution.py:1010
  7.9 50.5 %copy-start.56 = (s32[4]{0:T(128)S(1)}, s32[4]{0:T(128)}, u32[]{:S(2)}) copy-start(s32[4]{0:T(128)} %param.11) | copy-start | bytes 52
  7.9 54.2 %copy-start.55 = (bf16[4,1536]{1,0:T(4,128)(2,1)S(1)}, bf16[4,1536]{1,0:T(4,128)(2,1)}, u32[]{:S(2)}) copy-start(bf16[4,1536]{1,0:T(4,128)(2,1)} %param.10) | copy-start | bytes 36868
  7.9 155.9 %all-gather.11.cloned.1.call-start = ((), (), s32[]{:S(2)}) async-start(), calls=%async_computation.9 | async-start | bytes 4423680 | tf_op jit(solution)/shard_map/all_gather | solution.py:1000
  55.2 10.3 %copy-start.28 = (bf16[384,1536]{1,0:T(8,128)(2,1)S(1)}, bf16[384,1536]{1,0:T(8,128)(2,1)}, u32[]{:S(2)}) copy-start(bf16[384,1536]{1,0:T(8,128)(2,1)} %all-gather.9.cloned.1.call-done) | copy-start | bytes 3538948
  55.2 10.3 %copy-start.35 = (bf16[144,1536]{1,0:T(8,128)(2,1)S(1)}, bf16[144,1536]{1,0:T(8,128)(2,1)}, u32[]{:S(2)}) copy-start(bf16[144,1536]{1,0:T(8,128)(2,1)} %tokens.1) | copy-start | bytes 1327108
  55.3 216.4 %all-gather.13.cloned.1.call-start = ((), (), s32[]{:S(2)}) async-start(), calls=%async_computation.10 | async-start | bytes 5898240 | tf_op jit(solution)/shard_map/all_gather | solution.py:1000
  56.0 241.2 %all-gather.15.cloned.1.call-start = ((), (), s32[]{:S(2)}) async-start(), calls=%async_computation.11 | async-start | bytes 4915200 | tf_op jit(solution)/shard_map/all_gather | solution.py:1095
  58.3 357.2 %reduce-scatter.5.cloned.1.call-start = ((), (), s32[]{:S(2)}) async-start(), calls=%async_computation.4 | async-start | bytes 5898240 | tf_op jit(solution)/shard_map/reduce_scatter | solution.py:1005
  62.2 117.8 %copy-start.37 = (f32[1,1280]{1,0:T(1,128)}, f32[1,1280]{1,0:T(1,128)S(1)}, u32[]{:S(2)}) copy-start(f32[1,1280]{1,0:T(1,128)S(1)} %and_select_fusion.bias_ref) | copy-start | bytes 15364
  63.0 257.7 %copy-start.3 = (f32[1280,1]{1,0:T(8,128)}, f32[1280,1]{1,0:T(8,128)S(1)}, u32[]{:S(2)}) copy-start(f32[1280,1]{1,0:T(8,128)S(1)} %fusion.25.window_text.text.refs_4_) | copy-start | bytes 15364
  63.3 257.4 %copy-start.24 = (f32[160,1]{1,0:T(8,128)}, f32[160,1]{1,0:T(8,128)S(1)}, u32[]{:S(2)}) copy-start(f32[160,1]{1,0:T(8,128)S(1)} %convert_element_type.86.text.refs_11_) | copy-start | bytes 1924
  150.2 12.9 %copy-start.45 = (bf16[144,1536]{1,0:T(8,128)(2,1)}, bf16[144,1536]{1,0:T(8,128)(2,1)S(1)}, u32[]{:S(2)}) copy-start(bf16[144,1536]{1,0:T(8,128)(2,1)S(1)} %constant_dynamic-slice_fusion.3) | copy-start | bytes 1327108
  163.2 29.4 %copy-start.11 = (bf16[160,1536]{1,0:T(8,128)(2,1)}, bf16[160,1536]{1,0:T(8,128)(2,1)S(1)}, u32[]{:S(2)}) copy-start(bf16[160,1536]{1,0:T(8,128)(2,1)S(1)} %pad_maximum_fusion.5.tokens.refs_5_) | copy-start | bytes 1474564
  180.0 12.6 %copy-start.23 = (bf16[1280,576]{1,0:T(8,128)(2,1)}, bf16[1280,576]{1,0:T(8,128)(2,1)S(1)}, u32[]{:S(2)}) copy-start(bf16[1280,576]{1,0:T(8,128)(2,1)S(1)} %pad_maximum_fusion.4.projected) | copy-start | bytes 4423684
  180.0 12.6 %copy-start.27 = (bf16[2,2,96,1536]{3,2,1,0:T(8,128)(2,1)S(1)}, bf16[2,2,96,1536]{3,2,1,0:T(8,128)(2,1)}, u32[]{:S(2)}) copy-start(bf16[2,2,96,1536]{3,2,1,0:T(8,128)(2,1)} %copy-done.26) | copy-start | bytes 3538948
  289.7 240.6 %reduce-scatter.9.cloned.1.call-start = ((), (), s32[]{:S(2)}) async-start(), calls=%async_computation.6 | async-start | bytes 5898240 | tf_op jit(solution)/shard_map/reduce_scatter | solution.py:1005
  317.1 226.6 %reduce-scatter.7.cloned.1.call-start = ((), (), s32[]{:S(2)}) async-start(), calls=%async_computation.5 | async-start | bytes 4423680 | tf_op jit(solution)/shard_map/reduce_scatter | solution.py:1005
  319.1 67.2 %copy-start.12 = (bf16[160,1536]{1,0:T(8,128)(2,1)}, bf16[160,1536]{1,0:T(8,128)(2,1)S(1)}, u32[]{:S(2)}) copy-start(bf16[160,1536]{1,0:T(8,128)(2,1)S(1)} %pad_maximum_fusion.6.grad.refs_7_) | copy-start | bytes 1474564
  320.7 107.5 %copy-start.2 = (f32[160,1536]{1,0:T(8,128)}, f32[160,1536]{1,0:T(8,128)S(1)}, u32[]{:S(2)}) copy-start(f32[160,1536]{1,0:T(8,128)S(1)} %get-tuple-element.109.middle.refs_6_) | copy-start | bytes 2949124
  390.1 25.4 %copy-start.4 = (f32[1280,1]{1,0:T(8,128)S(1)}, f32[1280,1]{1,0:T(8,128)}, u32[]{:S(2)}) copy-start(f32[1280,1]{1,0:T(8,128)} %copy-done.3) | copy-start | bytes 15364
  427.1 148.5 %reduce-scatter.11.cloned.1.call-start = ((), (), s32[]{:S(2)}) async-start(), calls=%async_computation.7 | async-start | bytes 1474560 | tf_op jit(solution)/shard_map/reduce_scatter | solution.py:1005
  433.9 92.2 %copy-start.51 = (bf16[1,384,1536]{2,1,0:T(8,128)(2,1)S(1)}, bf16[1,384,1536]{2,1,0:T(8,128)(2,1)}, u32[]{:S(2)}) copy-start(bf16[1,384,1536]{2,1,0:T(8,128)(2,1)} %reduce-scatter.5.cloned.1.call-done) | copy-start | bytes 3538948
  530.3 13.5 %copy-start.29 = (bf16[1,8,96,768]{3,2,1,0:T(8,128)(2,1)S(1)}, bf16[1,8,96,768]{3,2,1,0:T(8,128)(2,1)}, u32[]{:S(2)}) copy-start(bf16[1,8,96,768]{3,2,1,0:T(8,128)(2,1)} %reduce-scatter.9.cloned.1.call-done) | copy-start | bytes 3538948
  (41 other events, 128.7 us)
Sparse Core Ops, SparseCore 0:
  9.6 45.5 all-gather.8
  56.8 73.8 all-gather.10
  132.2 87.9 all-gather.12
  222.3 74.8 all-gather.14
  299.3 83.8 reduce-scatter.4
  385.3 85.7 reduce-scatter.8
  473.5 70.2 reduce-scatter.6
  546.1 29.4 reduce-scatter.10

commit v8 on v6

--- a/solution.py
+++ b/solution.py
@@ -115,7 +115,7 @@
 
 
 def block_rows(rows):
-    return 256 if rows % 256 == 0 else 128
+    return 128
 
 
 def constant(shape):
@@ -241,7 +241,7 @@
 
 def weight_terms(plan, rows, grads, text, name, fold=0):
     width, cols = rows.shape[1], grads.shape[1]
-    chunk = 384 if width % 384 == 0 else width
+    chunk = 384 if fold else 256 if width % 256 == 0 else width
     shape = (2 * width // fold, fold // 2, 2 * cols) if fold else (2, width, cols)
     return pl.pallas_call(
         functools.partial(terms_kernel, plan, fold, chunk),
@@ -253,6 +253,73 @@
         cost_estimate=pl.CostEstimate(flops=3 * plan.rows * width * cols, bytes_accessed=1 << 23, transcendentals=0),
         name=name,
     )(rows, grads, text)
+
+
+def gelu(values):
+    return jax.nn.gelu(values, approximate=True)
+
+
+def in_blocks(plan, size, body):
+    def step(i, carry):
+        body(i, pl.ds(pl.multiple_of(i * size, size), size))
+        return carry
+
+    lax.fori_loop(0, plan.rows // size, step, 0)
+
+
+def blockwise(plan, i, size, block, pair, dims, mask, out):
+    @pl.when(i * size < plan.image_end)
+    def _():
+        out[...] = lax.dot_general(block, pair[0], dims, preferred_element_type=F32)
+
+    @pl.when(i * size + size > plan.text_start)
+    def _():
+        out[...] = jnp.where(mask > 0, lax.dot_general(block, pair[1], dims, preferred_element_type=F32), out[...])
+
+
+def project_kernel(plan, size, rows, pair, text, shift, scale, hidden, out, held):
+    def body(i, place):
+        mask = text[place]
+        normed, _ = norm_rows(rows[place].astype(F32))
+        block = (normed * (1.0 + pick_rows(scale[...], mask)) + pick_rows(shift[...], mask)).astype(BF16)
+        hidden[place] = block
+        blockwise(plan, i, size, block, pair, PLAIN, mask, held)
+        out[place] = held[...].astype(BF16)
+
+    in_blocks(plan, size, body)
+
+
+def up_kernel(plan, size, rows, pair, text, upper, activated):
+    def body(i, place):
+        blockwise(plan, i, size, rows[place], pair, PLAIN, text[place], upper.at[place])
+        activated[place] = gelu(upper[place]).astype(BF16)
+
+    in_blocks(plan, size, body)
+
+
+def down_back_kernel(plan, size, rows, pair, text, upper, out, held):
+    def body(i, place):
+        blockwise(plan, i, size, rows[place], pair, CONTRACT_LAST, text[place], held)
+        out[place] = jax.vjp(gelu, upper[place])[1](held[...])[0].astype(BF16)
+
+    in_blocks(plan, size, body)
+
+
+def stream_rows(plan, kernel, size, cols, held, name, outs, *operands):
+    spec = pl.BlockSpec(memory_space=pltpu.VMEM)
+    shapes = tuple(jax.ShapeDtypeStruct((plan.rows, width), dtype) for width, dtype in outs)
+    return pl.pallas_call(
+        functools.partial(kernel, plan, size),
+        out_shape=shapes,
+        in_specs=[spec] * len(operands),
+        out_specs=(spec,) * len(shapes),
+        scratch_shapes=[pltpu.VMEM((size, cols), F32)] if held else [],
+        compiler_params=pltpu.CompilerParams(vmem_limit_bytes=40 << 20),
+        cost_estimate=pl.CostEstimate(
+            flops=2 * plan.rows * plan.width * cols, bytes_accessed=1 << 24, transcendentals=0
+        ),
+        name=name,
+    )(*operands)
 
 
 VMEM = pl.BlockSpec(memory_space=pltpu.VMEM)
@@ -340,9 +407,8 @@
 def sum_scratch(plan, wire=BF16):
     half, own, width = plan.group // 2, plan.own, plan.width
     return [
+        pltpu.VMEM((half + 1, own, width), F32),
         pltpu.VMEM((half, own, width), F32),
-        pltpu.VMEM((half, own, width), F32),
-        pltpu.VMEM((own, width), F32),
         pltpu.VMEM((half - 1, own, width), wire),
         pltpu.VMEM((half - 1, own, width), wire),
         pltpu.SemaphoreType.DMA((half,)),
@@ -352,13 +418,13 @@
     ]
 
 
-SUM_SCRATCH = 9
+SUM_SCRATCH = 8
 
 
 def product(plan, rows, pair, text, dims, rank, out):
     block = load_block(plan, rows, rank)
     text_row = load_block(plan, text, rank) > 0
-    chunk = plan.width // 4
+    chunk = 256
 
     def step(i, carry):
         cols = pl.ds(pl.multiple_of(i * chunk, chunk), chunk)
@@ -369,14 +435,14 @@
         out[:, cols] = jnp.where(text_row, parts[1], parts[0])
         return carry
 
-    lax.fori_loop(0, 4, step, 0)
+    lax.fori_loop(0, plan.width // chunk, step, 0)
 
 
 def scatter_sum(*args):
     return scatter_start(*args)()
 
 
-def scatter_start(plan, seq, rank, rows, pair, text, dims, away, near, mine, going, coming,
+def scatter_start(plan, seq, rank, rows, pair, text, dims, away, near, going, coming,
                   pair_send, pair_recv, far_send, far_recv):
     half = plan.group // 2
     chip, core = lax.div(rank, 2), lax.rem(rank, 2)
@@ -390,29 +456,34 @@
         to = plan.device_of(seq, 2 * other(chip, step, half) + core)
         return remote(going.at[step - 1], coming.at[step - 1], far_send.at[step], far_recv.at[step], to)
 
-    def for_owner(step):
-        product(plan, rows, pair, text, dims, 2 * other(chip, step, half) + core, mine)
-        pair_copy(step).wait_recv()
-        mine[...] += near[step]
-
     def turn(i, carry):
-        step = other(i, 1, half)
-        product(plan, rows, pair, text, dims, 2 * other(chip, step, half) + 1 - core, away.at[step])
-        pair_copy(step).start()
-
-        @pl.when(i > 0)
+        for_partner = (i < 2) | (lax.rem(i, 2) == 1) & (i < 2 * half - 1)
+        place = jnp.where(i < 2, i, jnp.where(for_partner, lax.div(i + 1, 2), lax.div(i, 2) - 1))
+        place = jnp.where(i == 2 * half - 1, half - 1, place)
+        step = other(place, 1, half)
+        block = 2 * other(chip, step, half) + jnp.where(for_partner, 1 - core, core)
+        product(plan, rows, pair, text, dims, block, away.at[jnp.where(for_partner, step, half)])
+
+        @pl.when(for_partner)
         def _():
-            for_owner(i)
-            going[i - 1] = mine[...].astype(going.dtype)
-            far_copy(i).start()
+            pair_copy(step).start()
+
+        @pl.when(jnp.logical_not(for_partner))
+        def _():
+            pair_copy(step).wait_recv()
+            away[half] = away[half] + near[step]
+
+        @pl.when(jnp.logical_not(for_partner) & (place < half - 1))
+        def _():
+            going[step - 1] = away[half].astype(going.dtype)
+            far_copy(step).start()
 
         return carry
 
-    lax.fori_loop(0, half, turn, 0)
+    lax.fori_loop(0, 2 * half, turn, 0)
 
     def result():
-        for_owner(0)
-        total = mine[...]
+        total = away[half]
         for step in range(1, half):
             far_copy(step).wait_recv()
             total = total + coming[step - 1].astype(F32)
@@ -1023,24 +1094,6 @@
     return full.reshape(2, -1, weight.shape[1])
 
 
-def by_stream(plan, image_part, text_part, is_text):
-    start, end = plan.text_start, plan.image_end
-    mixed = jnp.where(is_text[start:end, None], text_part[: end - start], image_part[start:])
-    return jnp.concatenate([image_part[:start], mixed, text_part[end - start :]], axis=0)
-
-
-def stream_dot(plan, rows, pair, is_text):
-    image_part = jnp.dot(rows[: plan.image_end], pair[0], preferred_element_type=F32)
-    text_part = jnp.dot(rows[plan.text_start :], pair[1], preferred_element_type=F32)
-    return by_stream(plan, image_part, text_part, is_text)
-
-
-def stream_dot_back(plan, grads, pair, is_text):
-    image_part = lax.dot_general(grads[: plan.image_end], pair[0], CONTRACT_LAST, preferred_element_type=F32)
-    text_part = lax.dot_general(grads[plan.text_start :], pair[1], CONTRACT_LAST, preferred_element_type=F32)
-    return by_stream(plan, image_part, text_part, is_text)
-
-
 def pick(table, text_rows):
     return jnp.where(text_rows[:, None], table[1][None, :], table[0][None, :])
 
@@ -1094,9 +1147,11 @@
     shift_a, scale_a, gate_a, shift_b, scale_b, gate_b = jnp.split(mods, 6, axis=1)
     grad_window = jnp.where(valid[:, None], grad_window, jnp.zeros((), BF16))
 
-    normed_full, _ = layer_norm(token_window.astype(F32))
-    hidden_a = (normed_full * (1.0 + pick(scale_a, is_text)) + pick(shift_a, is_text)).astype(BF16)
-    projected = stream_dot(plan, hidden_a, project_pair, is_text).astype(BF16)
+    cols = project_pair.shape[2]
+    hidden_a, projected = stream_rows(
+        plan, project_kernel, 128, cols, True, "project", ((width, BF16), (cols, BF16)),
+        token_window, project_pair, window_text, shift_a, scale_a,
+    )
     attended = attend(plan, projected, bias)
 
     own_tokens = own_rows(plan, token_window, rank)
@@ -1108,16 +1163,19 @@
     middle = own_tokens.astype(F32) + pick(gate_a, own_text) * merged
     normed_b, inv_b = layer_norm(middle)
 
-    upper = stream_dot(plan, hidden_b, up_pair, is_text)
-    activated = jax.nn.gelu(upper, approximate=True).astype(BF16)
+    units = up_pair.shape[2]
+    upper, activated = stream_rows(
+        plan, up_kernel, 128, units, False, "up", ((units, F32), (units, BF16)), hidden_b, up_pair, window_text
+    )
     grad_lowered = (pick(gate_b, is_text) * grad_window.astype(F32)).astype(BF16)
     down_term = weight_terms(plan, activated, grad_lowered, window_text, "down_terms")
     down_term = down_term.reshape(plan.sequences, -1, width)
     down_term, grad_lowered = lax.optimization_barrier((down_term, grad_lowered))
     down_sum = over_sequences_sum(plan, down_term)
-    grad_activated = stream_dot_back(plan, grad_lowered, down_pair, is_text)
-    gelu_pull = jax.vjp(lambda value_in: jax.nn.gelu(value_in, approximate=True), upper)[1]
-    grad_upper = gelu_pull(grad_activated)[0].astype(BF16)
+    (grad_upper,) = stream_rows(
+        plan, down_back_kernel, 128, units, True, "down_back", ((units, BF16),),
+        grad_lowered, down_pair, window_text, upper,
+    )
     up_term = weight_terms(plan, hidden_b, grad_upper, window_text, "up_terms")
     up_term = up_term.reshape(plan.sequences, plan.group, mod_rows, -1)
     grad_upper, up_term = lax.optimization_barrier((grad_upper, up_term))

time: 589 us -> 593 us (level)
  Pallas kernels: 423 us -> 472 us
  waiting for transfers between devices: 38.7 us -> 21.3 us
  matrix products: 19.4 us -> 4.27 us
  other arithmetic: 35.6 us -> 26.3 us
    pallas_call x0 -> x3, Pallas kernels: none -> 34.9 us  [stream_rows(): pl.pallas_call(functools.partial(kernel, plan, size), out_shape=shapes, i...]
    dot_general x6 -> x0, matrix products: 15 us -> none  [the longest x1 5.68 us: stream_dot_back(): lax.dot_general(grads[:plan.image_end], pair[0], CONTRACT_LAST, preferred...]
    reduce_scatter x4, waiting for transfers between devices: 8.8 us -> 0.01 us  [over_sequences_sum(): lax.psum_scatter(pieces, 'dev', scatter_dimension=0, axis_index_groups=pl...]
    all_gather x1, waiting for transfers between devices: 24.4 us -> 15.8 us  [down_slices(): lax.all_gather(weight, 'dev', axis=0, axis_index_groups=plan.rank_groups())]
    unnamed x109 -> x101, local copies, waits for them, and re-layouts: 38.9 us -> 40.9 us
  transfers between devices with their start and end apart: 8 -> 8, of which waited for: 4 -> 2; matrix products, arithmetic and copies ran while one was open for 11% -> 7% of each run, Pallas kernels for 72% -> 80%
where the time goes in v8:
time: 593 us; the launch traced here: 591 us
  Pallas kernels  472 us (80%)
  local copies, waits for them, and re-layouts  50.9 us (9%)
  other arithmetic  26.3 us (4%)
  waiting for transfers between devices  21.3 us (4%)
  between operations  15.6 us (3%)
    pallas_call x6, Pallas kernels, call(): pl.pallas_call(kernel, out_shape=out_shape, in_specs=in_specs or [VMEM] *...  368 us
    unnamed x101, local copies, waits for them, and re-layouts  40.9 us
    pallas_call x3, Pallas kernels, stream_rows(): pl.pallas_call(functools.partial(kernel, plan, size), out_shape=shapes, i...  34.9 us
    pallas_call x1, Pallas kernels, attend_back(): pl.pallas_call(functools.partial(attend_back_kernel, plan.heads, rows //...  31.4 us
    pallas_call x4, Pallas kernels, weight_terms(): pl.pallas_call(functools.partial(terms_kernel, plan, fold, chunk), out_sh...  19.4 us
    pallas_call x1, Pallas kernels, attend(): pl.pallas_call(functools.partial(attend_kernel, plan.heads, block), out_s...  18.2 us
    all_gather x1, waiting for transfers between devices, down_slices(): lax.all_gather(weight, 'dev', axis=0, axis_index_groups=plan.rank_groups())  15.8 us
  transfers between devices with their start and end apart: 8, of which 2 were waited for; matrix products, arithmetic and copies ran while one was open for 7% of the time, Pallas kernels for 80%

profile of v8, /device:TPU:0, one launch (start us, length us, event | category | flops | bytes accessed | tf_op | source)
XLA Modules:
  0.0 590.8 jit_solution(1900134260734086868)
XLA Ops:
  10.4 28.9 %swap_in.1 = (bf16[8,48,1152]{2,1,0:T(8,128)(2,1)}, bf16[8,96,768]{2,1,0:T(8,128)(2,1)}) custom-call(bf16[96,4608]{1,0:T(8,128)(2,1)S(1)} %copy-done.31, bf16[96,6144]{1,0:T(8,128)(2,1)S(1)} %copy-done.28), custom_call_target="tpu_custom_call" | custom-call | tf_op jit(solution)/shard_map/swap_in/pallas_call | solution.py:374
  39.3 3.5 all-gather.9.cloned.1.call-done
  51.2 78.3 %entry.1 = (bf16[1280,1536]{1,0:T(8,128)(2,1)S(1)}, bf16[1280,1536]{1,0:T(8,128)(2,1)S(1)}, f32[8,2,9,128]{3,2,1,0:T(8,128)S(1)}, bf16[2,2,96,1536]{3,2,1,0:T(8,128)(2,1)S(1)}) custom-call(bf16[144,1536]{1,0:T(8,128)(2,1)S(1)} %copy-done.33, bf16[144,1536]{1,0:T(8,128)(2,1)S(1)} %copy-done.34, f32[8,4,9,128]{3,2,1,0:T(8,128)S(1)} %bitcast.53, ...), custom_call_target="tpu_custom_call" | custom-call | tf_op jit(solution)/shard_map/entry/pallas_call | solution.py:374
  137.7 5.5 multiply_convert_fusion
  143.3 3.3 fusion.10
  146.9 3.1 copy-done.9
  150.1 10.0 %project.3 = (bf16[1280,1536]{1,0:T(8,128)(2,1)S(1)}, bf16[1280,576]{1,0:T(8,128)(2,1)S(1)}) custom-call(bf16[1280,1536]{1,0:T(8,128)(2,1)S(1)} %copy-done.9, bf16[2,1536,576]{2,1,0:T(8,128)(2,1)S(1)} %bitcast.43, f32[1280,1]{1,0:T(8,128)S(1)} %fusion.text.window_text.refs_4_, f32[2,1536]{1,0:T(2,128)S(1)} %get-tuple-element.123.shift, ...), custom_call_target="tpu_custom_call" | custom-call | flops 2264924160 | bytes 16777216 | tf_op jit(solution)/shard_map/project/pallas_call | solution.py:311
  162.0 18.2 %attend.1.rows = bf16[1280,192]{1,0:T(8,128)(2,1)S(1)} custom-call(bf16[1280,576]{1,0:T(8,128)(2,1)S(1)} %get-tuple-element.58.projected, f32[1,1280]{1,0:T(1,128)S(1)} %and_select_fusion.bias_ref), custom_call_target="tpu_custom_call" | custom-call | flops 5033164800 | bytes 1966080 | tf_op jit(solution)/shard_map/attend/pallas_call | solution.py:128
  180.2 77.8 %middle.1 = (f32[160,1536]{1,0:T(8,128)S(1)}, bf16[1280,1536]{1,0:T(8,128)(2,1)S(1)}) custom-call(bf16[1280,192]{1,0:T(8,128)(2,1)S(1)} %attend.1.rows, bf16[2,192,1536]{2,1,0:T(8,128)(2,1)S(1)} %bitcast.51, f32[1280,1]{1,0:T(8,128)S(1)} %fusion.text.window_text.refs_4_, bf16[160,1536]{1,0:T(8,128)(2,1)S(1)} %pad_maximum_fusion.1.tokens.refs_5_, ...), custom_call_target="tpu_custom_call" | custom-call | tf_op jit(solution)/shard_map/middle/pallas_call | solution.py:374
  259.9 2.2 copy-done.40
  262.0 9.4 %up.3 = (f32[1280,768]{1,0:T(8,128)S(1)}, bf16[1280,768]{1,0:T(8,128)(2,1)S(1)}) custom-call(bf16[1280,1536]{1,0:T(8,128)(2,1)S(1)} %copy-done.40, bf16[2,1536,768]{2,1,0:T(8,128)(2,1)} %bitcast.58, f32[1280,1]{1,0:T(8,128)S(1)} %fusion.text.window_text.refs_4_), custom_call_target="tpu_custom_call" | custom-call | flops 3019898880 | bytes 16777216 | tf_op jit(solution)/shard_map/up/pallas_call | solution.py:311
  273.4 5.3 down_terms.1
  281.1 15.8 %all-gather.15.cloned.1.call-done = bf16[1536,1536]{1,0:T(8,128)(2,1)} async-done(((bf16[384,1536]{1,0:T(8,128)(2,1)}), bf16[1536,1536]{1,0:T(8,128)(2,1)}) %all-gather.15.cloned.1.call-update) | async-done | bytes 4718608 | tf_op jit(solution)/shard_map/all_gather | solution.py:1093
  301.1 15.5 %down_back.1.grads.rows = bf16[1280,768]{1,0:T(8,128)(2,1)S(1)} custom-call(bf16[1280,1536]{1,0:T(8,128)(2,1)S(1)} %copy-done.5, bf16[2,768,1536]{2,1,0:T(8,128)(2,1)} %bitcast.56, f32[1280,1]{1,0:T(8,128)S(1)} %fusion.text.window_text.refs_4_, f32[1280,768]{1,0:T(8,128)S(1)} %copy-done.20), custom_call_target="tpu_custom_call" | custom-call | flops 3019898880 | bytes 16777216 | tf_op jit(solution)/shard_map/down_back/pallas_call | solution.py:311
  316.6 6.5 %up_terms.1 = bf16[2,1536,768]{2,1,0:T(8,128)(2,1)S(1)} custom-call(bf16[1280,1536]{1,0:T(8,128)(2,1)S(1)} %copy-done.41, bf16[1280,768]{1,0:T(8,128)(2,1)S(1)} %down_back.1.grads.rows, f32[1280,1]{1,0:T(8,128)S(1)} %fusion.text.window_text.refs_4_), custom_call_target="tpu_custom_call" | custom-call | flops 4529848320 | bytes 8388608 | tf_op jit(solution)/shard_map/up_terms/pallas_call | solution.py:246
  323.2 2.2 copy-done.11
  330.9 65.6 %back.1 = (f32[160,1536]{1,0:T(8,128)S(1)}, f32[160,1536]{1,0:T(8,128)S(1)}, bf16[1280,1536]{1,0:T(8,128)(2,1)S(1)}) custom-call(bf16[1280,768]{1,0:T(8,128)(2,1)S(1)} %copy-done.7, bf16[2,1536,768]{2,1,0:T(8,128)(2,1)} %bitcast.59, f32[1280,1]{1,0:T(8,128)S(1)} %fusion.text.window_text.refs_4_, bf16[160,1536]{1,0:T(8,128)(2,1)S(1)} %pad_maximum_fusion.2.grad.refs_7_, ...), custom_call_target="tpu_custom_call" | custom-call | tf_op jit(solution)/shard_map/back/pallas_call | solution.py:374
  400.4 31.4 %attend_back.1.grads.refs_2_ = bf16[1280,576]{1,0:T(8,128)(2,1)} custom-call(bf16[1280,576]{1,0:T(8,128)(2,1)} %copy-done.42, bf16[1280,1536]{1,0:T(8,128)(2,1)} %copy-done.15, bf16[2,192,1536]{2,1,0:T(8,128)(2,1)} %bitcast.50, f32[1280,1]{1,0:T(8,128)} %copy-done.1, f32[1,1280]{1,0:T(1,128)} %copy-done.36), custom_call_target="tpu_custom_call" | custom-call | flops 12582912000 | bytes 3440640 | tf_op jit(solution)/shard_map/attend_back/pallas_call | solution.py:184
  435.4 6.3 %project_terms.1 = bf16[32,48,1152]{2,1,0:T(8,128)(2,1)S(1)} custom-call(bf16[1280,1536]{1,0:T(8,128)(2,1)S(1)} %copy-done.38, bf16[1280,576]{1,0:T(8,128)(2,1)S(1)} %copy-done.23, f32[1280,1]{1,0:T(8,128)S(1)} %copy-done.2), custom_call_target="tpu_custom_call" | custom-call | flops 3397386240 | bytes 8388608 | tf_op jit(solution)/shard_map/project_terms/pallas_call | solution.py:246
  444.5 2.6 multiply_reduce_fusion.1
  450.1 91.7 %last.1 = (bf16[144,1536]{1,0:T(8,128)(2,1)}, bf16[144,1536]{1,0:T(8,128)(2,1)}, f32[144,1536]{1,0:T(8,128)}, f32[144,1536]{1,0:T(8,128)}, f32[8,4,1,1152]{3,2,1...) custom-call(bf16[1280,768]{1,0:T(8,128)(2,1)} %copy-done.22, bf16[2,768,1536]{2,1,0:T(8,128)(2,1)} %bitcast.57, ...), custom_call_target="tpu_custom_call" | custom-call | tf_op jit(solution)/shard_map/last/pallas_call | solution.py:374
  543.1 2.5 fusion.13
  550.0 2.2 broadcast_select_fusion.1
  553.4 25.7 %finish.1 = (bf16[96,6144]{1,0:T(8,128)(2,1)S(1)}, bf16[96,4608]{1,0:T(8,128)(2,1)S(1)}) custom-call(bf16[8,96,768]{2,1,0:T(8,128)(2,1)S(1)} %bitcast.52, bf16[8,48,1152]{2,1,0:T(8,128)(2,1)S(1)} %bitcast.54), custom_call_target="tpu_custom_call" | custom-call | tf_op jit(solution)/shard_map/finish/pallas_call | solution.py:374
  (186 shorter events, 61.9 us)
Async XLA Ops:
  7.2 37.0 %copy-start.49 = (s32[4]{0:T(128)S(1)}, s32[4]{0:T(128)}, u32[]{:S(2)}) copy-start(s32[4]{0:T(128)} %param.11) | copy-start | bytes 52
  7.2 38.5 %copy-start.47 = (bf16[4,1536]{1,0:T(4,128)(2,1)S(1)}, bf16[4,1536]{1,0:T(4,128)(2,1)}, u32[]{:S(2)}) copy-start(bf16[4,1536]{1,0:T(4,128)(2,1)} %param.10) | copy-start | bytes 36868
  7.2 35.6 %all-gather.9.cloned.1.call-start = ((), (), s32[]{:S(2)}) async-start(), calls=%async_computation.8 | async-start | bytes 1474560 | tf_op jit(solution)/shard_map/all_gather | solution.py:1073
  7.9 135.3 %all-gather.11.cloned.1.call-start = ((), (), s32[]{:S(2)}) async-start(), calls=%async_computation.9 | async-start | bytes 4423680 | tf_op jit(solution)/shard_map/all_gather | solution.py:1063
  42.8 8.4 %copy-start.34 = (bf16[144,1536]{1,0:T(8,128)(2,1)S(1)}, bf16[144,1536]{1,0:T(8,128)(2,1)}, u32[]{:S(2)}) copy-start(bf16[144,1536]{1,0:T(8,128)(2,1)} %grads.1) | copy-start | bytes 1327108
  42.8 217.1 %all-gather.13.cloned.1.call-start = ((), (), s32[]{:S(2)}) async-start(), calls=%async_computation.10 | async-start | bytes 5898240 | tf_op jit(solution)/shard_map/all_gather | solution.py:1063
  43.5 253.3 %all-gather.15.cloned.1.call-start = ((), (), s32[]{:S(2)}) async-start(), calls=%async_computation.11 | async-start | bytes 5898240 | tf_op jit(solution)/shard_map/all_gather | solution.py:1093
  44.1 387.7 %reduce-scatter.5.cloned.1.call-start = ((), (), s32[]{:S(2)}) async-start(), calls=%async_computation.4 | async-start | bytes 5898240 | tf_op jit(solution)/shard_map/reduce_scatter | solution.py:1068
  49.6 279.3 %copy-start.24 = (f32[160,1]{1,0:T(8,128)}, f32[160,1]{1,0:T(8,128)S(1)}, u32[]{:S(2)}) copy-start(f32[160,1]{1,0:T(8,128)S(1)} %convert_element_type.71.text.refs_11_) | copy-start | bytes 1924
  50.3 111.7 %copy-start.36 = (f32[1,1280]{1,0:T(1,128)}, f32[1,1280]{1,0:T(1,128)S(1)}, u32[]{:S(2)}) copy-start(f32[1,1280]{1,0:T(1,128)S(1)} %and_select_fusion.bias_ref) | copy-start | bytes 15364
  51.1 277.8 %copy-start.1 = (f32[1280,1]{1,0:T(8,128)}, f32[1280,1]{1,0:T(8,128)S(1)}, u32[]{:S(2)}) copy-start(f32[1280,1]{1,0:T(8,128)S(1)} %fusion.text.window_text.refs_4_) | copy-start | bytes 15364
  137.1 43.1 %copy-start.13 = (bf16[160,1536]{1,0:T(8,128)(2,1)}, bf16[160,1536]{1,0:T(8,128)(2,1)S(1)}, u32[]{:S(2)}) copy-start(bf16[160,1536]{1,0:T(8,128)(2,1)S(1)} %pad_maximum_fusion.1.tokens.refs_5_) | copy-start | bytes 1474564
  137.7 9.2 %copy-start.35 = (f32[2,1536]{1,0:T(2,128)}, f32[2,1536]{1,0:T(2,128)S(1)}, u32[]{:S(2)}) copy-start(f32[2,1536]{1,0:T(2,128)S(1)} %get-tuple-element.122.scale.refs_10_) | copy-start | bytes 36868
  146.9 13.1 %copy-start = (bf16[32,96,576]{2,1,0:T(8,128)(2,1)}, bf16[32,96,576]{2,1,0:T(8,128)(2,1)S(1)}, u32[]{:S(2)}) copy-start(bf16[32,96,576]{2,1,0:T(8,128)(2,1)S(1)} %pad_maximum_fusion) | copy-start | bytes 10616836
  162.0 18.2 %copy-start.42 = (bf16[1280,576]{1,0:T(8,128)(2,1)}, bf16[1280,576]{1,0:T(8,128)(2,1)S(1)}, u32[]{:S(2)}) copy-start(bf16[1280,576]{1,0:T(8,128)(2,1)S(1)} %get-tuple-element.58.projected) | copy-start | bytes 4423684
  162.0 18.2 %copy-start.27 = (bf16[2,2,96,1536]{3,2,1,0:T(8,128)(2,1)S(1)}, bf16[2,2,96,1536]{3,2,1,0:T(8,128)(2,1)}, u32[]{:S(2)}) copy-start(bf16[2,2,96,1536]{3,2,1,0:T(8,128)(2,1)} %copy-done.26) | copy-start | bytes 3538948
  262.0 11.4 %copy-start.4 = (bf16[1280,1536]{1,0:T(8,128)(2,1)S(1)}, bf16[1280,1536]{1,0:T(8,128)(2,1)}, u32[]{:S(2)}) copy-start(bf16[1280,1536]{1,0:T(8,128)(2,1)} %get-tuple-element.64.grads.rows) | copy-start | bytes 11796484
  280.8 264.7 %reduce-scatter.9.cloned.1.call-start = ((), (), s32[]{:S(2)}) async-start(), calls=%async_computation.6 | async-start | bytes 5898240 | tf_op jit(solution)/shard_map/reduce_scatter | solution.py:1068
  301.1 15.5 %copy-start.41 = (bf16[1280,1536]{1,0:T(8,128)(2,1)S(1)}, bf16[1280,1536]{1,0:T(8,128)(2,1)}, u32[]{:S(2)}) copy-start(bf16[1280,1536]{1,0:T(8,128)(2,1)} %copy-done.39) | copy-start | bytes 11796484
  325.4 226.8 %reduce-scatter.7.cloned.1.call-start = ((), (), s32[]{:S(2)}) async-start(), calls=%async_computation.5 | async-start | bytes 4423680 | tf_op jit(solution)/shard_map/reduce_scatter | solution.py:1068
  327.4 69.0 %copy-start.14 = (bf16[160,1536]{1,0:T(8,128)(2,1)}, bf16[160,1536]{1,0:T(8,128)(2,1)S(1)}, u32[]{:S(2)}) copy-start(bf16[160,1536]{1,0:T(8,128)(2,1)S(1)} %pad_maximum_fusion.2.grad.refs_7_) | copy-start | bytes 1474564
  328.9 115.5 %copy-start.3 = (f32[160,1536]{1,0:T(8,128)}, f32[160,1536]{1,0:T(8,128)S(1)}, u32[]{:S(2)}) copy-start(f32[160,1536]{1,0:T(8,128)S(1)} %get-tuple-element.111.middle.refs_6_) | copy-start | bytes 2949124
  400.4 31.4 %copy-start.2 = (f32[1280,1]{1,0:T(8,128)S(1)}, f32[1280,1]{1,0:T(8,128)}, u32[]{:S(2)}) copy-start(f32[1280,1]{1,0:T(8,128)} %copy-done.1) | copy-start | bytes 15364
  443.4 138.8 %reduce-scatter.11.cloned.1.call-start = ((), (), s32[]{:S(2)}) async-start(), calls=%async_computation.7 | async-start | bytes 1474560 | tf_op jit(solution)/shard_map/reduce_scatter | solution.py:1068
  (34 other events, 98.9 us)
Sparse Core Ops, SparseCore 0:
  9.6 33.1 all-gather.8
  44.3 73.4 all-gather.10
  119.4 88.0 all-gather.12
  209.0 87.8 all-gather.14
  299.0 83.7 reduce-scatter.4
  385.0 85.7 reduce-scatter.8
  473.1 71.3 reduce-scatter.6
  552.4 27.7 reduce-scatter.10

commit v9 on v8

--- a/solution.py
+++ b/solution.py
@@ -114,8 +114,8 @@
     out_ref[...] = jnp.concatenate(outs, axis=1).astype(BF16)
 
 
-def block_rows(rows):
-    return 128
+def block_rows(rows, most):
+    return most if rows % most == 0 else 128
 
 
 def constant(shape):
@@ -124,7 +124,7 @@
 
 def attend(plan, projected, bias):
     rows, cols = projected.shape[0], projected.shape[1] // 3
-    block = block_rows(rows)
+    block = block_rows(rows, 128)
     return pl.pallas_call(
         functools.partial(attend_kernel, plan.heads, block),
         out_shape=jax.ShapeDtypeStruct((rows, cols), BF16),
@@ -180,7 +180,7 @@
 
 def attend_back(plan, projected, grad_merged, merge_pair, text, bias):
     rows, cols = projected.shape[0], projected.shape[1] // 3
-    block = block_rows(rows)
+    block = block_rows(rows, 256)
     return pl.pallas_call(
         functools.partial(attend_back_kernel, plan.heads, rows // block, block),
         out_shape=jax.ShapeDtypeStruct(projected.shape, BF16),
@@ -438,10 +438,6 @@
     lax.fori_loop(0, plan.width // chunk, step, 0)
 
 
-def scatter_sum(*args):
-    return scatter_start(*args)()
-
-
 def scatter_start(plan, seq, rank, rows, pair, text, dims, away, near, going, coming,
                   pair_send, pair_recv, far_send, far_recv):
     half = plan.group // 2
@@ -482,16 +478,24 @@
 
     lax.fori_loop(0, 2 * half, turn, 0)
 
-    def result():
-        total = away[half]
+    def result(use):
         for step in range(1, half):
             far_copy(step).wait_recv()
-            total = total + coming[step - 1].astype(F32)
+        size = 32 if plan.own % 32 == 0 else 16
+
+        def some(i, carry):
+            place = pl.ds(pl.multiple_of(i * size, size), size)
+            total = away[half, place]
+            for step in range(1, half):
+                total = total + coming[step - 1, place].astype(F32)
+            use(place, total)
+            return carry
+
+        lax.fori_loop(0, plan.own // size, some, 0)
         for step in range(half):
             pair_copy(step).wait_send()
         for step in range(1, half):
             far_copy(step).wait_send()
-        return total
 
     return result
 
@@ -787,12 +791,16 @@
 def middle_kernel(plan, rows, pair, window_text, tokens, gate_a, scale_b, shift_b, text, merged, window, own, *scratch):
     seq, rank = here(plan)
     meet(group_devices(plan, seq, rank))
-    total = scatter_sum(plan, seq, rank, rows, pair, window_text, PLAIN, *scratch[:SUM_SCRATCH])
-    merged[...] = total
-    mask = text[...]
-    middle = tokens[...].astype(F32) + pick_rows(gate_a[...], mask) * total
-    normed, _ = norm_rows(middle)
-    own[...] = (normed * (1.0 + pick_rows(scale_b[...], mask)) + pick_rows(shift_b[...], mask)).astype(BF16)
+    result = scatter_start(plan, seq, rank, rows, pair, window_text, PLAIN, *scratch[:SUM_SCRATCH])
+
+    def use(place, total):
+        merged[place] = total
+        mask = text[place]
+        middle = tokens[place].astype(F32) + pick_rows(gate_a[...], mask) * total
+        normed, _ = norm_rows(middle)
+        own[place] = (normed * (1.0 + pick_rows(scale_b[...], mask)) + pick_rows(shift_b[...], mask)).astype(BF16)
+
+    result(use)
     share_rows(plan, seq, rank, own_parts(plan, own), window, *scratch[SUM_SCRATCH:])
 
 
@@ -818,16 +826,20 @@
 def back_kernel(plan, rows, pair, window_text, grad, middle, gate_a, scale_b, text, grad_hidden, grad_middle, window, own, *scratch):
     seq, rank = here(plan)
     meet(group_devices(plan, seq, rank))
-    total = scatter_sum(plan, seq, rank, rows, pair, window_text, CONTRACT_LAST, *scratch[:SUM_SCRATCH])
-    grad_hidden[...] = total
-    mask = text[...]
-    normed, inv = norm_rows(middle[...])
-    inner = total * (1.0 + pick_rows(scale_b[...], mask))
-    mean_grad = jnp.mean(inner, axis=1, keepdims=True)
-    mean_cross = jnp.mean(inner * normed, axis=1, keepdims=True)
-    result = grad[...].astype(F32) + inv * (inner - mean_grad - normed * mean_cross)
-    grad_middle[...] = result
-    own[...] = (pick_rows(gate_a[...], mask) * result).astype(BF16)
+    result = scatter_start(plan, seq, rank, rows, pair, window_text, CONTRACT_LAST, *scratch[:SUM_SCRATCH])
+
+    def use(place, total):
+        grad_hidden[place] = total
+        mask = text[place]
+        normed, inv = norm_rows(middle[place])
+        inner = total * (1.0 + pick_rows(scale_b[...], mask))
+        mean_grad = jnp.mean(inner, axis=1, keepdims=True)
+        mean_cross = jnp.mean(inner * normed, axis=1, keepdims=True)
+        back = grad[place].astype(F32) + inv * (inner - mean_grad - normed * mean_cross)
+        grad_middle[place] = back
+        own[place] = (pick_rows(gate_a[...], mask) * back).astype(BF16)
+
+    result(use)
     share_rows(plan, seq, rank, own_parts(plan, own), window, *scratch[SUM_SCRATCH:])
 
 
@@ -902,22 +914,33 @@
             copy.start()
             swaps.append(copy)
             at.term_out[2 * j + core] = at.term[j, core]
-    text = at.text[...]
-    streams = (at.masks[:, 0:1], at.masks[:, 1:2])
     width = plan.width
-
-    lowered = low_sum()
-    at.layer_own[...] = (at.middle[...] + pick_rows(at.gate_b[...], text) * lowered).astype(BF16)
+    at.local[...] = jnp.zeros_like(at.local)
+    at.local[:, 2 * width : 5 * width] = at.rest[...]
+
+    def add(first, place, values):
+        masks = (at.masks[place, 0:1], at.masks[place, 1:2])
+        at.local[:, first * width : (first + 1) * width] += stream_sums(values, masks)
+
+    def use_low(place, lowered):
+        at.layer_own[place] = (at.middle[place] + pick_rows(at.gate_b[...], at.text[place]) * lowered).astype(BF16)
+        add(5, place, at.grad[place].astype(F32) * lowered)
+
+    low_sum(use_low)
     layer_edges = (at.layer_own, plan.rows_dev, at.layer_extra, at.l_send, at.l_recv)
     start_edges(plan, seq, rank, *layer_edges)
-    at.local[:, 5 * width :] = stream_sums(at.grad[...].astype(F32) * lowered, streams)
-    at.local[:, 2 * width : 5 * width] = at.rest[...]
     at.layer[...] = at.layer_own[pl.ds(0, plan.rows_dev)]
 
-    total = back_sum()
-    normed, inv = norm_rows(at.tokens[...].astype(F32))
-    at.local[:, :width] = stream_sums(total, streams)
-    at.local[:, width : 2 * width] = stream_sums(total * normed, streams)
+    def use_back(place, total):
+        normed, inv = norm_rows(at.tokens[place].astype(F32))
+        add(0, place, total)
+        add(1, place, total * normed)
+        inner = total * (1.0 + pick_rows(at.scale_a[...], at.text[place]))
+        mean_grad = jnp.mean(inner, axis=1, keepdims=True)
+        mean_cross = jnp.mean(inner * normed, axis=1, keepdims=True)
+        at.token_own[place] = at.grad_middle[place] + inv * (inner - mean_grad - normed * mean_cross)
+
+    back_sum(use_back)
     cols = 6 * width // plan.group
 
     def chunk(index):
@@ -931,10 +954,6 @@
         )
         copy.start()
         hops.append(copy)
-    inner = total * (1.0 + pick_rows(at.scale_a[...], text))
-    mean_grad = jnp.mean(inner, axis=1, keepdims=True)
-    mean_cross = jnp.mean(inner * normed, axis=1, keepdims=True)
-    at.token_own[...] = at.grad_middle[...] + inv * (inner - mean_grad - normed * mean_cross)
     token_edges = (at.token_own, plan.rows_dev, at.token_extra, at.e_send, at.e_recv)
     start_edges(plan, seq, rank, *token_edges)
     for copy in hops:
@@ -1173,7 +1192,7 @@
     down_term, grad_lowered = lax.optimization_barrier((down_term, grad_lowered))
     down_sum = over_sequences_sum(plan, down_term)
     (grad_upper,) = stream_rows(
-        plan, down_back_kernel, 128, units, True, "down_back", ((units, BF16),),
+        plan, down_back_kernel, block_rows(plan.rows, 256), units, True, "down_back", ((units, BF16),),
         grad_lowered, down_pair, window_text, upper,
     )
     up_term = weight_terms(plan, hidden_b, grad_upper, window_text, "up_terms")

time: 593 us -> 586 us (0.988)
  Pallas kernels: 472 us -> 463 us
    pallas_call x1, Pallas kernels: 31.4 us -> 24.9 us  [attend_back(): pl.pallas_call(functools.partial(attend_back_kernel, plan.heads, rows //...]
  transfers between devices with their start and end apart: 8 -> 8, of which waited for: 2 -> 4; matrix products, arithmetic and copies ran while one was open for 7% -> 7% of each run, Pallas kernels for 80% -> 79%
where the time goes in v9:
time: 586 us; the launch traced here: 585 us
  Pallas kernels  463 us (79%)
  local copies, waits for them, and re-layouts  51 us (9%)
  other arithmetic  26.3 us (4%)
  waiting for transfers between devices  24.4 us (4%)
  between operations  15.6 us (3%)
    pallas_call x6, Pallas kernels, call(): pl.pallas_call(kernel, out_shape=out_shape, in_specs=in_specs or [VMEM] *...  370 us
    unnamed x101, local copies, waits for them, and re-layouts  41 us
    pallas_call x3, Pallas kernels, stream_rows(): pl.pallas_call(functools.partial(kernel, plan, size), out_shape=shapes, i...  29.9 us
    pallas_call x1, Pallas kernels, attend_back(): pl.pallas_call(functools.partial(attend_back_kernel, plan.heads, rows //...  24.9 us
    pallas_call x4, Pallas kernels, weight_terms(): pl.pallas_call(functools.partial(terms_kernel, plan, fold, chunk), out_sh...  19.4 us
    pallas_call x1, Pallas kernels, attend(): pl.pallas_call(functools.partial(attend_kernel, plan.heads, block), out_s...  18.2 us
    all_gather x1, waiting for transfers between devices, down_slices(): lax.all_gather(weight, 'dev', axis=0, axis_index_groups=plan.rank_groups())  15.2 us
  transfers between devices with their start and end apart: 8, of which 4 were waited for; matrix products, arithmetic and copies ran while one was open for 7% of the time, Pallas kernels for 79%

profile of v9, /device:TPU:0, one launch (start us, length us, event | category | flops | bytes accessed | tf_op | source)
XLA Modules:
  0.0 585.0 jit_solution(12182486473863838457)
XLA Ops:
  10.4 28.9 %swap_in.1 = (bf16[8,48,1152]{2,1,0:T(8,128)(2,1)}, bf16[8,96,768]{2,1,0:T(8,128)(2,1)}) custom-call(bf16[96,4608]{1,0:T(8,128)(2,1)S(1)} %copy-done.31, bf16[96,6144]{1,0:T(8,128)(2,1)S(1)} %copy-done.28), custom_call_target="tpu_custom_call" | custom-call | tf_op jit(solution)/shard_map/swap_in/pallas_call | solution.py:374
  39.3 3.5 all-gather.9.cloned.1.call-done
  51.2 78.3 %entry.1 = (bf16[1280,1536]{1,0:T(8,128)(2,1)S(1)}, bf16[1280,1536]{1,0:T(8,128)(2,1)S(1)}, f32[8,2,9,128]{3,2,1,0:T(8,128)S(1)}, bf16[2,2,96,1536]{3,2,1,0:T(8,128)(2,1)S(1)}) custom-call(bf16[144,1536]{1,0:T(8,128)(2,1)S(1)} %copy-done.33, bf16[144,1536]{1,0:T(8,128)(2,1)S(1)} %copy-done.34, f32[8,4,9,128]{3,2,1,0:T(8,128)S(1)} %bitcast.53, ...), custom_call_target="tpu_custom_call" | custom-call | tf_op jit(solution)/shard_map/entry/pallas_call | solution.py:374
  137.7 5.5 multiply_convert_fusion
  143.3 3.3 fusion.10
  146.9 3.1 copy-done.9
  150.1 10.0 %project.3 = (bf16[1280,1536]{1,0:T(8,128)(2,1)S(1)}, bf16[1280,576]{1,0:T(8,128)(2,1)S(1)}) custom-call(bf16[1280,1536]{1,0:T(8,128)(2,1)S(1)} %copy-done.9, bf16[2,1536,576]{2,1,0:T(8,128)(2,1)S(1)} %bitcast.43, f32[1280,1]{1,0:T(8,128)S(1)} %fusion.text.window_text.refs_4_, f32[2,1536]{1,0:T(2,128)S(1)} %get-tuple-element.123.shift, ...), custom_call_target="tpu_custom_call" | custom-call | flops 2264924160 | bytes 16777216 | tf_op jit(solution)/shard_map/project/pallas_call | solution.py:311
  162.0 18.2 %attend.1.rows = bf16[1280,192]{1,0:T(8,128)(2,1)S(1)} custom-call(bf16[1280,576]{1,0:T(8,128)(2,1)S(1)} %get-tuple-element.58.projected, f32[1,1280]{1,0:T(1,128)S(1)} %and_select_fusion.bias_ref), custom_call_target="tpu_custom_call" | custom-call | flops 5033164800 | bytes 1966080 | tf_op jit(solution)/shard_map/attend/pallas_call | solution.py:128
  180.2 78.4 %middle.1 = (f32[160,1536]{1,0:T(8,128)S(1)}, bf16[1280,1536]{1,0:T(8,128)(2,1)S(1)}) custom-call(bf16[1280,192]{1,0:T(8,128)(2,1)S(1)} %attend.1.rows, bf16[2,192,1536]{2,1,0:T(8,128)(2,1)S(1)} %bitcast.51, f32[1280,1]{1,0:T(8,128)S(1)} %fusion.text.window_text.refs_4_, bf16[160,1536]{1,0:T(8,128)(2,1)S(1)} %pad_maximum_fusion.1.tokens.refs_5_, ...), custom_call_target="tpu_custom_call" | custom-call | tf_op jit(solution)/shard_map/middle/pallas_call | solution.py:374
  262.7 9.4 %up.3 = (f32[1280,768]{1,0:T(8,128)S(1)}, bf16[1280,768]{1,0:T(8,128)(2,1)S(1)}) custom-call(bf16[1280,1536]{1,0:T(8,128)(2,1)S(1)} %copy-done.40, bf16[2,1536,768]{2,1,0:T(8,128)(2,1)} %bitcast.58, f32[1280,1]{1,0:T(8,128)S(1)} %fusion.text.window_text.refs_4_), custom_call_target="tpu_custom_call" | custom-call | flops 3019898880 | bytes 16777216 | tf_op jit(solution)/shard_map/up/pallas_call | solution.py:311
  274.0 5.3 down_terms.1
  281.7 15.2 %all-gather.15.cloned.1.call-done = bf16[1536,1536]{1,0:T(8,128)(2,1)} async-done(((bf16[384,1536]{1,0:T(8,128)(2,1)}), bf16[1536,1536]{1,0:T(8,128)(2,1)}) %all-gather.15.cloned.1.call-update) | async-done | bytes 4718608 | tf_op jit(solution)/shard_map/all_gather | solution.py:1112
  301.1 10.5 %down_back.1.grads.rows = bf16[1280,768]{1,0:T(8,128)(2,1)S(1)} custom-call(bf16[1280,1536]{1,0:T(8,128)(2,1)S(1)} %copy-done.5, bf16[2,768,1536]{2,1,0:T(8,128)(2,1)} %bitcast.56, f32[1280,1]{1,0:T(8,128)S(1)} %fusion.text.window_text.refs_4_, f32[1280,768]{1,0:T(8,128)S(1)} %copy-done.20), custom_call_target="tpu_custom_call" | custom-call | flops 3019898880 | bytes 16777216 | tf_op jit(solution)/shard_map/down_back/pallas_call | solution.py:311
  311.6 6.5 %up_terms.1 = bf16[2,1536,768]{2,1,0:T(8,128)(2,1)S(1)} custom-call(bf16[1280,1536]{1,0:T(8,128)(2,1)S(1)} %copy-done.41, bf16[1280,768]{1,0:T(8,128)(2,1)S(1)} %down_back.1.grads.rows, f32[1280,1]{1,0:T(8,128)S(1)} %fusion.text.window_text.refs_4_), custom_call_target="tpu_custom_call" | custom-call | flops 4529848320 | bytes 8388608 | tf_op jit(solution)/shard_map/up_terms/pallas_call | solution.py:246
  318.2 2.2 copy-done.11
  325.8 66.3 %back.1 = (f32[160,1536]{1,0:T(8,128)S(1)}, f32[160,1536]{1,0:T(8,128)S(1)}, bf16[1280,1536]{1,0:T(8,128)(2,1)S(1)}) custom-call(bf16[1280,768]{1,0:T(8,128)(2,1)S(1)} %copy-done.7, bf16[2,1536,768]{2,1,0:T(8,128)(2,1)} %bitcast.59, f32[1280,1]{1,0:T(8,128)S(1)} %fusion.text.window_text.refs_4_, bf16[160,1536]{1,0:T(8,128)(2,1)S(1)} %pad_maximum_fusion.2.grad.refs_7_, ...), custom_call_target="tpu_custom_call" | custom-call | tf_op jit(solution)/shard_map/back/pallas_call | solution.py:374
  396.1 24.9 %attend_back.1.grads.refs_2_ = bf16[1280,576]{1,0:T(8,128)(2,1)} custom-call(bf16[1280,576]{1,0:T(8,128)(2,1)} %copy-done.42, bf16[1280,1536]{1,0:T(8,128)(2,1)} %copy-done.15, bf16[2,192,1536]{2,1,0:T(8,128)(2,1)} %bitcast.50, f32[1280,1]{1,0:T(8,128)} %copy-done.1, f32[1,1280]{1,0:T(1,128)} %copy-done.36), custom_call_target="tpu_custom_call" | custom-call | flops 12582912000 | bytes 3440640 | tf_op jit(solution)/shard_map/attend_back/pallas_call | solution.py:184
  422.5 2.2 copy-done.38
  424.7 6.3 %project_terms.1 = bf16[32,48,1152]{2,1,0:T(8,128)(2,1)S(1)} custom-call(bf16[1280,1536]{1,0:T(8,128)(2,1)S(1)} %copy-done.38, bf16[1280,576]{1,0:T(8,128)(2,1)S(1)} %copy-done.23, f32[1280,1]{1,0:T(8,128)S(1)} %copy-done.2), custom_call_target="tpu_custom_call" | custom-call | flops 3397386240 | bytes 8388608 | tf_op jit(solution)/shard_map/project_terms/pallas_call | solution.py:246
  433.8 2.6 multiply_reduce_fusion.1
  439.5 92.5 %last.1 = (bf16[144,1536]{1,0:T(8,128)(2,1)}, bf16[144,1536]{1,0:T(8,128)(2,1)}, f32[144,1536]{1,0:T(8,128)}, f32[144,1536]{1,0:T(8,128)}, f32[8,4,1,1152]{3,2,1...) custom-call(bf16[1280,768]{1,0:T(8,128)(2,1)} %copy-done.22, bf16[2,768,1536]{2,1,0:T(8,128)(2,1)} %bitcast.57, ...), custom_call_target="tpu_custom_call" | custom-call | tf_op jit(solution)/shard_map/last/pallas_call | solution.py:374
  533.2 2.5 fusion.13
  540.1 2.2 broadcast_select_fusion.1
  545.6 26.0 %finish.1 = (bf16[96,6144]{1,0:T(8,128)(2,1)S(1)}, bf16[96,4608]{1,0:T(8,128)(2,1)S(1)}) custom-call(bf16[8,96,768]{2,1,0:T(8,128)(2,1)S(1)} %bitcast.52, bf16[8,48,1152]{2,1,0:T(8,128)(2,1)S(1)} %bitcast.54), custom_call_target="tpu_custom_call" | custom-call | tf_op jit(solution)/shard_map/finish/pallas_call | solution.py:374
  (186 shorter events, 65.7 us)
Async XLA Ops:
  7.2 37.0 %copy-start.49 = (s32[4]{0:T(128)S(1)}, s32[4]{0:T(128)}, u32[]{:S(2)}) copy-start(s32[4]{0:T(128)} %param.11) | copy-start | bytes 52
  7.2 38.5 %copy-start.47 = (bf16[4,1536]{1,0:T(4,128)(2,1)S(1)}, bf16[4,1536]{1,0:T(4,128)(2,1)}, u32[]{:S(2)}) copy-start(bf16[4,1536]{1,0:T(4,128)(2,1)} %param.10) | copy-start | bytes 36868
  7.2 35.6 %all-gather.9.cloned.1.call-start = ((), (), s32[]{:S(2)}) async-start(), calls=%async_computation.8 | async-start | bytes 1474560 | tf_op jit(solution)/shard_map/all_gather | solution.py:1092
  7.9 135.3 %all-gather.11.cloned.1.call-start = ((), (), s32[]{:S(2)}) async-start(), calls=%async_computation.9 | async-start | bytes 4423680 | tf_op jit(solution)/shard_map/all_gather | solution.py:1082
  42.8 217.7 %all-gather.13.cloned.1.call-start = ((), (), s32[]{:S(2)}) async-start(), calls=%async_computation.10 | async-start | bytes 5898240 | tf_op jit(solution)/shard_map/all_gather | solution.py:1082
  43.5 253.3 %all-gather.15.cloned.1.call-start = ((), (), s32[]{:S(2)}) async-start(), calls=%async_computation.11 | async-start | bytes 5898240 | tf_op jit(solution)/shard_map/all_gather | solution.py:1112
  44.1 377.0 %reduce-scatter.5.cloned.1.call-start = ((), (), s32[]{:S(2)}) async-start(), calls=%async_computation.4 | async-start | bytes 5898240 | tf_op jit(solution)/shard_map/reduce_scatter | solution.py:1087
  49.6 274.3 %copy-start.24 = (f32[160,1]{1,0:T(8,128)}, f32[160,1]{1,0:T(8,128)S(1)}, u32[]{:S(2)}) copy-start(f32[160,1]{1,0:T(8,128)S(1)} %convert_element_type.71.text.refs_11_) | copy-start | bytes 1924
  50.3 111.7 %copy-start.36 = (f32[1,1280]{1,0:T(1,128)}, f32[1,1280]{1,0:T(1,128)S(1)}, u32[]{:S(2)}) copy-start(f32[1,1280]{1,0:T(1,128)S(1)} %and_select_fusion.bias_ref) | copy-start | bytes 15364
  51.1 272.8 %copy-start.1 = (f32[1280,1]{1,0:T(8,128)}, f32[1280,1]{1,0:T(8,128)S(1)}, u32[]{:S(2)}) copy-start(f32[1280,1]{1,0:T(8,128)S(1)} %fusion.text.window_text.refs_4_) | copy-start | bytes 15364
  137.1 43.1 %copy-start.13 = (bf16[160,1536]{1,0:T(8,128)(2,1)}, bf16[160,1536]{1,0:T(8,128)(2,1)S(1)}, u32[]{:S(2)}) copy-start(bf16[160,1536]{1,0:T(8,128)(2,1)S(1)} %pad_maximum_fusion.1.tokens.refs_5_) | copy-start | bytes 1474564
  137.7 9.2 %copy-start.35 = (f32[2,1536]{1,0:T(2,128)}, f32[2,1536]{1,0:T(2,128)S(1)}, u32[]{:S(2)}) copy-start(f32[2,1536]{1,0:T(2,128)S(1)} %get-tuple-element.122.scale.refs_10_) | copy-start | bytes 36868
  146.9 13.1 %copy-start = (bf16[32,96,576]{2,1,0:T(8,128)(2,1)}, bf16[32,96,576]{2,1,0:T(8,128)(2,1)S(1)}, u32[]{:S(2)}) copy-start(bf16[32,96,576]{2,1,0:T(8,128)(2,1)S(1)} %pad_maximum_fusion) | copy-start | bytes 10616836
  162.0 18.2 %copy-start.42 = (bf16[1280,576]{1,0:T(8,128)(2,1)}, bf16[1280,576]{1,0:T(8,128)(2,1)S(1)}, u32[]{:S(2)}) copy-start(bf16[1280,576]{1,0:T(8,128)(2,1)S(1)} %get-tuple-element.58.projected) | copy-start | bytes 4423684
  162.0 18.2 %copy-start.27 = (bf16[2,2,96,1536]{3,2,1,0:T(8,128)(2,1)S(1)}, bf16[2,2,96,1536]{3,2,1,0:T(8,128)(2,1)}, u32[]{:S(2)}) copy-start(bf16[2,2,96,1536]{3,2,1,0:T(8,128)(2,1)} %copy-done.26) | copy-start | bytes 3538948
  262.7 11.4 %copy-start.4 = (bf16[1280,1536]{1,0:T(8,128)(2,1)S(1)}, bf16[1280,1536]{1,0:T(8,128)(2,1)}, u32[]{:S(2)}) copy-start(bf16[1280,1536]{1,0:T(8,128)(2,1)} %get-tuple-element.64.grads.rows) | copy-start | bytes 11796484
  281.5 254.2 %reduce-scatter.9.cloned.1.call-start = ((), (), s32[]{:S(2)}) async-start(), calls=%async_computation.6 | async-start | bytes 5898240 | tf_op jit(solution)/shard_map/reduce_scatter | solution.py:1087
  301.1 10.5 %copy-start.41 = (bf16[1280,1536]{1,0:T(8,128)(2,1)S(1)}, bf16[1280,1536]{1,0:T(8,128)(2,1)}, u32[]{:S(2)}) copy-start(bf16[1280,1536]{1,0:T(8,128)(2,1)} %copy-done.39) | copy-start | bytes 11796484
  320.4 224.0 %reduce-scatter.7.cloned.1.call-start = ((), (), s32[]{:S(2)}) async-start(), calls=%async_computation.5 | async-start | bytes 4423680 | tf_op jit(solution)/shard_map/reduce_scatter | solution.py:1087
  322.4 69.8 %copy-start.14 = (bf16[160,1536]{1,0:T(8,128)(2,1)}, bf16[160,1536]{1,0:T(8,128)(2,1)S(1)}, u32[]{:S(2)}) copy-start(bf16[160,1536]{1,0:T(8,128)(2,1)S(1)} %pad_maximum_fusion.2.grad.refs_7_) | copy-start | bytes 1474564
  323.9 109.9 %copy-start.3 = (f32[160,1536]{1,0:T(8,128)}, f32[160,1536]{1,0:T(8,128)S(1)}, u32[]{:S(2)}) copy-start(f32[160,1536]{1,0:T(8,128)S(1)} %get-tuple-element.111.middle.refs_6_) | copy-start | bytes 2949124
  396.1 24.9 %copy-start.2 = (f32[1280,1]{1,0:T(8,128)S(1)}, f32[1280,1]{1,0:T(8,128)}, u32[]{:S(2)}) copy-start(f32[1280,1]{1,0:T(8,128)} %copy-done.1) | copy-start | bytes 15364
  432.8 143.6 %reduce-scatter.11.cloned.1.call-start = ((), (), s32[]{:S(2)}) async-start(), calls=%async_computation.7 | async-start | bytes 1474560 | tf_op jit(solution)/shard_map/reduce_scatter | solution.py:1087
  535.8 8.7 %copy-start.29 = (bf16[1,8,96,768]{3,2,1,0:T(8,128)(2,1)S(1)}, bf16[1,8,96,768]{3,2,1,0:T(8,128)(2,1)}, u32[]{:S(2)}) copy-start(bf16[1,8,96,768]{3,2,1,0:T(8,128)(2,1)} %reduce-scatter.9.cloned.1.call-done) | copy-start | bytes 3538948
  (34 other events, 100.7 us)
Sparse Core Ops, SparseCore 0:
  9.6 33.1 all-gather.8
  44.3 73.4 all-gather.10
  119.4 88.0 all-gather.12
  209.0 87.8 all-gather.14
  299.0 83.6 reduce-scatter.4
  384.9 85.7 reduce-scatter.8
  473.1 71.3 reduce-scatter.6
  546.7 29.5 reduce-scatter.10

commit v10 on v9

--- a/solution.py
+++ b/solution.py
@@ -747,11 +747,58 @@
             out[:, c : c + share] = piece[:, i * share : (i + 1) * share]
 
 
-def finish_kernel(plan, up, project, up_out, project_out, up_got, project_got, u_send, u_recv, p_send, p_recv):
+def line_sum(plan, seq, rank, term, out, up_in, up_out, down_in, down_out, up_send, up_recv, down_send, down_recv):
+    count = plan.sequences
+
+    def hop(source, target, send, recv, owner, to):
+        return remote(source.at[owner], target.at[owner], send.at[owner], recv.at[owner], plan.device_of(to, rank))
+
+    above, below = lax.rem(seq + 1, count), lax.rem(seq + count - 1, count)
+    ways = [
+        (list(range(count - 1, 0, -1)), above, below, up_in, up_out, up_send, up_recv, lambda owner: seq < owner, seq == 0),
+        (list(range(count - 1)), below, above, down_in, down_out, down_send, down_recv, lambda owner: seq > owner,
+         seq == count - 1),
+    ]
+    for turn in range(count - 1):
+        for owners, to, back, came, goes, send, recv, mine, first in ways:
+            owner = owners[turn]
+
+            @pl.when(mine(owner) & first)
+            def _():
+                hop(term, came, send, recv, owner, to).start()
+
+            @pl.when(mine(owner) & jnp.logical_not(first))
+            def _():
+                hop(goes, came, send, recv, owner, back).wait_recv()
+                goes[owner] = (term[owner].astype(F32) + came[owner].astype(F32)).astype(BF16)
+                hop(goes, came, send, recv, owner, to).start()
+
+    out[...] = term[seq].astype(F32)
+    for owners, to, back, came, goes, send, recv, mine, first in ways:
+        for owner in owners:
+            @pl.when(seq == owner)
+            def _():
+                hop(goes, came, send, recv, owner, back).wait_recv()
+                out[...] += came[owner].astype(F32)
+
+            @pl.when(mine(owner))
+            def _():
+                hop(goes, came, send, recv, owner, to).wait_send()
+
+
+def finish_kernel(plan, up, project, *refs):
+    if plan.chip_heads:
+        term, up_out, project_out, merge_out, *refs = refs
+        *refs, line = refs[:6] + [refs[6:]]
+    else:
+        up_out, project_out, *refs = refs
+    up_got, project_got, u_send, u_recv, p_send, p_recv = refs
     seq, rank = here(plan)
-    meet(group_devices(plan, seq, rank))
+    meet(group_devices(plan, seq, rank) + column_devices(plan, seq, rank))
     ups = start_swap(plan, seq, rank, up, up_got, u_send, u_recv)
     projects = start_swap(plan, seq, rank, project, project_got, p_send, p_recv)
+    if plan.chip_heads:
+        line_sum(plan, seq, rank, term, merge_out, *line)
     for copy in ups:
         copy.wait()
     place_columns(plan, up_got, up_out, lambda p, r: up_columns(p, r, up_out.shape[1]), False)
@@ -760,21 +807,23 @@
     place_columns(plan, project_got, project_out, project_columns, True)
 
 
-def finish(plan, up, project):
+def finish(plan, up, project, term):
     dma = pltpu.SemaphoreType.DMA
     rows = up.shape[1]
-    up_grad, project_grad = call(
-        functools.partial(finish_kernel, plan),
-        "finish",
-        6,
-        (
-            jax.ShapeDtypeStruct((rows, plan.group * up.shape[2]), BF16),
-            jax.ShapeDtypeStruct((rows, plan.group * project.shape[2] // 2), BF16),
-        ),
-        [pltpu.VMEM(up.shape, BF16), pltpu.VMEM(project.shape, BF16)] + [dma((plan.group,))] * 4,
-        (up, project),
-    )
-    return up_grad.astype(F32), project_grad.astype(F32)
+    shapes = (
+        jax.ShapeDtypeStruct((rows, plan.group * up.shape[2]), BF16),
+        jax.ShapeDtypeStruct((rows, plan.group * project.shape[2] // 2), BF16),
+    )
+    operands = (up, project)
+    scratch = [pltpu.VMEM(up.shape, BF16), pltpu.VMEM(project.shape, BF16)] + [dma((plan.group,))] * 4
+    if plan.chip_heads:
+        shapes += (jax.ShapeDtypeStruct(term.shape[1:], F32),)
+        operands += (term,)
+        scratch += [pltpu.VMEM(term.shape, BF16)] * 4 + [dma((plan.sequences,))] * 4
+    up_grad, project_grad, *merge_grad = call(
+        functools.partial(finish_kernel, plan), "finish", 6, shapes, scratch, operands
+    )
+    return up_grad.astype(F32), project_grad.astype(F32), merge_grad
 
 
 def pick_rows(table, text):
@@ -1098,8 +1147,6 @@
 
 
 def merge_sum(plan, term, rank):
-    if plan.chip_heads:
-        return over_sequences_sum(plan, term)
     half = plan.group // 2
     _, share, cols = term.shape
     mine = [jnp.where(lax.rem(rank, 2) == k, term, jnp.zeros((), BF16)) for k in range(2)]
@@ -1252,8 +1299,8 @@
         (got.term, project_sum, modulation_grad, down_grad, layer_out, tokens_grad, conditioning_grad)
     )
     modulation_grad, down_grad, layer_out, tokens_grad, conditioning_grad = done
-    merge_grad = merge_sum(plan, merge_out, rank).reshape(merge_weight.shape).astype(F32)
-    up_grad, project_grad = finish(plan, up_sum, project_sum)
+    up_grad, project_grad, merge_grad = finish(plan, up_sum, project_sum, merge_out)
+    merge_grad = merge_grad[0] if merge_grad else merge_sum(plan, merge_out, rank).astype(F32)
     return (
         layer_out,
         tokens_grad,

time: 586 us -> 592 us (1.010)
  Pallas kernels: 463 us -> 471 us
    pallas_call x6, Pallas kernels: 370 us -> 379 us  [call(): pl.pallas_call(kernel, out_shape=out_shape, in_specs=in_specs or [VMEM] *...]
    unnamed x101 -> x106, local copies, waits for them, and re-layouts: 41 us -> 41.9 us
  transfers between devices with their start and end apart: 8 -> 7, of which waited for: 4 -> 3; matrix products, arithmetic and copies ran while one was open for 7% -> 6% of each run, Pallas kernels for 79% -> 74%
where the time goes in v10:
time: 592 us; the launch traced here: 591 us
  Pallas kernels  471 us (80%)
  local copies, waits for them, and re-layouts  52.4 us (9%)
  other arithmetic  25.1 us (4%)
  waiting for transfers between devices  21.6 us (4%)
  between operations  15.6 us (3%)
    pallas_call x6, Pallas kernels, call(): pl.pallas_call(kernel, out_shape=out_shape, in_specs=in_specs or [VMEM] *...  379 us
    unnamed x106, local copies, waits for them, and re-layouts  41.9 us
    pallas_call x3, Pallas kernels, stream_rows(): pl.pallas_call(functools.partial(kernel, plan, size), out_shape=shapes, i...  29.8 us
    pallas_call x1, Pallas kernels, attend_back(): pl.pallas_call(functools.partial(attend_back_kernel, plan.heads, rows //...  24.9 us
    pallas_call x4, Pallas kernels, weight_terms(): pl.pallas_call(functools.partial(terms_kernel, plan, fold, chunk), out_sh...  19.4 us
    pallas_call x1, Pallas kernels, attend(): pl.pallas_call(functools.partial(attend_kernel, plan.heads, block), out_s...  18.2 us
    all_gather x1, waiting for transfers between devices, down_slices(): lax.all_gather(weight, 'dev', axis=0, axis_index_groups=plan.rank_groups())  15.1 us
  transfers between devices with their start and end apart: 7, of which 3 were waited for; matrix products, arithmetic and copies ran while one was open for 6% of the time, Pallas kernels for 74%

profile of v10, /device:TPU:0, one launch (start us, length us, event | category | flops | bytes accessed | tf_op | source)
XLA Modules:
  0.0 590.6 jit_solution(2729704953240659045)
XLA Ops:
  10.4 28.9 %swap_in.1 = (bf16[8,48,1152]{2,1,0:T(8,128)(2,1)}, bf16[8,96,768]{2,1,0:T(8,128)(2,1)}) custom-call(bf16[96,4608]{1,0:T(8,128)(2,1)S(1)} %copy-done.33, bf16[96,6144]{1,0:T(8,128)(2,1)S(1)} %copy-done.30), custom_call_target="tpu_custom_call" | custom-call | tf_op jit(solution)/shard_map/swap_in/pallas_call | solution.py:374
  39.3 3.5 all-gather.9.cloned.1.call-done
  51.2 78.3 %entry.1 = (bf16[1280,1536]{1,0:T(8,128)(2,1)S(1)}, bf16[1280,1536]{1,0:T(8,128)(2,1)S(1)}, f32[8,2,9,128]{3,2,1,0:T(8,128)S(1)}, bf16[2,2,96,1536]{3,2,1,0:T(8,128)(2,1)S(1)}) custom-call(bf16[144,1536]{1,0:T(8,128)(2,1)S(1)} %copy-done.34, bf16[144,1536]{1,0:T(8,128)(2,1)S(1)} %copy-done.35, f32[8,4,9,128]{3,2,1,0:T(8,128)S(1)} %bitcast.50, ...), custom_call_target="tpu_custom_call" | custom-call | tf_op jit(solution)/shard_map/entry/pallas_call | solution.py:374
  137.8 5.5 multiply_convert_fusion
  143.3 3.3 fusion.10
  147.0 3.1 copy-done.9
  150.1 10.0 %project.3 = (bf16[1280,1536]{1,0:T(8,128)(2,1)S(1)}, bf16[1280,576]{1,0:T(8,128)(2,1)S(1)}) custom-call(bf16[1280,1536]{1,0:T(8,128)(2,1)S(1)} %copy-done.9, bf16[2,1536,576]{2,1,0:T(8,128)(2,1)S(1)} %bitcast.40, f32[1280,1]{1,0:T(8,128)S(1)} %fusion.text.window_text.refs_4_, f32[2,1536]{1,0:T(2,128)S(1)} %get-tuple-element.125.shift, ...), custom_call_target="tpu_custom_call" | custom-call | flops 2264924160 | bytes 16777216 | tf_op jit(solution)/shard_map/project/pallas_call | solution.py:311
  162.1 18.2 %attend.1.rows = bf16[1280,192]{1,0:T(8,128)(2,1)S(1)} custom-call(bf16[1280,576]{1,0:T(8,128)(2,1)S(1)} %get-tuple-element.59.projected, f32[1,1280]{1,0:T(1,128)S(1)} %and_select_fusion.bias_ref), custom_call_target="tpu_custom_call" | custom-call | flops 5033164800 | bytes 1966080 | tf_op jit(solution)/shard_map/attend/pallas_call | solution.py:128
  180.3 78.4 %middle.1 = (f32[160,1536]{1,0:T(8,128)S(1)}, bf16[1280,1536]{1,0:T(8,128)(2,1)S(1)}) custom-call(bf16[1280,192]{1,0:T(8,128)(2,1)S(1)} %attend.1.rows, bf16[2,192,1536]{2,1,0:T(8,128)(2,1)S(1)} %bitcast.49, f32[1280,1]{1,0:T(8,128)S(1)} %fusion.text.window_text.refs_4_, bf16[160,1536]{1,0:T(8,128)(2,1)S(1)} %pad_maximum_fusion.1.tokens.refs_5_, ...), custom_call_target="tpu_custom_call" | custom-call | tf_op jit(solution)/shard_map/middle/pallas_call | solution.py:374
  262.7 9.4 %up.3 = (f32[1280,768]{1,0:T(8,128)S(1)}, bf16[1280,768]{1,0:T(8,128)(2,1)S(1)}) custom-call(bf16[1280,1536]{1,0:T(8,128)(2,1)S(1)} %copy-done.41, bf16[2,1536,768]{2,1,0:T(8,128)(2,1)} %bitcast.55, f32[1280,1]{1,0:T(8,128)S(1)} %fusion.text.window_text.refs_4_), custom_call_target="tpu_custom_call" | custom-call | flops 3019898880 | bytes 16777216 | tf_op jit(solution)/shard_map/up/pallas_call | solution.py:311
  274.1 5.3 down_terms.1
  281.8 15.1 %all-gather.15.cloned.1.call-done = bf16[1536,1536]{1,0:T(8,128)(2,1)} async-done(((bf16[384,1536]{1,0:T(8,128)(2,1)}), bf16[1536,1536]{1,0:T(8,128)(2,1)}) %all-gather.15.cloned.1.call-update) | async-done | bytes 4718608 | tf_op jit(solution)/shard_map/all_gather | solution.py:1159
  301.1 10.5 %down_back.1.grads.rows = bf16[1280,768]{1,0:T(8,128)(2,1)S(1)} custom-call(bf16[1280,1536]{1,0:T(8,128)(2,1)S(1)} %copy-done.5, bf16[2,768,1536]{2,1,0:T(8,128)(2,1)} %bitcast.53, f32[1280,1]{1,0:T(8,128)S(1)} %fusion.text.window_text.refs_4_, f32[1280,768]{1,0:T(8,128)S(1)} %copy-done.20), custom_call_target="tpu_custom_call" | custom-call | flops 3019898880 | bytes 16777216 | tf_op jit(solution)/shard_map/down_back/pallas_call | solution.py:311
  311.6 6.5 %up_terms.1 = bf16[2,1536,768]{2,1,0:T(8,128)(2,1)S(1)} custom-call(bf16[1280,1536]{1,0:T(8,128)(2,1)S(1)} %copy-done.42, bf16[1280,768]{1,0:T(8,128)(2,1)S(1)} %down_back.1.grads.rows, f32[1280,1]{1,0:T(8,128)S(1)} %fusion.text.window_text.refs_4_), custom_call_target="tpu_custom_call" | custom-call | flops 4529848320 | bytes 8388608 | tf_op jit(solution)/shard_map/up_terms/pallas_call | solution.py:246
  318.2 2.2 copy-done.11
  325.8 66.4 %back.1 = (f32[160,1536]{1,0:T(8,128)S(1)}, f32[160,1536]{1,0:T(8,128)S(1)}, bf16[1280,1536]{1,0:T(8,128)(2,1)S(1)}) custom-call(bf16[1280,768]{1,0:T(8,128)(2,1)S(1)} %copy-done.7, bf16[2,1536,768]{2,1,0:T(8,128)(2,1)} %bitcast.56, f32[1280,1]{1,0:T(8,128)S(1)} %fusion.text.window_text.refs_4_, bf16[160,1536]{1,0:T(8,128)(2,1)S(1)} %pad_maximum_fusion.2.grad.refs_7_, ...), custom_call_target="tpu_custom_call" | custom-call | tf_op jit(solution)/shard_map/back/pallas_call | solution.py:374
  396.2 24.9 %attend_back.1.grads.refs_2_ = bf16[1280,576]{1,0:T(8,128)(2,1)} custom-call(bf16[1280,576]{1,0:T(8,128)(2,1)} %copy-done.43, bf16[1280,1536]{1,0:T(8,128)(2,1)} %copy-done.15, bf16[2,192,1536]{2,1,0:T(8,128)(2,1)} %bitcast.48, f32[1280,1]{1,0:T(8,128)} %copy-done.1, f32[1,1280]{1,0:T(1,128)} %copy-done.37), custom_call_target="tpu_custom_call" | custom-call | flops 12582912000 | bytes 3440640 | tf_op jit(solution)/shard_map/attend_back/pallas_call | solution.py:184
  422.5 2.2 copy-done.39
  424.7 6.3 %project_terms.1 = bf16[32,48,1152]{2,1,0:T(8,128)(2,1)S(1)} custom-call(bf16[1280,1536]{1,0:T(8,128)(2,1)S(1)} %copy-done.39, bf16[1280,576]{1,0:T(8,128)(2,1)S(1)} %copy-done.23, f32[1280,1]{1,0:T(8,128)S(1)} %copy-done.2), custom_call_target="tpu_custom_call" | custom-call | flops 3397386240 | bytes 8388608 | tf_op jit(solution)/shard_map/project_terms/pallas_call | solution.py:246
  434.2 2.3 multiply_reduce_fusion.1
  439.5 92.6 %last.1 = (bf16[144,1536]{1,0:T(8,128)(2,1)}, bf16[144,1536]{1,0:T(8,128)(2,1)}, f32[144,1536]{1,0:T(8,128)}, f32[144,1536]{1,0:T(8,128)}, f32[8,4,1,1152]{3,2,1...) custom-call(bf16[1280,768]{1,0:T(8,128)(2,1)} %copy-done.22, bf16[2,768,1536]{2,1,0:T(8,128)(2,1)} %bitcast.54, ...), custom_call_target="tpu_custom_call" | custom-call | tf_op jit(solution)/shard_map/last/pallas_call | solution.py:374
  533.4 2.5 fusion.13
  541.0 2.5 broadcast_select_fusion.1
  545.6 34.4 %finish.1 = (bf16[96,6144]{1,0:T(8,128)(2,1)S(1)}, bf16[96,4608]{1,0:T(8,128)(2,1)S(1)}, f32[96,1536]{1,0:T(8,128)S(1)}) custom-call(bf16[8,96,768]{2,1,0:T(8,128)(2,1)S(1)} %bitcast.46, bf16[8,48,1152]{2,1,0:T(8,128)(2,1)S(1)} %bitcast.51, bf16[4,96,1536]{2,1,0:T(8,128)(2,1)S(1)} %copy-done.26), custom_call_target="tpu_custom_call" | custom-call | tf_op jit(solution)/shard_map/finish/pallas_call | solution.py:374
  (187 shorter events, 62.9 us)
Async XLA Ops:
  7.2 37.0 %copy-start.51 = (s32[4]{0:T(128)S(1)}, s32[4]{0:T(128)}, u32[]{:S(2)}) copy-start(s32[4]{0:T(128)} %param.11) | copy-start | bytes 52
  7.2 38.5 %copy-start.47 = (bf16[4,1536]{1,0:T(4,128)(2,1)S(1)}, bf16[4,1536]{1,0:T(4,128)(2,1)}, u32[]{:S(2)}) copy-start(bf16[4,1536]{1,0:T(4,128)(2,1)} %param.10) | copy-start | bytes 36868
  7.2 35.6 %all-gather.9.cloned.1.call-start = ((), (), s32[]{:S(2)}) async-start(), calls=%async_computation.6 | async-start | bytes 1474560 | tf_op jit(solution)/shard_map/all_gather | solution.py:1141
  7.9 135.4 %all-gather.11.cloned.1.call-start = ((), (), s32[]{:S(2)}) async-start(), calls=%async_computation.7 | async-start | bytes 4423680 | tf_op jit(solution)/shard_map/all_gather | solution.py:1131
  42.8 8.4 %copy-start.34 = (bf16[144,1536]{1,0:T(8,128)(2,1)S(1)}, bf16[144,1536]{1,0:T(8,128)(2,1)}, u32[]{:S(2)}) copy-start(bf16[144,1536]{1,0:T(8,128)(2,1)} %tokens.1) | copy-start | bytes 1327108
  42.8 8.4 %copy-start.35 = (bf16[144,1536]{1,0:T(8,128)(2,1)S(1)}, bf16[144,1536]{1,0:T(8,128)(2,1)}, u32[]{:S(2)}) copy-start(bf16[144,1536]{1,0:T(8,128)(2,1)} %grads.1) | copy-start | bytes 1327108
  42.8 217.8 %all-gather.13.cloned.1.call-start = ((), (), s32[]{:S(2)}) async-start(), calls=%async_computation.8 | async-start | bytes 5898240 | tf_op jit(solution)/shard_map/all_gather | solution.py:1131
  43.5 253.3 %all-gather.15.cloned.1.call-start = ((), (), s32[]{:S(2)}) async-start(), calls=%async_computation.9 | async-start | bytes 5898240 | tf_op jit(solution)/shard_map/all_gather | solution.py:1159
  44.1 377.0 %reduce-scatter.4.cloned.1.call-start = ((), (), s32[]{:S(2)}) async-start(), calls=%async_computation.3 | async-start | bytes 5898240 | tf_op jit(solution)/shard_map/reduce_scatter | solution.py:1136
  49.6 274.3 %copy-start.24 = (f32[160,1]{1,0:T(8,128)}, f32[160,1]{1,0:T(8,128)S(1)}, u32[]{:S(2)}) copy-start(f32[160,1]{1,0:T(8,128)S(1)} %convert_element_type.65.text.refs_11_) | copy-start | bytes 1924
  50.3 111.7 %copy-start.37 = (f32[1,1280]{1,0:T(1,128)}, f32[1,1280]{1,0:T(1,128)S(1)}, u32[]{:S(2)}) copy-start(f32[1,1280]{1,0:T(1,128)S(1)} %and_select_fusion.bias_ref) | copy-start | bytes 15364
  51.1 272.8 %copy-start.1 = (f32[1280,1]{1,0:T(8,128)}, f32[1280,1]{1,0:T(8,128)S(1)}, u32[]{:S(2)}) copy-start(f32[1280,1]{1,0:T(8,128)S(1)} %fusion.text.window_text.refs_4_) | copy-start | bytes 15364
  137.1 43.2 %copy-start.13 = (bf16[160,1536]{1,0:T(8,128)(2,1)}, bf16[160,1536]{1,0:T(8,128)(2,1)S(1)}, u32[]{:S(2)}) copy-start(bf16[160,1536]{1,0:T(8,128)(2,1)S(1)} %pad_maximum_fusion.1.tokens.refs_5_) | copy-start | bytes 1474564
  137.8 9.2 %copy-start.36 = (f32[2,1536]{1,0:T(2,128)}, f32[2,1536]{1,0:T(2,128)S(1)}, u32[]{:S(2)}) copy-start(f32[2,1536]{1,0:T(2,128)S(1)} %get-tuple-element.124.scale.refs_10_) | copy-start | bytes 36868
  146.9 13.1 %copy-start = (bf16[32,96,576]{2,1,0:T(8,128)(2,1)}, bf16[32,96,576]{2,1,0:T(8,128)(2,1)S(1)}, u32[]{:S(2)}) copy-start(bf16[32,96,576]{2,1,0:T(8,128)(2,1)S(1)} %pad_maximum_fusion) | copy-start | bytes 10616836
  162.0 18.2 %copy-start.43 = (bf16[1280,576]{1,0:T(8,128)(2,1)}, bf16[1280,576]{1,0:T(8,128)(2,1)S(1)}, u32[]{:S(2)}) copy-start(bf16[1280,576]{1,0:T(8,128)(2,1)S(1)} %get-tuple-element.59.projected) | copy-start | bytes 4423684
  162.1 18.2 %copy-start.29 = (bf16[2,2,96,1536]{3,2,1,0:T(8,128)(2,1)S(1)}, bf16[2,2,96,1536]{3,2,1,0:T(8,128)(2,1)}, u32[]{:S(2)}) copy-start(bf16[2,2,96,1536]{3,2,1,0:T(8,128)(2,1)} %copy-done.28) | copy-start | bytes 3538948
  262.7 11.4 %copy-start.4 = (bf16[1280,1536]{1,0:T(8,128)(2,1)S(1)}, bf16[1280,1536]{1,0:T(8,128)(2,1)}, u32[]{:S(2)}) copy-start(bf16[1280,1536]{1,0:T(8,128)(2,1)} %get-tuple-element.65.grads.rows) | copy-start | bytes 11796484
  281.5 254.3 %reduce-scatter.8.cloned.1.call-start = ((), (), s32[]{:S(2)}) async-start(), calls=%async_computation.5 | async-start | bytes 5898240 | tf_op jit(solution)/shard_map/reduce_scatter | solution.py:1136
  301.1 10.5 %copy-start.42 = (bf16[1280,1536]{1,0:T(8,128)(2,1)S(1)}, bf16[1280,1536]{1,0:T(8,128)(2,1)}, u32[]{:S(2)}) copy-start(bf16[1280,1536]{1,0:T(8,128)(2,1)} %copy-done.40) | copy-start | bytes 11796484
  320.4 224.1 %reduce-scatter.6.cloned.1.call-start = ((), (), s32[]{:S(2)}) async-start(), calls=%async_computation.4 | async-start | bytes 4423680 | tf_op jit(solution)/shard_map/reduce_scatter | solution.py:1136
  322.4 69.8 %copy-start.14 = (bf16[160,1536]{1,0:T(8,128)(2,1)}, bf16[160,1536]{1,0:T(8,128)(2,1)S(1)}, u32[]{:S(2)}) copy-start(bf16[160,1536]{1,0:T(8,128)(2,1)S(1)} %pad_maximum_fusion.2.grad.refs_7_) | copy-start | bytes 1474564
  323.9 110.2 %copy-start.3 = (f32[160,1536]{1,0:T(8,128)}, f32[160,1536]{1,0:T(8,128)S(1)}, u32[]{:S(2)}) copy-start(f32[160,1536]{1,0:T(8,128)S(1)} %get-tuple-element.113.middle.refs_6_) | copy-start | bytes 2949124
  396.2 24.9 %copy-start.2 = (f32[1280,1]{1,0:T(8,128)S(1)}, f32[1280,1]{1,0:T(8,128)}, u32[]{:S(2)}) copy-start(f32[1280,1]{1,0:T(8,128)} %copy-done.1) | copy-start | bytes 15364
  (35 other events, 98.7 us)
Sparse Core Ops, SparseCore 0:
  9.6 33.1 all-gather.8
  44.3 73.4 all-gather.10
  119.4 88.0 all-gather.12
  209.0 87.8 all-gather.14
  299.0 83.6 reduce-scatter.3
  384.9 85.7 reduce-scatter.7
  473.1 71.3 reduce-scatter.5

commit v11 on v10

--- a/solution.py
+++ b/solution.py
@@ -759,19 +759,30 @@
         (list(range(count - 1)), below, above, down_in, down_out, down_send, down_recv, lambda owner: seq > owner,
          seq == count - 1),
     ]
+    def pass_on(turn, way):
+        owners, to, back, came, goes, send, recv, mine, first = way
+        owner = owners[turn]
+
+        @pl.when(mine(owner) & first)
+        def _():
+            hop(term, came, send, recv, owner, to).start()
+
+        @pl.when(mine(owner) & jnp.logical_not(first))
+        def _():
+            hop(goes, came, send, recv, owner, back).wait_recv()
+            goes[owner] = (term[owner].astype(F32) + came[owner].astype(F32)).astype(BF16)
+            hop(goes, came, send, recv, owner, to).start()
+
     for turn in range(count - 1):
-        for owners, to, back, came, goes, send, recv, mine, first in ways:
-            owner = owners[turn]
-
-            @pl.when(mine(owner) & first)
-            def _():
-                hop(term, came, send, recv, owner, to).start()
-
-            @pl.when(mine(owner) & jnp.logical_not(first))
-            def _():
-                hop(goes, came, send, recv, owner, back).wait_recv()
-                goes[owner] = (term[owner].astype(F32) + came[owner].astype(F32)).astype(BF16)
-                hop(goes, came, send, recv, owner, to).start()
+        @pl.when(seq < count // 2)
+        def _():
+            pass_on(turn, ways[0])
+            pass_on(turn, ways[1])
+
+        @pl.when(seq >= count // 2)
+        def _():
+            pass_on(turn, ways[1])
+            pass_on(turn, ways[0])
 
     out[...] = term[seq].astype(F32)
     for owners, to, back, came, goes, send, recv, mine, first in ways:

time: 592 us -> 585 us (0.988)
  Pallas kernels: 471 us -> 464 us
    pallas_call x6, Pallas kernels: 379 us -> 372 us  [call(): pl.pallas_call(kernel, out_shape=out_shape, in_specs=in_specs or [VMEM] *...]
  transfers between devices with their start and end apart: 7 -> 7, of which waited for: 3 -> 3; matrix products, arithmetic and copies ran while one was open for 6% -> 6% of each run, Pallas kernels for 74% -> 75%
where the time goes in v11:
time: 585 us; the launch traced here: 584 us
  Pallas kernels  464 us (79%)
  local copies, waits for them, and re-layouts  52.4 us (9%)
  other arithmetic  25.1 us (4%)
  waiting for transfers between devices  21.6 us (4%)
  between operations  15.6 us (3%)
    pallas_call x6, Pallas kernels, call(): pl.pallas_call(kernel, out_shape=out_shape, in_specs=in_specs or [VMEM] *...  372 us
    unnamed x106, local copies, waits for them, and re-layouts  41.9 us
    pallas_call x3, Pallas kernels, stream_rows(): pl.pallas_call(functools.partial(kernel, plan, size), out_shape=shapes, i...  29.8 us
    pallas_call x1, Pallas kernels, attend_back(): pl.pallas_call(functools.partial(attend_back_kernel, plan.heads, rows //...  24.9 us
    pallas_call x4, Pallas kernels, weight_terms(): pl.pallas_call(functools.partial(terms_kernel, plan, fold, chunk), out_sh...  19.4 us
    pallas_call x1, Pallas kernels, attend(): pl.pallas_call(functools.partial(attend_kernel, plan.heads, block), out_s...  18.2 us
    all_gather x1, waiting for transfers between devices, down_slices(): lax.all_gather(weight, 'dev', axis=0, axis_index_groups=plan.rank_groups())  15.1 us
  transfers between devices with their start and end apart: 7, of which 3 were waited for; matrix products, arithmetic and copies ran while one was open for 6% of the time, Pallas kernels for 75%

profile of v11, /device:TPU:0, one launch (start us, length us, event | category | flops | bytes accessed | tf_op | source)
XLA Modules:
  0.0 583.7 jit_solution(3045824485694824045)
XLA Ops:
  10.4 28.9 %swap_in.1 = (bf16[8,48,1152]{2,1,0:T(8,128)(2,1)}, bf16[8,96,768]{2,1,0:T(8,128)(2,1)}) custom-call(bf16[96,4608]{1,0:T(8,128)(2,1)S(1)} %copy-done.33, bf16[96,6144]{1,0:T(8,128)(2,1)S(1)} %copy-done.30), custom_call_target="tpu_custom_call" | custom-call | tf_op jit(solution)/shard_map/swap_in/pallas_call | solution.py:374
  39.3 3.5 all-gather.9.cloned.1.call-done
  51.2 78.3 %entry.1 = (bf16[1280,1536]{1,0:T(8,128)(2,1)S(1)}, bf16[1280,1536]{1,0:T(8,128)(2,1)S(1)}, f32[8,2,9,128]{3,2,1,0:T(8,128)S(1)}, bf16[2,2,96,1536]{3,2,1,0:T(8,128)(2,1)S(1)}) custom-call(bf16[144,1536]{1,0:T(8,128)(2,1)S(1)} %copy-done.34, bf16[144,1536]{1,0:T(8,128)(2,1)S(1)} %copy-done.35, f32[8,4,9,128]{3,2,1,0:T(8,128)S(1)} %bitcast.50, ...), custom_call_target="tpu_custom_call" | custom-call | tf_op jit(solution)/shard_map/entry/pallas_call | solution.py:374
  137.8 5.5 multiply_convert_fusion
  143.3 3.3 fusion.10
  147.0 3.1 copy-done.9
  150.1 10.0 %project.3 = (bf16[1280,1536]{1,0:T(8,128)(2,1)S(1)}, bf16[1280,576]{1,0:T(8,128)(2,1)S(1)}) custom-call(bf16[1280,1536]{1,0:T(8,128)(2,1)S(1)} %copy-done.9, bf16[2,1536,576]{2,1,0:T(8,128)(2,1)S(1)} %bitcast.40, f32[1280,1]{1,0:T(8,128)S(1)} %fusion.text.window_text.refs_4_, f32[2,1536]{1,0:T(2,128)S(1)} %get-tuple-element.125.shift, ...), custom_call_target="tpu_custom_call" | custom-call | flops 2264924160 | bytes 16777216 | tf_op jit(solution)/shard_map/project/pallas_call | solution.py:311
  162.1 18.2 %attend.1.rows = bf16[1280,192]{1,0:T(8,128)(2,1)S(1)} custom-call(bf16[1280,576]{1,0:T(8,128)(2,1)S(1)} %get-tuple-element.59.projected, f32[1,1280]{1,0:T(1,128)S(1)} %and_select_fusion.bias_ref), custom_call_target="tpu_custom_call" | custom-call | flops 5033164800 | bytes 1966080 | tf_op jit(solution)/shard_map/attend/pallas_call | solution.py:128
  180.3 78.4 %middle.1 = (f32[160,1536]{1,0:T(8,128)S(1)}, bf16[1280,1536]{1,0:T(8,128)(2,1)S(1)}) custom-call(bf16[1280,192]{1,0:T(8,128)(2,1)S(1)} %attend.1.rows, bf16[2,192,1536]{2,1,0:T(8,128)(2,1)S(1)} %bitcast.49, f32[1280,1]{1,0:T(8,128)S(1)} %fusion.text.window_text.refs_4_, bf16[160,1536]{1,0:T(8,128)(2,1)S(1)} %pad_maximum_fusion.1.tokens.refs_5_, ...), custom_call_target="tpu_custom_call" | custom-call | tf_op jit(solution)/shard_map/middle/pallas_call | solution.py:374
  262.7 9.4 %up.3 = (f32[1280,768]{1,0:T(8,128)S(1)}, bf16[1280,768]{1,0:T(8,128)(2,1)S(1)}) custom-call(bf16[1280,1536]{1,0:T(8,128)(2,1)S(1)} %copy-done.41, bf16[2,1536,768]{2,1,0:T(8,128)(2,1)} %bitcast.55, f32[1280,1]{1,0:T(8,128)S(1)} %fusion.text.window_text.refs_4_), custom_call_target="tpu_custom_call" | custom-call | flops 3019898880 | bytes 16777216 | tf_op jit(solution)/shard_map/up/pallas_call | solution.py:311
  274.1 5.3 down_terms.1
  281.8 15.1 %all-gather.15.cloned.1.call-done = bf16[1536,1536]{1,0:T(8,128)(2,1)} async-done(((bf16[384,1536]{1,0:T(8,128)(2,1)}), bf16[1536,1536]{1,0:T(8,128)(2,1)}) %all-gather.15.cloned.1.call-update) | async-done | bytes 4718608 | tf_op jit(solution)/shard_map/all_gather | solution.py:1170
  301.1 10.5 %down_back.1.grads.rows = bf16[1280,768]{1,0:T(8,128)(2,1)S(1)} custom-call(bf16[1280,1536]{1,0:T(8,128)(2,1)S(1)} %copy-done.5, bf16[2,768,1536]{2,1,0:T(8,128)(2,1)} %bitcast.53, f32[1280,1]{1,0:T(8,128)S(1)} %fusion.text.window_text.refs_4_, f32[1280,768]{1,0:T(8,128)S(1)} %copy-done.20), custom_call_target="tpu_custom_call" | custom-call | flops 3019898880 | bytes 16777216 | tf_op jit(solution)/shard_map/down_back/pallas_call | solution.py:311
  311.6 6.5 %up_terms.1 = bf16[2,1536,768]{2,1,0:T(8,128)(2,1)S(1)} custom-call(bf16[1280,1536]{1,0:T(8,128)(2,1)S(1)} %copy-done.42, bf16[1280,768]{1,0:T(8,128)(2,1)S(1)} %down_back.1.grads.rows, f32[1280,1]{1,0:T(8,128)S(1)} %fusion.text.window_text.refs_4_), custom_call_target="tpu_custom_call" | custom-call | flops 4529848320 | bytes 8388608 | tf_op jit(solution)/shard_map/up_terms/pallas_call | solution.py:246
  318.2 2.2 copy-done.11
  325.8 66.4 %back.1 = (f32[160,1536]{1,0:T(8,128)S(1)}, f32[160,1536]{1,0:T(8,128)S(1)}, bf16[1280,1536]{1,0:T(8,128)(2,1)S(1)}) custom-call(bf16[1280,768]{1,0:T(8,128)(2,1)S(1)} %copy-done.7, bf16[2,1536,768]{2,1,0:T(8,128)(2,1)} %bitcast.56, f32[1280,1]{1,0:T(8,128)S(1)} %fusion.text.window_text.refs_4_, bf16[160,1536]{1,0:T(8,128)(2,1)S(1)} %pad_maximum_fusion.2.grad.refs_7_, ...), custom_call_target="tpu_custom_call" | custom-call | tf_op jit(solution)/shard_map/back/pallas_call | solution.py:374
  396.2 24.9 %attend_back.1.grads.refs_2_ = bf16[1280,576]{1,0:T(8,128)(2,1)} custom-call(bf16[1280,576]{1,0:T(8,128)(2,1)} %copy-done.43, bf16[1280,1536]{1,0:T(8,128)(2,1)} %copy-done.15, bf16[2,192,1536]{2,1,0:T(8,128)(2,1)} %bitcast.48, f32[1280,1]{1,0:T(8,128)} %copy-done.1, f32[1,1280]{1,0:T(1,128)} %copy-done.37), custom_call_target="tpu_custom_call" | custom-call | flops 12582912000 | bytes 3440640 | tf_op jit(solution)/shard_map/attend_back/pallas_call | solution.py:184
  422.5 2.2 copy-done.39
  424.7 6.3 %project_terms.1 = bf16[32,48,1152]{2,1,0:T(8,128)(2,1)S(1)} custom-call(bf16[1280,1536]{1,0:T(8,128)(2,1)S(1)} %copy-done.39, bf16[1280,576]{1,0:T(8,128)(2,1)S(1)} %copy-done.23, f32[1280,1]{1,0:T(8,128)S(1)} %copy-done.2), custom_call_target="tpu_custom_call" | custom-call | flops 3397386240 | bytes 8388608 | tf_op jit(solution)/shard_map/project_terms/pallas_call | solution.py:246
  434.2 2.3 multiply_reduce_fusion.1
  439.5 92.6 %last.1 = (bf16[144,1536]{1,0:T(8,128)(2,1)}, bf16[144,1536]{1,0:T(8,128)(2,1)}, f32[144,1536]{1,0:T(8,128)}, f32[144,1536]{1,0:T(8,128)}, f32[8,4,1,1152]{3,2,1...) custom-call(bf16[1280,768]{1,0:T(8,128)(2,1)} %copy-done.22, bf16[2,768,1536]{2,1,0:T(8,128)(2,1)} %bitcast.54, ...), custom_call_target="tpu_custom_call" | custom-call | tf_op jit(solution)/shard_map/last/pallas_call | solution.py:374
  533.4 2.5 fusion.13
  541.0 2.5 broadcast_select_fusion.1
  545.6 27.4 %finish.1 = (bf16[96,6144]{1,0:T(8,128)(2,1)S(1)}, bf16[96,4608]{1,0:T(8,128)(2,1)S(1)}, f32[96,1536]{1,0:T(8,128)S(1)}) custom-call(bf16[8,96,768]{2,1,0:T(8,128)(2,1)S(1)} %bitcast.46, bf16[8,48,1152]{2,1,0:T(8,128)(2,1)S(1)} %bitcast.51, bf16[4,96,1536]{2,1,0:T(8,128)(2,1)S(1)} %copy-done.26), custom_call_target="tpu_custom_call" | custom-call | tf_op jit(solution)/shard_map/finish/pallas_call | solution.py:374
  (187 shorter events, 62.9 us)
Async XLA Ops:
  7.2 37.0 %copy-start.51 = (s32[4]{0:T(128)S(1)}, s32[4]{0:T(128)}, u32[]{:S(2)}) copy-start(s32[4]{0:T(128)} %param.11) | copy-start | bytes 52
  7.2 38.5 %copy-start.47 = (bf16[4,1536]{1,0:T(4,128)(2,1)S(1)}, bf16[4,1536]{1,0:T(4,128)(2,1)}, u32[]{:S(2)}) copy-start(bf16[4,1536]{1,0:T(4,128)(2,1)} %param.10) | copy-start | bytes 36868
  7.2 35.6 %all-gather.9.cloned.1.call-start = ((), (), s32[]{:S(2)}) async-start(), calls=%async_computation.6 | async-start | bytes 1474560 | tf_op jit(solution)/shard_map/all_gather | solution.py:1152
  7.9 135.4 %all-gather.11.cloned.1.call-start = ((), (), s32[]{:S(2)}) async-start(), calls=%async_computation.7 | async-start | bytes 4423680 | tf_op jit(solution)/shard_map/all_gather | solution.py:1142
  42.8 8.4 %copy-start.34 = (bf16[144,1536]{1,0:T(8,128)(2,1)S(1)}, bf16[144,1536]{1,0:T(8,128)(2,1)}, u32[]{:S(2)}) copy-start(bf16[144,1536]{1,0:T(8,128)(2,1)} %tokens.1) | copy-start | bytes 1327108
  42.8 8.4 %copy-start.35 = (bf16[144,1536]{1,0:T(8,128)(2,1)S(1)}, bf16[144,1536]{1,0:T(8,128)(2,1)}, u32[]{:S(2)}) copy-start(bf16[144,1536]{1,0:T(8,128)(2,1)} %grads.1) | copy-start | bytes 1327108
  42.8 217.8 %all-gather.13.cloned.1.call-start = ((), (), s32[]{:S(2)}) async-start(), calls=%async_computation.8 | async-start | bytes 5898240 | tf_op jit(solution)/shard_map/all_gather | solution.py:1142
  43.5 253.3 %all-gather.15.cloned.1.call-start = ((), (), s32[]{:S(2)}) async-start(), calls=%async_computation.9 | async-start | bytes 5898240 | tf_op jit(solution)/shard_map/all_gather | solution.py:1170
  44.1 377.0 %reduce-scatter.4.cloned.1.call-start = ((), (), s32[]{:S(2)}) async-start(), calls=%async_computation.3 | async-start | bytes 5898240 | tf_op jit(solution)/shard_map/reduce_scatter | solution.py:1147
  49.6 274.3 %copy-start.24 = (f32[160,1]{1,0:T(8,128)}, f32[160,1]{1,0:T(8,128)S(1)}, u32[]{:S(2)}) copy-start(f32[160,1]{1,0:T(8,128)S(1)} %convert_element_type.65.text.refs_11_) | copy-start | bytes 1924
  50.3 111.7 %copy-start.37 = (f32[1,1280]{1,0:T(1,128)}, f32[1,1280]{1,0:T(1,128)S(1)}, u32[]{:S(2)}) copy-start(f32[1,1280]{1,0:T(1,128)S(1)} %and_select_fusion.bias_ref) | copy-start | bytes 15364
  51.1 272.8 %copy-start.1 = (f32[1280,1]{1,0:T(8,128)}, f32[1280,1]{1,0:T(8,128)S(1)}, u32[]{:S(2)}) copy-start(f32[1280,1]{1,0:T(8,128)S(1)} %fusion.text.window_text.refs_4_) | copy-start | bytes 15364
  137.1 43.2 %copy-start.13 = (bf16[160,1536]{1,0:T(8,128)(2,1)}, bf16[160,1536]{1,0:T(8,128)(2,1)S(1)}, u32[]{:S(2)}) copy-start(bf16[160,1536]{1,0:T(8,128)(2,1)S(1)} %pad_maximum_fusion.1.tokens.refs_5_) | copy-start | bytes 1474564
  137.8 9.2 %copy-start.36 = (f32[2,1536]{1,0:T(2,128)}, f32[2,1536]{1,0:T(2,128)S(1)}, u32[]{:S(2)}) copy-start(f32[2,1536]{1,0:T(2,128)S(1)} %get-tuple-element.124.scale.refs_10_) | copy-start | bytes 36868
  146.9 13.1 %copy-start = (bf16[32,96,576]{2,1,0:T(8,128)(2,1)}, bf16[32,96,576]{2,1,0:T(8,128)(2,1)S(1)}, u32[]{:S(2)}) copy-start(bf16[32,96,576]{2,1,0:T(8,128)(2,1)S(1)} %pad_maximum_fusion) | copy-start | bytes 10616836
  162.0 18.2 %copy-start.43 = (bf16[1280,576]{1,0:T(8,128)(2,1)}, bf16[1280,576]{1,0:T(8,128)(2,1)S(1)}, u32[]{:S(2)}) copy-start(bf16[1280,576]{1,0:T(8,128)(2,1)S(1)} %get-tuple-element.59.projected) | copy-start | bytes 4423684
  162.1 18.2 %copy-start.29 = (bf16[2,2,96,1536]{3,2,1,0:T(8,128)(2,1)S(1)}, bf16[2,2,96,1536]{3,2,1,0:T(8,128)(2,1)}, u32[]{:S(2)}) copy-start(bf16[2,2,96,1536]{3,2,1,0:T(8,128)(2,1)} %copy-done.28) | copy-start | bytes 3538948
  262.7 11.4 %copy-start.4 = (bf16[1280,1536]{1,0:T(8,128)(2,1)S(1)}, bf16[1280,1536]{1,0:T(8,128)(2,1)}, u32[]{:S(2)}) copy-start(bf16[1280,1536]{1,0:T(8,128)(2,1)} %get-tuple-element.65.grads.rows) | copy-start | bytes 11796484
  281.5 254.3 %reduce-scatter.8.cloned.1.call-start = ((), (), s32[]{:S(2)}) async-start(), calls=%async_computation.5 | async-start | bytes 5898240 | tf_op jit(solution)/shard_map/reduce_scatter | solution.py:1147
  301.1 10.5 %copy-start.42 = (bf16[1280,1536]{1,0:T(8,128)(2,1)S(1)}, bf16[1280,1536]{1,0:T(8,128)(2,1)}, u32[]{:S(2)}) copy-start(bf16[1280,1536]{1,0:T(8,128)(2,1)} %copy-done.40) | copy-start | bytes 11796484
  320.4 224.1 %reduce-scatter.6.cloned.1.call-start = ((), (), s32[]{:S(2)}) async-start(), calls=%async_computation.4 | async-start | bytes 4423680 | tf_op jit(solution)/shard_map/reduce_scatter | solution.py:1147
  322.4 69.8 %copy-start.14 = (bf16[160,1536]{1,0:T(8,128)(2,1)}, bf16[160,1536]{1,0:T(8,128)(2,1)S(1)}, u32[]{:S(2)}) copy-start(bf16[160,1536]{1,0:T(8,128)(2,1)S(1)} %pad_maximum_fusion.2.grad.refs_7_) | copy-start | bytes 1474564
  323.9 110.2 %copy-start.3 = (f32[160,1536]{1,0:T(8,128)}, f32[160,1536]{1,0:T(8,128)S(1)}, u32[]{:S(2)}) copy-start(f32[160,1536]{1,0:T(8,128)S(1)} %get-tuple-element.113.middle.refs_6_) | copy-start | bytes 2949124
  396.2 24.9 %copy-start.2 = (f32[1280,1]{1,0:T(8,128)S(1)}, f32[1280,1]{1,0:T(8,128)}, u32[]{:S(2)}) copy-start(f32[1280,1]{1,0:T(8,128)} %copy-done.1) | copy-start | bytes 15364
  (35 other events, 98.7 us)
Sparse Core Ops, SparseCore 0:
  9.6 33.1 all-gather.8
  44.3 73.4 all-gather.10
  119.4 88.0 all-gather.12
  209.0 87.8 all-gather.14
  299.0 83.6 reduce-scatter.3
  384.9 85.7 reduce-scatter.7
  473.1 71.3 reduce-scatter.5

commit v12 on v11

--- a/solution.py
+++ b/solution.py
@@ -744,7 +744,7 @@
         starts, share = columns(plan, source)
         piece = unfold_rows(got[source]) if unfold else got[source]
         for i, c in enumerate(starts):
-            out[:, c : c + share] = piece[:, i * share : (i + 1) * share]
+            out[:, c : c + share] = piece[:, i * share : (i + 1) * share].astype(out.dtype)
 
 
 def line_sum(plan, seq, rank, term, out, up_in, up_out, down_in, down_out, up_send, up_recv, down_send, down_recv):
@@ -799,42 +799,51 @@
 
 def finish_kernel(plan, up, project, *refs):
     if plan.chip_heads:
-        term, up_out, project_out, merge_out, *refs = refs
-        *refs, line = refs[:6] + [refs[6:]]
+        term, up_got, project_got, merge_out, *refs = refs
+        *refs, line = refs[:4] + [refs[4:]]
     else:
-        up_out, project_out, *refs = refs
-    up_got, project_got, u_send, u_recv, p_send, p_recv = refs
+        up_got, project_got, *refs = refs
+    u_send, u_recv, p_send, p_recv = refs
     seq, rank = here(plan)
     meet(group_devices(plan, seq, rank) + column_devices(plan, seq, rank))
     ups = start_swap(plan, seq, rank, up, up_got, u_send, u_recv)
     projects = start_swap(plan, seq, rank, project, project_got, p_send, p_recv)
     if plan.chip_heads:
         line_sum(plan, seq, rank, term, merge_out, *line)
-    for copy in ups:
+    for copy in ups + projects:
         copy.wait()
+
+
+def place_kernel(plan, up_got, project_got, up_out, project_out):
     place_columns(plan, up_got, up_out, lambda p, r: up_columns(p, r, up_out.shape[1]), False)
-    for copy in projects:
-        copy.wait()
     place_columns(plan, project_got, project_out, project_columns, True)
 
 
 def finish(plan, up, project, term):
     dma = pltpu.SemaphoreType.DMA
     rows = up.shape[1]
-    shapes = (
-        jax.ShapeDtypeStruct((rows, plan.group * up.shape[2]), BF16),
-        jax.ShapeDtypeStruct((rows, plan.group * project.shape[2] // 2), BF16),
-    )
+    shapes = tuple(jax.ShapeDtypeStruct(pieces.shape, BF16) for pieces in (up, project))
     operands = (up, project)
-    scratch = [pltpu.VMEM(up.shape, BF16), pltpu.VMEM(project.shape, BF16)] + [dma((plan.group,))] * 4
+    scratch = [dma((plan.group,))] * 4
     if plan.chip_heads:
         shapes += (jax.ShapeDtypeStruct(term.shape[1:], F32),)
         operands += (term,)
         scratch += [pltpu.VMEM(term.shape, BF16)] * 4 + [dma((plan.sequences,))] * 4
-    up_grad, project_grad, *merge_grad = call(
+    up_got, project_got, *merge_grad = call(
         functools.partial(finish_kernel, plan), "finish", 6, shapes, scratch, operands
     )
-    return up_grad.astype(F32), project_grad.astype(F32), merge_grad
+    up_grad, project_grad = pl.pallas_call(
+        functools.partial(place_kernel, plan),
+        out_shape=(
+            jax.ShapeDtypeStruct((rows, plan.group * up.shape[2]), F32),
+            jax.ShapeDtypeStruct((rows, plan.group * project.shape[2] // 2), F32),
+        ),
+        in_specs=[VMEM, VMEM],
+        out_specs=(VMEM, VMEM),
+        compiler_params=pltpu.CompilerParams(vmem_limit_bytes=24 << 20),
+        name="place",
+    )(up_got, project_got)
+    return up_grad, project_grad, merge_grad
 
 
 def pick_rows(table, text):

time: 585 us -> 584 us (level)
  no operation moved by 1% of the time
where the time goes in v12:
time: 584 us; the launch traced here: 583 us
  Pallas kernels  466 us (80%)
  local copies, waits for them, and re-layouts  52.5 us (9%)
  other arithmetic  22.1 us (4%)
  waiting for transfers between devices  21.5 us (4%)
  between operations  15.6 us (3%)
    pallas_call x6, Pallas kernels, call(): pl.pallas_call(kernel, out_shape=out_shape, in_specs=in_specs or [VMEM] *...  371 us
    unnamed x106, local copies, waits for them, and re-layouts  41.9 us
    pallas_call x3, Pallas kernels, stream_rows(): pl.pallas_call(functools.partial(kernel, plan, size), out_shape=shapes, i...  29.8 us
    pallas_call x1, Pallas kernels, attend_back(): pl.pallas_call(functools.partial(attend_back_kernel, plan.heads, rows //...  24.9 us
    pallas_call x4, Pallas kernels, weight_terms(): pl.pallas_call(functools.partial(terms_kernel, plan, fold, chunk), out_sh...  19.4 us
    pallas_call x1, Pallas kernels, attend(): pl.pallas_call(functools.partial(attend_kernel, plan.heads, block), out_s...  18.2 us
    all_gather x1, waiting for transfers between devices, down_slices(): lax.all_gather(weight, 'dev', axis=0, axis_index_groups=plan.rank_groups())  15.1 us
  transfers between devices with their start and end apart: 7, of which 3 were waited for; matrix products, arithmetic and copies ran while one was open for 6% of the time, Pallas kernels for 75%

profile of v12, /device:TPU:0, one launch (start us, length us, event | category | flops | bytes accessed | tf_op | source)
XLA Modules:
  0.0 582.7 jit_solution(10042576139632945198)
XLA Ops:
  10.4 28.9 %swap_in.1 = (bf16[8,48,1152]{2,1,0:T(8,128)(2,1)}, bf16[8,96,768]{2,1,0:T(8,128)(2,1)}) custom-call(bf16[96,4608]{1,0:T(8,128)(2,1)S(1)} %copy-done.33, bf16[96,6144]{1,0:T(8,128)(2,1)S(1)} %copy-done.30), custom_call_target="tpu_custom_call" | custom-call | tf_op jit(solution)/shard_map/swap_in/pallas_call | solution.py:374
  39.3 3.5 all-gather.9.cloned.1.call-done
  51.2 78.3 %entry.1 = (bf16[1280,1536]{1,0:T(8,128)(2,1)S(1)}, bf16[1280,1536]{1,0:T(8,128)(2,1)S(1)}, f32[8,2,9,128]{3,2,1,0:T(8,128)S(1)}, bf16[2,2,96,1536]{3,2,1,0:T(8,128)(2,1)S(1)}) custom-call(bf16[144,1536]{1,0:T(8,128)(2,1)S(1)} %copy-done.34, bf16[144,1536]{1,0:T(8,128)(2,1)S(1)} %copy-done.35, f32[8,4,9,128]{3,2,1,0:T(8,128)S(1)} %bitcast.50, ...), custom_call_target="tpu_custom_call" | custom-call | tf_op jit(solution)/shard_map/entry/pallas_call | solution.py:374
  137.8 5.5 multiply_convert_fusion
  143.3 3.3 fusion.10
  147.0 3.1 copy-done.9
  150.1 10.0 %project.3 = (bf16[1280,1536]{1,0:T(8,128)(2,1)S(1)}, bf16[1280,576]{1,0:T(8,128)(2,1)S(1)}) custom-call(bf16[1280,1536]{1,0:T(8,128)(2,1)S(1)} %copy-done.9, bf16[2,1536,576]{2,1,0:T(8,128)(2,1)S(1)} %bitcast.40, f32[1280,1]{1,0:T(8,128)S(1)} %fusion.text.window_text.refs_4_, f32[2,1536]{1,0:T(2,128)S(1)} %get-tuple-element.129.shift, ...), custom_call_target="tpu_custom_call" | custom-call | flops 2264924160 | bytes 16777216 | tf_op jit(solution)/shard_map/project/pallas_call | solution.py:311
  162.0 18.2 %attend.1.rows = bf16[1280,192]{1,0:T(8,128)(2,1)S(1)} custom-call(bf16[1280,576]{1,0:T(8,128)(2,1)S(1)} %get-tuple-element.61.projected, f32[1,1280]{1,0:T(1,128)S(1)} %and_select_fusion.bias_ref), custom_call_target="tpu_custom_call" | custom-call | flops 5033164800 | bytes 1966080 | tf_op jit(solution)/shard_map/attend/pallas_call | solution.py:128
  180.3 78.4 %middle.1 = (f32[160,1536]{1,0:T(8,128)S(1)}, bf16[1280,1536]{1,0:T(8,128)(2,1)S(1)}) custom-call(bf16[1280,192]{1,0:T(8,128)(2,1)S(1)} %attend.1.rows, bf16[2,192,1536]{2,1,0:T(8,128)(2,1)S(1)} %bitcast.49, f32[1280,1]{1,0:T(8,128)S(1)} %fusion.text.window_text.refs_4_, bf16[160,1536]{1,0:T(8,128)(2,1)S(1)} %pad_maximum_fusion.1.tokens.refs_5_, ...), custom_call_target="tpu_custom_call" | custom-call | tf_op jit(solution)/shard_map/middle/pallas_call | solution.py:374
  262.7 9.4 %up.3 = (f32[1280,768]{1,0:T(8,128)S(1)}, bf16[1280,768]{1,0:T(8,128)(2,1)S(1)}) custom-call(bf16[1280,1536]{1,0:T(8,128)(2,1)S(1)} %copy-done.41, bf16[2,1536,768]{2,1,0:T(8,128)(2,1)} %bitcast.55, f32[1280,1]{1,0:T(8,128)S(1)} %fusion.text.window_text.refs_4_), custom_call_target="tpu_custom_call" | custom-call | flops 3019898880 | bytes 16777216 | tf_op jit(solution)/shard_map/up/pallas_call | solution.py:311
  274.1 5.3 down_terms.1
  281.8 15.1 %all-gather.15.cloned.1.call-done = bf16[1536,1536]{1,0:T(8,128)(2,1)} async-done(((bf16[384,1536]{1,0:T(8,128)(2,1)}), bf16[1536,1536]{1,0:T(8,128)(2,1)}) %all-gather.15.cloned.1.call-update) | async-done | bytes 4718608 | tf_op jit(solution)/shard_map/all_gather | solution.py:1179
  301.1 10.5 %down_back.1.grads.rows = bf16[1280,768]{1,0:T(8,128)(2,1)S(1)} custom-call(bf16[1280,1536]{1,0:T(8,128)(2,1)S(1)} %copy-done.5, bf16[2,768,1536]{2,1,0:T(8,128)(2,1)} %bitcast.53, f32[1280,1]{1,0:T(8,128)S(1)} %fusion.text.window_text.refs_4_, f32[1280,768]{1,0:T(8,128)S(1)} %copy-done.20), custom_call_target="tpu_custom_call" | custom-call | flops 3019898880 | bytes 16777216 | tf_op jit(solution)/shard_map/down_back/pallas_call | solution.py:311
  311.6 6.5 %up_terms.1 = bf16[2,1536,768]{2,1,0:T(8,128)(2,1)S(1)} custom-call(bf16[1280,1536]{1,0:T(8,128)(2,1)S(1)} %copy-done.42, bf16[1280,768]{1,0:T(8,128)(2,1)S(1)} %down_back.1.grads.rows, f32[1280,1]{1,0:T(8,128)S(1)} %fusion.text.window_text.refs_4_), custom_call_target="tpu_custom_call" | custom-call | flops 4529848320 | bytes 8388608 | tf_op jit(solution)/shard_map/up_terms/pallas_call | solution.py:246
  325.8 66.3 %back.1 = (f32[160,1536]{1,0:T(8,128)S(1)}, f32[160,1536]{1,0:T(8,128)S(1)}, bf16[1280,1536]{1,0:T(8,128)(2,1)S(1)}) custom-call(bf16[1280,768]{1,0:T(8,128)(2,1)S(1)} %copy-done.7, bf16[2,1536,768]{2,1,0:T(8,128)(2,1)} %bitcast.56, f32[1280,1]{1,0:T(8,128)S(1)} %fusion.text.window_text.refs_4_, bf16[160,1536]{1,0:T(8,128)(2,1)S(1)} %pad_maximum_fusion.2.grad.refs_7_, ...), custom_call_target="tpu_custom_call" | custom-call | tf_op jit(solution)/shard_map/back/pallas_call | solution.py:374
  396.2 24.9 %attend_back.1.grads.refs_2_ = bf16[1280,576]{1,0:T(8,128)(2,1)} custom-call(bf16[1280,576]{1,0:T(8,128)(2,1)} %copy-done.43, bf16[1280,1536]{1,0:T(8,128)(2,1)} %copy-done.15, bf16[2,192,1536]{2,1,0:T(8,128)(2,1)} %bitcast.48, f32[1280,1]{1,0:T(8,128)} %copy-done.1, f32[1,1280]{1,0:T(1,128)} %copy-done.37), custom_call_target="tpu_custom_call" | custom-call | flops 12582912000 | bytes 3440640 | tf_op jit(solution)/shard_map/attend_back/pallas_call | solution.py:184
  422.5 2.2 copy-done.39
  424.7 6.3 %project_terms.1 = bf16[32,48,1152]{2,1,0:T(8,128)(2,1)S(1)} custom-call(bf16[1280,1536]{1,0:T(8,128)(2,1)S(1)} %copy-done.39, bf16[1280,576]{1,0:T(8,128)(2,1)S(1)} %copy-done.23, f32[1280,1]{1,0:T(8,128)S(1)} %copy-done.2), custom_call_target="tpu_custom_call" | custom-call | flops 3397386240 | bytes 8388608 | tf_op jit(solution)/shard_map/project_terms/pallas_call | solution.py:246
  434.1 2.3 multiply_reduce_fusion.1
  439.5 92.7 %last.1 = (bf16[144,1536]{1,0:T(8,128)(2,1)}, bf16[144,1536]{1,0:T(8,128)(2,1)}, f32[144,1536]{1,0:T(8,128)}, f32[144,1536]{1,0:T(8,128)}, f32[8,4,1,1152]{3,2,1...) custom-call(bf16[1280,768]{1,0:T(8,128)(2,1)} %copy-done.22, bf16[2,768,1536]{2,1,0:T(8,128)(2,1)} %bitcast.54, ...), custom_call_target="tpu_custom_call" | custom-call | tf_op jit(solution)/shard_map/last/pallas_call | solution.py:374
  533.4 2.5 fusion.13
  541.0 2.5 broadcast_select_fusion.1
  545.6 26.7 %finish.1 = (bf16[8,96,768]{2,1,0:T(8,128)(2,1)S(1)}, bf16[8,48,1152]{2,1,0:T(8,128)(2,1)S(1)}, f32[96,1536]{1,0:T(8,128)S(1)}) custom-call(bf16[8,96,768]{2,1,0:T(8,128)(2,1)S(1)} %bitcast.46, bf16[8,48,1152]{2,1,0:T(8,128)(2,1)S(1)} %bitcast.51, bf16[4,96,1536]{2,1,0:T(8,128)(2,1)S(1)} %copy-done.26), custom_call_target="tpu_custom_call" | custom-call | tf_op jit(solution)/shard_map/finish/pallas_call | solution.py:374
  572.3 2.7 place.1
  (186 shorter events, 62.1 us)
Async XLA Ops:
  7.2 37.0 %copy-start.51 = (s32[4]{0:T(128)S(1)}, s32[4]{0:T(128)}, u32[]{:S(2)}) copy-start(s32[4]{0:T(128)} %param.11) | copy-start | bytes 52
  7.2 38.5 %copy-start.47 = (bf16[4,1536]{1,0:T(4,128)(2,1)S(1)}, bf16[4,1536]{1,0:T(4,128)(2,1)}, u32[]{:S(2)}) copy-start(bf16[4,1536]{1,0:T(4,128)(2,1)} %param.10) | copy-start | bytes 36868
  7.2 35.6 %all-gather.9.cloned.1.call-start = ((), (), s32[]{:S(2)}) async-start(), calls=%async_computation.6 | async-start | bytes 1474560 | tf_op jit(solution)/shard_map/all_gather | solution.py:1161
  7.9 135.4 %all-gather.11.cloned.1.call-start = ((), (), s32[]{:S(2)}) async-start(), calls=%async_computation.7 | async-start | bytes 4423680 | tf_op jit(solution)/shard_map/all_gather | solution.py:1151
  42.8 8.4 %copy-start.34 = (bf16[144,1536]{1,0:T(8,128)(2,1)S(1)}, bf16[144,1536]{1,0:T(8,128)(2,1)}, u32[]{:S(2)}) copy-start(bf16[144,1536]{1,0:T(8,128)(2,1)} %tokens.1) | copy-start | bytes 1327108
  42.8 8.4 %copy-start.35 = (bf16[144,1536]{1,0:T(8,128)(2,1)S(1)}, bf16[144,1536]{1,0:T(8,128)(2,1)}, u32[]{:S(2)}) copy-start(bf16[144,1536]{1,0:T(8,128)(2,1)} %grads.1) | copy-start | bytes 1327108
  42.8 217.8 %all-gather.13.cloned.1.call-start = ((), (), s32[]{:S(2)}) async-start(), calls=%async_computation.8 | async-start | bytes 5898240 | tf_op jit(solution)/shard_map/all_gather | solution.py:1151
  43.5 253.4 %all-gather.15.cloned.1.call-start = ((), (), s32[]{:S(2)}) async-start(), calls=%async_computation.9 | async-start | bytes 5898240 | tf_op jit(solution)/shard_map/all_gather | solution.py:1179
  44.1 377.0 %reduce-scatter.4.cloned.1.call-start = ((), (), s32[]{:S(2)}) async-start(), calls=%async_computation.3 | async-start | bytes 5898240 | tf_op jit(solution)/shard_map/reduce_scatter | solution.py:1156
  49.6 274.3 %copy-start.24 = (f32[160,1]{1,0:T(8,128)}, f32[160,1]{1,0:T(8,128)S(1)}, u32[]{:S(2)}) copy-start(f32[160,1]{1,0:T(8,128)S(1)} %convert_element_type.59.text.refs_11_) | copy-start | bytes 1924
  50.3 111.7 %copy-start.37 = (f32[1,1280]{1,0:T(1,128)}, f32[1,1280]{1,0:T(1,128)S(1)}, u32[]{:S(2)}) copy-start(f32[1,1280]{1,0:T(1,128)S(1)} %and_select_fusion.bias_ref) | copy-start | bytes 15364
  51.1 272.8 %copy-start.1 = (f32[1280,1]{1,0:T(8,128)}, f32[1280,1]{1,0:T(8,128)S(1)}, u32[]{:S(2)}) copy-start(f32[1280,1]{1,0:T(8,128)S(1)} %fusion.text.window_text.refs_4_) | copy-start | bytes 15364
  137.1 43.2 %copy-start.13 = (bf16[160,1536]{1,0:T(8,128)(2,1)}, bf16[160,1536]{1,0:T(8,128)(2,1)S(1)}, u32[]{:S(2)}) copy-start(bf16[160,1536]{1,0:T(8,128)(2,1)S(1)} %pad_maximum_fusion.1.tokens.refs_5_) | copy-start | bytes 1474564
  137.8 9.2 %copy-start.36 = (f32[2,1536]{1,0:T(2,128)}, f32[2,1536]{1,0:T(2,128)S(1)}, u32[]{:S(2)}) copy-start(f32[2,1536]{1,0:T(2,128)S(1)} %get-tuple-element.128.scale.refs_10_) | copy-start | bytes 36868
  147.0 13.1 %copy-start = (bf16[32,96,576]{2,1,0:T(8,128)(2,1)}, bf16[32,96,576]{2,1,0:T(8,128)(2,1)S(1)}, u32[]{:S(2)}) copy-start(bf16[32,96,576]{2,1,0:T(8,128)(2,1)S(1)} %pad_maximum_fusion) | copy-start | bytes 10616836
  162.0 18.2 %copy-start.43 = (bf16[1280,576]{1,0:T(8,128)(2,1)}, bf16[1280,576]{1,0:T(8,128)(2,1)S(1)}, u32[]{:S(2)}) copy-start(bf16[1280,576]{1,0:T(8,128)(2,1)S(1)} %get-tuple-element.61.projected) | copy-start | bytes 4423684
  162.0 18.2 %copy-start.29 = (bf16[2,2,96,1536]{3,2,1,0:T(8,128)(2,1)S(1)}, bf16[2,2,96,1536]{3,2,1,0:T(8,128)(2,1)}, u32[]{:S(2)}) copy-start(bf16[2,2,96,1536]{3,2,1,0:T(8,128)(2,1)} %copy-done.28) | copy-start | bytes 3538948
  262.7 11.4 %copy-start.4 = (bf16[1280,1536]{1,0:T(8,128)(2,1)S(1)}, bf16[1280,1536]{1,0:T(8,128)(2,1)}, u32[]{:S(2)}) copy-start(bf16[1280,1536]{1,0:T(8,128)(2,1)} %get-tuple-element.67.grads.rows) | copy-start | bytes 11796484
  281.5 254.3 %reduce-scatter.8.cloned.1.call-start = ((), (), s32[]{:S(2)}) async-start(), calls=%async_computation.5 | async-start | bytes 5898240 | tf_op jit(solution)/shard_map/reduce_scatter | solution.py:1156
  301.1 10.5 %copy-start.42 = (bf16[1280,1536]{1,0:T(8,128)(2,1)S(1)}, bf16[1280,1536]{1,0:T(8,128)(2,1)}, u32[]{:S(2)}) copy-start(bf16[1280,1536]{1,0:T(8,128)(2,1)} %copy-done.40) | copy-start | bytes 11796484
  320.4 224.1 %reduce-scatter.6.cloned.1.call-start = ((), (), s32[]{:S(2)}) async-start(), calls=%async_computation.4 | async-start | bytes 4423680 | tf_op jit(solution)/shard_map/reduce_scatter | solution.py:1156
  322.4 69.8 %copy-start.14 = (bf16[160,1536]{1,0:T(8,128)(2,1)}, bf16[160,1536]{1,0:T(8,128)(2,1)S(1)}, u32[]{:S(2)}) copy-start(bf16[160,1536]{1,0:T(8,128)(2,1)S(1)} %pad_maximum_fusion.2.grad.refs_7_) | copy-start | bytes 1474564
  323.9 110.2 %copy-start.3 = (f32[160,1536]{1,0:T(8,128)}, f32[160,1536]{1,0:T(8,128)S(1)}, u32[]{:S(2)}) copy-start(f32[160,1536]{1,0:T(8,128)S(1)} %get-tuple-element.117.middle.refs_6_) | copy-start | bytes 2949124
  396.2 24.9 %copy-start.2 = (f32[1280,1]{1,0:T(8,128)S(1)}, f32[1280,1]{1,0:T(8,128)}, u32[]{:S(2)}) copy-start(f32[1280,1]{1,0:T(8,128)} %copy-done.1) | copy-start | bytes 15364
  (35 other events, 98.6 us)
Sparse Core Ops, SparseCore 0:
  9.6 33.1 all-gather.8
  44.3 73.4 all-gather.10
  119.4 88.0 all-gather.12
  209.0 87.8 all-gather.14
  299.0 83.6 reduce-scatter.3
  384.9 85.7 reduce-scatter.7
  473.1 71.3 reduce-scatter.5

commit v13 on v11

--- a/solution.py
+++ b/solution.py
@@ -241,7 +241,7 @@
 
 def weight_terms(plan, rows, grads, text, name, fold=0):
     width, cols = rows.shape[1], grads.shape[1]
-    chunk = 384 if fold else 256 if width % 256 == 0 else width
+    chunk = 384 if width % 384 == 0 else width
     shape = (2 * width // fold, fold // 2, 2 * cols) if fold else (2, width, cols)
     return pl.pallas_call(
         functools.partial(terms_kernel, plan, fold, chunk),

time: 585 us -> 585 us (level)
  transfers between devices with their start and end apart: 7 -> 7, of which waited for: 3 -> 3; matrix products, arithmetic and copies ran while one was open for 6% -> 6% of each run, Pallas kernels for 75% -> 74%
where the time goes in v13:
time: 585 us; the launch traced here: 584 us
  Pallas kernels  462 us (79%)
  local copies, waits for them, and re-layouts  52.4 us (9%)
  other arithmetic  25 us (4%)
  waiting for transfers between devices  24.4 us (4%)
  between operations  15.6 us (3%)
    pallas_call x6, Pallas kernels, call(): pl.pallas_call(kernel, out_shape=out_shape, in_specs=in_specs or [VMEM] *...  370 us
    unnamed x106, local copies, waits for them, and re-layouts  41.8 us
    pallas_call x3, Pallas kernels, stream_rows(): pl.pallas_call(functools.partial(kernel, plan, size), out_shape=shapes, i...  29.8 us
    pallas_call x1, Pallas kernels, attend_back(): pl.pallas_call(functools.partial(attend_back_kernel, plan.heads, rows //...  24.9 us
    pallas_call x4, Pallas kernels, weight_terms(): pl.pallas_call(functools.partial(terms_kernel, plan, fold, chunk), out_sh...  18.2 us
    pallas_call x1, Pallas kernels, attend(): pl.pallas_call(functools.partial(attend_kernel, plan.heads, block), out_s...  18.2 us
    all_gather x1, waiting for transfers between devices, down_slices(): lax.all_gather(weight, 'dev', axis=0, axis_index_groups=plan.rank_groups())  15.5 us
  transfers between devices with their start and end apart: 7, of which 3 were waited for; matrix products, arithmetic and copies ran while one was open for 6% of the time, Pallas kernels for 74%

profile of v13, /device:TPU:0, one launch (start us, length us, event | category | flops | bytes accessed | tf_op | source)
XLA Modules:
  0.0 583.7 jit_solution(14105599928234608025)
XLA Ops:
  10.4 28.9 %swap_in.1 = (bf16[8,48,1152]{2,1,0:T(8,128)(2,1)}, bf16[8,96,768]{2,1,0:T(8,128)(2,1)}) custom-call(bf16[96,4608]{1,0:T(8,128)(2,1)S(1)} %copy-done.33, bf16[96,6144]{1,0:T(8,128)(2,1)S(1)} %copy-done.30), custom_call_target="tpu_custom_call" | custom-call | tf_op jit(solution)/shard_map/swap_in/pallas_call | solution.py:374
  39.3 3.5 all-gather.9.cloned.1.call-done
  51.2 78.3 %entry.1 = (bf16[1280,1536]{1,0:T(8,128)(2,1)S(1)}, bf16[1280,1536]{1,0:T(8,128)(2,1)S(1)}, f32[8,2,9,128]{3,2,1,0:T(8,128)S(1)}, bf16[2,2,96,1536]{3,2,1,0:T(8,128)(2,1)S(1)}) custom-call(bf16[144,1536]{1,0:T(8,128)(2,1)S(1)} %copy-done.34, bf16[144,1536]{1,0:T(8,128)(2,1)S(1)} %copy-done.35, f32[8,4,9,128]{3,2,1,0:T(8,128)S(1)} %bitcast.50, ...), custom_call_target="tpu_custom_call" | custom-call | tf_op jit(solution)/shard_map/entry/pallas_call | solution.py:374
  137.8 5.5 multiply_convert_fusion
  143.3 3.3 fusion.10
  147.0 3.1 copy-done.9
  150.1 10.0 %project.3 = (bf16[1280,1536]{1,0:T(8,128)(2,1)S(1)}, bf16[1280,576]{1,0:T(8,128)(2,1)S(1)}) custom-call(bf16[1280,1536]{1,0:T(8,128)(2,1)S(1)} %copy-done.9, bf16[2,1536,576]{2,1,0:T(8,128)(2,1)S(1)} %bitcast.40, f32[1280,1]{1,0:T(8,128)S(1)} %fusion.text.window_text.refs_4_, f32[2,1536]{1,0:T(2,128)S(1)} %get-tuple-element.125.shift, ...), custom_call_target="tpu_custom_call" | custom-call | flops 2264924160 | bytes 16777216 | tf_op jit(solution)/shard_map/project/pallas_call | solution.py:311
  162.1 18.2 %attend.1.rows = bf16[1280,192]{1,0:T(8,128)(2,1)S(1)} custom-call(bf16[1280,576]{1,0:T(8,128)(2,1)S(1)} %get-tuple-element.59.projected, f32[1,1280]{1,0:T(1,128)S(1)} %and_select_fusion.bias_ref), custom_call_target="tpu_custom_call" | custom-call | flops 5033164800 | bytes 1966080 | tf_op jit(solution)/shard_map/attend/pallas_call | solution.py:128
  180.3 78.4 %middle.1 = (f32[160,1536]{1,0:T(8,128)S(1)}, bf16[1280,1536]{1,0:T(8,128)(2,1)S(1)}) custom-call(bf16[1280,192]{1,0:T(8,128)(2,1)S(1)} %attend.1.rows, bf16[2,192,1536]{2,1,0:T(8,128)(2,1)S(1)} %bitcast.49, f32[1280,1]{1,0:T(8,128)S(1)} %fusion.text.window_text.refs_4_, bf16[160,1536]{1,0:T(8,128)(2,1)S(1)} %pad_maximum_fusion.1.tokens.refs_5_, ...), custom_call_target="tpu_custom_call" | custom-call | tf_op jit(solution)/shard_map/middle/pallas_call | solution.py:374
  262.7 9.4 %up.3 = (f32[1280,768]{1,0:T(8,128)S(1)}, bf16[1280,768]{1,0:T(8,128)(2,1)S(1)}) custom-call(bf16[1280,1536]{1,0:T(8,128)(2,1)S(1)} %copy-done.41, bf16[2,1536,768]{2,1,0:T(8,128)(2,1)} %bitcast.55, f32[1280,1]{1,0:T(8,128)S(1)} %fusion.text.window_text.refs_4_), custom_call_target="tpu_custom_call" | custom-call | flops 3019898880 | bytes 16777216 | tf_op jit(solution)/shard_map/up/pallas_call | solution.py:311
  274.1 4.9 down_terms.1
  281.4 15.5 %all-gather.15.cloned.1.call-done = bf16[1536,1536]{1,0:T(8,128)(2,1)} async-done(((bf16[384,1536]{1,0:T(8,128)(2,1)}), bf16[1536,1536]{1,0:T(8,128)(2,1)}) %all-gather.15.cloned.1.call-update) | async-done | bytes 4718608 | tf_op jit(solution)/shard_map/all_gather | solution.py:1170
  301.1 10.5 %down_back.1.grads.rows = bf16[1280,768]{1,0:T(8,128)(2,1)S(1)} custom-call(bf16[1280,1536]{1,0:T(8,128)(2,1)S(1)} %copy-done.5, bf16[2,768,1536]{2,1,0:T(8,128)(2,1)} %bitcast.53, f32[1280,1]{1,0:T(8,128)S(1)} %fusion.text.window_text.refs_4_, f32[1280,768]{1,0:T(8,128)S(1)} %copy-done.20), custom_call_target="tpu_custom_call" | custom-call | flops 3019898880 | bytes 16777216 | tf_op jit(solution)/shard_map/down_back/pallas_call | solution.py:311
  311.6 5.8 up_terms.1
  317.4 2.2 copy-done.11
  325.1 66.4 %back.1 = (f32[160,1536]{1,0:T(8,128)S(1)}, f32[160,1536]{1,0:T(8,128)S(1)}, bf16[1280,1536]{1,0:T(8,128)(2,1)S(1)}) custom-call(bf16[1280,768]{1,0:T(8,128)(2,1)S(1)} %copy-done.7, bf16[2,1536,768]{2,1,0:T(8,128)(2,1)} %bitcast.56, f32[1280,1]{1,0:T(8,128)S(1)} %fusion.text.window_text.refs_4_, bf16[160,1536]{1,0:T(8,128)(2,1)S(1)} %pad_maximum_fusion.2.grad.refs_7_, ...), custom_call_target="tpu_custom_call" | custom-call | tf_op jit(solution)/shard_map/back/pallas_call | solution.py:374
  395.5 24.9 %attend_back.1.grads.refs_2_ = bf16[1280,576]{1,0:T(8,128)(2,1)} custom-call(bf16[1280,576]{1,0:T(8,128)(2,1)} %copy-done.43, bf16[1280,1536]{1,0:T(8,128)(2,1)} %copy-done.15, bf16[2,192,1536]{2,1,0:T(8,128)(2,1)} %bitcast.48, f32[1280,1]{1,0:T(8,128)} %copy-done.1, f32[1,1280]{1,0:T(1,128)} %copy-done.37), custom_call_target="tpu_custom_call" | custom-call | flops 12582912000 | bytes 3440640 | tf_op jit(solution)/shard_map/attend_back/pallas_call | solution.py:184
  423.9 6.3 %project_terms.1 = bf16[32,48,1152]{2,1,0:T(8,128)(2,1)S(1)} custom-call(bf16[1280,1536]{1,0:T(8,128)(2,1)S(1)} %copy-done.39, bf16[1280,576]{1,0:T(8,128)(2,1)S(1)} %copy-done.23, f32[1280,1]{1,0:T(8,128)S(1)} %copy-done.2), custom_call_target="tpu_custom_call" | custom-call | flops 3397386240 | bytes 8388608 | tf_op jit(solution)/shard_map/project_terms/pallas_call | solution.py:246
  433.4 2.3 multiply_reduce_fusion.1
  438.7 91.0 %last.1 = (bf16[144,1536]{1,0:T(8,128)(2,1)}, bf16[144,1536]{1,0:T(8,128)(2,1)}, f32[144,1536]{1,0:T(8,128)}, f32[144,1536]{1,0:T(8,128)}, f32[8,4,1,1152]{3,2,1...) custom-call(bf16[1280,768]{1,0:T(8,128)(2,1)} %copy-done.22, bf16[2,768,1536]{2,1,0:T(8,128)(2,1)} %bitcast.54, ...), custom_call_target="tpu_custom_call" | custom-call | tf_op jit(solution)/shard_map/last/pallas_call | solution.py:374
  531.0 2.5 fusion.13
  538.5 2.5 broadcast_select_fusion.1
  541.0 3.4 reduce-scatter.6.cloned.1.call-done
  545.6 27.4 %finish.1 = (bf16[96,6144]{1,0:T(8,128)(2,1)S(1)}, bf16[96,4608]{1,0:T(8,128)(2,1)S(1)}, f32[96,1536]{1,0:T(8,128)S(1)}) custom-call(bf16[8,96,768]{2,1,0:T(8,128)(2,1)S(1)} %bitcast.46, bf16[8,48,1152]{2,1,0:T(8,128)(2,1)S(1)} %bitcast.51, bf16[4,96,1536]{2,1,0:T(8,128)(2,1)S(1)} %copy-done.26), custom_call_target="tpu_custom_call" | custom-call | tf_op jit(solution)/shard_map/finish/pallas_call | solution.py:374
  (187 shorter events, 64.0 us)
Async XLA Ops:
  7.2 37.0 %copy-start.51 = (s32[4]{0:T(128)S(1)}, s32[4]{0:T(128)}, u32[]{:S(2)}) copy-start(s32[4]{0:T(128)} %param.11) | copy-start | bytes 52
  7.2 38.5 %copy-start.47 = (bf16[4,1536]{1,0:T(4,128)(2,1)S(1)}, bf16[4,1536]{1,0:T(4,128)(2,1)}, u32[]{:S(2)}) copy-start(bf16[4,1536]{1,0:T(4,128)(2,1)} %param.10) | copy-start | bytes 36868
  7.2 35.6 %all-gather.9.cloned.1.call-start = ((), (), s32[]{:S(2)}) async-start(), calls=%async_computation.6 | async-start | bytes 1474560 | tf_op jit(solution)/shard_map/all_gather | solution.py:1152
  7.9 135.4 %all-gather.11.cloned.1.call-start = ((), (), s32[]{:S(2)}) async-start(), calls=%async_computation.7 | async-start | bytes 4423680 | tf_op jit(solution)/shard_map/all_gather | solution.py:1142
  42.8 217.8 %all-gather.13.cloned.1.call-start = ((), (), s32[]{:S(2)}) async-start(), calls=%async_computation.8 | async-start | bytes 5898240 | tf_op jit(solution)/shard_map/all_gather | solution.py:1142
  43.5 253.3 %all-gather.15.cloned.1.call-start = ((), (), s32[]{:S(2)}) async-start(), calls=%async_computation.9 | async-start | bytes 5898240 | tf_op jit(solution)/shard_map/all_gather | solution.py:1170
  44.1 376.3 %reduce-scatter.4.cloned.1.call-start = ((), (), s32[]{:S(2)}) async-start(), calls=%async_computation.3 | async-start | bytes 5898240 | tf_op jit(solution)/shard_map/reduce_scatter | solution.py:1147
  49.6 273.5 %copy-start.24 = (f32[160,1]{1,0:T(8,128)}, f32[160,1]{1,0:T(8,128)S(1)}, u32[]{:S(2)}) copy-start(f32[160,1]{1,0:T(8,128)S(1)} %convert_element_type.65.text.refs_11_) | copy-start | bytes 1924
  50.3 111.7 %copy-start.37 = (f32[1,1280]{1,0:T(1,128)}, f32[1,1280]{1,0:T(1,128)S(1)}, u32[]{:S(2)}) copy-start(f32[1,1280]{1,0:T(1,128)S(1)} %and_select_fusion.bias_ref) | copy-start | bytes 15364
  51.1 272.0 %copy-start.1 = (f32[1280,1]{1,0:T(8,128)}, f32[1280,1]{1,0:T(8,128)S(1)}, u32[]{:S(2)}) copy-start(f32[1280,1]{1,0:T(8,128)S(1)} %fusion.text.window_text.refs_4_) | copy-start | bytes 15364
  137.1 43.2 %copy-start.13 = (bf16[160,1536]{1,0:T(8,128)(2,1)}, bf16[160,1536]{1,0:T(8,128)(2,1)S(1)}, u32[]{:S(2)}) copy-start(bf16[160,1536]{1,0:T(8,128)(2,1)S(1)} %pad_maximum_fusion.1.tokens.refs_5_) | copy-start | bytes 1474564
  137.8 9.2 %copy-start.36 = (f32[2,1536]{1,0:T(2,128)}, f32[2,1536]{1,0:T(2,128)S(1)}, u32[]{:S(2)}) copy-start(f32[2,1536]{1,0:T(2,128)S(1)} %get-tuple-element.124.scale.refs_10_) | copy-start | bytes 36868
  146.9 13.1 %copy-start = (bf16[32,96,576]{2,1,0:T(8,128)(2,1)}, bf16[32,96,576]{2,1,0:T(8,128)(2,1)S(1)}, u32[]{:S(2)}) copy-start(bf16[32,96,576]{2,1,0:T(8,128)(2,1)S(1)} %pad_maximum_fusion) | copy-start | bytes 10616836
  162.0 18.2 %copy-start.43 = (bf16[1280,576]{1,0:T(8,128)(2,1)}, bf16[1280,576]{1,0:T(8,128)(2,1)S(1)}, u32[]{:S(2)}) copy-start(bf16[1280,576]{1,0:T(8,128)(2,1)S(1)} %get-tuple-element.59.projected) | copy-start | bytes 4423684
  162.1 18.2 %copy-start.29 = (bf16[2,2,96,1536]{3,2,1,0:T(8,128)(2,1)S(1)}, bf16[2,2,96,1536]{3,2,1,0:T(8,128)(2,1)}, u32[]{:S(2)}) copy-start(bf16[2,2,96,1536]{3,2,1,0:T(8,128)(2,1)} %copy-done.28) | copy-start | bytes 3538948
  262.7 11.4 %copy-start.4 = (bf16[1280,1536]{1,0:T(8,128)(2,1)S(1)}, bf16[1280,1536]{1,0:T(8,128)(2,1)}, u32[]{:S(2)}) copy-start(bf16[1280,1536]{1,0:T(8,128)(2,1)} %get-tuple-element.65.grads.rows) | copy-start | bytes 11796484
  281.2 252.2 %reduce-scatter.8.cloned.1.call-start = ((), (), s32[]{:S(2)}) async-start(), calls=%async_computation.5 | async-start | bytes 5898240 | tf_op jit(solution)/shard_map/reduce_scatter | solution.py:1147
  301.1 10.5 %copy-start.42 = (bf16[1280,1536]{1,0:T(8,128)(2,1)S(1)}, bf16[1280,1536]{1,0:T(8,128)(2,1)}, u32[]{:S(2)}) copy-start(bf16[1280,1536]{1,0:T(8,128)(2,1)} %copy-done.40) | copy-start | bytes 11796484
  319.6 224.8 %reduce-scatter.6.cloned.1.call-start = ((), (), s32[]{:S(2)}) async-start(), calls=%async_computation.4 | async-start | bytes 4423680 | tf_op jit(solution)/shard_map/reduce_scatter | solution.py:1147
  321.6 69.9 %copy-start.14 = (bf16[160,1536]{1,0:T(8,128)(2,1)}, bf16[160,1536]{1,0:T(8,128)(2,1)S(1)}, u32[]{:S(2)}) copy-start(bf16[160,1536]{1,0:T(8,128)(2,1)S(1)} %pad_maximum_fusion.2.grad.refs_7_) | copy-start | bytes 1474564
  323.1 110.2 %copy-start.3 = (f32[160,1536]{1,0:T(8,128)}, f32[160,1536]{1,0:T(8,128)S(1)}, u32[]{:S(2)}) copy-start(f32[160,1536]{1,0:T(8,128)S(1)} %get-tuple-element.113.middle.refs_6_) | copy-start | bytes 2949124
  395.4 24.9 %copy-start.2 = (f32[1280,1]{1,0:T(8,128)S(1)}, f32[1280,1]{1,0:T(8,128)}, u32[]{:S(2)}) copy-start(f32[1280,1]{1,0:T(8,128)} %copy-done.1) | copy-start | bytes 15364
  534.1 10.3 %copy-start.25 = (bf16[1,8,96,768]{3,2,1,0:T(8,128)(2,1)S(1)}, bf16[1,8,96,768]{3,2,1,0:T(8,128)(2,1)}, u32[]{:S(2)}) copy-start(bf16[1,8,96,768]{3,2,1,0:T(8,128)(2,1)} %reduce-scatter.8.cloned.1.call-done) | copy-start | bytes 3538948
  534.1 10.3 %copy-start.26 = (bf16[4,96,1536]{2,1,0:T(8,128)(2,1)S(1)}, bf16[4,96,1536]{2,1,0:T(8,128)(2,1)}, u32[]{:S(2)}) copy-start(bf16[4,96,1536]{2,1,0:T(8,128)(2,1)} %get-tuple-element.93.refs_0_) | copy-start | bytes 3538948
  (35 other events, 98.6 us)
Sparse Core Ops, SparseCore 0:
  9.6 33.1 all-gather.8
  44.3 73.4 all-gather.10
  119.4 88.0 all-gather.12
  209.0 87.8 all-gather.14
  299.0 83.6 reduce-scatter.3
  384.9 85.7 reduce-scatter.7
  473.1 71.3 reduce-scatter.5
